TPU v7x, 512 devices: a whole 4x8x8 slice. The times are simulated.
512 devices in a mesh: slab: 16 (over z, core), blk: 32 (over x, y).
Axes of the slice: x: 4, y: 8, z: 8, core: 2. Of those that a mesh axis runs over, the one named last changes fastest.
Arguments:
- voltage: float32 [64, 256, 512], P('slab', 'blk'), may hold values from -1 to 1.2
- voltage_lag: float32 [64, 256, 512], P('slab', 'blk'), may hold values from -1 to 1.2
- tissue: int32 [64, 256, 512], P('slab', 'blk'), may hold values from 0 to 1, as said below
- fiber: int32 [64, 256, 512], P('slab', 'blk'), may hold values from 0 to 15
- conductivity: float32 [6, 16], replicated, may hold values from -0.036 to 0.12, as said below
- worker: int32 [64, 256], P('slab', 'blk'), may hold values from -1 to 511, as said below
- gates: float32 [12, 8192, 512], P(None, ('slab', 'blk')), may hold values from 0.02 to 0.98
- gate_half: float32 [12], replicated, may hold values from -0.6 to 0.6
- gate_steep: float32 [12], replicated, may hold values from -8 to 8
- gate_tmin: float32 [12], replicated, may hold values from 0.1 to 0.5
- gate_tspan: float32 [12], replicated, may hold values from 0.2 to 3
- channel: float32 [6], replicated, may hold values from 0.5 to 3
Outputs:
- voltage_out: float32 [64, 256, 512], P('slab', 'blk')
- gates_out: float32 [12, 8192, 512], P(None, ('slab', 'blk'))
- charge: float32 [3, 64, 256, 512], P(None, 'slab', 'blk')
Inputs may be any that keep to these rules, and one draw needn't show every extreme that they name: `worker`: -1 marks a tile with no tissue. Otherwise the entry is w * 16 + k: the tile's gating variables are row k of the 16 rows of gates held by the device with blk index w in the same slab group. Every such row is named by exactly one tile of its slab group. The tiles of one device name one blk index at most 1 times, and some device does so exactly 1 times. `tissue`: 1 only in tiles whose worker entry is not -1; every such tile holds some tissue. `conductivity`: the first three rows are positive; each class's tensor is positive definite.
All inputs are finite; a program needn't handle non-finite values.
Results may differ from a plain program's by a relative error of at most 0.000088.
Values sent between devices are 32-bit elements; how exact they have to be, the bound alone decides.
No kernel may reach another device: no remote copies, remote signals or barrier semaphores. Data moves between devices by JAX's collectives and lax.ppermute only.
A program may use at most 64 MiB of HBM per device.

v0:
```python
import jax
import jax.numpy as jnp
from jax import lax
from jax.sharding import PartitionSpec as P

FIB = 16
STEPS = 3


STEP_DT = 0.1
PHASE_REF = -0.2
PHASE_SOFT = 0.5
COMPONENT = ((1, 4, 5), (4, 2, 6), (5, 6, 3))


def extended(x, sides, width):
    edges = {}
    for axis, dim in sides:
        size, length = (lax.axis_size(axis), x.shape[dim])
        up = [(i, (i + 1) % size) for i in range(size - 1)]
        last = lax.slice_in_dim(x, length - width, length, axis=dim)
        first = lax.slice_in_dim(x, 0, width, axis=dim)
        edges[dim] = (
            lax.ppermute(last, axis, up),
            lax.ppermute(first, axis, [(b, a) for a, b in up]),
        )
    done = []
    for _, dim in sides:
        low, high = edges[dim]
        around = [(width, width) if d in done else (0, 0) for d in range(x.ndim)]
        x = jnp.concatenate([jnp.pad(low, around), x, jnp.pad(high, around)], axis=dim)
        done.append(dim)
    return x


def padded(x, sides, width):
    for axis, dim in sides:
        size, length = (lax.axis_size(axis), x.shape[dim])
        up = [(i, (i + 1) % size) for i in range(size - 1)]
        down = [(j, i) for i, j in up]
        last = lax.slice_in_dim(x, length - width, length, axis=dim)
        first = lax.slice_in_dim(x, 0, width, axis=dim)
        before = lax.ppermute(last, axis, up)
        after = lax.ppermute(first, axis, down)
        x = jnp.concatenate([before, x, after], axis=dim)
    return x


def basis(direction, amount):
    return tuple((amount if position == direction else 0 for position in range(3)))


def combine(first, second):
    return tuple((left_part + right_part for left_part, right_part in zip(first, second)))


def window(array, starts, extent):
    leading = array.ndim - 3
    begin = (0,) * leading + tuple(starts)
    finish = tuple(array.shape[:leading]) + tuple(
        (first + count for first, count in zip(starts, extent))
    )
    return lax.slice(array, begin, finish)


def shifted(array, direction, offset, extent):
    starts = tuple(
        ((0 if position == direction else 1) + offset[position] for position in range(3))
    )
    sizes = tuple(
        (
            extent[position] + 1 if position == direction else extent[position]
            for position in range(3)
        )
    )
    return window(array, starts, sizes)


def coefficient_stack(weights, fiber, conductivity):
    classes = (fiber[None] == jnp.arange(FIB, dtype=jnp.int32)[:, None, None, None]).astype(
        jnp.float32
    )
    sigma = jnp.tensordot(conductivity, classes, axes=(1, 0), precision=lax.Precision.HIGHEST)
    return jnp.concatenate([weights[None], weights[None] * sigma], axis=0)


def face_terms(padded_stack, extent):
    result = []
    for direction in range(3):
        lower = shifted(padded_stack, direction, (0, 0, 0), extent)
        upper = shifted(padded_stack, direction, basis(direction, 1), extent)
        face_mask = lower[0] * upper[0]
        result.append(
            [
                0.5
                * (lower[COMPONENT[direction][other]] + upper[COMPONENT[direction][other]])
                * face_mask
                for other in range(3)
            ]
        )
    return result


def diffuse(padded_field, faces, extent):
    total = jnp.zeros(extent, jnp.float32)
    for direction in range(3):
        along = basis(direction, 1)
        flux = faces[direction][direction] * (
            shifted(padded_field, direction, along, extent)
            - shifted(padded_field, direction, (0, 0, 0), extent)
        )
        for other in range(3):
            if other != direction:
                upward = basis(other, 1)
                downward = basis(other, -1)
                slope = (
                    shifted(padded_field, direction, upward, extent)
                    + shifted(padded_field, direction, combine(along, upward), extent)
                    - shifted(padded_field, direction, downward, extent)
                    - shifted(padded_field, direction, combine(along, downward), extent)
                ) * 0.25
                flux = flux + faces[direction][other] * slope
        total = total + jnp.diff(flux, axis=direction)
    return total


def react(potential, states, params):
    gate_half, gate_steep, gate_tmin, gate_tspan, channel = params
    level = potential[None]
    centre = gate_half[:, None, None]
    target = jax.nn.sigmoid(gate_steep[:, None, None] * (level - centre))
    relax = gate_tmin[:, None, None] + gate_tspan[:, None, None] / (
        1.0 + 4.0 * (level - centre) * (level - centre)
    )
    fresh = target + (states - target) * jnp.exp(-STEP_DT / relax)
    sodium = (
        channel[0] * states[0] * states[0] * states[0] * states[1] * states[2] * (potential - 1.2)
    )
    calcium = channel[1] * states[3] * states[4] * states[5] * states[6] * (potential - 1.0)
    transient = channel[2] * states[7] * states[8] * (potential + 0.9)
    rapid_delayed = channel[3] * states[9] * states[10] * (potential + 0.9)
    slow_delayed = channel[4] * states[11] * states[11] * (potential + 0.8)
    inward_rect = channel[5] * (potential + 0.9) / (1.0 + jnp.exp(4.0 * (potential + 0.6)))
    return (fresh, sodium + calcium + transient + rapid_delayed + slow_delayed + inward_rect)


def edge_term(first, second):
    cross = first[0] * second[1] - first[1] * second[0]
    inner = first[0] * second[0] + first[1] * second[1]
    norm_value = jnp.sqrt(
        (first[0] * first[0] + first[1] * first[1])
        * (second[0] * second[0] + second[1] * second[1])
    )
    return 2.0 * jnp.arctan(cross / (norm_value + inner + PHASE_SOFT))


def charges(padded_phase, extent):
    results = []
    for first_dim, second_dim in ((0, 1), (1, 2), (0, 2)):
        corners = [
            basis(first_dim, 1),
            basis(second_dim, 1),
            basis(first_dim, -1),
            basis(second_dim, -1),
        ]
        points = [
            window(padded_phase, tuple((1 + value for value in corner)), extent)
            for corner in corners
        ]
        circulation = jnp.zeros(extent, jnp.float32)
        for position in range(4):
            circulation = circulation + edge_term(points[position], points[(position + 1) % 4])
        results.append(circulation)
    return jnp.stack(results)


def pad_depth(array):
    return jnp.pad(array, [(0, 0)] * (array.ndim - 1) + [(1, 1)])


def pair_layout(targets, live, capacity, blocks, pair_slots):
    holder = jnp.where(live, targets // capacity, -1)
    row_slot = jnp.where(live, targets % capacity, capacity)
    ranks = jnp.arange(targets.shape[0], dtype=jnp.int32)
    earlier = (
        (holder[:, None] == holder[None, :]) & live[None, :] & (ranks[None, :] < ranks[:, None])
    )
    order = jnp.sum(earlier.astype(jnp.int32), axis=1)
    position = jnp.where(live, holder * pair_slots + order, blocks * pair_slots)
    claims = (
        jnp.full((blocks * pair_slots + 1,), capacity, jnp.int32).at[position].set(row_slot)[:-1]
    )
    return (position, claims.reshape(blocks, pair_slots))


def on_device(
    voltage,
    voltage_lag,
    tissue,
    fiber,
    conductivity,
    worker,
    gates,
    gate_half,
    gate_steep,
    gate_tmin,
    gate_tspan,
    channel,
):
    extent = voltage.shape
    depth = extent[2]
    gate_count = gates.shape[0]
    params = (gate_half, gate_steep, gate_tmin, gate_tspan, channel)
    blocks = lax.axis_size("blk")
    weights = tissue.astype(jnp.float32)
    packed = fiber * 2 + tissue
    packed_rim = extended(packed, (("slab", 0), ("blk", 1)), 1)
    rim_weights = (packed_rim % 2).astype(jnp.float32)
    stack_rim = coefficient_stack(rim_weights, packed_rim // 2, conductivity)
    faces = face_terms(pad_depth(stack_rim), extent)
    targets = worker.reshape(-1)
    live = targets >= 0
    tile_count = targets.shape[0]
    capacity = gates.shape[1]
    pair_slots = tile_count // blocks
    position, claims = pair_layout(targets, live, capacity, blocks, pair_slots)
    arrived = lax.all_to_all(claims, "blk", split_axis=0, concat_axis=0, tiled=True)
    padded_states = jnp.concatenate([gates, jnp.zeros((gate_count, 1, depth), jnp.float32)], axis=1)
    leaving = padded_states[:, arrived.reshape(-1)].reshape(gate_count, blocks, pair_slots, depth)
    coming = lax.all_to_all(leaving, "blk", split_axis=1, concat_axis=1, tiled=True)
    states = coming.reshape(gate_count, blocks * pair_slots, depth)[
        :, jnp.minimum(position, blocks * pair_slots - 1)
    ]
    potential = voltage
    for timestep in range(STEPS):
        tile_volts = potential.reshape(tile_count, depth)
        states, tile_current = react(tile_volts, states, params)
        current = jnp.where(live[:, None], tile_current, 0.0)
        field_rim = padded(weights * potential, (("slab", 0), ("blk", 1)), 1)
        spread = diffuse(pad_depth(field_rim), faces, extent)
        potential = potential + weights * (spread - STEP_DT * current.reshape(extent))
    home_rows = (
        jnp.zeros((gate_count, blocks * pair_slots + 1, depth), jnp.float32)
        .at[:, position]
        .set(states)[:, :-1]
    )
    returned_states = lax.all_to_all(
        home_rows.reshape(gate_count, blocks, pair_slots, depth),
        "blk",
        split_axis=1,
        concat_axis=1,
        tiled=True,
    )
    gates_out = (
        jnp.zeros((gate_count, capacity + 1, depth), jnp.float32)
        .at[:, arrived.reshape(-1)]
        .set(returned_states.reshape(gate_count, -1, depth))[:, :capacity]
    )
    phase = jnp.stack([weights * (potential - PHASE_REF), weights * (voltage_lag - PHASE_REF)])
    phase_rim = extended(phase, (("slab", 1), ("blk", 2)), 1)
    return (potential, gates_out, charges(pad_depth(phase_rim), extent))


def solution(mesh):
    in_specs = (
        P("slab", "blk", None),
        P("slab", "blk", None),
        P("slab", "blk", None),
        P("slab", "blk", None),
        P(),
        P("slab", "blk"),
        P(None, ("slab", "blk"), None),
        P(),
        P(),
        P(),
        P(),
        P(),
    )
    out_specs = (
        P("slab", "blk", None),
        P(None, ("slab", "blk"), None),
        P(None, "slab", "blk", None),
    )
    return jax.shard_map(
        on_device, mesh=mesh, in_specs=in_specs, out_specs=out_specs, check_vma=False
    )
```

profile of v0, /device:TPU:199, one launch (start us, length us, event | category | flops | bytes accessed | tf_op | source)
XLA Modules:
  0.0 152.6 jit_solution(14557017206843129013)
XLA Ops:
  0.6 0.9 multiply_bitcast_fusion
  1.6 2.6 %collective-permute-start.4 = (f32[1,8,512]{2,1,0:T(8,128)S(1)}, f32[1,8,512]{2,1,0:T(8,128)S(1)}, u32[]{:S(2)}, u32[]{:S(2)}) collective-permute-start(f32[1,8,512]{2,1,0:T(8,128)S(1)} %get-tuple-element.98), channel_id=1, source_target_pairs={{32,0},{64,32},{96,64},{128,96},{160,128},{192,160},{224,192},{256... | collective-permute-start | bytes 49160 | tf_op jit(solution)/shard_map/ppermute | solution.py:44
  4.2 5.1 %collective-permute-start.5 = (f32[1,8,512]{2,1,0:T(8,128)S(1)}, f32[1,8,512]{2,1,0:T(8,128)S(1)}, u32[]{:S(2)}, u32[]{:S(2)}) collective-permute-start(f32[1,8,512]{2,1,0:T(8,128)S(1)} %get-tuple-element.97), channel_id=1, source_target_pairs={{0,32},{32,64},{64,96},{96,128},{128,160},{160,192},{192,224},{224... | collective-permute-start | bytes 49160 | tf_op jit(solution)/shard_map/ppermute | solution.py:43
  9.3 0.9 multiply_add_fusion
  10.2 3.2 %collective-permute-start = (s32[4,1,512]{2,1,0:T(1,128)S(1)}, s32[4,1,512]{2,1,0:T(1,128)S(1)}, u32[]{:S(2)}, u32[]{:S(2)}) collective-permute-start(s32[4,1,512]{2,1,0:T(1,128)S(1)} %get-tuple-element.93), channel_id=1, source_target_pairs={{0,1},{1,2},{2,3},{3,4},{4,5},{5,6},{6,7},{7,8},{8,9},{9,10},{10,1... | collective-permute-start | bytes 24584 | tf_op jit(solution)/shard_map/ppermute | solution.py:24
  13.4 4.2 %collective-permute-start.3 = (s32[4,1,512]{2,1,0:T(1,128)S(1)}, s32[4,1,512]{2,1,0:T(1,128)S(1)}, u32[]{:S(2)}, u32[]{:S(2)}) collective-permute-start(s32[4,1,512]{2,1,0:T(1,128)S(1)} %get-tuple-element.94), channel_id=1, source_target_pairs={{1,0},{2,1},{3,2},{4,3},{5,4},{6,5},{7,6},{8,7},{9,8},{10,9},{11,1... | collective-permute-start | bytes 24584 | tf_op jit(solution)/shard_map/ppermute | solution.py:25
  17.6 3.0 %collective-permute-start.1 = (s32[1,8,512]{2,1,0:T(8,128)S(1)}, s32[1,8,512]{2,1,0:T(8,128)S(1)}, u32[]{:S(2)}, u32[]{:S(2)}) collective-permute-start(s32[1,8,512]{2,1,0:T(8,128)S(1)} %get-tuple-element.95), channel_id=1, source_target_pairs={{0,32},{32,64},{64,96},{96,128},{128,160},{160,192},{192,224},{224... | collective-permute-start | bytes 49160 | tf_op jit(solution)/shard_map/ppermute | solution.py:24
  20.6 0.8 reshape.630
  21.4 0.8 reshape.629
  23.8 8.8 %all-to-all-start = ((s32[32,1,1]{2,1,0:T(1,128)}), s32[32,1,1]{2,1,0:T(1,128)S(1)}, u32[]{:S(2)}, u32[]{:S(2)}) async-start(s32[32,1,1]{2,1,0:T(1,128)} %copy.149), calls=%async_computation | async-start | bytes 32768 | tf_op jit(solution)/shard_map/all_to_all | solution.py:227
  33.2 1.6 %fusion.251 = (f32[1]{0:T(128)}, f32[1]{0:T(128)}, f32[1]{0:T(128)}, f32[1]{0:T(128)}, f32[1]{0:T(128)}, /*index=5*/f32[1]{0:T(128)}) fusion(f32[6]{0:T(128)} %param.23), kind=kLoop, calls=%fused_computation.498 | loop fusion | bytes 48 | tf_op jit(solution)/shard_map/slice | solution.py:137
  34.8 1.2 copy.148
  36.1 3.5 %all-to-all-done = s32[32,1,1]{2,1,0:T(1,128)S(1)} async-done(((s32[32,1,1]{2,1,0:T(1,128)}), s32[32,1,1]{2,1,0:T(1,128)S(1)}, u32[]{:S(2)}, u32[]{:S(2)}) %all-to-all-start) | async-done | bytes 160 | tf_op jit(solution)/shard_map/all_to_all | solution.py:227
  40.8 1.7 %copy.150 = f32[12,32,1,512]{3,2,0,1:T(1,128)} copy(f32[12,32,1,512]{3,0,1,2:T(8,128)S(1)} %bitcast.169) | data formatting | bytes 1572864 | tf_op jit(solution)/shard_map/reshape | solution.py:229
  42.5 5.8 %all-to-all-start.1 = ((f32[12,32,1,512]{3,2,0,1:T(1,128)}), f32[12,32,1,512]{3,2,0,1:T(1,128)S(1)}, u32[]{:S(2)}, u32[]{:S(2)}) async-start(f32[12,32,1,512]{3,2,0,1:T(1,128)} %copy.150), calls=%async_computation.1 | async-start | bytes 1572864 | tf_op jit(solution)/shard_map/all_to_all | solution.py:230
  48.3 2.8 %collective-permute-start.2 = (s32[1,8,512]{2,1,0:T(8,128)S(1)}, s32[1,8,512]{2,1,0:T(8,128)S(1)}, u32[]{:S(2)}, u32[]{:S(2)}) collective-permute-start(s32[1,8,512]{2,1,0:T(8,128)S(1)} %get-tuple-element.96), channel_id=1, source_target_pairs={{32,0},{64,32},{96,64},{128,96},{160,128},{192,160},{224,192},{256... | collective-permute-start | bytes 49160 | tf_op jit(solution)/shard_map/ppermute | solution.py:25
  51.3 4.6 %collective-permute-start.6 = (f32[6,1,512]{2,1,0:T(1,128)S(1)}, f32[6,1,512]{2,1,0:T(1,128)S(1)}, u32[]{:S(2)}, u32[]{:S(2)}) collective-permute-start(f32[6,1,512]{2,1,0:T(1,128)S(1)} %get-tuple-element.86), channel_id=1, source_target_pairs={{1,0},{2,1},{3,2},{4,3},{5,4},{6,5},{7,6},{8,7},{9,8},{10,9},{11,1... | collective-permute-start | bytes 36872 | tf_op jit(solution)/shard_map/ppermute | solution.py:44
  55.8 1.9 %collective-permute-start.7 = (f32[6,1,512]{2,1,0:T(1,128)S(1)}, f32[6,1,512]{2,1,0:T(1,128)S(1)}, u32[]{:S(2)}, u32[]{:S(2)}) collective-permute-start(f32[6,1,512]{2,1,0:T(1,128)S(1)} %get-tuple-element.85), channel_id=1, source_target_pairs={{0,1},{1,2},{2,3},{3,4},{4,5},{5,6},{6,7},{7,8},{8,9},{9,10},{10,1... | collective-permute-start | bytes 36872 | tf_op jit(solution)/shard_map/ppermute | solution.py:43
  59.8 6.2 %collective-permute-done.6 = f32[6,1,512]{2,1,0:T(1,128)S(1)} collective-permute-done((f32[6,1,512]{2,1,0:T(1,128)S(1)}, f32[6,1,512]{2,1,0:T(1,128)S(1)}, u32[]{:S(2)}, u32[]{:S(2)}) %collective-permute-start.6) | collective-permute-done | bytes 12320 | tf_op jit(solution)/shard_map/ppermute | solution.py:44
  67.7 2.4 %fusion.245 = (f32[1,32,512]{2,0,1:T(1,128)S(1)}, f32[1,32,512]{2,0,1:T(1,128)S(1)}, f32[1,32,512]{2,0,1:T(1,128)S(1)}, f32[1,32,512]{2,0,1:T(1,128)S(1)}, f32[1...) fusion(f32[12,32,512]{2,0,1:T(8,128)S(1)} %bitcast.167, f32[]{:T(128)} %bitcast.27, ...), kind=kLoop, calls=%fused_computation.492 | loop fusion | flops 131072 | bytes 1245196 | tf_op jit(solution)/shard_map/slice | solution.py:137
  70.2 2.0 %convert_multiply_fusion.1 = (f32[4,8,512]{2,1,0:T(8,128)S(1)}, f32[4,8,512]{2,1,0:T(8,128)S(1)}) fusion(s32[4,8,512]{2,1,0:T(8,128)S(1)} %copy-done.1, f32[4,8,512]{2,1,0:T(8,128)S(1)} %copy-done.2, f32[]{:T(128)} %bitcast.30, f32[1,32,512]{2,0,1:T(1,128)S(1)} %get-tuple-element.63, f32[]{:T(128)} %bitcast.29, f32[1,32,512]{2,0,1:T(1,128)S(1)} %get-tuple-element.65, ...), kind=kLoop, calls=%fused_computation.442 | loop fusion | flops 622592 | bytes 1114156 | tf_op jit(solution)/shard_map/mul | solution.py:239
  72.2 5.8 %collective-permute-start.8 = (f32[1,8,512]{2,1,0:T(8,128)S(1)}, f32[1,8,512]{2,1,0:T(8,128)S(1)}, u32[]{:S(2)}, u32[]{:S(2)}) collective-permute-start(f32[1,8,512]{2,1,0:T(8,128)S(1)} %get-tuple-element.92), channel_id=1, source_target_pairs={{32,0},{64,32},{96,64},{128,96},{160,128},{192,160},{224,192},{256... | collective-permute-start | bytes 49160 | tf_op jit(solution)/shard_map/ppermute | solution.py:44
  78.0 3.0 %collective-permute-start.9 = (f32[1,8,512]{2,1,0:T(8,128)S(1)}, f32[1,8,512]{2,1,0:T(8,128)S(1)}, u32[]{:S(2)}, u32[]{:S(2)}) collective-permute-start(f32[1,8,512]{2,1,0:T(8,128)S(1)} %get-tuple-element.91), channel_id=1, source_target_pairs={{0,32},{32,64},{64,96},{96,128},{128,160},{160,192},{192,224},{224... | collective-permute-start | bytes 49160 | tf_op jit(solution)/shard_map/ppermute | solution.py:43
  81.1 0.8 fusion.13
  81.9 3.3 %collective-permute-start.10 = (f32[6,1,512]{2,1,0:T(1,128)S(1)}, f32[6,1,512]{2,1,0:T(1,128)S(1)}, u32[]{:S(2)}, u32[]{:S(2)}) collective-permute-start(f32[6,1,512]{2,1,0:T(1,128)S(1)} %get-tuple-element.82), channel_id=1, source_target_pairs={{1,0},{2,1},{3,2},{4,3},{5,4},{6,5},{7,6},{8,7},{9,8},{10,9},{11,1... | collective-permute-start | bytes 36872 | tf_op jit(solution)/shard_map/ppermute | solution.py:44
  85.2 2.1 %collective-permute-start.11 = (f32[6,1,512]{2,1,0:T(1,128)S(1)}, f32[6,1,512]{2,1,0:T(1,128)S(1)}, u32[]{:S(2)}, u32[]{:S(2)}) collective-permute-start(f32[6,1,512]{2,1,0:T(1,128)S(1)} %get-tuple-element.81), channel_id=1, source_target_pairs={{0,1},{1,2},{2,3},{3,4},{4,5},{5,6},{6,7},{7,8},{8,9},{9,10},{10,1... | collective-permute-start | bytes 36872 | tf_op jit(solution)/shard_map/ppermute | solution.py:43
  87.2 2.4 %fusion.244 = (f32[1,32,512]{2,0,1:T(1,128)S(1)}, f32[1,32,512]{2,0,1:T(1,128)S(1)}, f32[1,32,512]{2,0,1:T(1,128)S(1)}, f32[1,32,512]{2,0,1:T(1,128)S(1)}, f32[1...) fusion(f32[12,32,512]{2,0,1:T(8,128)S(1)} %fusion.13, f32[]{:T(128)} %bitcast.26, ...), kind=kLoop, calls=%fused_computation.491 | loop fusion | flops 131072 | bytes 1245196 | tf_op jit(solution)/shard_map/slice | solution.py:137
  89.7 2.0 %collective-permute-done.11 = f32[6,1,512]{2,1,0:T(1,128)S(1)} collective-permute-done((f32[6,1,512]{2,1,0:T(1,128)S(1)}, f32[6,1,512]{2,1,0:T(1,128)S(1)}, u32[]{:S(2)}, u32[]{:S(2)}) %collective-permute-start.11) | collective-permute-done | bytes 12320 | tf_op jit(solution)/shard_map/ppermute | solution.py:43
  92.4 2.0 %convert_multiply_fusion = (f32[4,8,512]{2,1,0:T(8,128)S(1)}, f32[4,8,512]{2,1,0:T(8,128)S(1)}) fusion(s32[4,8,512]{2,1,0:T(8,128)S(1)} %copy-done.1, f32[4,8,512]{2,1,0:T(8,128)S(1)} %get-tuple-element.33, f32[]{:T(128)} %bitcast.30, f32[1,32,512]{2,0,1:T(1,128)S(1)} %get-tuple-element.56, f32[]{:T(128)} %bitcast.29, ...), kind=kLoop, calls=%fused_computation.441 | loop fusion | flops 622592 | bytes 1114156 | tf_op jit(solution)/shard_map/mul | solution.py:239
  95.0 4.5 %collective-permute-start.12 = (f32[1,8,512]{2,1,0:T(8,128)}, f32[1,8,512]{2,1,0:T(8,128)S(1)}, u32[]{:S(2)}, u32[]{:S(2)}) collective-permute-start(f32[1,8,512]{2,1,0:T(8,128)} %get-tuple-element.90), channel_id=1, source_target_pairs={{32,0},{64,32},{96,64},{128,96},{160,128},{192,160},{224,192},{256... | collective-permute-start | bytes 49160 | tf_op jit(solution)/shard_map/ppermute | solution.py:44
  99.6 4.4 %collective-permute-start.13 = (f32[1,8,512]{2,1,0:T(8,128)}, f32[1,8,512]{2,1,0:T(8,128)S(1)}, u32[]{:S(2)}, u32[]{:S(2)}) collective-permute-start(f32[1,8,512]{2,1,0:T(8,128)} %get-tuple-element.89), channel_id=1, source_target_pairs={{0,32},{32,64},{64,96},{96,128},{128,160},{160,192},{192,224},{224... | collective-permute-start | bytes 49160 | tf_op jit(solution)/shard_map/ppermute | solution.py:43
  104.0 2.2 %fusion.36 = (f32[32,12,512]{2,1,0:T(8,128)S(1)}, f32[12,32,512]{2,0,1:T(8,128)S(1)}) fusion(f32[32,512]{1,0:T(8,128)S(1)} %bitcast.173, f32[12]{0:T(128)S(1)} %copy-done.7, f32[12]{0:T(128)S(1)} %copy-done.8, f32[12]{0:T(128)S(1)} %copy-done.9, f32[12]{0:T(128)S(1)} %copy-done.10, f32[32,512]{1,0:T(8,128)S(1)} %bitcast.174, ...), kind=kLoop, calls=%fused_computation.58 | loop fusion | flops 8257536 | bytes 2556096 | tf_op jit(solution)/shard_map/add | solution.py:135
  106.1 3.2 %fusion.243 = (f32[1,32,512]{2,0,1:T(1,128)S(1)}, f32[1,32,512]{2,0,1:T(1,128)S(1)}, f32[1,32,512]{2,0,1:T(1,128)S(1)}, f32[1,32,512]{2,0,1:T(1,128)}, f32[1,32,...) fusion(f32[12,32,512]{2,0,1:T(8,128)S(1)} %get-tuple-element.29, f32[]{:T(128)} %bitcast.26, ...), kind=kLoop, calls=%fused_computation.490 | loop fusion | flops 131072 | bytes 1245196 | tf_op jit(solution)/shard_map/slice | solution.py:137
  109.4 1.6 %scatter_fusion = f32[12,33,512]{2,0,1:T(8,128)S(1)} fusion(f32[12,33,512]{2,0,1:T(8,128)S(1)} %broadcast_in_dim.37, s32[32]{0:T(128)S(1)} %fusion.224, f32[32,12,512]{2,1,0:T(8,128)S(1)} %get-tuple-element.28), kind=kCustom, calls=%fused_computation.3 | custom fusion | bytes 2359424 | tf_op jit(solution)/shard_map/scatter | solution.py:245
  111.1 2.5 %collective-permute-start.14 = (f32[6,1,512]{2,1,0:T(1,128)S(1)}, f32[6,1,512]{2,1,0:T(1,128)S(1)}, u32[]{:S(2)}, u32[]{:S(2)}) collective-permute-start(f32[6,1,512]{2,1,0:T(1,128)S(1)} %get-tuple-element.78), channel_id=1, source_target_pairs={{1,0},{2,1},{3,2},{4,3},{5,4},{6,5},{7,6},{8,7},{9,8},{10,9},{11,1... | collective-permute-start | bytes 36872 | tf_op jit(solution)/shard_map/ppermute | solution.py:44
  113.5 2.8 %collective-permute-start.15 = (f32[6,1,512]{2,1,0:T(1,128)S(1)}, f32[6,1,512]{2,1,0:T(1,128)S(1)}, u32[]{:S(2)}, u32[]{:S(2)}) collective-permute-start(f32[6,1,512]{2,1,0:T(1,128)S(1)} %get-tuple-element.77), channel_id=1, source_target_pairs={{0,1},{1,2},{2,3},{3,4},{4,5},{5,6},{6,7},{7,8},{8,9},{9,10},{10,1... | collective-permute-start | bytes 36872 | tf_op jit(solution)/shard_map/ppermute | solution.py:43
  116.5 1.7 %copy.153 = f32[12,32,1,512]{3,2,0,1:T(1,128)} copy(f32[12,32,1,512]{3,0,1,2:T(8,128)S(1)} %slice_bitcast_fusion) | data formatting | bytes 1572864 | tf_op jit(solution)/shard_map/reshape | solution.py:248
  118.2 7.1 %all-to-all-start.2 = ((f32[12,32,1,512]{3,2,0,1:T(1,128)}), f32[12,32,1,512]{3,2,0,1:T(1,128)S(1)}, u32[]{:S(2)}, u32[]{:S(2)}) async-start(f32[12,32,1,512]{3,2,0,1:T(1,128)} %copy.153), calls=%async_computation.2 | async-start | bytes 1572864 | tf_op jit(solution)/shard_map/all_to_all | solution.py:247
  126.5 2.6 %multiply_bitcast_fusion.1 = (f32[1,4,8,512]{3,2,1,0:T(8,128)S(1)}, f32[4,8,512]{2,1,0:T(8,128)}) fusion(s32[4,8,512]{2,1,0:T(8,128)S(1)} %copy-done.1, f32[4,8,512]{2,1,0:T(8,128)S(1)} %get-tuple-element.31, f32[]{:T(128)} %bitcast.30, f32[1,32,512]{2,0,1:T(1,128)S(1)} %copy-done.3, f32[]{:T(128)} %bitcast.29, f32[1,32,512]{2,0,1:T(1,128)S(1)} %get-tuple-element.50, ...), kind=kLoop, calls=%fused_computation.439 | loop fusion | flops 638976 | bytes 1114156 | tf_op jit(solution)/shard_map/stack | solution.py:259
  129.1 1.9 %collective-permute-start.16 = (f32[2,1,8,512]{3,2,1,0:T(8,128)S(1)}, f32[2,1,8,512]{3,2,1,0:T(8,128)S(1)}, u32[]{:S(2)}, u32[]{:S(2)}) collective-permute-start(f32[2,1,8,512]{3,2,1,0:T(8,128)S(1)} %get-tuple-element.70), channel_id=1, source_target_pairs={{32,0},{64,32},{96,64},{128,96},{160,128},{192,160},{224,192},{256... | collective-permute-start | bytes 98312 | tf_op jit(solution)/shard_map/ppermute | solution.py:25
  131.1 4.9 %collective-permute-start.17 = (f32[2,1,8,512]{3,2,1,0:T(8,128)S(1)}, f32[2,1,8,512]{3,2,1,0:T(8,128)S(1)}, u32[]{:S(2)}, u32[]{:S(2)}) collective-permute-start(f32[2,1,8,512]{3,2,1,0:T(8,128)S(1)} %get-tuple-element.69), channel_id=1, source_target_pairs={{0,32},{32,64},{64,96},{96,128},{128,160},{160,192},{192,224},{224... | collective-permute-start | bytes 98312 | tf_op jit(solution)/shard_map/ppermute | solution.py:24
  135.9 4.6 %collective-permute-start.18 = (f32[2,4,1,512]{3,2,1,0:T(1,128)S(1)}, f32[2,4,1,512]{3,2,1,0:T(1,128)S(1)}, u32[]{:S(2)}, u32[]{:S(2)}) collective-permute-start(f32[2,4,1,512]{3,2,1,0:T(1,128)S(1)} %get-tuple-element.72), channel_id=1, source_target_pairs={{1,0},{2,1},{3,2},{4,3},{5,4},{6,5},{7,6},{8,7},{9,8},{10,9},{11,1... | collective-permute-start | bytes 49160 | tf_op jit(solution)/shard_map/ppermute | solution.py:25
  140.5 1.9 %collective-permute-start.19 = (f32[2,4,1,512]{3,2,1,0:T(1,128)S(1)}, f32[2,4,1,512]{3,2,1,0:T(1,128)S(1)}, u32[]{:S(2)}, u32[]{:S(2)}) collective-permute-start(f32[2,4,1,512]{3,2,1,0:T(1,128)S(1)} %get-tuple-element.71), channel_id=1, source_target_pairs={{0,1},{1,2},{2,3},{3,4},{4,5},{5,6},{6,7},{7,8},{8,9},{9,10},{10,1... | collective-permute-start | bytes 49160 | tf_op jit(solution)/shard_map/ppermute | solution.py:24
  142.5 1.6 %collective-permute-done.18 = f32[2,4,1,512]{3,2,1,0:T(1,128)S(1)} collective-permute-done((f32[2,4,1,512]{3,2,1,0:T(1,128)S(1)}, f32[2,4,1,512]{3,2,1,0:T(1,128)S(1)}, u32[]{:S(2)}, u32[]{:S(2)}) %collective-permute-start.18) | collective-permute-done | bytes 16416 | tf_op jit(solution)/shard_map/ppermute | solution.py:25
  144.1 3.0 %collective-permute-done.19 = f32[2,4,1,512]{3,2,1,0:T(1,128)S(1)} collective-permute-done((f32[2,4,1,512]{3,2,1,0:T(1,128)S(1)}, f32[2,4,1,512]{3,2,1,0:T(1,128)S(1)}, u32[]{:S(2)}, u32[]{:S(2)}) %collective-permute-start.19) | collective-permute-done | bytes 16416 | tf_op jit(solution)/shard_map/ppermute | solution.py:24
  149.1 0.7 pad_maximum_fusion.3
  150.0 1.6 %scatter_fusion.1 = f32[12,17,512]{2,0,1:T(8,128)S(1)} fusion(f32[12,17,512]{2,0,1:T(8,128)S(1)} %broadcast_in_dim.36, s32[32]{0:T(128)S(1)} %fusion.225, f32[32,12,512]{2,1,0:T(8,128)S(1)} %bitcast.168), kind=kCustom, calls=%fused_computation.4 | custom fusion | bytes 2359424 | tf_op jit(solution)/shard_map/scatter | solution.py:257
  151.6 1.0 copy.156
  (101 shorter events, 12.2 us)
Async XLA Ops:
  0.6 57.4 %copy-start = (f32[6,16]{1,0:T(8,128)S(1)}, f32[6,16]{1,0:T(8,128)}, u32[]{:S(2)}) copy-start(f32[6,16]{1,0:T(8,128)} %param.16) | copy-start | bytes 1156
  1.6 49.6 %collective-permute-start.4 = (f32[1,8,512]{2,1,0:T(8,128)S(1)}, f32[1,8,512]{2,1,0:T(8,128)S(1)}, u32[]{:S(2)}, u32[]{:S(2)}) collective-permute-start(f32[1,8,512]{2,1,0:T(8,128)S(1)} %get-tuple-element.98), channel_id=1, source_target_pairs={{32,0},{64,32},{96,64},{128,96},{160,128},{192,160},{224,192},{256... | collective-permute-start | bytes 49160 | tf_op jit(solution)/shard_map/ppermute | solution.py:44
  4.2 47.0 %collective-permute-start.5 = (f32[1,8,512]{2,1,0:T(8,128)S(1)}, f32[1,8,512]{2,1,0:T(8,128)S(1)}, u32[]{:S(2)}, u32[]{:S(2)}) collective-permute-start(f32[1,8,512]{2,1,0:T(8,128)S(1)} %get-tuple-element.97), channel_id=1, source_target_pairs={{0,32},{32,64},{64,96},{96,128},{128,160},{160,192},{192,224},{224... | collective-permute-start | bytes 49160 | tf_op jit(solution)/shard_map/ppermute | solution.py:43
  10.2 38.1 %collective-permute-start = (s32[4,1,512]{2,1,0:T(1,128)S(1)}, s32[4,1,512]{2,1,0:T(1,128)S(1)}, u32[]{:S(2)}, u32[]{:S(2)}) collective-permute-start(s32[4,1,512]{2,1,0:T(1,128)S(1)} %get-tuple-element.93), channel_id=1, source_target_pairs={{0,1},{1,2},{2,3},{3,4},{4,5},{5,6},{6,7},{7,8},{8,9},{9,10},{10,1... | collective-permute-start | bytes 24584 | tf_op jit(solution)/shard_map/ppermute | solution.py:24
  13.4 37.8 %collective-permute-start.3 = (s32[4,1,512]{2,1,0:T(1,128)S(1)}, s32[4,1,512]{2,1,0:T(1,128)S(1)}, u32[]{:S(2)}, u32[]{:S(2)}) collective-permute-start(s32[4,1,512]{2,1,0:T(1,128)S(1)} %get-tuple-element.94), channel_id=1, source_target_pairs={{1,0},{2,1},{3,2},{4,3},{5,4},{6,5},{7,6},{8,7},{9,8},{10,9},{11,1... | collective-permute-start | bytes 24584 | tf_op jit(solution)/shard_map/ppermute | solution.py:25
  17.6 40.2 %collective-permute-start.1 = (s32[1,8,512]{2,1,0:T(8,128)S(1)}, s32[1,8,512]{2,1,0:T(8,128)S(1)}, u32[]{:S(2)}, u32[]{:S(2)}) collective-permute-start(s32[1,8,512]{2,1,0:T(8,128)S(1)} %get-tuple-element.95), channel_id=1, source_target_pairs={{0,32},{32,64},{64,96},{96,128},{128,160},{160,192},{192,224},{224... | collective-permute-start | bytes 49160 | tf_op jit(solution)/shard_map/ppermute | solution.py:24
  23.8 15.8 %all-to-all-start = ((s32[32,1,1]{2,1,0:T(1,128)}), s32[32,1,1]{2,1,0:T(1,128)S(1)}, u32[]{:S(2)}, u32[]{:S(2)}) async-start(s32[32,1,1]{2,1,0:T(1,128)} %copy.149), calls=%async_computation | async-start | bytes 32768 | tf_op jit(solution)/shard_map/all_to_all | solution.py:227
  42.5 24.4 %all-to-all-start.1 = ((f32[12,32,1,512]{3,2,0,1:T(1,128)}), f32[12,32,1,512]{3,2,0,1:T(1,128)S(1)}, u32[]{:S(2)}, u32[]{:S(2)}) async-start(f32[12,32,1,512]{3,2,0,1:T(1,128)} %copy.150), calls=%async_computation.1 | async-start | bytes 1572864 | tf_op jit(solution)/shard_map/all_to_all | solution.py:230
  48.3 9.4 %collective-permute-start.2 = (s32[1,8,512]{2,1,0:T(8,128)S(1)}, s32[1,8,512]{2,1,0:T(8,128)S(1)}, u32[]{:S(2)}, u32[]{:S(2)}) collective-permute-start(s32[1,8,512]{2,1,0:T(8,128)S(1)} %get-tuple-element.96), channel_id=1, source_target_pairs={{32,0},{64,32},{96,64},{128,96},{160,128},{192,160},{224,192},{256... | collective-permute-start | bytes 49160 | tf_op jit(solution)/shard_map/ppermute | solution.py:25
  51.3 14.7 %collective-permute-start.6 = (f32[6,1,512]{2,1,0:T(1,128)S(1)}, f32[6,1,512]{2,1,0:T(1,128)S(1)}, u32[]{:S(2)}, u32[]{:S(2)}) collective-permute-start(f32[6,1,512]{2,1,0:T(1,128)S(1)} %get-tuple-element.86), channel_id=1, source_target_pairs={{1,0},{2,1},{3,2},{4,3},{5,4},{6,5},{7,6},{8,7},{9,8},{10,9},{11,1... | collective-permute-start | bytes 36872 | tf_op jit(solution)/shard_map/ppermute | solution.py:44
  55.8 10.1 %collective-permute-start.7 = (f32[6,1,512]{2,1,0:T(1,128)S(1)}, f32[6,1,512]{2,1,0:T(1,128)S(1)}, u32[]{:S(2)}, u32[]{:S(2)}) collective-permute-start(f32[6,1,512]{2,1,0:T(1,128)S(1)} %get-tuple-element.85), channel_id=1, source_target_pairs={{0,1},{1,2},{2,3},{3,4},{4,5},{5,6},{6,7},{7,8},{8,9},{9,10},{10,1... | collective-permute-start | bytes 36872 | tf_op jit(solution)/shard_map/ppermute | solution.py:43
  67.0 3.1 %copy-start.1 = (s32[4,8,512]{2,1,0:T(8,128)S(1)}, s32[4,8,512]{2,1,0:T(8,128)}, u32[]{:S(2)}) copy-start(s32[4,8,512]{2,1,0:T(8,128)} %param.14) | copy-start | bytes 196612
  67.0 3.1 %copy-start.2 = (f32[4,8,512]{2,1,0:T(8,128)S(1)}, f32[4,8,512]{2,1,0:T(8,128)}, u32[]{:S(2)}) copy-start(f32[4,8,512]{2,1,0:T(8,128)} %param.12) | copy-start | bytes 196612
  67.0 14.0 %copy-start.7 = (f32[12]{0:T(128)S(1)}, f32[12]{0:T(128)}, u32[]{:S(2)}) copy-start(f32[12]{0:T(128)} %param.22) | copy-start | bytes 148
  67.1 14.0 %copy-start.8 = (f32[12]{0:T(128)S(1)}, f32[12]{0:T(128)}, u32[]{:S(2)}) copy-start(f32[12]{0:T(128)} %param.21) | copy-start | bytes 148
  67.1 14.0 %copy-start.9 = (f32[12]{0:T(128)S(1)}, f32[12]{0:T(128)}, u32[]{:S(2)}) copy-start(f32[12]{0:T(128)} %param.19) | copy-start | bytes 148
  67.1 14.0 %copy-start.10 = (f32[12]{0:T(128)S(1)}, f32[12]{0:T(128)}, u32[]{:S(2)}) copy-start(f32[12]{0:T(128)} %param.20) | copy-start | bytes 148
  72.2 9.7 %collective-permute-start.8 = (f32[1,8,512]{2,1,0:T(8,128)S(1)}, f32[1,8,512]{2,1,0:T(8,128)S(1)}, u32[]{:S(2)}, u32[]{:S(2)}) collective-permute-start(f32[1,8,512]{2,1,0:T(8,128)S(1)} %get-tuple-element.92), channel_id=1, source_target_pairs={{32,0},{64,32},{96,64},{128,96},{160,128},{192,160},{224,192},{256... | collective-permute-start | bytes 49160 | tf_op jit(solution)/shard_map/ppermute | solution.py:44
  78.0 3.9 %collective-permute-start.9 = (f32[1,8,512]{2,1,0:T(8,128)S(1)}, f32[1,8,512]{2,1,0:T(8,128)S(1)}, u32[]{:S(2)}, u32[]{:S(2)}) collective-permute-start(f32[1,8,512]{2,1,0:T(8,128)S(1)} %get-tuple-element.91), channel_id=1, source_target_pairs={{0,32},{32,64},{64,96},{96,128},{128,160},{160,192},{192,224},{224... | collective-permute-start | bytes 49160 | tf_op jit(solution)/shard_map/ppermute | solution.py:43
  81.9 7.8 %collective-permute-start.10 = (f32[6,1,512]{2,1,0:T(1,128)S(1)}, f32[6,1,512]{2,1,0:T(1,128)S(1)}, u32[]{:S(2)}, u32[]{:S(2)}) collective-permute-start(f32[6,1,512]{2,1,0:T(1,128)S(1)} %get-tuple-element.82), channel_id=1, source_target_pairs={{1,0},{2,1},{3,2},{4,3},{5,4},{6,5},{7,6},{8,7},{9,8},{10,9},{11,1... | collective-permute-start | bytes 36872 | tf_op jit(solution)/shard_map/ppermute | solution.py:44
  85.2 6.5 %collective-permute-start.11 = (f32[6,1,512]{2,1,0:T(1,128)S(1)}, f32[6,1,512]{2,1,0:T(1,128)S(1)}, u32[]{:S(2)}, u32[]{:S(2)}) collective-permute-start(f32[6,1,512]{2,1,0:T(1,128)S(1)} %get-tuple-element.81), channel_id=1, source_target_pairs={{0,1},{1,2},{2,3},{3,4},{4,5},{5,6},{6,7},{7,8},{8,9},{9,10},{10,1... | collective-permute-start | bytes 36872 | tf_op jit(solution)/shard_map/ppermute | solution.py:43
  95.0 16.0 %collective-permute-start.12 = (f32[1,8,512]{2,1,0:T(8,128)}, f32[1,8,512]{2,1,0:T(8,128)S(1)}, u32[]{:S(2)}, u32[]{:S(2)}) collective-permute-start(f32[1,8,512]{2,1,0:T(8,128)} %get-tuple-element.90), channel_id=1, source_target_pairs={{32,0},{64,32},{96,64},{128,96},{160,128},{192,160},{224,192},{256... | collective-permute-start | bytes 49160 | tf_op jit(solution)/shard_map/ppermute | solution.py:44
  99.6 11.5 %collective-permute-start.13 = (f32[1,8,512]{2,1,0:T(8,128)}, f32[1,8,512]{2,1,0:T(8,128)S(1)}, u32[]{:S(2)}, u32[]{:S(2)}) collective-permute-start(f32[1,8,512]{2,1,0:T(8,128)} %get-tuple-element.89), channel_id=1, source_target_pairs={{0,32},{32,64},{64,96},{96,128},{128,160},{160,192},{192,224},{224... | collective-permute-start | bytes 49160 | tf_op jit(solution)/shard_map/ppermute | solution.py:43
  111.1 14.2 %collective-permute-start.14 = (f32[6,1,512]{2,1,0:T(1,128)S(1)}, f32[6,1,512]{2,1,0:T(1,128)S(1)}, u32[]{:S(2)}, u32[]{:S(2)}) collective-permute-start(f32[6,1,512]{2,1,0:T(1,128)S(1)} %get-tuple-element.78), channel_id=1, source_target_pairs={{1,0},{2,1},{3,2},{4,3},{5,4},{6,5},{7,6},{8,7},{9,8},{10,9},{11,1... | collective-permute-start | bytes 36872 | tf_op jit(solution)/shard_map/ppermute | solution.py:44
  113.5 11.8 %collective-permute-start.15 = (f32[6,1,512]{2,1,0:T(1,128)S(1)}, f32[6,1,512]{2,1,0:T(1,128)S(1)}, u32[]{:S(2)}, u32[]{:S(2)}) collective-permute-start(f32[6,1,512]{2,1,0:T(1,128)S(1)} %get-tuple-element.77), channel_id=1, source_target_pairs={{0,1},{1,2},{2,3},{3,4},{4,5},{5,6},{6,7},{7,8},{8,9},{9,10},{10,1... | collective-permute-start | bytes 36872 | tf_op jit(solution)/shard_map/ppermute | solution.py:43
  118.2 31.6 %all-to-all-start.2 = ((f32[12,32,1,512]{3,2,0,1:T(1,128)}), f32[12,32,1,512]{3,2,0,1:T(1,128)S(1)}, u32[]{:S(2)}, u32[]{:S(2)}) async-start(f32[12,32,1,512]{3,2,0,1:T(1,128)} %copy.153), calls=%async_computation.2 | async-start | bytes 1572864 | tf_op jit(solution)/shard_map/all_to_all | solution.py:247
  125.6 0.8 copy-start.3
  125.6 0.9 copy-start.4
  125.6 0.9 copy-start.5
  125.6 0.9 copy-start.6
  129.1 18.0 %collective-permute-start.16 = (f32[2,1,8,512]{3,2,1,0:T(8,128)S(1)}, f32[2,1,8,512]{3,2,1,0:T(8,128)S(1)}, u32[]{:S(2)}, u32[]{:S(2)}) collective-permute-start(f32[2,1,8,512]{3,2,1,0:T(8,128)S(1)} %get-tuple-element.70), channel_id=1, source_target_pairs={{32,0},{64,32},{96,64},{128,96},{160,128},{192,160},{224,192},{256... | collective-permute-start | bytes 98312 | tf_op jit(solution)/shard_map/ppermute | solution.py:25
  131.1 16.1 %collective-permute-start.17 = (f32[2,1,8,512]{3,2,1,0:T(8,128)S(1)}, f32[2,1,8,512]{3,2,1,0:T(8,128)S(1)}, u32[]{:S(2)}, u32[]{:S(2)}) collective-permute-start(f32[2,1,8,512]{3,2,1,0:T(8,128)S(1)} %get-tuple-element.69), channel_id=1, source_target_pairs={{0,32},{32,64},{64,96},{96,128},{128,160},{160,192},{192,224},{224... | collective-permute-start | bytes 98312 | tf_op jit(solution)/shard_map/ppermute | solution.py:24
  135.9 8.1 %collective-permute-start.18 = (f32[2,4,1,512]{3,2,1,0:T(1,128)S(1)}, f32[2,4,1,512]{3,2,1,0:T(1,128)S(1)}, u32[]{:S(2)}, u32[]{:S(2)}) collective-permute-start(f32[2,4,1,512]{3,2,1,0:T(1,128)S(1)} %get-tuple-element.72), channel_id=1, source_target_pairs={{1,0},{2,1},{3,2},{4,3},{5,4},{6,5},{7,6},{8,7},{9,8},{10,9},{11,1... | collective-permute-start | bytes 49160 | tf_op jit(solution)/shard_map/ppermute | solution.py:25
  140.5 6.6 %collective-permute-start.19 = (f32[2,4,1,512]{3,2,1,0:T(1,128)S(1)}, f32[2,4,1,512]{3,2,1,0:T(1,128)S(1)}, u32[]{:S(2)}, u32[]{:S(2)}) collective-permute-start(f32[2,4,1,512]{3,2,1,0:T(1,128)S(1)} %get-tuple-element.71), channel_id=1, source_target_pairs={{0,1},{1,2},{2,3},{3,4},{4,5},{5,6},{6,7},{7,8},{8,9},{9,10},{10,1... | collective-permute-start | bytes 49160 | tf_op jit(solution)/shard_map/ppermute | solution.py:24
where the time goes:
time: 154 us; the launch traced here: 153 us
  starting transfers between devices  90.7 us (59%)
  other arithmetic  27.2 us (18%)
  local copies, waits for them, and re-layouts  16.3 us (11%)
  waiting for transfers between devices  16.3 us (11%)
    ppermute x6, starting transfers between devices, padded(): after = lax.ppermute(first, axis, down)  23.3 us
    ppermute x6, starting transfers between devices, padded(): before = lax.ppermute(last, axis, up)  19.3 us
    ppermute x4, starting transfers between devices, extended(): lax.ppermute(first, axis, [(b, a) for a, b in up])  13.5 us
    ppermute x4, starting transfers between devices, extended(): lax.ppermute(last, axis, up)  12.9 us
    all_to_all x1, starting transfers between devices, on_device(): lax.all_to_all(claims, 'blk', split_axis=0, concat_axis=0, tiled=True)  8.78 us
    slice x3, other arithmetic, react(): states[0]  8.01 us
    all_to_all x1, starting transfers between devices, on_device(): lax.all_to_all(home_rows.reshape(gate_count, blocks, pair_slots, depth),...  7.14 us
    ppermute x6, waiting for transfers between devices, padded(): after = lax.ppermute(first, axis, down)  6.18 us
  transfers between devices with their start and end apart: 23, of which 5 were waited for; matrix products, arithmetic and copies ran while one was open for 21% of the time, Pallas kernels for 0%

commit v1 on v0

v1 whole, which is shorter than its diff:
```python
import jax
import jax.numpy as jnp
from jax import lax
from jax.sharding import PartitionSpec as P

FIB = 16
STEPS = 3


STEP_DT = 0.1
PHASE_REF = -0.2
PHASE_SOFT = 0.5
COMPONENT = ((1, 4, 5), (4, 2, 6), (5, 6, 3))


def basis(direction, amount):
    return tuple((amount if position == direction else 0 for position in range(3)))


def combine(first, second):
    return tuple((left_part + right_part for left_part, right_part in zip(first, second)))


def window(array, starts, extent):
    leading = array.ndim - 3
    begin = (0,) * leading + tuple(starts)
    finish = tuple(array.shape[:leading]) + tuple(
        (first + count for first, count in zip(starts, extent))
    )
    return lax.slice(array, begin, finish)


def shifted(array, direction, offset, extent):
    starts = tuple(
        ((0 if position == direction else 1) + offset[position] for position in range(3))
    )
    sizes = tuple(
        (
            extent[position] + 1 if position == direction else extent[position]
            for position in range(3)
        )
    )
    return window(array, starts, sizes)


def coefficient_stack(weights, fiber, conductivity):
    classes = (fiber[None] == jnp.arange(FIB, dtype=jnp.int32)[:, None, None, None]).astype(
        jnp.float32
    )
    sigma = jnp.tensordot(conductivity, classes, axes=(1, 0), precision=lax.Precision.HIGHEST)
    return jnp.concatenate([weights[None], weights[None] * sigma], axis=0)


def face_terms(padded_stack, extent):
    result = []
    for direction in range(3):
        lower = shifted(padded_stack, direction, (0, 0, 0), extent)
        upper = shifted(padded_stack, direction, basis(direction, 1), extent)
        face_mask = lower[0] * upper[0]
        result.append(
            [
                0.5
                * (lower[COMPONENT[direction][other]] + upper[COMPONENT[direction][other]])
                * face_mask
                for other in range(3)
            ]
        )
    return result


def diffuse(padded_field, faces, extent):
    total = jnp.zeros(extent, jnp.float32)
    for direction in range(3):
        along = basis(direction, 1)
        flux = faces[direction][direction] * (
            shifted(padded_field, direction, along, extent)
            - shifted(padded_field, direction, (0, 0, 0), extent)
        )
        for other in range(3):
            if other != direction:
                upward = basis(other, 1)
                downward = basis(other, -1)
                slope = (
                    shifted(padded_field, direction, upward, extent)
                    + shifted(padded_field, direction, combine(along, upward), extent)
                    - shifted(padded_field, direction, downward, extent)
                    - shifted(padded_field, direction, combine(along, downward), extent)
                ) * 0.25
                flux = flux + faces[direction][other] * slope
        total = total + jnp.diff(flux, axis=direction)
    return total


def edge_term(first, second):
    cross = first[0] * second[1] - first[1] * second[0]
    inner = first[0] * second[0] + first[1] * second[1]
    norm_value = jnp.sqrt(
        (first[0] * first[0] + first[1] * first[1])
        * (second[0] * second[0] + second[1] * second[1])
    )
    return 2.0 * jnp.arctan(cross / (norm_value + inner + PHASE_SOFT))


def charges(padded_phase, extent):
    results = []
    for first_dim, second_dim in ((0, 1), (1, 2), (0, 2)):
        corners = [
            basis(first_dim, 1),
            basis(second_dim, 1),
            basis(first_dim, -1),
            basis(second_dim, -1),
        ]
        points = [
            window(padded_phase, tuple((1 + value for value in corner)), extent)
            for corner in corners
        ]
        circulation = jnp.zeros(extent, jnp.float32)
        for position in range(4):
            circulation = circulation + edge_term(points[position], points[(position + 1) % 4])
        results.append(circulation)
    return jnp.stack(results)


def pad_depth(array):
    return jnp.pad(array, [(0, 0)] * (array.ndim - 1) + [(1, 1)])


def shift_pair(axis, last, first):
    size = lax.axis_size(axis)
    up = [(i, i + 1) for i in range(size - 1)]
    return (lax.ppermute(last, axis, up), lax.ppermute(first, axis, [(b, a) for a, b in up]))


def gate_update(level, states, params):
    gate_half, gate_steep, gate_tmin, gate_tspan, _ = params
    offset = level[None] - gate_half[:, None, None]
    target = jax.nn.sigmoid(gate_steep[:, None, None] * offset)
    relax = gate_tmin[:, None, None] + gate_tspan[:, None, None] / (1.0 + 4.0 * offset * offset)
    return target + (states - target) * jnp.exp(-STEP_DT / relax)


def ionic_current(level, states, channel):
    sodium = channel[0] * states[0] * states[0] * states[0] * states[1] * states[2] * (level - 1.2)
    calcium = channel[1] * states[3] * states[4] * states[5] * states[6] * (level - 1.0)
    transient = channel[2] * states[7] * states[8] * (level + 0.9)
    rapid_delayed = channel[3] * states[9] * states[10] * (level + 0.9)
    slow_delayed = channel[4] * states[11] * states[11] * (level + 0.8)
    inward_rect = channel[5] * (level + 0.9) / (1.0 + jnp.exp(4.0 * (level + 0.6)))
    return sodium + calcium + transient + rapid_delayed + slow_delayed + inward_rect


def swap_blocks(x):
    return lax.all_to_all(x, "blk", split_axis=0, concat_axis=0, tiled=True)


def inner_faces(faces):
    return [
        [lax.slice_in_dim(lax.slice_in_dim(f, 1, f.shape[0] - 1, axis=0), 1, f.shape[1] - 1, axis=1) for f in row]
        for row in faces
    ]


def on_device(
    voltage,
    voltage_lag,
    tissue,
    fiber,
    conductivity,
    worker,
    gates,
    gate_half,
    gate_steep,
    gate_tmin,
    gate_tspan,
    channel,
):
    extent = voltage.shape
    planes, rows, depth = extent
    gate_count, capacity, _ = gates.shape
    params = (gate_half, gate_steep, gate_tmin, gate_tspan, channel)
    blocks = lax.axis_size("blk")
    lanes = 128
    chunks = depth // lanes
    weights = tissue.astype(jnp.float32)

    targets = worker.reshape(-1)
    tile_count = targets.shape[0]
    live = targets >= 0
    holder = jnp.where(live, targets // capacity, -1)
    claimed = holder[None, :] == jnp.arange(blocks, dtype=jnp.int32)[:, None]
    claims = jnp.sum(jnp.where(claimed, targets % capacity + 1, 0), axis=1) - 1
    tile_of = jnp.sum(jnp.where(claimed, jnp.arange(tile_count, dtype=jnp.int32)[None, :], 0), axis=1)
    arrived = swap_blocks(jnp.broadcast_to(claims[:, None, None], (blocks, 1, lanes)))[:, 0, 0]

    by_row = gates.transpose(1, 0, 2).reshape(capacity, gate_count * chunks, lanes)
    leaving = by_row[jnp.maximum(arrived, 0)]
    coming = swap_blocks(leaving)
    states = (
        coming[jnp.maximum(holder, 0)].reshape(tile_count, gate_count, depth).transpose(1, 0, 2)
    )

    field = weights * voltage
    lag = weights * (voltage_lag - PHASE_REF)
    fiber_f = fiber.astype(jnp.float32)
    low, high = shift_pair(
        "slab",
        jnp.concatenate([field[-1:], lag[-1:], fiber_f[-2:], weights[-2:]]),
        jnp.concatenate([field[:1], lag[:1], fiber_f[:2], weights[:2]]),
    )
    field_s = jnp.concatenate([low[0:1], field, high[0:1]])
    lag_s = jnp.concatenate([low[1:2], lag, high[1:2]])
    fiber_s = jnp.concatenate([low[2:4], fiber_f, high[2:4]])
    weights_s = jnp.concatenate([low[4:6], weights, high[4:6]])
    low, high = shift_pair(
        "blk",
        jnp.concatenate([field_s[:, -1], lag_s[1:-1, -1], fiber_s[:, -2], fiber_s[:, -1], weights_s[:, -2], weights_s[:, -1]]),
        jnp.concatenate([field_s[:, 0], lag_s[1:-1, 0], fiber_s[:, 0], fiber_s[:, 1], weights_s[:, 0], weights_s[:, 1]]),
    )
    n1, n2 = planes + 2, planes + 4

    def column(part, start, count):
        return part[start : start + count, None]

    def two(part, start):
        return jnp.concatenate([column(part, start, n2), column(part, start + n2, n2)], axis=1)

    field_e = jnp.concatenate([column(low, 0, n1), field_s, column(high, 0, n1)], axis=1)
    lag_rim = (column(low, n1, planes), column(high, n1, planes))
    at = n1 + planes
    fiber_e = jnp.concatenate([two(low, at), fiber_s, two(high, at)], axis=1)
    at = at + 2 * n2
    weights_e = jnp.concatenate([two(low, at), weights_s, two(high, at)], axis=1)
    stack_e = coefficient_stack(weights_e, fiber_e.astype(jnp.int32), conductivity)
    ring = (planes + 2, rows + 2, depth)
    faces_ring = face_terms(pad_depth(stack_e), ring)
    faces = inner_faces(faces_ring)
    weights_ring = weights_e[1:-1, 1:-1]

    def current_of(potential, states):
        found = ionic_current(potential.reshape(tile_count, depth), states, channel)
        return jnp.where(live[:, None], found, 0.0).reshape(extent)

    spread = diffuse(pad_depth(field_e), faces, extent)
    v0 = voltage
    v1 = v0 + weights * (spread - STEP_DT * current_of(v0, states))
    states = gate_update(v0.reshape(tile_count, depth), states, params)
    current = current_of(v1, states)
    low, high = shift_pair(
        "slab",
        jnp.concatenate([v1[-2:], current[-1:]]),
        jnp.concatenate([v1[:2], current[:1]]),
    )
    v1_s = jnp.concatenate([low[:2], v1, high[:2]])
    current_s = jnp.concatenate([low[2:], current, high[2:]])
    low, high = shift_pair(
        "blk",
        jnp.concatenate([v1_s[:, -2], v1_s[:, -1], current_s[:, -1]]),
        jnp.concatenate([v1_s[:, 0], v1_s[:, 1], current_s[:, 0]]),
    )
    v1_e = jnp.concatenate([two(low, 0), v1_s, two(high, 0)], axis=1)
    current_e = jnp.concatenate([column(low, 2 * n2, n1), current_s, column(high, 2 * n2, n1)], axis=1)
    states = gate_update(v1.reshape(tile_count, depth), states, params)
    spread = diffuse(pad_depth(weights_e * v1_e), faces_ring, ring)
    v2_e = v1_e[1:-1, 1:-1] + weights_ring * (spread - STEP_DT * current_e)
    v2 = v2_e[1:-1, 1:-1]

    used = jnp.stack([v.reshape(tile_count, chunks, lanes) for v in (v0, v1, v2)], axis=1)
    used = used.reshape(tile_count, 3 * chunks, lanes)[tile_of]
    returned = swap_blocks(used)

    spread = diffuse(pad_depth(weights_ring * v2_e), faces, extent)
    v3 = v2 + weights * (spread - STEP_DT * current_of(v2, states))

    ours = weights * (v3 - PHASE_REF)
    below, above = shift_pair("slab", ours[-1:], ours[:1])
    left, right = shift_pair("blk", ours[:, -1:], ours[:, :1])

    def plus(array, low0, high0, low1, high1):
        tall = jnp.concatenate([low0, array, high0], axis=0)
        around = [(1, 1), (0, 0), (0, 0)]
        return jnp.concatenate([jnp.pad(low1, around), tall, jnp.pad(high1, around)], axis=1)

    phase = jnp.stack(
        [
            plus(ours, below, above, left, right),
            plus(lag, lag_s[:1], lag_s[-1:], *lag_rim),
        ]
    )
    charge = charges(pad_depth(phase), extent)

    mine = arrived[None, :] == jnp.arange(capacity, dtype=jnp.int32)[:, None]
    source = jnp.sum(jnp.where(mine, jnp.arange(blocks, dtype=jnp.int32)[None, :], 0), axis=1)
    seen = returned[source].reshape(capacity, 3, depth)
    gates_out = gates
    for step in range(STEPS):
        gates_out = gate_update(seen[:, step], gates_out, params)
    return (v3, gates_out, charge)

def solution(mesh):
    in_specs = (
        P("slab", "blk", None),
        P("slab", "blk", None),
        P("slab", "blk", None),
        P("slab", "blk", None),
        P(),
        P("slab", "blk"),
        P(None, ("slab", "blk"), None),
        P(),
        P(),
        P(),
        P(),
        P(),
    )
    out_specs = (
        P("slab", "blk", None),
        P(None, ("slab", "blk"), None),
        P(None, "slab", "blk", None),
    )
    return jax.shard_map(
        on_device, mesh=mesh, in_specs=in_specs, out_specs=out_specs, check_vma=False
    )
```

time: 154 us -> 151 us (0.981)
  the two profiles are of different devices: /device:TPU:199 before, /device:TPU:201 now
where the time goes in v1:
time: 151 us; the launch traced here: 150 us
  starting transfers between devices  63.6 us (42%)
  other arithmetic  35.1 us (23%)
  waiting for transfers between devices  33.4 us (22%)
  local copies, waits for them, and re-layouts  14.9 us (10%)
  between operations  2.05 us (1%)
    all_to_all x3, starting transfers between devices, swap_blocks(): return lax.all_to_all(x, 'blk', split_axis=0, concat_axis=0, tiled=True)  27.9 us
    ppermute x6, starting transfers between devices, shift_pair(): lax.ppermute(last, axis, up)  23.1 us
    ppermute x6, starting transfers between devices, shift_pair(): lax.ppermute(first, axis, [(b, a) for a, b in up])  12.6 us
    ppermute x6, waiting for transfers between devices, shift_pair(): lax.ppermute(last, axis, up)  12.4 us
    all_to_all x3, waiting for transfers between devices, swap_blocks(): return lax.all_to_all(x, 'blk', split_axis=0, concat_axis=0, tiled=True)  11.6 us
    ppermute x6, waiting for transfers between devices, shift_pair(): lax.ppermute(first, axis, [(b, a) for a, b in up])  9.44 us
    select_n x2, other arithmetic, current_of(): return jnp.where(live[:, None], found, 0.0).reshape(extent)  7.08 us
    mul x1, other arithmetic, on_device(): ours = weights * (v3 - PHASE_REF)  4.43 us
  transfers between devices with their start and end apart: 15, of which 6 were waited for; matrix products, arithmetic and copies ran while one was open for 18% of the time, Pallas kernels for 0%

profile of v1, /device:TPU:201, one launch (start us, length us, event | category | flops | bytes accessed | tf_op | source)
XLA Modules:
  0.0 150.1 jit_solution(16020695042883222924)
XLA Ops:
  0.7 0.9 copy_convert_fusion.1
  1.6 0.9 copy_convert_fusion
  2.5 1.0 copy_multiply_fusion.2
  3.7 5.8 %collective-permute-start = (f32[6,8,512]{2,0,1:T(8,128)S(1)}, f32[6,8,512]{2,0,1:T(8,128)S(1)}, u32[]{:S(2)}, u32[]{:S(2)}) collective-permute-start(f32[6,8,512]{2,0,1:T(8,128)S(1)} %pad_maximum_fusion.11), channel_id=1, source_target_pairs={{0,32},{32,64},{64,96},{96,128},{128,160},{160,192},{192,224},{224... | collective-permute-start | bytes 294920 | tf_op jit(solution)/shard_map/ppermute | solution.py:131
  9.6 1.9 %collective-permute-start.1 = (f32[6,8,512]{2,0,1:T(8,128)S(1)}, f32[6,8,512]{2,0,1:T(8,128)S(1)}, u32[]{:S(2)}, u32[]{:S(2)}) collective-permute-start(f32[6,8,512]{2,0,1:T(8,128)S(1)} %pad_maximum_fusion.12), channel_id=1, source_target_pairs={{32,0},{64,32},{96,64},{128,96},{160,128},{192,160},{224,192},{256... | collective-permute-start | bytes 294920 | tf_op jit(solution)/shard_map/ppermute | solution.py:131
  11.5 0.8 reshape.383
  13.1 9.6 %all-to-all-start = ((s32[32,1,128]{2,1,0:T(1,128)}), s32[32,1,128]{2,1,0:T(1,128)S(1)}, u32[]{:S(2)}, u32[]{:S(2)}) async-start(s32[32,1,128]{2,1,0:T(1,128)} %broadcast_in_dim.156), calls=%async_computation | async-start | bytes 32768 | tf_op jit(solution)/shard_map/all_to_all | solution.py:153
  22.7 0.8 reshape.384
  24.7 1.5 %fusion.298 = (f32[1]{0:T(128)}, f32[1]{0:T(128)}, f32[1]{0:T(128)}, f32[1]{0:T(128)}, f32[1]{0:T(128)}, /*index=5*/f32[1]{0:T(128)}) fusion(f32[6]{0:T(128)} %param.23), kind=kLoop, calls=%fused_computation.610 | loop fusion | bytes 48 | tf_op jit(solution)/shard_map/slice | solution.py:144
  26.2 1.5 stack_reshape.9
  28.0 2.4 %all-to-all-done = s32[32,1,128]{2,1,0:T(1,128)S(1)} async-done(((s32[32,1,128]{2,1,0:T(1,128)}), s32[32,1,128]{2,1,0:T(1,128)S(1)}, u32[]{:S(2)}, u32[]{:S(2)}) %all-to-all-start) | async-done | bytes 16416 | tf_op jit(solution)/shard_map/all_to_all | solution.py:153
  30.4 1.2 slice_reduce_fusion
  31.7 1.5 %gather_fusion = f32[32,48,128]{2,1,0:T(8,128)} fusion(f32[16,48,128]{2,1,0:T(8,128)S(1)} %reshape.382, s32[1024]{0:T(1024)S(1)} %get-tuple-element.107), kind=kCustom, calls=%fused_computation | custom fusion | bytes 1572992 | tf_op jit(solution)/shard_map/gather | solution.py:196
  33.2 6.8 %all-to-all-start.1 = ((f32[32,48,128]{2,1,0:T(8,128)}), f32[32,48,128]{2,1,0:T(8,128)S(1)}, u32[]{:S(2)}, u32[]{:S(2)}) async-start(f32[32,48,128]{2,1,0:T(8,128)} %gather_fusion), calls=%async_computation.1 | async-start | bytes 1572864 | tf_op jit(solution)/shard_map/all_to_all | solution.py:153
  41.0 3.1 %collective-permute-start.2 = (f32[42,512]{1,0:T(8,128)S(1)}, f32[42,512]{1,0:T(8,128)S(1)}, u32[]{:S(2)}, u32[]{:S(2)}) collective-permute-start(f32[42,512]{1,0:T(8,128)S(1)} %concatenate.112), channel_id=1, source_target_pairs={{0,1},{1,2},{2,3},{3,4},{4,5},{5,6},{6,7},{7,8},{8,9},{9,10},{10,1... | collective-permute-start | bytes 258056 | tf_op jit(solution)/shard_map/ppermute | solution.py:131
  44.6 2.4 %collective-permute-start.3 = (f32[42,512]{1,0:T(8,128)S(1)}, f32[42,512]{1,0:T(8,128)S(1)}, u32[]{:S(2)}, u32[]{:S(2)}) collective-permute-start(f32[42,512]{1,0:T(8,128)S(1)} %concatenate.113), channel_id=1, source_target_pairs={{1,0},{2,1},{3,2},{4,3},{5,4},{6,5},{7,6},{8,7},{9,8},{10,9},{11,1... | collective-permute-start | bytes 258056 | tf_op jit(solution)/shard_map/ppermute | solution.py:131
  47.1 12.4 %collective-permute-done.2 = f32[42,512]{1,0:T(8,128)S(1)} collective-permute-done((f32[42,512]{1,0:T(8,128)S(1)}, f32[42,512]{1,0:T(8,128)S(1)}, u32[]{:S(2)}, u32[]{:S(2)}) %collective-permute-start.2) | collective-permute-done | bytes 86048 | tf_op jit(solution)/shard_map/ppermute | solution.py:131
  59.6 1.8 %collective-permute-done.3 = f32[42,512]{1,0:T(8,128)S(1)} collective-permute-done((f32[42,512]{1,0:T(8,128)S(1)}, f32[42,512]{1,0:T(8,128)S(1)}, u32[]{:S(2)}, u32[]{:S(2)}) %collective-permute-start.3) | collective-permute-done | bytes 86048 | tf_op jit(solution)/shard_map/ppermute | solution.py:131
  61.9 1.1 multiply_bitcast_fusion
  64.2 1.1 select_maximum_fusion
  65.6 1.4 fusion.107
  67.1 0.8 slice_bitcast_fusion.37
  68.7 0.8 slice_bitcast_fusion.31
  69.5 0.7 pad_maximum_fusion.2
  71.1 0.8 fusion.285
  71.9 0.7 fusion.239
  73.4 1.5 fusion.13
  74.9 3.9 %fusion.207 = (f32[4,8,512]{2,1,0:T(8,128)S(1)}, f32[1,32,512]{2,1,0:T(8,128)S(1)}, f32[4,8,512]{2,1,0:T(8,128)S(1)}) fusion(f32[12,32,512]{2,1,0:T(8,128)S(1)} %get-tuple-element.26, f32[]{:T(128)} %bitcast.50, f32[]{:T(128)} %bitcast.48, f32[]{:T(128)} %bitcast.35, pred[4,8]{1,0:T(4,128)(4,1)S(1)} %broadcast_compare_fusion, f32[]{:T(128)} %bitcast.44, ...), kind=kLoop, calls=%fused_computation.373 | loop fusion | flops 1212416 | bytes 1966136 | tf_op jit(solution)/shard_map/jit(_where)/select_n | solution.py:241
  78.9 3.2 %fusion.197 = f32[32,512]{1,0:T(8,128)S(1)} fusion(f32[1,32,512]{2,1,0:T(8,128)S(1)} %get-tuple-element.24, f32[12,32,512]{2,1,0:T(8,128)S(1)} %get-tuple-element.26, f32[]{:T(128)} %bitcast.50, f32[]{:T(128)} %bitcast.48, f32[]{:T(128)} %bitcast.35, pred[32]{0:T(512)(128)(4,1)S(1)} %copy-done.27, f32[]{:T(128)} %bitcast.44, f32[]{:T(128)} %bitcast.46, ...), kind=kLoop, calls=%fused_computation.363 | loop fusion | flops 507904 | bytes 720948 | tf_op jit(solution)/shard_map/jit(_where)/select_n | solution.py:241
  82.2 3.1 %collective-permute-start.4 = (f32[3,8,512]{2,0,1:T(4,128)S(1)}, f32[3,8,512]{2,0,1:T(4,128)S(1)}, u32[]{:S(2)}, u32[]{:S(2)}) collective-permute-start(f32[3,8,512]{2,0,1:T(4,128)S(1)} %pad_maximum_fusion.17), channel_id=1, source_target_pairs={{0,32},{32,64},{64,96},{96,128},{128,160},{160,192},{192,224},{224... | collective-permute-start | bytes 147464 | tf_op jit(solution)/shard_map/ppermute | solution.py:131
  85.3 1.9 %collective-permute-start.5 = (f32[3,8,512]{2,0,1:T(4,128)S(1)}, f32[3,8,512]{2,0,1:T(4,128)S(1)}, u32[]{:S(2)}, u32[]{:S(2)}) collective-permute-start(f32[3,8,512]{2,0,1:T(4,128)S(1)} %pad_maximum_fusion.18), channel_id=1, source_target_pairs={{32,0},{64,32},{96,64},{128,96},{160,128},{192,160},{224,192},{256... | collective-permute-start | bytes 147464 | tf_op jit(solution)/shard_map/ppermute | solution.py:131
  87.2 0.8 fusion.24
  88.1 4.0 %collective-permute-done.5 = f32[3,8,512]{2,0,1:T(4,128)S(1)} collective-permute-done((f32[3,8,512]{2,0,1:T(4,128)S(1)}, f32[3,8,512]{2,0,1:T(4,128)S(1)}, u32[]{:S(2)}, u32[]{:S(2)}) %collective-permute-start.5) | collective-permute-done | bytes 49184 | tf_op jit(solution)/shard_map/ppermute | solution.py:131
  92.3 2.9 %collective-permute-start.6 = (f32[22,512]{1,0:T(8,128)S(1)}, f32[22,512]{1,0:T(8,128)S(1)}, u32[]{:S(2)}, u32[]{:S(2)}) collective-permute-start(f32[22,512]{1,0:T(8,128)S(1)} %pad_maximum_fusion.19), channel_id=1, source_target_pairs={{0,1},{1,2},{2,3},{3,4},{4,5},{5,6},{6,7},{7,8},{8,9},{9,10},{10,1... | collective-permute-start | bytes 135176 | tf_op jit(solution)/shard_map/ppermute | solution.py:131
  95.3 2.6 %collective-permute-start.7 = (f32[22,512]{1,0:T(8,128)S(1)}, f32[22,512]{1,0:T(8,128)S(1)}, u32[]{:S(2)}, u32[]{:S(2)}) collective-permute-start(f32[22,512]{1,0:T(8,128)S(1)} %pad_maximum_fusion.20), channel_id=1, source_target_pairs={{1,0},{2,1},{3,2},{4,3},{5,4},{6,5},{7,6},{8,7},{9,8},{10,9},{11,1... | collective-permute-start | bytes 135176 | tf_op jit(solution)/shard_map/ppermute | solution.py:131
  97.9 3.7 %collective-permute-done.7 = f32[22,512]{1,0:T(8,128)S(1)} collective-permute-done((f32[22,512]{1,0:T(8,128)S(1)}, f32[22,512]{1,0:T(8,128)S(1)}, u32[]{:S(2)}, u32[]{:S(2)}) %collective-permute-start.7) | collective-permute-done | bytes 45088 | tf_op jit(solution)/shard_map/ppermute | solution.py:131
  103.5 1.2 fusion.167
  104.8 1.4 fusion.144
  106.4 4.4 %add_multiply_fusion.13 = (f32[4,8,512]{2,1,0:T(8,128)S(1)}, f32[4,8,512]{2,1,0:T(8,128)}) fusion(f32[4,8,512]{2,0,1:T(4,128)S(1)} %copy_convert_fusion.1, f32[]{:T(128)} %bitcast.50, f32[12,32,512]{2,1,0:T(8,128)S(1)} %fusion.24, f32[]{:T(128)} %bitcast.48, f32[]{:T(128)} %bitcast.46, f32[]{:T(128)} %bitcast.44, f32[]{:T(128)} %bitcast.42, f32[]{:T(128)} %bitcast.35, ...), kind=kLoop, calls=%fused_computation.503 | loop fusion | flops 720896 | bytes 1310776 | tf_op jit(solution)/shard_map/mul | solution.py:274
  110.9 1.9 %collective-permute-start.10 = (f32[1,8,512]{2,1,0:T(8,128)S(1)}, f32[1,8,512]{2,1,0:T(8,128)S(1)}, u32[]{:S(2)}, u32[]{:S(2)}) collective-permute-start(f32[1,8,512]{2,1,0:T(8,128)S(1)} %get-tuple-element.79), channel_id=1, source_target_pairs={{32,0},{64,32},{96,64},{128,96},{160,128},{192,160},{224,192},{256... | collective-permute-start | bytes 49160 | tf_op jit(solution)/shard_map/ppermute | solution.py:131
  112.8 4.9 %collective-permute-start.9 = (f32[1,8,512]{2,1,0:T(8,128)S(1)}, f32[1,8,512]{2,1,0:T(8,128)S(1)}, u32[]{:S(2)}, u32[]{:S(2)}) collective-permute-start(f32[1,8,512]{2,1,0:T(8,128)S(1)} %get-tuple-element.78), channel_id=1, source_target_pairs={{0,32},{32,64},{64,96},{96,128},{128,160},{160,192},{192,224},{224... | collective-permute-start | bytes 49160 | tf_op jit(solution)/shard_map/ppermute | solution.py:131
  117.7 1.9 %collective-permute-start.11 = (f32[4,1,512]{2,1,0:T(1,128)S(1)}, f32[4,1,512]{2,1,0:T(1,128)S(1)}, u32[]{:S(2)}, u32[]{:S(2)}) collective-permute-start(f32[4,1,512]{2,1,0:T(1,128)S(1)} %get-tuple-element.81), channel_id=1, source_target_pairs={{1,0},{2,1},{3,2},{4,3},{5,4},{6,5},{7,6},{8,7},{9,8},{10,9},{11,1... | collective-permute-start | bytes 24584 | tf_op jit(solution)/shard_map/ppermute | solution.py:131
  119.6 3.4 %collective-permute-start.8 = (f32[4,1,512]{2,1,0:T(1,128)S(1)}, f32[4,1,512]{2,1,0:T(1,128)S(1)}, u32[]{:S(2)}, u32[]{:S(2)}) collective-permute-start(f32[4,1,512]{2,1,0:T(1,128)S(1)} %get-tuple-element.80), channel_id=1, source_target_pairs={{0,1},{1,2},{2,3},{3,4},{4,5},{5,6},{6,7},{7,8},{8,9},{9,10},{10,1... | collective-permute-start | bytes 24584 | tf_op jit(solution)/shard_map/ppermute | solution.py:131
  123.2 1.3 gather_fusion.2
  124.5 11.5 %all-to-all-start.2 = ((f32[32,12,128]{2,1,0:T(8,128)}), f32[32,12,128]{2,1,0:T(8,128)S(1)}, u32[]{:S(2)}, u32[]{:S(2)}) async-start(f32[32,12,128]{2,1,0:T(8,128)} %gather_fusion.2), calls=%async_computation.2 | async-start | bytes 524288 | tf_op jit(solution)/shard_map/all_to_all | solution.py:153
  136.8 1.0 add_multiply_fusion.11
  138.5 9.2 %all-to-all-done.2 = f32[32,12,128]{2,1,0:T(8,128)S(1)} async-done(((f32[32,12,128]{2,1,0:T(8,128)}), f32[32,12,128]{2,1,0:T(8,128)S(1)}, u32[]{:S(2)}, u32[]{:S(2)}) %all-to-all-start.2) | async-done | bytes 196640 | tf_op jit(solution)/shard_map/all_to_all | solution.py:153
  148.4 1.6 %fusion.36 = f32[12,16,512]{2,1,0:T(8,128)} fusion(f32[12,16,512]{2,1,0:T(8,128)S(1)} %copy-done.17, f32[12]{0:T(128)S(1)} %copy-done.22, f32[12]{0:T(128)S(1)} %copy-done.23, f32[16,512]{1,0:T(8,128)S(1)} %bitcast.336, f32[16,512]{1,0:T(8,128)S(1)} %bitcast.337, f32[12]{0:T(128)S(1)} %copy-done.24, f32[16,512]{1,0:T(8,128)S(1)} %bitcast.338, ...), kind=kLoop, calls=%fused_computation.82 | loop fusion | flops 4128768 | bytes 884928 | tf_op jit(solution)/shard_map/add | solution.py:139
  (194 shorter events, 13.2 us)
Async XLA Ops:
  0.6 61.3 %copy-start = (f32[6,16]{1,0:T(8,128)S(1)}, f32[6,16]{1,0:T(8,128)}, u32[]{:S(2)}) copy-start(f32[6,16]{1,0:T(8,128)} %param.16) | copy-start | bytes 1156
  0.6 27.1 %copy-start.16 = (f32[12,16,512]{2,1,0:T(8,128)S(1)}, f32[12,16,512]{2,1,0:T(8,128)}, u32[]{:S(2)}) copy-start(f32[12,16,512]{2,1,0:T(8,128)} %param.18) | copy-start | bytes 1179652
  3.7 36.4 %collective-permute-start = (f32[6,8,512]{2,0,1:T(8,128)S(1)}, f32[6,8,512]{2,0,1:T(8,128)S(1)}, u32[]{:S(2)}, u32[]{:S(2)}) collective-permute-start(f32[6,8,512]{2,0,1:T(8,128)S(1)} %pad_maximum_fusion.11), channel_id=1, source_target_pairs={{0,32},{32,64},{64,96},{96,128},{128,160},{160,192},{192,224},{224... | collective-permute-start | bytes 294920 | tf_op jit(solution)/shard_map/ppermute | solution.py:131
  9.6 30.6 %collective-permute-start.1 = (f32[6,8,512]{2,0,1:T(8,128)S(1)}, f32[6,8,512]{2,0,1:T(8,128)S(1)}, u32[]{:S(2)}, u32[]{:S(2)}) collective-permute-start(f32[6,8,512]{2,0,1:T(8,128)S(1)} %pad_maximum_fusion.12), channel_id=1, source_target_pairs={{32,0},{64,32},{96,64},{128,96},{160,128},{192,160},{224,192},{256... | collective-permute-start | bytes 294920 | tf_op jit(solution)/shard_map/ppermute | solution.py:131
  13.1 17.3 %all-to-all-start = ((s32[32,1,128]{2,1,0:T(1,128)}), s32[32,1,128]{2,1,0:T(1,128)S(1)}, u32[]{:S(2)}, u32[]{:S(2)}) async-start(s32[32,1,128]{2,1,0:T(1,128)} %broadcast_in_dim.156), calls=%async_computation | async-start | bytes 32768 | tf_op jit(solution)/shard_map/all_to_all | solution.py:153
  33.2 39.4 %all-to-all-start.1 = ((f32[32,48,128]{2,1,0:T(8,128)}), f32[32,48,128]{2,1,0:T(8,128)S(1)}, u32[]{:S(2)}, u32[]{:S(2)}) async-start(f32[32,48,128]{2,1,0:T(8,128)} %gather_fusion), calls=%async_computation.1 | async-start | bytes 1572864 | tf_op jit(solution)/shard_map/all_to_all | solution.py:153
  41.0 18.5 %collective-permute-start.2 = (f32[42,512]{1,0:T(8,128)S(1)}, f32[42,512]{1,0:T(8,128)S(1)}, u32[]{:S(2)}, u32[]{:S(2)}) collective-permute-start(f32[42,512]{1,0:T(8,128)S(1)} %concatenate.112), channel_id=1, source_target_pairs={{0,1},{1,2},{2,3},{3,4},{4,5},{5,6},{6,7},{7,8},{8,9},{9,10},{10,1... | collective-permute-start | bytes 258056 | tf_op jit(solution)/shard_map/ppermute | solution.py:131
  44.6 16.8 %collective-permute-start.3 = (f32[42,512]{1,0:T(8,128)S(1)}, f32[42,512]{1,0:T(8,128)S(1)}, u32[]{:S(2)}, u32[]{:S(2)}) collective-permute-start(f32[42,512]{1,0:T(8,128)S(1)} %concatenate.113), channel_id=1, source_target_pairs={{1,0},{2,1},{3,2},{4,3},{5,4},{6,5},{7,6},{8,7},{9,8},{10,9},{11,1... | collective-permute-start | bytes 258056 | tf_op jit(solution)/shard_map/ppermute | solution.py:131
  59.5 2.1 %copy-start.21 = (f32[42,512]{1,0:T(8,128)}, f32[42,512]{1,0:T(8,128)S(1)}, u32[]{:S(2)}) copy-start(f32[42,512]{1,0:T(8,128)S(1)} %collective-permute-done.2) | copy-start | bytes 258052
  64.2 1.3 copy-start.1
  65.3 5.5 %copy-start.3 = (f32[1,7,10,512]{3,1,2,0:T(8,128)}, f32[1,7,10,512]{3,1,2,0:T(8,128)S(1)}, u32[]{:S(2)}) copy-start(f32[1,7,10,512]{3,1,2,0:T(8,128)S(1)} %copy.1295) | copy-start | bytes 430084
  65.4 5.4 %copy-start.5 = (f32[1,7,10,512]{3,1,2,0:T(8,128)}, f32[1,7,10,512]{3,1,2,0:T(8,128)S(1)}, u32[]{:S(2)}) copy-start(f32[1,7,10,512]{3,1,2,0:T(8,128)S(1)} %copy.1296) | copy-start | bytes 430084
  65.4 5.4 %copy-start.7 = (f32[1,7,10,512]{3,1,2,0:T(8,128)}, f32[1,7,10,512]{3,1,2,0:T(8,128)S(1)}, u32[]{:S(2)}) copy-start(f32[1,7,10,512]{3,1,2,0:T(8,128)S(1)} %copy.1297) | copy-start | bytes 430084
  65.5 5.6 %copy-start.14 = (f32[1,6,11,512]{3,1,2,0:T(8,128)}, f32[1,6,11,512]{3,1,2,0:T(8,128)S(1)}, u32[]{:S(2)}) copy-start(f32[1,6,11,512]{3,1,2,0:T(8,128)S(1)} %copy.1292) | copy-start | bytes 405508
  65.6 5.5 %copy-start.15 = (f32[1,6,11,512]{3,1,2,0:T(8,128)}, f32[1,6,11,512]{3,1,2,0:T(8,128)S(1)}, u32[]{:S(2)}) copy-start(f32[1,6,11,512]{3,1,2,0:T(8,128)S(1)} %copy.1294) | copy-start | bytes 405508
  67.0 4.0 %copy-start.10 = (f32[1,6,10,513]{3,1,2,0:T(8,128)}, f32[1,6,10,513]{3,1,2,0:T(8,128)S(1)}, u32[]{:S(2)}) copy-start(f32[1,6,10,513]{3,1,2,0:T(8,128)S(1)} %copy.1289) | copy-start | bytes 369364
  67.1 4.0 %copy-start.11 = (f32[1,6,10,513]{3,1,2,0:T(8,128)}, f32[1,6,10,513]{3,1,2,0:T(8,128)S(1)}, u32[]{:S(2)}) copy-start(f32[1,6,10,513]{3,1,2,0:T(8,128)S(1)} %copy.1290) | copy-start | bytes 369364
  67.1 3.9 %copy-start.12 = (f32[1,6,10,513]{3,1,2,0:T(8,128)}, f32[1,6,10,513]{3,1,2,0:T(8,128)S(1)}, u32[]{:S(2)}) copy-start(f32[1,6,10,513]{3,1,2,0:T(8,128)S(1)} %copy.1291) | copy-start | bytes 369364
  71.9 1.5 copy-start.9
  71.9 1.5 copy-start.22
  71.9 1.5 %copy-start.23 = (f32[12]{0:T(128)S(1)}, f32[12]{0:T(128)}, u32[]{:S(2)}) copy-start(f32[12]{0:T(128)} %param.21) | copy-start | bytes 148
  73.4 1.5 %copy-start.19 = (f32[4,8,512]{2,0,1:T(4,128)S(1)}, f32[4,8,512]{2,0,1:T(4,128)}, u32[]{:S(2)}) copy-start(f32[4,8,512]{2,0,1:T(4,128)} %fusion.239) | copy-start | bytes 196612
  73.4 5.5 %copy-start.27 = (pred[32]{0:T(512)(128)(4,1)S(1)}, pred[32]{0:T(512)(128)(4,1)}, u32[]{:S(2)}) copy-start(pred[32]{0:T(512)(128)(4,1)} %broadcast_compare_fusion.1) | copy-start | bytes 100
  74.9 12.4 %copy-start.24 = (f32[12]{0:T(128)S(1)}, f32[12]{0:T(128)}, u32[]{:S(2)}) copy-start(f32[12]{0:T(128)} %param.19) | copy-start | bytes 148
  74.9 12.4 %copy-start.25 = (f32[12]{0:T(128)S(1)}, f32[12]{0:T(128)}, u32[]{:S(2)}) copy-start(f32[12]{0:T(128)} %param.20) | copy-start | bytes 148
  82.2 5.9 %collective-permute-start.4 = (f32[3,8,512]{2,0,1:T(4,128)S(1)}, f32[3,8,512]{2,0,1:T(4,128)S(1)}, u32[]{:S(2)}, u32[]{:S(2)}) collective-permute-start(f32[3,8,512]{2,0,1:T(4,128)S(1)} %pad_maximum_fusion.17), channel_id=1, source_target_pairs={{0,32},{32,64},{64,96},{96,128},{128,160},{160,192},{192,224},{224... | collective-permute-start | bytes 147464 | tf_op jit(solution)/shard_map/ppermute | solution.py:131
  85.3 6.8 %collective-permute-start.5 = (f32[3,8,512]{2,0,1:T(4,128)S(1)}, f32[3,8,512]{2,0,1:T(4,128)S(1)}, u32[]{:S(2)}, u32[]{:S(2)}) collective-permute-start(f32[3,8,512]{2,0,1:T(4,128)S(1)} %pad_maximum_fusion.18), channel_id=1, source_target_pairs={{32,0},{64,32},{96,64},{128,96},{160,128},{192,160},{224,192},{256... | collective-permute-start | bytes 147464 | tf_op jit(solution)/shard_map/ppermute | solution.py:131
  88.0 13.9 %copy-start.2 = (f32[1,6,11,512]{3,0,2,1:T(1,128)S(1)}, f32[1,6,11,512]{3,0,2,1:T(1,128)}, u32[]{:S(2)}) copy-start(f32[1,6,11,512]{3,0,2,1:T(1,128)} %copy-done.1) | copy-start | bytes 405508
  92.3 5.5 %collective-permute-start.6 = (f32[22,512]{1,0:T(8,128)S(1)}, f32[22,512]{1,0:T(8,128)S(1)}, u32[]{:S(2)}, u32[]{:S(2)}) collective-permute-start(f32[22,512]{1,0:T(8,128)S(1)} %pad_maximum_fusion.19), channel_id=1, source_target_pairs={{0,1},{1,2},{2,3},{3,4},{4,5},{5,6},{6,7},{7,8},{8,9},{9,10},{10,1... | collective-permute-start | bytes 135176 | tf_op jit(solution)/shard_map/ppermute | solution.py:131
  95.3 6.4 %collective-permute-start.7 = (f32[22,512]{1,0:T(8,128)S(1)}, f32[22,512]{1,0:T(8,128)S(1)}, u32[]{:S(2)}, u32[]{:S(2)}) collective-permute-start(f32[22,512]{1,0:T(8,128)S(1)} %pad_maximum_fusion.20), channel_id=1, source_target_pairs={{1,0},{2,1},{3,2},{4,3},{5,4},{6,5},{7,6},{8,7},{9,8},{10,9},{11,1... | collective-permute-start | bytes 135176 | tf_op jit(solution)/shard_map/ppermute | solution.py:131
  102.0 0.9 copy-start.13
  102.2 1.0 copy-start.4
  102.2 1.0 copy-start.6
  102.2 1.1 copy-start.8
  102.9 3.4 %copy-start.18 = (f32[4,9,512]{2,0,1:T(4,128)S(1)}, f32[4,9,512]{2,0,1:T(4,128)}, u32[]{:S(2)}) copy-start(f32[4,9,512]{2,0,1:T(4,128)} %get-tuple-element.39) | copy-start | bytes 221188
  103.5 19.5 %copy-start.20 = (f32[32,1,4,128]{3,2,0,1:T(4,128)S(1)}, f32[32,1,4,128]{3,2,0,1:T(4,128)}, u32[]{:S(2)}) copy-start(f32[32,1,4,128]{3,2,0,1:T(4,128)} %stack_reshape.9) | copy-start | bytes 196612
  110.9 25.2 %collective-permute-start.10 = (f32[1,8,512]{2,1,0:T(8,128)S(1)}, f32[1,8,512]{2,1,0:T(8,128)S(1)}, u32[]{:S(2)}, u32[]{:S(2)}) collective-permute-start(f32[1,8,512]{2,1,0:T(8,128)S(1)} %get-tuple-element.79), channel_id=1, source_target_pairs={{32,0},{64,32},{96,64},{128,96},{160,128},{192,160},{224,192},{256... | collective-permute-start | bytes 49160 | tf_op jit(solution)/shard_map/ppermute | solution.py:131
  112.8 23.3 %collective-permute-start.9 = (f32[1,8,512]{2,1,0:T(8,128)S(1)}, f32[1,8,512]{2,1,0:T(8,128)S(1)}, u32[]{:S(2)}, u32[]{:S(2)}) collective-permute-start(f32[1,8,512]{2,1,0:T(8,128)S(1)} %get-tuple-element.78), channel_id=1, source_target_pairs={{0,32},{32,64},{64,96},{96,128},{128,160},{160,192},{192,224},{224... | collective-permute-start | bytes 49160 | tf_op jit(solution)/shard_map/ppermute | solution.py:131
  117.7 18.4 %collective-permute-start.11 = (f32[4,1,512]{2,1,0:T(1,128)S(1)}, f32[4,1,512]{2,1,0:T(1,128)S(1)}, u32[]{:S(2)}, u32[]{:S(2)}) collective-permute-start(f32[4,1,512]{2,1,0:T(1,128)S(1)} %get-tuple-element.81), channel_id=1, source_target_pairs={{1,0},{2,1},{3,2},{4,3},{5,4},{6,5},{7,6},{8,7},{9,8},{10,9},{11,1... | collective-permute-start | bytes 24584 | tf_op jit(solution)/shard_map/ppermute | solution.py:131
  119.6 16.5 %collective-permute-start.8 = (f32[4,1,512]{2,1,0:T(1,128)S(1)}, f32[4,1,512]{2,1,0:T(1,128)S(1)}, u32[]{:S(2)}, u32[]{:S(2)}) collective-permute-start(f32[4,1,512]{2,1,0:T(1,128)S(1)} %get-tuple-element.80), channel_id=1, source_target_pairs={{0,1},{1,2},{2,3},{3,4},{4,5},{5,6},{6,7},{7,8},{8,9},{9,10},{10,1... | collective-permute-start | bytes 24584 | tf_op jit(solution)/shard_map/ppermute | solution.py:131
  124.5 23.2 %all-to-all-start.2 = ((f32[32,12,128]{2,1,0:T(8,128)}), f32[32,12,128]{2,1,0:T(8,128)S(1)}, u32[]{:S(2)}, u32[]{:S(2)}) async-start(f32[32,12,128]{2,1,0:T(8,128)} %gather_fusion.2), calls=%async_computation.2 | async-start | bytes 524288 | tf_op jit(solution)/shard_map/all_to_all | solution.py:153
  136.0 12.4 %copy-start.17 = (f32[12,16,512]{2,1,0:T(8,128)S(1)}, f32[12,16,512]{2,1,0:T(8,128)}, u32[]{:S(2)}) copy-start(f32[12,16,512]{2,1,0:T(8,128)} %param.18) | copy-start | bytes 1179652
  136.0 12.4 %copy-start.26 = (f32[12]{0:T(128)S(1)}, f32[12]{0:T(128)}, u32[]{:S(2)}) copy-start(f32[12]{0:T(128)} %param.20) | copy-start | bytes 148

commit v2 on v1

v2 whole, which is shorter than its diff:
```python
import functools

import jax
import jax.numpy as jnp
from jax import lax
from jax.experimental import pallas as pl
from jax.experimental.pallas import tpu as pltpu
from jax.sharding import PartitionSpec as P

FIB = 16
STEPS = 3
GATES = 12
CX, CY, CZ = 4, 8, 512
TILES = CX * CY
LANES = 128
CHUNKS = CZ // LANES
CAP = 16
NI, NJ = CX + 4, 16


STEP_DT = 0.1
PHASE_REF = -0.2
PHASE_SOFT = 0.5
COMPONENT = ((0, 3, 4), (3, 1, 5), (4, 5, 2))
HALF, STEEP, TMIN, TSPAN, CHANNEL = 0, 12, 24, 36, 48

f32 = jnp.float32
VM = pl.BlockSpec(memory_space=pltpu.VMEM)
SM = pl.BlockSpec(memory_space=pltpu.SMEM)


def kernel_call(body, outs, ins, scratch=(), flops=1_000_000):
    return pl.pallas_call(
        body,
        out_shape=[jax.ShapeDtypeStruct(shape, f32) for shape in outs],
        in_specs=ins,
        out_specs=[VM] * len(outs),
        scratch_shapes=[pltpu.VMEM(shape, f32) for shape in scratch],
        cost_estimate=pl.CostEstimate(flops=flops, bytes_accessed=1_000_000, transcendentals=0),
        compiler_params=pltpu.CompilerParams(vmem_limit_bytes=40 * 1024 * 1024),
    )


def chunk(c):
    return pl.ds(c * LANES, LANES)


def to_dense(dense_ref, plane, i):
    for c in range(CHUNKS):
        dense_ref[pl.ds(i * CY * CHUNKS + c, CY, stride=CHUNKS), :] = plane[:, c * LANES : (c + 1) * LANES]


def from_dense(dense_ref, i, c):
    return dense_ref[pl.ds(i * CY * CHUNKS + c, CY, stride=CHUNKS), :]


def updated(level, state, par_ref, g):
    offset = level - par_ref[HALF + g]
    target = 1.0 / (1.0 + jnp.exp(-par_ref[STEEP + g] * offset))
    bell = 1.0 + 4.0 * (offset * offset)
    decay = jnp.exp((-STEP_DT * bell) / (par_ref[TMIN + g] * bell + par_ref[TSPAN + g]))
    return target + (state - target) * decay


def factors(s, par_ref):
    return (
        par_ref[CHANNEL] * s[0] * s[0] * s[0] * s[1] * s[2],
        par_ref[CHANNEL + 1] * s[3] * s[4] * s[5] * s[6],
        par_ref[CHANNEL + 2] * s[7] * s[8] + par_ref[CHANNEL + 3] * s[9] * s[10],
        par_ref[CHANNEL + 4] * s[11] * s[11],
    )


def current_from(level, parts, par_ref):
    inward = par_ref[CHANNEL + 5] * (level + 0.9) / (1.0 + jnp.exp(4.0 * (level + 0.6)))
    return (
        parts[0] * (level - 1.2)
        + parts[1] * (level - 1.0)
        + parts[2] * (level + 0.9)
        + parts[3] * (level + 0.8)
        + inward
    )


def start_body(voltage, lag, tissue, fiber, up_ref, down_ref):
    for ref, outer, pair in ((up_ref, CX - 1, (CX - 2, CX - 1)), (down_ref, 0, (0, 1))):
        w = tissue[outer].astype(f32)
        ref[0] = w * voltage[outer]
        ref[1] = w * (lag[outer] - PHASE_REF)
        for n, i in enumerate(pair):
            ref[2 + n] = fiber[i].astype(f32)
            ref[4 + n] = tissue[i].astype(f32)


def columns_body(voltage, lag, tissue, fiber, low, high, up_ref, down_ref):
    for ref, outer, pair in ((up_ref, CY - 1, (CY - 2, CY - 1)), (down_ref, 0, (0, 1))):
        one = slice(outer, outer + 1)
        ref[0:1] = low[0, one]
        ref[CX + 1 : CX + 2] = high[0, one]
        for i in range(CX):
            w = tissue[i, one].astype(f32)
            ref[1 + i : 2 + i] = w * voltage[i, one]
            ref[CX + 2 + i : CX + 3 + i] = w * (lag[i, one] - PHASE_REF)
        at = 2 * CX + 2
        for n, j in enumerate(pair):
            one = slice(j, j + 1)
            for m in range(2):
                for kind, base in ((2, at + n * NI), (4, at + (2 + n) * NI)):
                    ref[base + m : base + m + 1] = low[kind + m, one]
                    ref[base + CX + 2 + m : base + CX + 3 + m] = high[kind + m, one]
            for i in range(CX):
                ref[at + n * NI + 2 + i : at + n * NI + 3 + i] = fiber[i, one].astype(f32)
                ref[at + (2 + n) * NI + 2 + i : at + (2 + n) * NI + 3 + i] = tissue[i, one].astype(f32)


def by_row_body(gates, out_ref):
    for g in range(GATES):
        for c in range(CHUNKS):
            for k in range(0, CAP, 8):
                out_ref[pl.ds(k * GATES * CHUNKS + g * CHUNKS + c, 8, stride=GATES * CHUNKS), :] = gates[g, k : k + 8, chunk(c)]


def pack_body(slots, arrived, by_row, out_ref):
    for d in range(slots):
        k = jnp.maximum(arrived[d], 0)
        out_ref[d] = by_row[pl.ds(pl.multiple_of(k * GATES * CHUNKS, 8), GATES * CHUNKS), :]


def up_j(x):
    return pltpu.roll(x, NJ - 1, 0)


def down_j(x):
    return pltpu.roll(x, 1, 0)


def up_z(x):
    return pltpu.roll(x, CZ - 1, 1)


def down_z(x):
    return pltpu.roll(x, 1, 1)


def spread_of(f, face, first, last):
    z = lax.broadcasted_iota(jnp.int32, (NJ, CZ), 1)
    dy, dz = {}, {}
    for i in range(first - 1, last + 2):
        dy[i] = up_j(f[i]) - down_j(f[i])
        dz[i] = jnp.where(z == CZ - 1, 0.0, up_z(f[i])) - jnp.where(z == 0, 0.0, down_z(f[i]))
    along = {}
    for i in range(first - 1, last + 1):
        along[i] = (
            face(0, i) * (f[i + 1] - f[i])
            + face(1, i) * (0.25 * (dy[i] + dy[i + 1]))
            + face(2, i) * (0.25 * (dz[i] + dz[i + 1]))
        )
    total = {}
    for i in range(first, last + 1):
        dx = f[i + 1] - f[i - 1]
        flux_y = (
            face(4, i) * (up_j(f[i]) - f[i])
            + face(3, i) * (0.25 * (dx + up_j(dx)))
            + face(5, i) * (0.25 * (dz[i] + up_j(dz[i])))
        )
        flux_z = (
            face(8, i) * (up_z(f[i]) - f[i])
            + face(6, i) * (0.25 * (dx + up_z(dx)))
            + face(7, i) * (0.25 * (dy[i] + up_z(dy[i])))
        )
        total[i] = along[i] - along[i - 1] + flux_y - down_j(flux_y) + flux_z - down_z(flux_z)
    return total


def faces_body(voltage, tissue, fiber, low, high, left, right, cond, faces_ref, weights_ref, base_ref, field_ref, fib_ref, stack_ref):
    zero = jnp.zeros((NI, NJ, CZ), f32)
    field_ref[...] = zero
    fib_ref[...] = zero
    weights_ref[...] = zero
    own = slice(2, 2 + CY)
    for i in range(CX):
        w = tissue[i].astype(f32)
        field_ref[2 + i, own, :] = w * voltage[i]
        weights_ref[2 + i, own, :] = w
        fib_ref[2 + i, own, :] = fiber[i].astype(f32)
    for ref, base, at in ((low, 0, 1), (high, CX + 2, CX + 2)):
        field_ref[at, own, :] = ref[0]
        for m in range(2):
            fib_ref[base + m, own, :] = ref[2 + m]
            weights_ref[base + m, own, :] = ref[4 + m]
    at = 2 * CX + 2
    for ref, outer, cols in ((left, 1, (0, 1)), (right, 2 + CY, (2 + CY, 3 + CY))):
        for i in range(CX + 2):
            field_ref[1 + i, outer : outer + 1, :] = ref[i : i + 1, :]
        for n, j in enumerate(cols):
            for i in range(NI):
                fib_ref[i, j : j + 1, :] = ref[at + n * NI + i : at + n * NI + i + 1, :]
                weights_ref[i, j : j + 1, :] = ref[at + (2 + n) * NI + i : at + (2 + n) * NI + i + 1, :]

    def classes(i, carry):
        for c in range(CHUNKS):
            fib = fib_ref[i, :, chunk(c)]
            w = weights_ref[i, :, chunk(c)]
            found = [jnp.full((NJ, LANES), cond[n * FIB]) for n in range(6)]
            for k in range(1, FIB):
                here = fib == float(k)
                found = [jnp.where(here, cond[n * FIB + k], old) for n, old in enumerate(found)]
            for n in range(6):
                stack_ref[n, i, :, chunk(c)] = 0.5 * (w * found[n])
        return carry

    lax.fori_loop(0, NI, classes, 0)
    z = lax.broadcasted_iota(jnp.int32, (NJ, CZ), 1)
    for i in range(NI - 1):
        w = weights_ref[i]
        both = w * weights_ref[i + 1]
        for n, comp in enumerate(COMPONENT[0]):
            faces_ref[n, i] = (stack_ref[comp, i] + stack_ref[comp, i + 1]) * both
        if i == 0:
            continue
        both = w * up_j(w)
        for n, comp in enumerate(COMPONENT[1]):
            here = stack_ref[comp, i]
            faces_ref[3 + n, i] = (here + up_j(here)) * both
        both = w * jnp.where(z == CZ - 1, 0.0, up_z(w))
        for n, comp in enumerate(COMPONENT[2]):
            here = stack_ref[comp, i]
            faces_ref[6 + n, i] = (here + up_z(here)) * both
    field = {i: field_ref[i] for i in range(1, NI - 1)}
    spread = spread_of(field, lambda n, i: faces_ref[n, i], 2, CX + 1)
    for i in range(CX):
        base_ref[i] = voltage[i] + tissue[i].astype(f32) * spread[2 + i][2 : 2 + CY]


def react_body(holder, par, coming, voltage, base, tissue, live, v1_ref, current_ref, states_ref, v_d, base_d, w_d, live_d, out_d, cur_d):
    for i in range(CX):
        mask = jnp.concatenate([live[i]] * CHUNKS, axis=1)
        to_dense(v_d, voltage[i], i)
        to_dense(base_d, base[i], i)
        to_dense(w_d, tissue[i].astype(f32) * mask, i)
        to_dense(live_d, mask, i)

    def pair(p, carry):
        rows = pl.ds(pl.multiple_of(p * 8, 8), 8)
        first, second = holder[2 * p], holder[2 * p + 1]
        level = v_d[rows, :]
        states = [
            jnp.concatenate([coming[first, pl.ds(g * CHUNKS, CHUNKS), :], coming[second, pl.ds(g * CHUNKS, CHUNKS), :]], axis=0)
            for g in range(GATES)
        ]
        after = base_d[rows, :] - w_d[rows, :] * (STEP_DT * current_from(level, factors(states, par), par))
        states = [updated(level, s, par, g) for g, s in enumerate(states)]
        for g in range(GATES):
            states_ref[g, rows, :] = states[g]
        out_d[rows, :] = after
        cur_d[rows, :] = live_d[rows, :] * current_from(after, factors(states, par), par)
        return carry

    lax.fori_loop(0, TILES // 2, pair, 0)
    for i in range(CX):
        for c in range(CHUNKS):
            v1_ref[i, :, chunk(c)] = from_dense(out_d, i, c)
            current_ref[i, :, chunk(c)] = from_dense(cur_d, i, c)


def second_body(par, states_in, v1, parts_ref, v_d, parts_d):
    for i in range(CX):
        to_dense(v_d, v1[i], i)

    def pair(p, carry):
        rows = pl.ds(pl.multiple_of(p * 8, 8), 8)
        level = v_d[rows, :]
        states = [updated(level, states_in[g, rows, :], par, g) for g in range(GATES)]
        for n, part in enumerate(factors(states, par)):
            parts_d[n, rows, :] = part
        return carry

    lax.fori_loop(0, TILES // 2, pair, 0)
    for n in range(4):
        for i in range(CX):
            for c in range(CHUNKS):
                parts_ref[n, i, :, chunk(c)] = from_dense(parts_d.at[n], i, c)


def columns2_body(v1, current, low, high, up_ref, down_ref):
    for ref, pair in ((up_ref, (CY - 2, CY - 1)), (down_ref, (0, 1))):
        outer = CY - 1 if ref is up_ref else 0
        for n, j in enumerate(pair):
            one = slice(j, j + 1)
            for m in range(2):
                ref[n * NI + m : n * NI + m + 1] = low[m, one]
                ref[n * NI + CX + 2 + m : n * NI + CX + 3 + m] = high[m, one]
            for i in range(CX):
                ref[n * NI + 2 + i : n * NI + 3 + i] = v1[i, one]
        one = slice(outer, outer + 1)
        at = 2 * NI
        ref[at : at + 1] = low[2, one]
        ref[at + CX + 1 : at + CX + 2] = high[2, one]
        for i in range(CX):
            ref[at + 1 + i : at + 2 + i] = current[i, one]


def steps_body(slots, tile_of, par, v0, v1, current, low, high, left, right, weights, faces, parts, live, v3_ref, ours_ref, used_ref, v_ref, cur_ref, next_ref, rows_ref):
    v_ref[...] = jnp.zeros((NI, NJ, CZ), f32)
    cur_ref[...] = jnp.zeros((NI, NJ, CZ), f32)
    own = slice(2, 2 + CY)
    for i in range(CX):
        v_ref[2 + i, own, :] = v1[i]
        cur_ref[2 + i, own, :] = current[i]
    for m in range(2):
        v_ref[m, own, :] = low[m]
        v_ref[CX + 2 + m, own, :] = high[m]
    cur_ref[1, own, :] = low[2]
    cur_ref[CX + 2, own, :] = high[2]
    for ref, cols, outer in ((left, (0, 1), 1), (right, (2 + CY, 3 + CY), 2 + CY)):
        for n, j in enumerate(cols):
            for i in range(NI):
                v_ref[i, j : j + 1, :] = ref[n * NI + i : n * NI + i + 1, :]
        for i in range(CX + 2):
            cur_ref[1 + i, outer : outer + 1, :] = ref[2 * NI + i : 2 * NI + i + 1, :]
    face = lambda n, i: faces[n, i]
    field = {i: weights[i] * v_ref[i] for i in range(NI)}
    spread = spread_of(field, face, 1, NI - 2)
    for i in range(1, NI - 1):
        next_ref[i] = v_ref[i] + weights[i] * (spread[i] - STEP_DT * cur_ref[i])
    field = {i: weights[i] * next_ref[i] for i in range(1, NI - 1)}
    spread = spread_of(field, face, 2, CX + 1)
    for i in range(CX):
        v2 = next_ref[2 + i, own, :]
        w = weights[2 + i, own, :]
        mask = jnp.concatenate([live[i]] * CHUNKS, axis=1)
        found = mask * current_from(v2, [parts[n, i] for n in range(4)], par)
        v3 = v2 + w * (spread[2 + i][own] - STEP_DT * found)
        v3_ref[i] = v3
        ours_ref[i] = w * (v3 - PHASE_REF)
        for n, v in enumerate((v0[i], v1[i], v2)):
            for c in range(CHUNKS):
                rows_ref[pl.ds(i * CY * 16 + n * CHUNKS + c, CY, stride=16), :] = v[:, c * LANES : (c + 1) * LANES]
        for c in range(CHUNKS):
            rows_ref[pl.ds(i * CY * 16 + 3 * CHUNKS + c, CY, stride=16), :] = jnp.zeros((CY, LANES), f32)
    for d in range(slots):
        used_ref[d] = rows_ref[pl.ds(pl.multiple_of(tile_of[d] * 16, 16), 16), :]


def last_body(slots, arrived, par, returned, gates, out_ref, rows_ref):
    for d in range(slots):
        k = arrived[d]
        row = jnp.where(k >= 0, k, CAP)
        rows_ref[pl.ds(pl.multiple_of(row * 16, 16), 16), :] = returned[d]

    def one(g, carry):
        for k in range(0, CAP, 8):
            for c in range(CHUNKS):
                state = gates[g, k : k + 8, chunk(c)]
                for n in range(STEPS):
                    state = updated(rows_ref[pl.ds(k * 16 + n * CHUNKS + c, 8, stride=16), :], state, par, g)
                out_ref[g, k : k + 8, chunk(c)] = state
        return carry

    lax.fori_loop(0, GATES, one, 0)


def shift_pair(axis, last, first):
    size = lax.axis_size(axis)
    up = [(i, i + 1) for i in range(size - 1)]
    return (lax.ppermute(last, axis, up), lax.ppermute(first, axis, [(b, a) for a, b in up]))


def swap_blocks(x):
    return lax.all_to_all(x, "blk", split_axis=0, concat_axis=0, tiled=True)


def basis(direction, amount):
    return tuple((amount if position == direction else 0 for position in range(3)))


def window(array, starts, extent):
    leading = array.ndim - 3
    begin = (0,) * leading + tuple(starts)
    finish = tuple(array.shape[:leading]) + tuple(
        (first + count for first, count in zip(starts, extent))
    )
    return lax.slice(array, begin, finish)


def edge_term(first, second):
    cross = first[0] * second[1] - first[1] * second[0]
    inner = first[0] * second[0] + first[1] * second[1]
    norm_value = jnp.sqrt(
        (first[0] * first[0] + first[1] * first[1])
        * (second[0] * second[0] + second[1] * second[1])
    )
    return 2.0 * jnp.arctan(cross / (norm_value + inner + PHASE_SOFT))


def charges(padded_phase, extent):
    results = []
    for first_dim, second_dim in ((0, 1), (1, 2), (0, 2)):
        corners = [
            basis(first_dim, 1),
            basis(second_dim, 1),
            basis(first_dim, -1),
            basis(second_dim, -1),
        ]
        points = [
            window(padded_phase, tuple((1 + value for value in corner)), extent)
            for corner in corners
        ]
        circulation = jnp.zeros(extent, jnp.float32)
        for position in range(4):
            circulation = circulation + edge_term(points[position], points[(position + 1) % 4])
        results.append(circulation)
    return jnp.stack(results)


def pad_depth(array):
    return jnp.pad(array, [(0, 0)] * (array.ndim - 1) + [(1, 1)])


def on_device(
    voltage,
    voltage_lag,
    tissue,
    fiber,
    conductivity,
    worker,
    gates,
    gate_half,
    gate_steep,
    gate_tmin,
    gate_tspan,
    channel,
):
    block = voltage.shape
    slots = lax.axis_size("blk")
    par = jnp.concatenate([gate_half, gate_steep, gate_tmin, gate_tspan, channel])
    cond = conductivity.reshape(-1)

    targets = worker.reshape(-1)
    live = targets >= 0
    holder = jnp.where(live, targets // CAP, -1)
    claimed = holder[None, :] == jnp.arange(slots, dtype=jnp.int32)[:, None]
    claims = jnp.sum(jnp.where(claimed, targets % CAP + 1, 0), axis=1) - 1
    tile_of = jnp.sum(jnp.where(claimed, jnp.arange(TILES, dtype=jnp.int32)[None, :], 0), axis=1)
    arrived = swap_blocks(jnp.broadcast_to(claims[:, None, None], (slots, 1, LANES)))[:, 0, 0]
    mask = jnp.broadcast_to((worker >= 0).astype(f32)[:, :, None], (CX, CY, LANES))

    rim = (6, CY, CZ)
    up, down = kernel_call(start_body, [rim, rim], [VM] * 4)(voltage, voltage_lag, tissue, fiber)
    low, high = shift_pair("slab", up, down)
    (by_row,) = kernel_call(by_row_body, [(CAP * GATES * CHUNKS, LANES)], [VM])(gates)

    run = (slots, GATES * CHUNKS, LANES)
    (leaving,) = kernel_call(functools.partial(pack_body, slots), [run], [SM, VM])(arrived, by_row)
    coming = swap_blocks(leaving)

    side = (2 * CX + 2 + 4 * NI, CZ)
    up, down = kernel_call(columns_body, [side, side], [VM] * 6)(voltage, voltage_lag, tissue, fiber, low, high)
    left, right = shift_pair("blk", up, down)
    wide = (NI, NJ, CZ)
    faces, weights_e, base = kernel_call(
        faces_body, [(9, *wide), wide, block], [VM] * 7 + [SM], [wide, wide, (6, *wide)]
    )(voltage, tissue, fiber, low, high, left, right, cond)
    lag_low, lag_high = low[1:2], high[1:2]
    lag_left, lag_right = (x[CX + 2 : 2 * CX + 2, None] for x in (left, right))

    dense = (TILES * CHUNKS, LANES)
    v1, current, states = kernel_call(
        react_body, [block, block, (GATES, *dense)], [SM, SM] + [VM] * 5, [dense] * 6
    )(jnp.maximum(holder, 0), par, coming, voltage, base, tissue, mask)

    low, high = shift_pair(
        "slab", jnp.concatenate([v1[-2:], current[-1:]]), jnp.concatenate([v1[:2], current[:1]])
    )
    (parts,) = kernel_call(second_body, [(4, *block)], [SM, VM, VM], [dense, (4, *dense)])(par, states, v1)
    side = (2 * NI + CX + 2, CZ)
    up, down = kernel_call(columns2_body, [side, side], [VM] * 4)(v1, current, low, high)
    left, right = shift_pair("blk", up, down)

    v3, ours, used = kernel_call(
        functools.partial(steps_body, slots),
        [block, block, (slots, 16, LANES)],
        [SM, SM] + [VM] * 11,
        [wide, wide, wide, (TILES * 16, LANES)],
    )(tile_of, par, voltage, v1, current, low, high, left, right, weights_e, faces, parts, mask)
    returned = swap_blocks(used)

    below, above = shift_pair("slab", ours[-1:], ours[:1])
    left, right = shift_pair("blk", ours[:, -1:], ours[:, :1])

    def plus(array, low0, high0, low1, high1):
        tall = jnp.concatenate([low0, array, high0], axis=0)
        around = [(1, 1), (0, 0), (0, 0)]
        return jnp.concatenate([jnp.pad(low1, around), tall, jnp.pad(high1, around)], axis=1)

    lag = tissue.astype(f32) * (voltage_lag - PHASE_REF)
    phase = jnp.stack(
        [plus(ours, below, above, left, right), plus(lag, lag_low, lag_high, lag_left, lag_right)]
    )
    charge = charges(pad_depth(phase), block)

    (gates_out,) = kernel_call(
        functools.partial(last_body, slots), [gates.shape], [SM, SM, VM, VM], [((CAP + 1) * 16, LANES)]
    )(arrived, par, returned, gates)
    return (v3, gates_out, charge)


def solution(mesh):
    in_specs = (
        P("slab", "blk", None),
        P("slab", "blk", None),
        P("slab", "blk", None),
        P("slab", "blk", None),
        P(),
        P("slab", "blk"),
        P(None, ("slab", "blk"), None),
        P(),
        P(),
        P(),
        P(),
        P(),
    )
    out_specs = (
        P("slab", "blk", None),
        P(None, ("slab", "blk"), None),
        P(None, "slab", "blk", None),
    )
    return jax.shard_map(on_device, mesh=mesh, in_specs=in_specs, out_specs=out_specs, check_vma=False)
```

time: 151 us -> 119 us (0.79)
  the two profiles are of different devices: /device:TPU:201 before, /device:TPU:200 now
where the time goes in v2:
time: 119 us; the launch traced here: 118 us
  starting transfers between devices  62.4 us (52%)
  waiting for transfers between devices  28.5 us (24%)
  Pallas kernels  12.7 us (11%)
  local copies, waits for them, and re-layouts  11.2 us (9%)
  other arithmetic  2.63 us (2%)
    all_to_all x3, starting transfers between devices, swap_blocks(): return lax.all_to_all(x, 'blk', split_axis=0, concat_axis=0, tiled=True)  25.6 us
    ppermute x6, starting transfers between devices, shift_pair(): lax.ppermute(last, axis, up)  23 us
    all_to_all x3, waiting for transfers between devices, swap_blocks(): return lax.all_to_all(x, 'blk', split_axis=0, concat_axis=0, tiled=True)  18 us
    ppermute x6, starting transfers between devices, shift_pair(): lax.ppermute(first, axis, [(b, a) for a, b in up])  13.8 us
    ppermute x6, waiting for transfers between devices, shift_pair(): lax.ppermute(first, axis, [(b, a) for a, b in up])  7.38 us
    unnamed x46, local copies, waits for them, and re-layouts  7.19 us
    ppermute x6, waiting for transfers between devices, shift_pair(): lax.ppermute(last, axis, up)  3.07 us
    pallas_call x1, Pallas kernels, on_device(): kernel_call(faces_body, [(9, *wide), wide, block], [VM] * 7 + [SM], [wide...  2.9 us
  transfers between devices with their start and end apart: 15, of which 8 were waited for; matrix products, arithmetic and copies ran while one was open for 4% of the time, Pallas kernels for 4%

profile of v2, /device:TPU:200, one launch (start us, length us, event | category | flops | bytes accessed | tf_op | source)
XLA Modules:
  0.0 118.5 jit_solution(4025347518611694196)
XLA Ops:
  0.7 0.8 reshape.51
  1.6 0.7 broadcast_in_dim.44
  2.3 10.2 %all-to-all-start = ((s32[32,1,128]{2,1,0:T(1,128)}), s32[32,1,128]{2,1,0:T(1,128)S(1)}, u32[]{:S(2)}, u32[]{:S(2)}) async-start(s32[32,1,128]{2,1,0:T(1,128)} %broadcast_in_dim.44), calls=%async_computation | async-start | bytes 32768 | tf_op jit(solution)/shard_map/all_to_all | solution.py:370
  12.5 1.0 copy-done.2
  13.5 0.1 shard_map.139.by_row
  13.7 7.4 %all-to-all-done = s32[32,1,128]{2,1,0:T(1,128)S(1)} async-done(((s32[32,1,128]{2,1,0:T(1,128)}), s32[32,1,128]{2,1,0:T(1,128)S(1)}, u32[]{:S(2)}, u32[]{:S(2)}) %all-to-all-start) | async-done | bytes 16416 | tf_op jit(solution)/shard_map/all_to_all | solution.py:370
  21.0 0.7 slice_reduce_fusion.arrived
  21.7 1.5 %shard_map.140 = f32[32,48,128]{2,1,0:T(8,128)} custom-call(s32[32]{0:T(128)S(1)} %slice_reduce_fusion.arrived, f32[768,128]{1,0:T(8,128)S(1)} %shard_map.139.by_row), custom_call_target="tpu_custom_call" | custom-call | flops 1000000 | bytes 1000000 | tf_op jit(solution)/shard_map/pallas_call | solution.py:454
  23.2 5.0 %all-to-all-start.1 = ((f32[32,48,128]{2,1,0:T(8,128)}), f32[32,48,128]{2,1,0:T(8,128)S(1)}, u32[]{:S(2)}, u32[]{:S(2)}) async-start(f32[32,48,128]{2,1,0:T(8,128)} %shard_map.140), calls=%async_computation.1 | async-start | bytes 1572864 | tf_op jit(solution)/shard_map/all_to_all | solution.py:370
  28.3 1.9 %collective-permute-start = (f32[6,8,512]{2,1,0:T(8,128)S(1)}, f32[6,8,512]{2,1,0:T(8,128)S(1)}, u32[]{:S(2)}, u32[]{:S(2)}) collective-permute-start(f32[6,8,512]{2,1,0:T(8,128)S(1)} %get-tuple-element.18), channel_id=1, source_target_pairs={{0,32},{32,64},{64,96},{96,128},{128,160},{160,192},{192,224},{224... | collective-permute-start | bytes 294920 | tf_op jit(solution)/shard_map/ppermute | solution.py:366
  30.2 3.6 %collective-permute-start.1 = (f32[6,8,512]{2,1,0:T(8,128)S(1)}, f32[6,8,512]{2,1,0:T(8,128)S(1)}, u32[]{:S(2)}, u32[]{:S(2)}) collective-permute-start(f32[6,8,512]{2,1,0:T(8,128)S(1)} %get-tuple-element.19), channel_id=1, source_target_pairs={{32,0},{64,32},{96,64},{128,96},{160,128},{192,160},{224,192},{256... | collective-permute-start | bytes 294920 | tf_op jit(solution)/shard_map/ppermute | solution.py:366
  33.8 0.4 collective-permute-done.low
  34.2 2.4 %collective-permute-done.1.high = f32[6,8,512]{2,1,0:T(8,128)S(1)} collective-permute-done((f32[6,8,512]{2,1,0:T(8,128)S(1)}, f32[6,8,512]{2,1,0:T(8,128)S(1)}, u32[]{:S(2)}, u32[]{:S(2)}) %collective-permute-start.1) | collective-permute-done | bytes 98336 | tf_op jit(solution)/shard_map/ppermute | solution.py:366
  36.6 3.4 %collective-permute-start.2 = (f32[42,512]{1,0:T(8,128)S(1)}, f32[42,512]{1,0:T(8,128)S(1)}, u32[]{:S(2)}, u32[]{:S(2)}) collective-permute-start(f32[42,512]{1,0:T(8,128)S(1)} %get-tuple-element.20), channel_id=1, source_target_pairs={{0,1},{1,2},{2,3},{3,4},{4,5},{5,6},{6,7},{7,8},{8,9},{9,10},{10,1... | collective-permute-start | bytes 258056 | tf_op jit(solution)/shard_map/ppermute | solution.py:366
  40.0 2.5 %collective-permute-start.3 = (f32[42,512]{1,0:T(8,128)S(1)}, f32[42,512]{1,0:T(8,128)S(1)}, u32[]{:S(2)}, u32[]{:S(2)}) collective-permute-start(f32[42,512]{1,0:T(8,128)S(1)} %get-tuple-element.21), channel_id=1, source_target_pairs={{1,0},{2,1},{3,2},{4,3},{5,4},{6,5},{7,6},{8,7},{9,8},{10,9},{11,1... | collective-permute-start | bytes 258056 | tf_op jit(solution)/shard_map/ppermute | solution.py:366
  42.7 2.7 %collective-permute-done.2.left = f32[42,512]{1,0:T(8,128)S(1)} collective-permute-done((f32[42,512]{1,0:T(8,128)S(1)}, f32[42,512]{1,0:T(8,128)S(1)}, u32[]{:S(2)}, u32[]{:S(2)}) %collective-permute-start.2) | collective-permute-done | bytes 86048 | tf_op jit(solution)/shard_map/ppermute | solution.py:366
  45.4 0.6 copy-done.10
  46.1 0.8 collective-permute-done.3.right
  46.9 0.6 copy-done.12
  47.5 0.9 copy-done.7
  48.4 0.9 copy-done.11
  49.3 0.9 copy-done.13
  50.2 2.9 %shard_map.143 = (f32[9,8,16,512]{3,2,1,0:T(8,128)S(1)}, f32[8,16,512]{2,1,0:T(8,128)S(1)}, f32[4,8,512]{2,1,0:T(8,128)S(1)}) custom-call(f32[4,8,512]{2,1,0:T(8,128)S(1)} %copy-done.1, s32[4,8,512]{2,1,0:T(8,128)S(1)} %copy-done, s32[4,8,512]{2,1,0:T(8,128)S(1)} %copy-done.5, f32[6,8,512]{2,1,0:T(8,128)S(1)} %collective-permute-done.low, ...), custom_call_target="tpu_custom_call" | custom-call | flops 1000000 | bytes 1000000 | tf_op jit(solution)/shard_map/pallas_call | solution.py:461
  53.1 0.7 copy-done.8
  53.8 0.6 copy-done.14
  54.5 0.9 copy-done.15
  55.4 1.7 %shard_map.144 = (f32[4,8,512]{2,1,0:T(8,128)S(1)}, f32[4,8,512]{2,1,0:T(8,128)S(1)}, f32[12,128,128]{2,1,0:T(8,128)S(1)}) custom-call(s32[32]{0:T(128)S(1)} %get-tuple-element.35.holder, f32[54]{0:T(128)S(1)} %concatenate.21.par, f32[32,48,128]{2,1,0:T(8,128)S(1)} %all-to-all-done.1.coming, f32[4,8,512]{2,1,0:T(8,128)S(1)} %copy-done.1, ...), custom_call_target="tpu_custom_call" | custom-call | flops 1000000 | bytes 1000000 | tf_op jit(solution)/shard_map/pallas_call | solution.py:468
  57.1 5.2 %collective-permute-start.4 = (f32[3,8,512]{2,1,0:T(8,128)S(1)}, f32[3,8,512]{2,1,0:T(8,128)S(1)}, u32[]{:S(2)}, u32[]{:S(2)}) collective-permute-start(f32[3,8,512]{2,1,0:T(8,128)S(1)} %pad_maximum_fusion.1), channel_id=1, source_target_pairs={{0,32},{32,64},{64,96},{96,128},{128,160},{160,192},{192,224},{224... | collective-permute-start | bytes 147464 | tf_op jit(solution)/shard_map/ppermute | solution.py:366
  62.3 1.9 %collective-permute-start.5 = (f32[3,8,512]{2,1,0:T(8,128)S(1)}, f32[3,8,512]{2,1,0:T(8,128)S(1)}, u32[]{:S(2)}, u32[]{:S(2)}) collective-permute-start(f32[3,8,512]{2,1,0:T(8,128)S(1)} %pad_maximum_fusion.2), channel_id=1, source_target_pairs={{32,0},{64,32},{96,64},{128,96},{160,128},{192,160},{224,192},{256... | collective-permute-start | bytes 147464 | tf_op jit(solution)/shard_map/ppermute | solution.py:366
  64.3 2.8 %collective-permute-done.5.high = f32[3,8,512]{2,1,0:T(8,128)S(1)} collective-permute-done((f32[3,8,512]{2,1,0:T(8,128)S(1)}, f32[3,8,512]{2,1,0:T(8,128)S(1)}, u32[]{:S(2)}, u32[]{:S(2)}) %collective-permute-start.5) | collective-permute-done | bytes 49184 | tf_op jit(solution)/shard_map/ppermute | solution.py:366
  67.1 4.1 %collective-permute-start.6 = (f32[22,512]{1,0:T(8,128)S(1)}, f32[22,512]{1,0:T(8,128)S(1)}, u32[]{:S(2)}, u32[]{:S(2)}) collective-permute-start(f32[22,512]{1,0:T(8,128)S(1)} %get-tuple-element.25), channel_id=1, source_target_pairs={{0,1},{1,2},{2,3},{3,4},{4,5},{5,6},{6,7},{7,8},{8,9},{9,10},{10,1... | collective-permute-start | bytes 135176 | tf_op jit(solution)/shard_map/ppermute | solution.py:366
  71.2 1.9 %collective-permute-start.7 = (f32[22,512]{1,0:T(8,128)S(1)}, f32[22,512]{1,0:T(8,128)S(1)}, u32[]{:S(2)}, u32[]{:S(2)}) collective-permute-start(f32[22,512]{1,0:T(8,128)S(1)} %get-tuple-element.26), channel_id=1, source_target_pairs={{1,0},{2,1},{3,2},{4,3},{5,4},{6,5},{7,6},{8,7},{9,8},{10,9},{11,1... | collective-permute-start | bytes 135176 | tf_op jit(solution)/shard_map/ppermute | solution.py:366
  73.2 0.8 slice.101
  73.9 0.8 slice.104
  74.7 1.5 %shard_map.146.parts = f32[4,4,8,512]{3,2,1,0:T(8,128)S(1)} custom-call(f32[54]{0:T(128)S(1)} %concatenate.21.par, f32[12,128,128]{2,1,0:T(8,128)S(1)} %get-tuple-element.29.states_in, f32[4,8,512]{2,1,0:T(8,128)S(1)} %get-tuple-element.23.v1), custom_call_target="tpu_custom_call" | custom-call | flops 1000000 | bytes 1000000 | tf_op jit(solution)/shard_map/pallas_call | solution.py:475
  76.2 1.3 %collective-permute-done.7.right = f32[22,512]{1,0:T(8,128)S(1)} collective-permute-done((f32[22,512]{1,0:T(8,128)S(1)}, f32[22,512]{1,0:T(8,128)S(1)}, u32[]{:S(2)}, u32[]{:S(2)}) %collective-permute-start.7) | collective-permute-done | bytes 45088 | tf_op jit(solution)/shard_map/ppermute | solution.py:366
  77.5 2.5 %shard_map.147 = (f32[4,8,512]{2,1,0:T(8,128)}, f32[4,8,512]{2,1,0:T(8,128)S(1)}, f32[32,16,128]{2,1,0:T(8,128)}) custom-call(s32[32]{0:T(128)S(1)} %get-tuple-element.34.tile_of, f32[54]{0:T(128)S(1)} %concatenate.21.par, f32[4,8,512]{2,1,0:T(8,128)S(1)} %copy-done.1, f32[4,8,512]{2,1,0:T(8,128)S(1)} %get-tuple-element.23.v1, ...), custom_call_target="tpu_custom_call" | custom-call | flops 1000000 | bytes 1000000 | tf_op jit(solution)/shard_map/pallas_call | solution.py:480
  80.0 4.1 %collective-permute-start.8 = (f32[4,1,512]{2,1,0:T(1,128)S(1)}, f32[4,1,512]{2,1,0:T(1,128)S(1)}, u32[]{:S(2)}, u32[]{:S(2)}) collective-permute-start(f32[4,1,512]{2,1,0:T(1,128)S(1)} %get-tuple-element.41), channel_id=1, source_target_pairs={{0,1},{1,2},{2,3},{3,4},{4,5},{5,6},{6,7},{7,8},{8,9},{9,10},{10,1... | collective-permute-start | bytes 24584 | tf_op jit(solution)/shard_map/ppermute | solution.py:366
  84.1 1.9 %collective-permute-start.11 = (f32[4,1,512]{2,1,0:T(1,128)S(1)}, f32[4,1,512]{2,1,0:T(1,128)S(1)}, u32[]{:S(2)}, u32[]{:S(2)}) collective-permute-start(f32[4,1,512]{2,1,0:T(1,128)S(1)} %get-tuple-element.42), channel_id=1, source_target_pairs={{1,0},{2,1},{3,2},{4,3},{5,4},{6,5},{7,6},{8,7},{9,8},{10,9},{11,1... | collective-permute-start | bytes 24584 | tf_op jit(solution)/shard_map/ppermute | solution.py:366
  86.0 4.4 %collective-permute-start.9 = (f32[1,8,512]{2,1,0:T(8,128)S(1)}, f32[1,8,512]{2,1,0:T(8,128)S(1)}, u32[]{:S(2)}, u32[]{:S(2)}) collective-permute-start(f32[1,8,512]{2,1,0:T(8,128)S(1)} %get-tuple-element.39), channel_id=1, source_target_pairs={{0,32},{32,64},{64,96},{96,128},{128,160},{160,192},{192,224},{224... | collective-permute-start | bytes 49160 | tf_op jit(solution)/shard_map/ppermute | solution.py:366
  90.4 1.9 %collective-permute-start.10 = (f32[1,8,512]{2,1,0:T(8,128)S(1)}, f32[1,8,512]{2,1,0:T(8,128)S(1)}, u32[]{:S(2)}, u32[]{:S(2)}) collective-permute-start(f32[1,8,512]{2,1,0:T(8,128)S(1)} %get-tuple-element.40), channel_id=1, source_target_pairs={{32,0},{64,32},{96,64},{128,96},{160,128},{192,160},{224,192},{256... | collective-permute-start | bytes 49160 | tf_op jit(solution)/shard_map/ppermute | solution.py:366
  92.4 10.5 %all-to-all-start.2 = ((f32[32,16,128]{2,1,0:T(8,128)}), f32[32,16,128]{2,1,0:T(8,128)S(1)}, u32[]{:S(2)}, u32[]{:S(2)}) async-start(f32[32,16,128]{2,1,0:T(8,128)} %get-tuple-element.31), calls=%async_computation.2 | async-start | bytes 524288 | tf_op jit(solution)/shard_map/all_to_all | solution.py:370
  102.9 0.5 add_multiply_fusion.10
  103.5 0.2 select_maximum_fusion
  103.7 1.0 add_multiply_fusion.9
  104.7 0.7 pad_maximum_fusion
  105.3 10.7 %all-to-all-done.2.returned = f32[32,16,128]{2,1,0:T(8,128)S(1)} async-done(((f32[32,16,128]{2,1,0:T(8,128)}), f32[32,16,128]{2,1,0:T(8,128)S(1)}, u32[]{:S(2)}, u32[]{:S(2)}) %all-to-all-start.2) | async-done | bytes 262176 | tf_op jit(solution)/shard_map/all_to_all | solution.py:370
  116.0 2.5 %shard_map.148 = f32[12,16,512]{2,1,0:T(8,128)} custom-call(s32[32]{0:T(128)S(1)} %slice_reduce_fusion.arrived, f32[54]{0:T(128)S(1)} %concatenate.21.par, f32[32,16,128]{2,1,0:T(8,128)S(1)} %all-to-all-done.2.returned, f32[12,16,512]{2,1,0:T(8,128)S(1)} %copy-done.3), custom_call_target="tpu_custom_call" | custom-call | flops 1000000 | bytes 1000000 | tf_op jit(solution)/shard_map/pallas_call | solution.py:502
  (68 shorter events, 0.7 us)
Async XLA Ops:
  0.6 27.6 %copy-start = (s32[4,8,512]{2,1,0:T(8,128)S(1)}, s32[4,8,512]{2,1,0:T(8,128)}, u32[]{:S(2)}) copy-start(s32[4,8,512]{2,1,0:T(8,128)} %tissue.7) | copy-start | bytes 196612
  0.6 27.6 %copy-start.1 = (f32[4,8,512]{2,1,0:T(8,128)S(1)}, f32[4,8,512]{2,1,0:T(8,128)}, u32[]{:S(2)}) copy-start(f32[4,8,512]{2,1,0:T(8,128)} %v0.1) | copy-start | bytes 196612
  2.3 18.7 %all-to-all-start = ((s32[32,1,128]{2,1,0:T(1,128)}), s32[32,1,128]{2,1,0:T(1,128)S(1)}, u32[]{:S(2)}, u32[]{:S(2)}) async-start(s32[32,1,128]{2,1,0:T(1,128)} %broadcast_in_dim.44), calls=%async_computation | async-start | bytes 32768 | tf_op jit(solution)/shard_map/all_to_all | solution.py:370
  12.5 1.0 copy-start.2
  13.5 14.8 %copy-start.4 = (f32[4,8,512]{2,1,0:T(8,128)S(1)}, f32[4,8,512]{2,1,0:T(8,128)}, u32[]{:S(2)}) copy-start(f32[4,8,512]{2,1,0:T(8,128)} %lag.3) | copy-start | bytes 196612
  13.5 14.8 %copy-start.5 = (s32[4,8,512]{2,1,0:T(8,128)S(1)}, s32[4,8,512]{2,1,0:T(8,128)}, u32[]{:S(2)}) copy-start(s32[4,8,512]{2,1,0:T(8,128)} %fiber.5) | copy-start | bytes 196612
  13.5 29.0 %copy-start.16 = (s32[4,8]{1,0:T(4,128)S(1)}, s32[4,8]{1,0:T(4,128)}, u32[]{:S(2)}) copy-start(s32[4,8]{1,0:T(4,128)} %param.17) | copy-start | bytes 388
  13.5 29.0 %copy-start.17 = (f32[6,16]{1,0:T(8,128)S(1)}, f32[6,16]{1,0:T(8,128)}, u32[]{:S(2)}) copy-start(f32[6,16]{1,0:T(8,128)} %param.16) | copy-start | bytes 1156
  13.5 29.1 %copy-start.18 = (f32[12]{0:T(128)S(1)}, f32[12]{0:T(128)}, u32[]{:S(2)}) copy-start(f32[12]{0:T(128)} %param.19) | copy-start | bytes 148
  13.5 29.1 %copy-start.19 = (f32[12]{0:T(128)S(1)}, f32[12]{0:T(128)}, u32[]{:S(2)}) copy-start(f32[12]{0:T(128)} %param.20) | copy-start | bytes 148
  13.5 29.1 %copy-start.20 = (f32[12]{0:T(128)S(1)}, f32[12]{0:T(128)}, u32[]{:S(2)}) copy-start(f32[12]{0:T(128)} %param.21) | copy-start | bytes 148
  13.5 29.1 %copy-start.21 = (f32[12]{0:T(128)S(1)}, f32[12]{0:T(128)}, u32[]{:S(2)}) copy-start(f32[12]{0:T(128)} %param.22) | copy-start | bytes 148
  13.5 29.1 %copy-start.22 = (f32[6]{0:T(128)S(1)}, f32[6]{0:T(128)}, u32[]{:S(2)}) copy-start(f32[6]{0:T(128)} %param.23) | copy-start | bytes 76
  23.2 31.2 %all-to-all-start.1 = ((f32[32,48,128]{2,1,0:T(8,128)}), f32[32,48,128]{2,1,0:T(8,128)S(1)}, u32[]{:S(2)}, u32[]{:S(2)}) async-start(f32[32,48,128]{2,1,0:T(8,128)} %shard_map.140), calls=%async_computation.1 | async-start | bytes 1572864 | tf_op jit(solution)/shard_map/all_to_all | solution.py:370
  28.3 5.9 %collective-permute-start = (f32[6,8,512]{2,1,0:T(8,128)S(1)}, f32[6,8,512]{2,1,0:T(8,128)S(1)}, u32[]{:S(2)}, u32[]{:S(2)}) collective-permute-start(f32[6,8,512]{2,1,0:T(8,128)S(1)} %get-tuple-element.18), channel_id=1, source_target_pairs={{0,32},{32,64},{64,96},{96,128},{128,160},{160,192},{192,224},{224... | collective-permute-start | bytes 294920 | tf_op jit(solution)/shard_map/ppermute | solution.py:366
  30.2 6.4 %collective-permute-start.1 = (f32[6,8,512]{2,1,0:T(8,128)S(1)}, f32[6,8,512]{2,1,0:T(8,128)S(1)}, u32[]{:S(2)}, u32[]{:S(2)}) collective-permute-start(f32[6,8,512]{2,1,0:T(8,128)S(1)} %get-tuple-element.19), channel_id=1, source_target_pairs={{32,0},{64,32},{96,64},{128,96},{160,128},{192,160},{224,192},{256... | collective-permute-start | bytes 294920 | tf_op jit(solution)/shard_map/ppermute | solution.py:366
  36.6 8.8 %copy-start.6 = (f32[6,8,512]{2,1,0:T(8,128)}, f32[6,8,512]{2,1,0:T(8,128)S(1)}, u32[]{:S(2)}) copy-start(f32[6,8,512]{2,1,0:T(8,128)S(1)} %collective-permute-done.1.high) | copy-start | bytes 294916
  36.6 8.8 %collective-permute-start.2 = (f32[42,512]{1,0:T(8,128)S(1)}, f32[42,512]{1,0:T(8,128)S(1)}, u32[]{:S(2)}, u32[]{:S(2)}) collective-permute-start(f32[42,512]{1,0:T(8,128)S(1)} %get-tuple-element.20), channel_id=1, source_target_pairs={{0,1},{1,2},{2,3},{3,4},{4,5},{5,6},{6,7},{7,8},{8,9},{9,10},{10,1... | collective-permute-start | bytes 258056 | tf_op jit(solution)/shard_map/ppermute | solution.py:366
  40.0 6.9 %collective-permute-start.3 = (f32[42,512]{1,0:T(8,128)S(1)}, f32[42,512]{1,0:T(8,128)S(1)}, u32[]{:S(2)}, u32[]{:S(2)}) collective-permute-start(f32[42,512]{1,0:T(8,128)S(1)} %get-tuple-element.21), channel_id=1, source_target_pairs={{1,0},{2,1},{3,2},{4,3},{5,4},{6,5},{7,6},{8,7},{9,8},{10,9},{11,1... | collective-permute-start | bytes 258056 | tf_op jit(solution)/shard_map/ppermute | solution.py:366
  45.4 0.6 copy-start.10
  46.9 0.6 copy-start.12
  47.5 0.9 copy-start.7
  48.4 0.9 copy-start.11
  49.3 0.9 copy-start.13
  53.1 0.7 copy-start.8
  53.8 0.6 copy-start.14
  54.4 23.1 %copy-start.9 = (f32[8,16,512]{2,1,0:T(8,128)S(1)}, f32[8,16,512]{2,1,0:T(8,128)}, u32[]{:S(2)}) copy-start(f32[8,16,512]{2,1,0:T(8,128)} %copy-done.8) | copy-start | bytes 786436
  54.5 0.9 copy-start.15
  57.1 7.1 %collective-permute-start.4 = (f32[3,8,512]{2,1,0:T(8,128)S(1)}, f32[3,8,512]{2,1,0:T(8,128)S(1)}, u32[]{:S(2)}, u32[]{:S(2)}) collective-permute-start(f32[3,8,512]{2,1,0:T(8,128)S(1)} %pad_maximum_fusion.1), channel_id=1, source_target_pairs={{0,32},{32,64},{64,96},{96,128},{128,160},{160,192},{192,224},{224... | collective-permute-start | bytes 147464 | tf_op jit(solution)/shard_map/ppermute | solution.py:366
  62.3 4.8 %collective-permute-start.5 = (f32[3,8,512]{2,1,0:T(8,128)S(1)}, f32[3,8,512]{2,1,0:T(8,128)S(1)}, u32[]{:S(2)}, u32[]{:S(2)}) collective-permute-start(f32[3,8,512]{2,1,0:T(8,128)S(1)} %pad_maximum_fusion.2), channel_id=1, source_target_pairs={{32,0},{64,32},{96,64},{128,96},{160,128},{192,160},{224,192},{256... | collective-permute-start | bytes 147464 | tf_op jit(solution)/shard_map/ppermute | solution.py:366
  67.1 9.1 %collective-permute-start.6 = (f32[22,512]{1,0:T(8,128)S(1)}, f32[22,512]{1,0:T(8,128)S(1)}, u32[]{:S(2)}, u32[]{:S(2)}) collective-permute-start(f32[22,512]{1,0:T(8,128)S(1)} %get-tuple-element.25), channel_id=1, source_target_pairs={{0,1},{1,2},{2,3},{3,4},{4,5},{5,6},{6,7},{7,8},{8,9},{9,10},{10,1... | collective-permute-start | bytes 135176 | tf_op jit(solution)/shard_map/ppermute | solution.py:366
  71.2 6.3 %collective-permute-start.7 = (f32[22,512]{1,0:T(8,128)S(1)}, f32[22,512]{1,0:T(8,128)S(1)}, u32[]{:S(2)}, u32[]{:S(2)}) collective-permute-start(f32[22,512]{1,0:T(8,128)S(1)} %get-tuple-element.26), channel_id=1, source_target_pairs={{1,0},{2,1},{3,2},{4,3},{5,4},{6,5},{7,6},{8,7},{9,8},{10,9},{11,1... | collective-permute-start | bytes 135176 | tf_op jit(solution)/shard_map/ppermute | solution.py:366
  73.1 19.2 %slice-start = ((f32[6,8,512]{2,1,0:T(8,128)}), f32[1,8,512]{2,1,0:T(8,128)S(1)}, s32[]{:S(2)}) async-start(f32[6,8,512]{2,1,0:T(8,128)} %copy-done.6), calls=%async_computation.3 | async-start | bytes 32768 | tf_op jit(solution)/shard_map/slice | solution.py:464
  80.0 36.0 %copy-start.3 = (f32[12,16,512]{2,1,0:T(8,128)S(1)}, f32[12,16,512]{2,1,0:T(8,128)}, u32[]{:S(2)}) copy-start(f32[12,16,512]{2,1,0:T(8,128)} %gates.3) | copy-start | bytes 1179652
  80.0 22.8 %collective-permute-start.8 = (f32[4,1,512]{2,1,0:T(1,128)S(1)}, f32[4,1,512]{2,1,0:T(1,128)S(1)}, u32[]{:S(2)}, u32[]{:S(2)}) collective-permute-start(f32[4,1,512]{2,1,0:T(1,128)S(1)} %get-tuple-element.41), channel_id=1, source_target_pairs={{0,1},{1,2},{2,3},{3,4},{4,5},{5,6},{6,7},{7,8},{8,9},{9,10},{10,1... | collective-permute-start | bytes 24584 | tf_op jit(solution)/shard_map/ppermute | solution.py:366
  84.1 18.8 %collective-permute-start.11 = (f32[4,1,512]{2,1,0:T(1,128)S(1)}, f32[4,1,512]{2,1,0:T(1,128)S(1)}, u32[]{:S(2)}, u32[]{:S(2)}) collective-permute-start(f32[4,1,512]{2,1,0:T(1,128)S(1)} %get-tuple-element.42), channel_id=1, source_target_pairs={{1,0},{2,1},{3,2},{4,3},{5,4},{6,5},{7,6},{8,7},{9,8},{10,9},{11,1... | collective-permute-start | bytes 24584 | tf_op jit(solution)/shard_map/ppermute | solution.py:366
  86.0 16.9 %collective-permute-start.9 = (f32[1,8,512]{2,1,0:T(8,128)S(1)}, f32[1,8,512]{2,1,0:T(8,128)S(1)}, u32[]{:S(2)}, u32[]{:S(2)}) collective-permute-start(f32[1,8,512]{2,1,0:T(8,128)S(1)} %get-tuple-element.39), channel_id=1, source_target_pairs={{0,32},{32,64},{64,96},{96,128},{128,160},{160,192},{192,224},{224... | collective-permute-start | bytes 49160 | tf_op jit(solution)/shard_map/ppermute | solution.py:366
  90.4 12.5 %collective-permute-start.10 = (f32[1,8,512]{2,1,0:T(8,128)S(1)}, f32[1,8,512]{2,1,0:T(8,128)S(1)}, u32[]{:S(2)}, u32[]{:S(2)}) collective-permute-start(f32[1,8,512]{2,1,0:T(8,128)S(1)} %get-tuple-element.40), channel_id=1, source_target_pairs={{32,0},{64,32},{96,64},{128,96},{160,128},{192,160},{224,192},{256... | collective-permute-start | bytes 49160 | tf_op jit(solution)/shard_map/ppermute | solution.py:366
  92.4 23.6 %all-to-all-start.2 = ((f32[32,16,128]{2,1,0:T(8,128)}), f32[32,16,128]{2,1,0:T(8,128)S(1)}, u32[]{:S(2)}, u32[]{:S(2)}) async-start(f32[32,16,128]{2,1,0:T(8,128)} %get-tuple-element.31), calls=%async_computation.2 | async-start | bytes 524288 | tf_op jit(solution)/shard_map/all_to_all | solution.py:370

commit v3 on v2

--- a/solution.py
+++ b/solution.py
@@ -27,17 +27,18 @@
 f32 = jnp.float32
 VM = pl.BlockSpec(memory_space=pltpu.VMEM)
 SM = pl.BlockSpec(memory_space=pltpu.SMEM)
-
-
-def kernel_call(body, outs, ins, scratch=(), flops=1_000_000):
+HB = pl.BlockSpec(memory_space=pltpu.HBM)
+
+
+def kernel_call(body, outs, ins, scratch=(), flops=1_000_000, limit=6, specs=None):
     return pl.pallas_call(
         body,
         out_shape=[jax.ShapeDtypeStruct(shape, f32) for shape in outs],
         in_specs=ins,
-        out_specs=[VM] * len(outs),
-        scratch_shapes=[pltpu.VMEM(shape, f32) for shape in scratch],
+        out_specs=specs or [VM] * len(outs),
+        scratch_shapes=[pltpu.VMEM(s, f32) if isinstance(s, tuple) else s for s in scratch],
         cost_estimate=pl.CostEstimate(flops=flops, bytes_accessed=1_000_000, transcendentals=0),
-        compiler_params=pltpu.CompilerParams(vmem_limit_bytes=40 * 1024 * 1024),
+        compiler_params=pltpu.CompilerParams(vmem_limit_bytes=limit * 1024 * 1024),
     )
 
 
@@ -172,7 +173,7 @@
     return total
 
 
-def faces_body(voltage, tissue, fiber, low, high, left, right, cond, faces_ref, weights_ref, base_ref, field_ref, fib_ref, stack_ref):
+def faces_body(voltage, tissue, fiber, low, high, left, right, cond, faces_out, weights_ref, base_ref, lag_ref, faces_ref, field_ref, fib_ref, stack_ref, sems):
     zero = jnp.zeros((NI, NJ, CZ), f32)
     field_ref[...] = zero
     fib_ref[...] = zero
@@ -210,26 +211,40 @@
         return carry
 
     lax.fori_loop(0, NI, classes, 0)
+    lag_ref[0:CY] = low[1]
+    lag_ref[CY : 2 * CY] = high[1]
+    lag_ref[2 * CY : 2 * CY + CX] = left[CX + 2 : 2 * CX + 2]
+    lag_ref[2 * CY + CX : 2 * CY + 2 * CX] = right[CX + 2 : 2 * CX + 2]
     z = lax.broadcasted_iota(jnp.int32, (NJ, CZ), 1)
+    copies = []
     for i in range(NI - 1):
+        if i > 1:
+            copies.append(pltpu.make_async_copy(faces_ref.at[i - 1], faces_out.at[i - 1], sems.at[i - 1]))
+            copies[-1].start()
         w = weights_ref[i]
         both = w * weights_ref[i + 1]
         for n, comp in enumerate(COMPONENT[0]):
-            faces_ref[n, i] = (stack_ref[comp, i] + stack_ref[comp, i + 1]) * both
+            faces_ref[i, n] = (stack_ref[comp, i] + stack_ref[comp, i + 1]) * both
         if i == 0:
+            faces_ref[0, 3:] = jnp.zeros((6, NJ, CZ), f32)
             continue
         both = w * up_j(w)
         for n, comp in enumerate(COMPONENT[1]):
             here = stack_ref[comp, i]
-            faces_ref[3 + n, i] = (here + up_j(here)) * both
+            faces_ref[i, 3 + n] = (here + up_j(here)) * both
         both = w * jnp.where(z == CZ - 1, 0.0, up_z(w))
         for n, comp in enumerate(COMPONENT[2]):
             here = stack_ref[comp, i]
-            faces_ref[6 + n, i] = (here + up_z(here)) * both
+            faces_ref[i, 6 + n] = (here + up_z(here)) * both
+    for i in (0, NI - 2):
+        copies.append(pltpu.make_async_copy(faces_ref.at[i], faces_out.at[i], sems.at[i]))
+        copies[-1].start()
     field = {i: field_ref[i] for i in range(1, NI - 1)}
-    spread = spread_of(field, lambda n, i: faces_ref[n, i], 2, CX + 1)
+    spread = spread_of(field, lambda n, i: faces_ref[i, n], 2, CX + 1)
     for i in range(CX):
         base_ref[i] = voltage[i] + tissue[i].astype(f32) * spread[2 + i][2 : 2 + CY]
+    for copy in copies:
+        copy.wait()
 
 
 def react_body(holder, par, coming, voltage, base, tissue, live, v1_ref, current_ref, states_ref, v_d, base_d, w_d, live_d, out_d, cur_d):
@@ -300,7 +315,9 @@
             ref[at + 1 + i : at + 2 + i] = current[i, one]
 
 
-def steps_body(slots, tile_of, par, v0, v1, current, low, high, left, right, weights, faces, parts, live, v3_ref, ours_ref, used_ref, v_ref, cur_ref, next_ref, rows_ref):
+def steps_body(slots, tile_of, par, v0, v1, current, low, high, left, right, weights, faces_in, parts, live, v3_ref, ours_ref, used_ref, faces, v_ref, cur_ref, next_ref, rows_ref, sem):
+    fetch = pltpu.make_async_copy(faces_in, faces, sem)
+    fetch.start()
     v_ref[...] = jnp.zeros((NI, NJ, CZ), f32)
     cur_ref[...] = jnp.zeros((NI, NJ, CZ), f32)
     own = slice(2, 2 + CY)
@@ -318,8 +335,9 @@
                 v_ref[i, j : j + 1, :] = ref[n * NI + i : n * NI + i + 1, :]
         for i in range(CX + 2):
             cur_ref[1 + i, outer : outer + 1, :] = ref[2 * NI + i : 2 * NI + i + 1, :]
-    face = lambda n, i: faces[n, i]
+    face = lambda n, i: faces[i, n]
     field = {i: weights[i] * v_ref[i] for i in range(NI)}
+    fetch.wait()
     spread = spread_of(field, face, 1, NI - 2)
     for i in range(1, NI - 1):
         next_ref[i] = v_ref[i] + weights[i] * (spread[i] - STEP_DT * cur_ref[i])
@@ -360,6 +378,53 @@
     lax.fori_loop(0, GATES, one, 0)
 
 
+def arctan_of(cross, den):
+    size = jnp.abs(cross)
+    big = size > 2.414213562373095 * den
+    mid = size > 0.4142135623730950 * den
+    num = jnp.where(big, -den, jnp.where(mid, size - den, size))
+    x = num / jnp.where(big, size, jnp.where(mid, size + den, den))
+    z = x * x
+    tail = ((8.05374449538e-2 * z - 1.38776856032e-1) * z + 1.99777106478e-1) * z - 3.33329491539e-1
+    found = jnp.where(big, 1.5707963267948966, jnp.where(mid, 0.7853981633974483, 0.0)) + (tail * z * x + x)
+    return jnp.where(cross < 0.0, -found, found)
+
+
+def edge_of(p, q):
+    cross = p[0] * q[1] - p[1] * q[0]
+    inner = p[0] * q[0] + p[1] * q[1]
+    return arctan_of(cross, p[2] * q[2] + inner + PHASE_SOFT)
+
+
+def charge_body(ours, below, above, left, right, lag, tissue, lag_rim, out_ref):
+    row = lax.broadcasted_iota(jnp.int32, (CY, CZ), 0)
+    z = lax.broadcasted_iota(jnp.int32, (CY, CZ), 1)
+
+    def point(a, b):
+        return (a, b, jnp.sqrt(a * a + b * b))
+
+    a = {-1: below[0], CX: above[0]} | {i: ours[i] for i in range(CX)}
+    b = {-1: lag_rim[0:CY], CX: lag_rim[CY : 2 * CY]} | {i: tissue[i].astype(f32) * (lag[i] - PHASE_REF) for i in range(CX)}
+    plane = {i: point(a[i], b[i]) for i in range(-1, CX + 1)}
+    for i in range(CX):
+        at, beyond = 2 * CY + i, 2 * CY + CX + i
+
+        def later(x, edge):
+            return jnp.where(row == CY - 1, jnp.broadcast_to(edge, (CY, CZ)), pltpu.roll(x, CY - 1, 0))
+
+        def earlier(x, edge):
+            return jnp.where(row == 0, jnp.broadcast_to(edge, (CY, CZ)), pltpu.roll(x, 1, 0))
+
+        y_up = point(later(a[i], right[i]), later(b[i], lag_rim[beyond : beyond + 1]))
+        y_down = point(earlier(a[i], left[i]), earlier(b[i], lag_rim[at : at + 1]))
+        z_up = tuple(jnp.where(z == CZ - 1, 0.0, up_z(x)) for x in plane[i])
+        z_down = tuple(jnp.where(z == 0, 0.0, down_z(x)) for x in plane[i])
+        x_up, x_down = plane[i + 1], plane[i - 1]
+        for n, ring in enumerate(((x_up, y_up, x_down, y_down), (y_up, z_up, y_down, z_down), (x_up, z_up, x_down, z_down))):
+            total = edge_of(ring[0], ring[1]) + edge_of(ring[1], ring[2]) + edge_of(ring[2], ring[3]) + edge_of(ring[3], ring[0])
+            out_ref[n, i] = 2.0 * total
+
+
 def shift_pair(axis, last, first):
     size = lax.axis_size(axis)
     up = [(i, i + 1) for i in range(size - 1)]
@@ -368,53 +433,6 @@
 
 def swap_blocks(x):
     return lax.all_to_all(x, "blk", split_axis=0, concat_axis=0, tiled=True)
-
-
-def basis(direction, amount):
-    return tuple((amount if position == direction else 0 for position in range(3)))
-
-
-def window(array, starts, extent):
-    leading = array.ndim - 3
-    begin = (0,) * leading + tuple(starts)
-    finish = tuple(array.shape[:leading]) + tuple(
-        (first + count for first, count in zip(starts, extent))
-    )
-    return lax.slice(array, begin, finish)
-
-
-def edge_term(first, second):
-    cross = first[0] * second[1] - first[1] * second[0]
-    inner = first[0] * second[0] + first[1] * second[1]
-    norm_value = jnp.sqrt(
-        (first[0] * first[0] + first[1] * first[1])
-        * (second[0] * second[0] + second[1] * second[1])
-    )
-    return 2.0 * jnp.arctan(cross / (norm_value + inner + PHASE_SOFT))
-
-
-def charges(padded_phase, extent):
-    results = []
-    for first_dim, second_dim in ((0, 1), (1, 2), (0, 2)):
-        corners = [
-            basis(first_dim, 1),
-            basis(second_dim, 1),
-            basis(first_dim, -1),
-            basis(second_dim, -1),
-        ]
-        points = [
-            window(padded_phase, tuple((1 + value for value in corner)), extent)
-            for corner in corners
-        ]
-        circulation = jnp.zeros(extent, jnp.float32)
-        for position in range(4):
-            circulation = circulation + edge_term(points[position], points[(position + 1) % 4])
-        results.append(circulation)
-    return jnp.stack(results)
-
-
-def pad_depth(array):
-    return jnp.pad(array, [(0, 0)] * (array.ndim - 1) + [(1, 1)])
 
 
 def on_device(
@@ -436,14 +454,14 @@
     par = jnp.concatenate([gate_half, gate_steep, gate_tmin, gate_tspan, channel])
     cond = conductivity.reshape(-1)
 
-    targets = worker.reshape(-1)
-    live = targets >= 0
-    holder = jnp.where(live, targets // CAP, -1)
-    claimed = holder[None, :] == jnp.arange(slots, dtype=jnp.int32)[:, None]
-    claims = jnp.sum(jnp.where(claimed, targets % CAP + 1, 0), axis=1) - 1
-    tile_of = jnp.sum(jnp.where(claimed, jnp.arange(TILES, dtype=jnp.int32)[None, :], 0), axis=1)
+    live = worker >= 0
+    holder = jnp.where(live, worker // CAP, -1)
+    claimed = holder[None] == jnp.arange(slots, dtype=jnp.int32)[:, None, None]
+    tiles = CY * jnp.arange(CX, dtype=jnp.int32)[:, None] + jnp.arange(CY, dtype=jnp.int32)[None, :]
+    claims = jnp.sum(jnp.where(claimed, worker % CAP + 1, 0), axis=(1, 2)) - 1
+    tile_of = jnp.sum(jnp.where(claimed, tiles[None], 0), axis=(1, 2))
     arrived = swap_blocks(jnp.broadcast_to(claims[:, None, None], (slots, 1, LANES)))[:, 0, 0]
-    mask = jnp.broadcast_to((worker >= 0).astype(f32)[:, :, None], (CX, CY, LANES))
+    mask = jnp.broadcast_to(live.astype(f32)[:, :, None], (CX, CY, LANES))
 
     rim = (6, CY, CZ)
     up, down = kernel_call(start_body, [rim, rim], [VM] * 4)(voltage, voltage_lag, tissue, fiber)
@@ -458,16 +476,20 @@
     up, down = kernel_call(columns_body, [side, side], [VM] * 6)(voltage, voltage_lag, tissue, fiber, low, high)
     left, right = shift_pair("blk", up, down)
     wide = (NI, NJ, CZ)
-    faces, weights_e, base = kernel_call(
-        faces_body, [(9, *wide), wide, block], [VM] * 7 + [SM], [wide, wide, (6, *wide)]
+    sheets = (NI - 1, 9, NJ, CZ)
+    faces, weights_e, base, lag_rim = kernel_call(
+        faces_body,
+        [sheets, wide, block, (2 * CY + 2 * CX, CZ)],
+        [VM] * 7 + [SM],
+        [sheets, wide, wide, (6, *wide), pltpu.SemaphoreType.DMA((NI - 1,))],
+        specs=[HB, VM, VM, VM],
+        limit=12,
     )(voltage, tissue, fiber, low, high, left, right, cond)
-    lag_low, lag_high = low[1:2], high[1:2]
-    lag_left, lag_right = (x[CX + 2 : 2 * CX + 2, None] for x in (left, right))
 
     dense = (TILES * CHUNKS, LANES)
     v1, current, states = kernel_call(
         react_body, [block, block, (GATES, *dense)], [SM, SM] + [VM] * 5, [dense] * 6
-    )(jnp.maximum(holder, 0), par, coming, voltage, base, tissue, mask)
+    )(jnp.maximum(holder, 0).reshape(-1), par, coming, voltage, base, tissue, mask)
 
     low, high = shift_pair(
         "slab", jnp.concatenate([v1[-2:], current[-1:]]), jnp.concatenate([v1[:2], current[:1]])
@@ -480,24 +502,18 @@
     v3, ours, used = kernel_call(
         functools.partial(steps_body, slots),
         [block, block, (slots, 16, LANES)],
-        [SM, SM] + [VM] * 11,
-        [wide, wide, wide, (TILES * 16, LANES)],
+        [SM, SM] + [VM] * 8 + [HB, VM, VM],
+        [sheets, wide, wide, wide, (TILES * 16, LANES), pltpu.SemaphoreType.DMA],
+        limit=12,
     )(tile_of, par, voltage, v1, current, low, high, left, right, weights_e, faces, parts, mask)
     returned = swap_blocks(used)
 
     below, above = shift_pair("slab", ours[-1:], ours[:1])
     left, right = shift_pair("blk", ours[:, -1:], ours[:, :1])
 
-    def plus(array, low0, high0, low1, high1):
-        tall = jnp.concatenate([low0, array, high0], axis=0)
-        around = [(1, 1), (0, 0), (0, 0)]
-        return jnp.concatenate([jnp.pad(low1, around), tall, jnp.pad(high1, around)], axis=1)
-
-    lag = tissue.astype(f32) * (voltage_lag - PHASE_REF)
-    phase = jnp.stack(
-        [plus(ours, below, above, left, right), plus(lag, lag_low, lag_high, lag_left, lag_right)]
-    )
-    charge = charges(pad_depth(phase), block)
+    (charge,) = kernel_call(charge_body, [(3, *block)], [VM] * 8)(
+        ours, below, above, left, right, voltage_lag, tissue, lag_rim
+    )
 
     (gates_out,) = kernel_call(
         functools.partial(last_body, slots), [gates.shape], [SM, SM, VM, VM], [((CAP + 1) * 16, LANES)]

time: 119 us -> 116 us (0.975)
  the two profiles are of different devices: /device:TPU:200 before, /device:TPU:199 now
where the time goes in v3:
time: 116 us; the launch traced here: 115 us
  starting transfers between devices  65 us (56%)
  waiting for transfers between devices  20.6 us (18%)
  Pallas kernels  15.9 us (14%)
  local copies, waits for them, and re-layouts  10.5 us (9%)
  other arithmetic  1.99 us (2%)
    ppermute x6, starting transfers between devices, shift_pair(): lax.ppermute(last, axis, up)  23.4 us
    all_to_all x3, starting transfers between devices, swap_blocks(): return lax.all_to_all(x, 'blk', split_axis=0, concat_axis=0, tiled=True)  22.1 us
    ppermute x6, starting transfers between devices, shift_pair(): lax.ppermute(first, axis, [(b, a) for a, b in up])  19.5 us
    ppermute x6, waiting for transfers between devices, shift_pair(): lax.ppermute(first, axis, [(b, a) for a, b in up])  10.2 us
    unnamed x50, local copies, waits for them, and re-layouts  6.48 us
    all_to_all x3, waiting for transfers between devices, swap_blocks(): return lax.all_to_all(x, 'blk', split_axis=0, concat_axis=0, tiled=True)  5.8 us
    ppermute x6, waiting for transfers between devices, shift_pair(): lax.ppermute(last, axis, up)  4.58 us
    pallas_call x1, Pallas kernels, on_device(): kernel_call(faces_body, [sheets, wide, block, (2 * CY + 2 * CX, CZ)], [VM...  3.8 us
  transfers between devices with their start and end apart: 15, of which 4 were waited for; matrix products, arithmetic and copies ran while one was open for 2% of the time, Pallas kernels for 6%

profile of v3, /device:TPU:199, one launch (start us, length us, event | category | flops | bytes accessed | tf_op | source)
XLA Modules:
  0.0 115.1 jit_solution(1286585232017797720)
XLA Ops:
  0.7 0.8 broadcast_maximum_fusion
  1.4 0.6 select_reduce_fusion
  2.1 0.7 broadcast_in_dim.40
  2.8 9.7 %all-to-all-start = ((s32[32,1,128]{2,1,0:T(1,128)}), s32[32,1,128]{2,1,0:T(1,128)S(1)}, u32[]{:S(2)}, u32[]{:S(2)}) async-start(s32[32,1,128]{2,1,0:T(1,128)} %broadcast_in_dim.40), calls=%async_computation | async-start | bytes 32768 | tf_op jit(solution)/shard_map/all_to_all | solution.py:435
  12.5 1.0 copy-done.2
  13.5 0.0 copy-start.20
  13.5 0.0 copy-start.21
  13.5 0.0 copy-start.24
  13.5 0.1 shard_map.139.by_row
  13.6 5.8 %all-to-all-done = s32[32,1,128]{2,1,0:T(1,128)S(1)} async-done(((s32[32,1,128]{2,1,0:T(1,128)}), s32[32,1,128]{2,1,0:T(1,128)S(1)}, u32[]{:S(2)}, u32[]{:S(2)}) %all-to-all-start) | async-done | bytes 16416 | tf_op jit(solution)/shard_map/all_to_all | solution.py:435
  19.4 0.7 slice_reduce_fusion.arrived
  20.1 1.5 %shard_map.140 = f32[32,48,128]{2,1,0:T(8,128)} custom-call(s32[32]{0:T(128)S(1)} %slice_reduce_fusion.arrived, f32[768,128]{1,0:T(8,128)S(1)} %shard_map.139.by_row), custom_call_target="tpu_custom_call" | custom-call | flops 1000000 | bytes 1000000 | tf_op jit(solution)/shard_map/pallas_call | solution.py:472
  21.6 5.5 %all-to-all-start.1 = ((f32[32,48,128]{2,1,0:T(8,128)}), f32[32,48,128]{2,1,0:T(8,128)S(1)}, u32[]{:S(2)}, u32[]{:S(2)}) async-start(f32[32,48,128]{2,1,0:T(8,128)} %shard_map.140), calls=%async_computation.1 | async-start | bytes 1572864 | tf_op jit(solution)/shard_map/all_to_all | solution.py:435
  27.2 7.5 %collective-permute-start = (f32[6,8,512]{2,1,0:T(8,128)S(1)}, f32[6,8,512]{2,1,0:T(8,128)S(1)}, u32[]{:S(2)}, u32[]{:S(2)}) collective-permute-start(f32[6,8,512]{2,1,0:T(8,128)S(1)} %get-tuple-element.19), channel_id=1, source_target_pairs={{0,32},{32,64},{64,96},{96,128},{128,160},{160,192},{192,224},{224... | collective-permute-start | bytes 294920 | tf_op jit(solution)/shard_map/ppermute | solution.py:431
  34.7 1.9 %collective-permute-start.1 = (f32[6,8,512]{2,1,0:T(8,128)S(1)}, f32[6,8,512]{2,1,0:T(8,128)S(1)}, u32[]{:S(2)}, u32[]{:S(2)}) collective-permute-start(f32[6,8,512]{2,1,0:T(8,128)S(1)} %get-tuple-element.20), channel_id=1, source_target_pairs={{32,0},{64,32},{96,64},{128,96},{160,128},{192,160},{224,192},{256... | collective-permute-start | bytes 294920 | tf_op jit(solution)/shard_map/ppermute | solution.py:431
  36.6 5.5 %collective-permute-done.1.high = f32[6,8,512]{2,1,0:T(8,128)S(1)} collective-permute-done((f32[6,8,512]{2,1,0:T(8,128)S(1)}, f32[6,8,512]{2,1,0:T(8,128)S(1)}, u32[]{:S(2)}, u32[]{:S(2)}) %collective-permute-start.1) | collective-permute-done | bytes 98336 | tf_op jit(solution)/shard_map/ppermute | solution.py:431
  42.2 3.1 %collective-permute-start.2 = (f32[42,512]{1,0:T(8,128)S(1)}, f32[42,512]{1,0:T(8,128)S(1)}, u32[]{:S(2)}, u32[]{:S(2)}) collective-permute-start(f32[42,512]{1,0:T(8,128)S(1)} %get-tuple-element.21), channel_id=1, source_target_pairs={{0,1},{1,2},{2,3},{3,4},{4,5},{5,6},{6,7},{7,8},{8,9},{9,10},{10,1... | collective-permute-start | bytes 258056 | tf_op jit(solution)/shard_map/ppermute | solution.py:431
  45.3 4.3 %collective-permute-start.3 = (f32[42,512]{1,0:T(8,128)S(1)}, f32[42,512]{1,0:T(8,128)S(1)}, u32[]{:S(2)}, u32[]{:S(2)}) collective-permute-start(f32[42,512]{1,0:T(8,128)S(1)} %get-tuple-element.22), channel_id=1, source_target_pairs={{1,0},{2,1},{3,2},{4,3},{5,4},{6,5},{7,6},{8,7},{9,8},{10,9},{11,1... | collective-permute-start | bytes 258056 | tf_op jit(solution)/shard_map/ppermute | solution.py:431
  49.6 0.6 fusion.3
  50.2 0.6 reshape.44.cond
  50.8 0.6 reshape.43.holder
  51.4 0.7 concatenate.9.par
  52.1 0.7 copy-done.16
  52.7 3.8 %shard_map.143 = (f32[7,9,16,512]{3,2,1,0:T(8,128)S(1)}, f32[8,16,512]{2,1,0:T(8,128)S(1)}, f32[4,8,512]{2,1,0:T(8,128)S(1)}, f32[24,512]{1,0:T(8,128)S(1)}) custom-call(f32[4,8,512]{2,1,0:T(8,128)S(1)} %copy-done, s32[4,8,512]{2,1,0:T(8,128)S(1)} %copy-done.1, s32[4,8,512]{2,1,0:T(8,128)S(1)} %copy-done.5, f32[6,8,512]{2,1,0:T(8,128)S(1)} %collective-permute-done.low, ...), custom_call_target="tpu_custom_call" | custom-call | flops 1000000 | bytes 1000000 | tf_op jit(solution)/shard_map/pallas_call | solution.py:480
  56.6 0.7 copy-done.6
  57.3 0.6 copy-done.8
  57.9 0.8 broadcast_in_dim.41.live
  58.7 0.8 copy-done.9
  59.5 0.7 copy-done.10
  60.2 0.6 copy-done.15
  60.8 1.7 %shard_map.144 = (f32[4,8,512]{2,1,0:T(8,128)S(1)}, f32[4,8,512]{2,1,0:T(8,128)S(1)}, f32[12,128,128]{2,1,0:T(8,128)S(1)}) custom-call(s32[32]{0:T(128)S(1)} %copy-done.15, f32[54]{0:T(128)S(1)} %copy-done.10, f32[32,48,128]{2,1,0:T(8,128)S(1)} %all-to-all-done.1.coming, f32[4,8,512]{2,1,0:T(8,128)S(1)} %copy-done, f32[4,8,512]{2,1,0:T(8,128)S(1)} %copy-done.9, ...), custom_call_target="tpu_custom_call" | custom-call | flops 1000000 | bytes 1000000 | tf_op jit(solution)/shard_map/pallas_call | solution.py:490
  62.6 3.5 %collective-permute-start.4 = (f32[3,8,512]{2,1,0:T(8,128)S(1)}, f32[3,8,512]{2,1,0:T(8,128)S(1)}, u32[]{:S(2)}, u32[]{:S(2)}) collective-permute-start(f32[3,8,512]{2,1,0:T(8,128)S(1)} %pad_maximum_fusion), channel_id=1, source_target_pairs={{0,32},{32,64},{64,96},{96,128},{128,160},{160,192},{192,224},{224... | collective-permute-start | bytes 147464 | tf_op jit(solution)/shard_map/ppermute | solution.py:431
  66.1 1.9 %collective-permute-start.5 = (f32[3,8,512]{2,1,0:T(8,128)S(1)}, f32[3,8,512]{2,1,0:T(8,128)S(1)}, u32[]{:S(2)}, u32[]{:S(2)}) collective-permute-start(f32[3,8,512]{2,1,0:T(8,128)S(1)} %pad_maximum_fusion.1), channel_id=1, source_target_pairs={{32,0},{64,32},{96,64},{128,96},{160,128},{192,160},{224,192},{256... | collective-permute-start | bytes 147464 | tf_op jit(solution)/shard_map/ppermute | solution.py:431
  68.0 4.7 %collective-permute-done.5.high = f32[3,8,512]{2,1,0:T(8,128)S(1)} collective-permute-done((f32[3,8,512]{2,1,0:T(8,128)S(1)}, f32[3,8,512]{2,1,0:T(8,128)S(1)}, u32[]{:S(2)}, u32[]{:S(2)}) %collective-permute-start.5) | collective-permute-done | bytes 49184 | tf_op jit(solution)/shard_map/ppermute | solution.py:431
  72.8 2.5 %collective-permute-start.6 = (f32[22,512]{1,0:T(8,128)S(1)}, f32[22,512]{1,0:T(8,128)S(1)}, u32[]{:S(2)}, u32[]{:S(2)}) collective-permute-start(f32[22,512]{1,0:T(8,128)S(1)} %get-tuple-element.26), channel_id=1, source_target_pairs={{0,1},{1,2},{2,3},{3,4},{4,5},{5,6},{6,7},{7,8},{8,9},{9,10},{10,1... | collective-permute-start | bytes 135176 | tf_op jit(solution)/shard_map/ppermute | solution.py:431
  75.3 4.9 %collective-permute-start.7 = (f32[22,512]{1,0:T(8,128)S(1)}, f32[22,512]{1,0:T(8,128)S(1)}, u32[]{:S(2)}, u32[]{:S(2)}) collective-permute-start(f32[22,512]{1,0:T(8,128)S(1)} %get-tuple-element.27), channel_id=1, source_target_pairs={{1,0},{2,1},{3,2},{4,3},{5,4},{6,5},{7,6},{8,7},{9,8},{10,9},{11,1... | collective-permute-start | bytes 135176 | tf_op jit(solution)/shard_map/ppermute | solution.py:431
  80.2 0.7 copy-done.11
  80.8 1.5 %shard_map.146.parts = f32[4,4,8,512]{3,2,1,0:T(8,128)S(1)} custom-call(f32[54]{0:T(128)S(1)} %copy-done.11, f32[12,128,128]{2,1,0:T(8,128)S(1)} %get-tuple-element.30.states_in, f32[4,8,512]{2,1,0:T(8,128)S(1)} %get-tuple-element.24.v1), custom_call_target="tpu_custom_call" | custom-call | flops 1000000 | bytes 1000000 | tf_op jit(solution)/shard_map/pallas_call | solution.py:497
  82.4 0.6 copy-done.17
  83.0 2.9 %shard_map.147 = (f32[4,8,512]{2,1,0:T(8,128)}, f32[4,8,512]{2,1,0:T(8,128)S(1)}, f32[32,16,128]{2,1,0:T(8,128)}) custom-call(s32[32]{0:T(128)S(1)} %copy-done.17, f32[54]{0:T(128)S(1)} %copy-done.12, f32[4,8,512]{2,1,0:T(8,128)S(1)} %copy-done, f32[4,8,512]{2,1,0:T(8,128)S(1)} %get-tuple-element.24.v1, f32[4,8,512]{2,1,0:T(8,128)S(1)} %get-tuple-element.25.current, ...), custom_call_target="tpu_custom_call" | custom-call | flops 1000000 | bytes 1000000 | tf_op jit(solution)/shard_map/pallas_call | solution.py:502
  85.9 6.9 %all-to-all-start.2 = ((f32[32,16,128]{2,1,0:T(8,128)}), f32[32,16,128]{2,1,0:T(8,128)S(1)}, u32[]{:S(2)}, u32[]{:S(2)}) async-start(f32[32,16,128]{2,1,0:T(8,128)} %get-tuple-element.32), calls=%async_computation.2 | async-start | bytes 524288 | tf_op jit(solution)/shard_map/all_to_all | solution.py:435
  92.9 1.9 %collective-permute-start.9 = (f32[1,8,512]{2,1,0:T(8,128)S(1)}, f32[1,8,512]{2,1,0:T(8,128)S(1)}, u32[]{:S(2)}, u32[]{:S(2)}) collective-permute-start(f32[1,8,512]{2,1,0:T(8,128)S(1)} %get-tuple-element.41), channel_id=1, source_target_pairs={{32,0},{64,32},{96,64},{128,96},{160,128},{192,160},{224,192},{256... | collective-permute-start | bytes 49160 | tf_op jit(solution)/shard_map/ppermute | solution.py:431
  94.8 4.9 %collective-permute-start.8 = (f32[1,8,512]{2,1,0:T(8,128)S(1)}, f32[1,8,512]{2,1,0:T(8,128)S(1)}, u32[]{:S(2)}, u32[]{:S(2)}) collective-permute-start(f32[1,8,512]{2,1,0:T(8,128)S(1)} %get-tuple-element.42), channel_id=1, source_target_pairs={{0,32},{32,64},{64,96},{96,128},{128,160},{160,192},{192,224},{224... | collective-permute-start | bytes 49160 | tf_op jit(solution)/shard_map/ppermute | solution.py:431
  99.7 4.6 %collective-permute-start.11 = (f32[4,1,512]{2,1,0:T(1,128)S(1)}, f32[4,1,512]{2,1,0:T(1,128)S(1)}, u32[]{:S(2)}, u32[]{:S(2)}) collective-permute-start(f32[4,1,512]{2,1,0:T(1,128)S(1)} %get-tuple-element.39), channel_id=1, source_target_pairs={{1,0},{2,1},{3,2},{4,3},{5,4},{6,5},{7,6},{8,7},{9,8},{10,9},{11,1... | collective-permute-start | bytes 24584 | tf_op jit(solution)/shard_map/ppermute | solution.py:431
  104.3 1.9 %collective-permute-start.10 = (f32[4,1,512]{2,1,0:T(1,128)S(1)}, f32[4,1,512]{2,1,0:T(1,128)S(1)}, u32[]{:S(2)}, u32[]{:S(2)}) collective-permute-start(f32[4,1,512]{2,1,0:T(1,128)S(1)} %get-tuple-element.40), channel_id=1, source_target_pairs={{0,1},{1,2},{2,3},{3,4},{4,5},{5,6},{6,7},{7,8},{8,9},{9,10},{10,1... | collective-permute-start | bytes 24584 | tf_op jit(solution)/shard_map/ppermute | solution.py:431
  106.2 4.6 %collective-permute-done.10.left = f32[4,1,512]{2,1,0:T(1,128)S(1)} collective-permute-done((f32[4,1,512]{2,1,0:T(1,128)S(1)}, f32[4,1,512]{2,1,0:T(1,128)S(1)}, u32[]{:S(2)}, u32[]{:S(2)}) %collective-permute-start.10) | collective-permute-done | bytes 8224 | tf_op jit(solution)/shard_map/ppermute | solution.py:431
  110.8 1.9 %shard_map.149 = f32[3,4,8,512]{3,2,1,0:T(8,128)} custom-call(f32[4,8,512]{2,1,0:T(8,128)S(1)} %get-tuple-element.33.ours, f32[1,8,512]{2,1,0:T(8,128)S(1)} %collective-permute-done.8.below, f32[1,8,512]{2,1,0:T(8,128)S(1)} %collective-permute-done.9.above, f32[4,1,512]{2,1,0:T(1,128)S(1)} %collective-permute-done.10.left, ...), custom_call_target="tpu_custom_call" | custom-call | flops 1000000 | bytes 1000000 | tf_op jit(solution)/shard_map/pallas_call | solution.py:514
  112.6 2.5 %shard_map.148 = f32[12,16,512]{2,1,0:T(8,128)} custom-call(s32[32]{0:T(128)S(1)} %copy-done.14, f32[54]{0:T(128)S(1)} %copy-done.12, f32[32,16,128]{2,1,0:T(8,128)S(1)} %all-to-all-done.2.returned, f32[12,16,512]{2,1,0:T(8,128)S(1)} %copy-done.3), custom_call_target="tpu_custom_call" | custom-call | flops 1000000 | bytes 1000000 | tf_op jit(solution)/shard_map/pallas_call | solution.py:518
  (60 shorter events, 0.3 us)
Async XLA Ops:
  0.6 26.5 %copy-start.1 = (s32[4,8,512]{2,1,0:T(8,128)S(1)}, s32[4,8,512]{2,1,0:T(8,128)}, u32[]{:S(2)}) copy-start(s32[4,8,512]{2,1,0:T(8,128)} %tissue.9) | copy-start | bytes 196612
  0.6 26.5 %copy-start = (f32[4,8,512]{2,1,0:T(8,128)S(1)}, f32[4,8,512]{2,1,0:T(8,128)}, u32[]{:S(2)}) copy-start(f32[4,8,512]{2,1,0:T(8,128)} %v0.1) | copy-start | bytes 196612
  2.8 16.7 %all-to-all-start = ((s32[32,1,128]{2,1,0:T(1,128)}), s32[32,1,128]{2,1,0:T(1,128)S(1)}, u32[]{:S(2)}, u32[]{:S(2)}) async-start(s32[32,1,128]{2,1,0:T(1,128)} %broadcast_in_dim.40), calls=%async_computation | async-start | bytes 32768 | tf_op jit(solution)/shard_map/all_to_all | solution.py:435
  12.4 1.0 copy-start.2
  13.4 13.7 %copy-start.4 = (f32[4,8,512]{2,1,0:T(8,128)S(1)}, f32[4,8,512]{2,1,0:T(8,128)}, u32[]{:S(2)}) copy-start(f32[4,8,512]{2,1,0:T(8,128)} %lag.5) | copy-start | bytes 196612
  13.4 13.7 %copy-start.5 = (s32[4,8,512]{2,1,0:T(8,128)S(1)}, s32[4,8,512]{2,1,0:T(8,128)}, u32[]{:S(2)}) copy-start(s32[4,8,512]{2,1,0:T(8,128)} %fiber.5) | copy-start | bytes 196612
  13.4 36.1 %copy-start.18 = (s32[4,8]{1,0:T(4,128)S(1)}, s32[4,8]{1,0:T(4,128)}, u32[]{:S(2)}) copy-start(s32[4,8]{1,0:T(4,128)} %param.17) | copy-start | bytes 388
  13.5 36.7 %copy-start.19 = (f32[6,16]{1,0:T(8,128)S(1)}, f32[6,16]{1,0:T(8,128)}, u32[]{:S(2)}) copy-start(f32[6,16]{1,0:T(8,128)} %param.16) | copy-start | bytes 1156
  13.5 37.9 %copy-start.20 = (f32[12]{0:T(128)S(1)}, f32[12]{0:T(128)}, u32[]{:S(2)}) copy-start(f32[12]{0:T(128)} %param.19) | copy-start | bytes 148
  13.5 37.9 %copy-start.21 = (f32[12]{0:T(128)S(1)}, f32[12]{0:T(128)}, u32[]{:S(2)}) copy-start(f32[12]{0:T(128)} %param.20) | copy-start | bytes 148
  13.5 37.9 %copy-start.22 = (f32[12]{0:T(128)S(1)}, f32[12]{0:T(128)}, u32[]{:S(2)}) copy-start(f32[12]{0:T(128)} %param.21) | copy-start | bytes 148
  13.5 37.9 %copy-start.23 = (f32[12]{0:T(128)S(1)}, f32[12]{0:T(128)}, u32[]{:S(2)}) copy-start(f32[12]{0:T(128)} %param.22) | copy-start | bytes 148
  13.5 37.9 %copy-start.24 = (f32[6]{0:T(128)S(1)}, f32[6]{0:T(128)}, u32[]{:S(2)}) copy-start(f32[6]{0:T(128)} %param.23) | copy-start | bytes 76
  20.1 1.5 %copy-start.13 = (s32[32]{0:T(128)}, s32[32]{0:T(128)S(1)}, u32[]{:S(2)}) copy-start(s32[32]{0:T(128)S(1)} %slice_reduce_fusion.arrived) | copy-start | bytes 388
  21.6 36.3 %all-to-all-start.1 = ((f32[32,48,128]{2,1,0:T(8,128)}), f32[32,48,128]{2,1,0:T(8,128)S(1)}, u32[]{:S(2)}, u32[]{:S(2)}) async-start(f32[32,48,128]{2,1,0:T(8,128)} %shard_map.140), calls=%async_computation.1 | async-start | bytes 1572864 | tf_op jit(solution)/shard_map/all_to_all | solution.py:435
  27.2 9.4 %collective-permute-start = (f32[6,8,512]{2,1,0:T(8,128)S(1)}, f32[6,8,512]{2,1,0:T(8,128)S(1)}, u32[]{:S(2)}, u32[]{:S(2)}) collective-permute-start(f32[6,8,512]{2,1,0:T(8,128)S(1)} %get-tuple-element.19), channel_id=1, source_target_pairs={{0,32},{32,64},{64,96},{96,128},{128,160},{160,192},{192,224},{224... | collective-permute-start | bytes 294920 | tf_op jit(solution)/shard_map/ppermute | solution.py:431
  34.7 7.4 %collective-permute-start.1 = (f32[6,8,512]{2,1,0:T(8,128)S(1)}, f32[6,8,512]{2,1,0:T(8,128)S(1)}, u32[]{:S(2)}, u32[]{:S(2)}) collective-permute-start(f32[6,8,512]{2,1,0:T(8,128)S(1)} %get-tuple-element.20), channel_id=1, source_target_pairs={{32,0},{64,32},{96,64},{128,96},{160,128},{192,160},{224,192},{256... | collective-permute-start | bytes 294920 | tf_op jit(solution)/shard_map/ppermute | solution.py:431
  42.2 9.9 %collective-permute-start.2 = (f32[42,512]{1,0:T(8,128)S(1)}, f32[42,512]{1,0:T(8,128)S(1)}, u32[]{:S(2)}, u32[]{:S(2)}) collective-permute-start(f32[42,512]{1,0:T(8,128)S(1)} %get-tuple-element.21), channel_id=1, source_target_pairs={{0,1},{1,2},{2,3},{3,4},{4,5},{5,6},{6,7},{7,8},{8,9},{9,10},{10,1... | collective-permute-start | bytes 258056 | tf_op jit(solution)/shard_map/ppermute | solution.py:431
  45.3 6.8 %collective-permute-start.3 = (f32[42,512]{1,0:T(8,128)S(1)}, f32[42,512]{1,0:T(8,128)S(1)}, u32[]{:S(2)}, u32[]{:S(2)}) collective-permute-start(f32[42,512]{1,0:T(8,128)S(1)} %get-tuple-element.22), channel_id=1, source_target_pairs={{1,0},{2,1},{3,2},{4,3},{5,4},{6,5},{7,6},{8,7},{9,8},{10,9},{11,1... | collective-permute-start | bytes 258056 | tf_op jit(solution)/shard_map/ppermute | solution.py:431
  52.1 0.7 copy-start.16
  56.5 0.7 copy-start.6
  57.3 0.6 copy-start.8
  57.9 24.5 %copy-start.7 = (f32[8,16,512]{2,1,0:T(8,128)S(1)}, f32[8,16,512]{2,1,0:T(8,128)}, u32[]{:S(2)}) copy-start(f32[8,16,512]{2,1,0:T(8,128)} %copy-done.6) | copy-start | bytes 786436
  58.7 0.8 copy-start.9
  59.5 0.7 copy-start.10
  60.2 0.6 copy-start.15
  60.8 21.5 %copy-start.12 = (f32[54]{0:T(128)S(1)}, f32[54]{0:T(128)}, u32[]{:S(2)}) copy-start(f32[54]{0:T(128)} %concatenate.9.par) | copy-start | bytes 652
  62.6 5.5 %collective-permute-start.4 = (f32[3,8,512]{2,1,0:T(8,128)S(1)}, f32[3,8,512]{2,1,0:T(8,128)S(1)}, u32[]{:S(2)}, u32[]{:S(2)}) collective-permute-start(f32[3,8,512]{2,1,0:T(8,128)S(1)} %pad_maximum_fusion), channel_id=1, source_target_pairs={{0,32},{32,64},{64,96},{96,128},{128,160},{160,192},{192,224},{224... | collective-permute-start | bytes 147464 | tf_op jit(solution)/shard_map/ppermute | solution.py:431
  66.1 6.6 %collective-permute-start.5 = (f32[3,8,512]{2,1,0:T(8,128)S(1)}, f32[3,8,512]{2,1,0:T(8,128)S(1)}, u32[]{:S(2)}, u32[]{:S(2)}) collective-permute-start(f32[3,8,512]{2,1,0:T(8,128)S(1)} %pad_maximum_fusion.1), channel_id=1, source_target_pairs={{32,0},{64,32},{96,64},{128,96},{160,128},{192,160},{224,192},{256... | collective-permute-start | bytes 147464 | tf_op jit(solution)/shard_map/ppermute | solution.py:431
  72.8 9.5 %collective-permute-start.6 = (f32[22,512]{1,0:T(8,128)S(1)}, f32[22,512]{1,0:T(8,128)S(1)}, u32[]{:S(2)}, u32[]{:S(2)}) collective-permute-start(f32[22,512]{1,0:T(8,128)S(1)} %get-tuple-element.26), channel_id=1, source_target_pairs={{0,1},{1,2},{2,3},{3,4},{4,5},{5,6},{6,7},{7,8},{8,9},{9,10},{10,1... | collective-permute-start | bytes 135176 | tf_op jit(solution)/shard_map/ppermute | solution.py:431
  75.3 7.1 %collective-permute-start.7 = (f32[22,512]{1,0:T(8,128)S(1)}, f32[22,512]{1,0:T(8,128)S(1)}, u32[]{:S(2)}, u32[]{:S(2)}) collective-permute-start(f32[22,512]{1,0:T(8,128)S(1)} %get-tuple-element.27), channel_id=1, source_target_pairs={{1,0},{2,1},{3,2},{4,3},{5,4},{6,5},{7,6},{8,7},{9,8},{10,9},{11,1... | collective-permute-start | bytes 135176 | tf_op jit(solution)/shard_map/ppermute | solution.py:431
  80.2 0.7 copy-start.11
  82.3 30.3 %copy-start.3 = (f32[12,16,512]{2,1,0:T(8,128)S(1)}, f32[12,16,512]{2,1,0:T(8,128)}, u32[]{:S(2)}) copy-start(f32[12,16,512]{2,1,0:T(8,128)} %gates.3) | copy-start | bytes 1179652
  82.3 30.3 %copy-start.14 = (s32[32]{0:T(128)S(1)}, s32[32]{0:T(128)}, u32[]{:S(2)}) copy-start(s32[32]{0:T(128)} %copy-done.13) | copy-start | bytes 388
  82.4 0.6 copy-start.17
  85.9 26.7 %all-to-all-start.2 = ((f32[32,16,128]{2,1,0:T(8,128)}), f32[32,16,128]{2,1,0:T(8,128)S(1)}, u32[]{:S(2)}, u32[]{:S(2)}) async-start(f32[32,16,128]{2,1,0:T(8,128)} %get-tuple-element.32), calls=%async_computation.2 | async-start | bytes 524288 | tf_op jit(solution)/shard_map/all_to_all | solution.py:435
  92.9 17.9 %collective-permute-start.9 = (f32[1,8,512]{2,1,0:T(8,128)S(1)}, f32[1,8,512]{2,1,0:T(8,128)S(1)}, u32[]{:S(2)}, u32[]{:S(2)}) collective-permute-start(f32[1,8,512]{2,1,0:T(8,128)S(1)} %get-tuple-element.41), channel_id=1, source_target_pairs={{32,0},{64,32},{96,64},{128,96},{160,128},{192,160},{224,192},{256... | collective-permute-start | bytes 49160 | tf_op jit(solution)/shard_map/ppermute | solution.py:431
  94.8 16.0 %collective-permute-start.8 = (f32[1,8,512]{2,1,0:T(8,128)S(1)}, f32[1,8,512]{2,1,0:T(8,128)S(1)}, u32[]{:S(2)}, u32[]{:S(2)}) collective-permute-start(f32[1,8,512]{2,1,0:T(8,128)S(1)} %get-tuple-element.42), channel_id=1, source_target_pairs={{0,32},{32,64},{64,96},{96,128},{128,160},{160,192},{192,224},{224... | collective-permute-start | bytes 49160 | tf_op jit(solution)/shard_map/ppermute | solution.py:431
  99.7 6.5 %collective-permute-start.11 = (f32[4,1,512]{2,1,0:T(1,128)S(1)}, f32[4,1,512]{2,1,0:T(1,128)S(1)}, u32[]{:S(2)}, u32[]{:S(2)}) collective-permute-start(f32[4,1,512]{2,1,0:T(1,128)S(1)} %get-tuple-element.39), channel_id=1, source_target_pairs={{1,0},{2,1},{3,2},{4,3},{5,4},{6,5},{7,6},{8,7},{9,8},{10,9},{11,1... | collective-permute-start | bytes 24584 | tf_op jit(solution)/shard_map/ppermute | solution.py:431
  104.3 6.5 %collective-permute-start.10 = (f32[4,1,512]{2,1,0:T(1,128)S(1)}, f32[4,1,512]{2,1,0:T(1,128)S(1)}, u32[]{:S(2)}, u32[]{:S(2)}) collective-permute-start(f32[4,1,512]{2,1,0:T(1,128)S(1)} %get-tuple-element.40), channel_id=1, source_target_pairs={{0,1},{1,2},{2,3},{3,4},{4,5},{5,6},{6,7},{7,8},{8,9},{9,10},{10,1... | collective-permute-start | bytes 24584 | tf_op jit(solution)/shard_map/ppermute | solution.py:431

commit v4 on v3

--- a/solution.py
+++ b/solution.py
@@ -22,7 +22,7 @@
 PHASE_REF = -0.2
 PHASE_SOFT = 0.5
 COMPONENT = ((0, 3, 4), (3, 1, 5), (4, 5, 2))
-HALF, STEEP, TMIN, TSPAN, CHANNEL = 0, 12, 24, 36, 48
+HALF, STEEP, TMIN, TSPAN, CHANNEL, COND, PARAMS = 0, 12, 24, 36, 48, 54, 256
 
 f32 = jnp.float32
 VM = pl.BlockSpec(memory_space=pltpu.VMEM)
@@ -42,6 +42,21 @@
     )
 
 
+def fetched(pairs, sems):
+    copies = [pltpu.make_async_copy(a, b, sems.at[n]) for n, (a, b) in enumerate(pairs)]
+    for copy in copies:
+        copy.start()
+    return copies
+
+
+def live_plane(worker, i):
+    row = lax.broadcasted_iota(jnp.int32, (CY, CZ), 0)
+    mask = jnp.zeros((CY, CZ), f32)
+    for j in range(CY):
+        mask = jnp.where(row == j, jnp.where(worker[i, j] >= 0, 1.0, 0.0), mask)
+    return mask
+
+
 def chunk(c):
     return pl.ds(c * LANES, LANES)
 
@@ -83,7 +98,9 @@
     )
 
 
-def start_body(voltage, lag, tissue, fiber, up_ref, down_ref):
+def start_body(voltage_in, lag_in, tissue_in, fiber_in, up_ref, down_ref, right_ref, left_ref, voltage, lag, tissue, fiber, sems):
+    for copy in fetched(((voltage_in, voltage), (lag_in, lag), (tissue_in, tissue), (fiber_in, fiber)), sems):
+        copy.wait()
     for ref, outer, pair in ((up_ref, CX - 1, (CX - 2, CX - 1)), (down_ref, 0, (0, 1))):
         w = tissue[outer].astype(f32)
         ref[0] = w * voltage[outer]
@@ -91,13 +108,9 @@
         for n, i in enumerate(pair):
             ref[2 + n] = fiber[i].astype(f32)
             ref[4 + n] = tissue[i].astype(f32)
-
-
-def columns_body(voltage, lag, tissue, fiber, low, high, up_ref, down_ref):
-    for ref, outer, pair in ((up_ref, CY - 1, (CY - 2, CY - 1)), (down_ref, 0, (0, 1))):
+    for ref, outer, pair in ((right_ref, CY - 1, (CY - 2, CY - 1)), (left_ref, 0, (0, 1))):
+        ref[...] = jnp.zeros(ref.shape, f32)
         one = slice(outer, outer + 1)
-        ref[0:1] = low[0, one]
-        ref[CX + 1 : CX + 2] = high[0, one]
         for i in range(CX):
             w = tissue[i, one].astype(f32)
             ref[1 + i : 2 + i] = w * voltage[i, one]
@@ -105,13 +118,24 @@
         at = 2 * CX + 2
         for n, j in enumerate(pair):
             one = slice(j, j + 1)
+            for i in range(CX):
+                ref[at + n * NI + 2 + i : at + n * NI + 3 + i] = fiber[i, one].astype(f32)
+                ref[at + (2 + n) * NI + 2 + i : at + (2 + n) * NI + 3 + i] = tissue[i, one].astype(f32)
+
+
+def columns_body(right_in, left_in, low, high, up_ref, down_ref):
+    for ref, own, outer, pair in ((up_ref, right_in, CY - 1, (CY - 2, CY - 1)), (down_ref, left_in, 0, (0, 1))):
+        ref[...] = own[...]
+        one = slice(outer, outer + 1)
+        ref[0:1] = low[0, one]
+        ref[CX + 1 : CX + 2] = high[0, one]
+        at = 2 * CX + 2
+        for n, j in enumerate(pair):
+            one = slice(j, j + 1)
             for m in range(2):
                 for kind, base in ((2, at + n * NI), (4, at + (2 + n) * NI)):
                     ref[base + m : base + m + 1] = low[kind + m, one]
                     ref[base + CX + 2 + m : base + CX + 3 + m] = high[kind + m, one]
-            for i in range(CX):
-                ref[at + n * NI + 2 + i : at + n * NI + 3 + i] = fiber[i, one].astype(f32)
-                ref[at + (2 + n) * NI + 2 + i : at + (2 + n) * NI + 3 + i] = tissue[i, one].astype(f32)
 
 
 def by_row_body(gates, out_ref):
@@ -173,12 +197,19 @@
     return total
 
 
-def faces_body(voltage, tissue, fiber, low, high, left, right, cond, faces_out, weights_ref, base_ref, lag_ref, faces_ref, field_ref, fib_ref, stack_ref, sems):
+def faces_body(
+    voltage_in, tissue_in, fiber_in, par_in, low, high, left, right,
+    faces_out, weights_out, base_out, lag_out,
+    voltage, tissue, fiber, cond, faces_ref, weights_ref, base_ref, lag_ref, field_ref, fib_ref, stack_ref, sems, in_sems,
+):
+    coming = fetched(((voltage_in, voltage), (tissue_in, tissue), (fiber_in, fiber), (par_in, cond)), in_sems)
     zero = jnp.zeros((NI, NJ, CZ), f32)
     field_ref[...] = zero
     fib_ref[...] = zero
     weights_ref[...] = zero
     own = slice(2, 2 + CY)
+    for copy in coming:
+        copy.wait()
     for i in range(CX):
         w = tissue[i].astype(f32)
         field_ref[2 + i, own, :] = w * voltage[i]
@@ -202,10 +233,10 @@
         for c in range(CHUNKS):
             fib = fib_ref[i, :, chunk(c)]
             w = weights_ref[i, :, chunk(c)]
-            found = [jnp.full((NJ, LANES), cond[n * FIB]) for n in range(6)]
+            found = [jnp.full((NJ, LANES), cond[COND + n * FIB]) for n in range(6)]
             for k in range(1, FIB):
                 here = fib == float(k)
-                found = [jnp.where(here, cond[n * FIB + k], old) for n, old in enumerate(found)]
+                found = [jnp.where(here, cond[COND + n * FIB + k], old) for n, old in enumerate(found)]
             for n in range(6):
                 stack_ref[n, i, :, chunk(c)] = 0.5 * (w * found[n])
         return carry
@@ -216,10 +247,11 @@
     lag_ref[2 * CY : 2 * CY + CX] = left[CX + 2 : 2 * CX + 2]
     lag_ref[2 * CY + CX : 2 * CY + 2 * CX] = right[CX + 2 : 2 * CX + 2]
     z = lax.broadcasted_iota(jnp.int32, (NJ, CZ), 1)
-    copies = []
+    copies = fetched(((weights_ref, weights_out), (lag_ref, lag_out)), sems)
+    late = 2
     for i in range(NI - 1):
         if i > 1:
-            copies.append(pltpu.make_async_copy(faces_ref.at[i - 1], faces_out.at[i - 1], sems.at[i - 1]))
+            copies.append(pltpu.make_async_copy(faces_ref.at[i - 1], faces_out.at[i - 1], sems.at[late + i - 1]))
             copies[-1].start()
         w = weights_ref[i]
         both = w * weights_ref[i + 1]
@@ -237,38 +269,46 @@
             here = stack_ref[comp, i]
             faces_ref[i, 6 + n] = (here + up_z(here)) * both
     for i in (0, NI - 2):
-        copies.append(pltpu.make_async_copy(faces_ref.at[i], faces_out.at[i], sems.at[i]))
+        copies.append(pltpu.make_async_copy(faces_ref.at[i], faces_out.at[i], sems.at[late + i]))
         copies[-1].start()
     field = {i: field_ref[i] for i in range(1, NI - 1)}
     spread = spread_of(field, lambda n, i: faces_ref[i, n], 2, CX + 1)
     for i in range(CX):
         base_ref[i] = voltage[i] + tissue[i].astype(f32) * spread[2 + i][2 : 2 + CY]
+    copies.append(pltpu.make_async_copy(base_ref, base_out, sems.at[late + NI - 1]))
+    copies[-1].start()
     for copy in copies:
         copy.wait()
 
 
-def react_body(holder, par, coming, voltage, base, tissue, live, v1_ref, current_ref, states_ref, v_d, base_d, w_d, live_d, out_d, cur_d):
-    for i in range(CX):
-        mask = jnp.concatenate([live[i]] * CHUNKS, axis=1)
+def react_body(
+    worker, voltage_in, base_in, tissue_in, par_in, coming,
+    v1_ref, current_ref, states_ref, voltage, base, tissue, par, v_d, base_d, w_d, out_d, cur_d, sems,
+):
+    for copy in fetched(((voltage_in, voltage), (base_in, base), (tissue_in, tissue), (par_in, par)), sems):
+        copy.wait()
+    for i in range(CX):
         to_dense(v_d, voltage[i], i)
         to_dense(base_d, base[i], i)
-        to_dense(w_d, tissue[i].astype(f32) * mask, i)
-        to_dense(live_d, mask, i)
+        to_dense(w_d, tissue[i].astype(f32), i)
+    low_half = lax.broadcasted_iota(jnp.int32, (8, LANES), 0) < CHUNKS
 
     def pair(p, carry):
         rows = pl.ds(pl.multiple_of(p * 8, 8), 8)
-        first, second = holder[2 * p], holder[2 * p + 1]
+        owners = [worker[p // (CY // 2), 2 * (p % (CY // 2)) + m] for m in range(2)]
+        first, second = [jnp.maximum(k, 0) // CAP for k in owners]
+        live = jnp.where(low_half, *[jnp.where(k >= 0, 1.0, 0.0) for k in owners])
         level = v_d[rows, :]
         states = [
             jnp.concatenate([coming[first, pl.ds(g * CHUNKS, CHUNKS), :], coming[second, pl.ds(g * CHUNKS, CHUNKS), :]], axis=0)
             for g in range(GATES)
         ]
-        after = base_d[rows, :] - w_d[rows, :] * (STEP_DT * current_from(level, factors(states, par), par))
+        after = base_d[rows, :] - w_d[rows, :] * (STEP_DT * (live * current_from(level, factors(states, par), par)))
         states = [updated(level, s, par, g) for g, s in enumerate(states)]
         for g in range(GATES):
             states_ref[g, rows, :] = states[g]
         out_d[rows, :] = after
-        cur_d[rows, :] = live_d[rows, :] * current_from(after, factors(states, par), par)
+        cur_d[rows, :] = live * current_from(after, factors(states, par), par)
         return carry
 
     lax.fori_loop(0, TILES // 2, pair, 0)
@@ -278,7 +318,10 @@
             current_ref[i, :, chunk(c)] = from_dense(cur_d, i, c)
 
 
-def second_body(par, states_in, v1, parts_ref, v_d, parts_d):
+def second_body(par_in, states_in, v1, parts_ref, v_d, parts_d, par, sem):
+    fetch = pltpu.make_async_copy(par_in, par, sem)
+    fetch.start()
+    fetch.wait()
     for i in range(CX):
         to_dense(v_d, v1[i], i)
 
@@ -315,9 +358,13 @@
             ref[at + 1 + i : at + 2 + i] = current[i, one]
 
 
-def steps_body(slots, tile_of, par, v0, v1, current, low, high, left, right, weights, faces_in, parts, live, v3_ref, ours_ref, used_ref, faces, v_ref, cur_ref, next_ref, rows_ref, sem):
-    fetch = pltpu.make_async_copy(faces_in, faces, sem)
-    fetch.start()
+def steps_body(
+    slots, worker, tile_of_in, par_in, v0, weights, faces, v1, current, low, high, left, right, parts,
+    v3_ref, ours_ref, used_ref, tile_of, par, v_ref, cur_ref, next_ref, rows_ref, sems,
+):
+    fetches = fetched(
+        ((par_in, par), (tile_of_in, tile_of)), sems
+    )
     v_ref[...] = jnp.zeros((NI, NJ, CZ), f32)
     cur_ref[...] = jnp.zeros((NI, NJ, CZ), f32)
     own = slice(2, 2 + CY)
@@ -336,8 +383,9 @@
         for i in range(CX + 2):
             cur_ref[1 + i, outer : outer + 1, :] = ref[2 * NI + i : 2 * NI + i + 1, :]
     face = lambda n, i: faces[i, n]
+    for fetch in fetches:
+        fetch.wait()
     field = {i: weights[i] * v_ref[i] for i in range(NI)}
-    fetch.wait()
     spread = spread_of(field, face, 1, NI - 2)
     for i in range(1, NI - 1):
         next_ref[i] = v_ref[i] + weights[i] * (spread[i] - STEP_DT * cur_ref[i])
@@ -346,8 +394,7 @@
     for i in range(CX):
         v2 = next_ref[2 + i, own, :]
         w = weights[2 + i, own, :]
-        mask = jnp.concatenate([live[i]] * CHUNKS, axis=1)
-        found = mask * current_from(v2, [parts[n, i] for n in range(4)], par)
+        found = live_plane(worker, i) * current_from(v2, [parts[n, i] for n in range(4)], par)
         v3 = v2 + w * (spread[2 + i][own] - STEP_DT * found)
         v3_ref[i] = v3
         ours_ref[i] = w * (v3 - PHASE_REF)
@@ -360,18 +407,22 @@
         used_ref[d] = rows_ref[pl.ds(pl.multiple_of(tile_of[d] * 16, 16), 16), :]
 
 
-def last_body(slots, arrived, par, returned, gates, out_ref, rows_ref):
+def last_body(slots, arrived, par, returned, gates, out_ref, rows_ref, seen_ref):
     for d in range(slots):
         k = arrived[d]
         row = jnp.where(k >= 0, k, CAP)
         rows_ref[pl.ds(pl.multiple_of(row * 16, 16), 16), :] = returned[d]
+    for n in range(STEPS):
+        for k in range(0, CAP, 8):
+            for c in range(CHUNKS):
+                seen_ref[n, k : k + 8, chunk(c)] = rows_ref[pl.ds(k * 16 + n * CHUNKS + c, 8, stride=16), :]
 
     def one(g, carry):
         for k in range(0, CAP, 8):
             for c in range(CHUNKS):
                 state = gates[g, k : k + 8, chunk(c)]
                 for n in range(STEPS):
-                    state = updated(rows_ref[pl.ds(k * 16 + n * CHUNKS + c, 8, stride=16), :], state, par, g)
+                    state = updated(seen_ref[n, k : k + 8, chunk(c)], state, par, g)
                 out_ref[g, k : k + 8, chunk(c)] = state
         return carry
 
@@ -451,8 +502,11 @@
 ):
     block = voltage.shape
     slots = lax.axis_size("blk")
-    par = jnp.concatenate([gate_half, gate_steep, gate_tmin, gate_tspan, channel])
-    cond = conductivity.reshape(-1)
+    par = jnp.concatenate([gate_half, gate_steep, gate_tmin, gate_tspan, channel, *conductivity])
+    par = jnp.pad(par, (0, PARAMS - par.shape[0]))
+    smem = pltpu.SMEM((PARAMS,), f32)
+    dma = lambda n: pltpu.SemaphoreType.DMA((n,))
+    whole_i = pltpu.VMEM(block, jnp.int32)
 
     live = worker >= 0
     holder = jnp.where(live, worker // CAP, -1)
@@ -461,10 +515,11 @@
     claims = jnp.sum(jnp.where(claimed, worker % CAP + 1, 0), axis=(1, 2)) - 1
     tile_of = jnp.sum(jnp.where(claimed, tiles[None], 0), axis=(1, 2))
     arrived = swap_blocks(jnp.broadcast_to(claims[:, None, None], (slots, 1, LANES)))[:, 0, 0]
-    mask = jnp.broadcast_to(live.astype(f32)[:, :, None], (CX, CY, LANES))
-
     rim = (6, CY, CZ)
-    up, down = kernel_call(start_body, [rim, rim], [VM] * 4)(voltage, voltage_lag, tissue, fiber)
+    side = (2 * CX + 2 + 4 * NI, CZ)
+    up, down, right, left = kernel_call(
+        start_body, [rim, rim, side, side], [HB] * 4, [block, block, whole_i, whole_i, dma(4)]
+    )(voltage, voltage_lag, tissue, fiber)
     low, high = shift_pair("slab", up, down)
     (by_row,) = kernel_call(by_row_body, [(CAP * GATES * CHUNKS, LANES)], [VM])(gates)
 
@@ -472,29 +527,32 @@
     (leaving,) = kernel_call(functools.partial(pack_body, slots), [run], [SM, VM])(arrived, by_row)
     coming = swap_blocks(leaving)
 
-    side = (2 * CX + 2 + 4 * NI, CZ)
-    up, down = kernel_call(columns_body, [side, side], [VM] * 6)(voltage, voltage_lag, tissue, fiber, low, high)
+    up, down = kernel_call(columns_body, [side, side], [VM] * 4)(right, left, low, high)
     left, right = shift_pair("blk", up, down)
     wide = (NI, NJ, CZ)
-    sheets = (NI - 1, 9, NJ, CZ)
+    sheets = (NI, 9, NJ, CZ)
+    lags = (2 * CY + 2 * CX, CZ)
     faces, weights_e, base, lag_rim = kernel_call(
         faces_body,
-        [sheets, wide, block, (2 * CY + 2 * CX, CZ)],
-        [VM] * 7 + [SM],
-        [sheets, wide, wide, (6, *wide), pltpu.SemaphoreType.DMA((NI - 1,))],
-        specs=[HB, VM, VM, VM],
-        limit=12,
-    )(voltage, tissue, fiber, low, high, left, right, cond)
+        [sheets, wide, block, lags],
+        [HB] * 4 + [VM] * 4,
+        [block, whole_i, whole_i, smem, sheets, wide, block, lags, wide, wide, (6, *wide), dma(NI + 2), dma(4)],
+        limit=61,
+        specs=[HB] * 4,
+    )(voltage, tissue, fiber, par, low, high, left, right)
 
     dense = (TILES * CHUNKS, LANES)
     v1, current, states = kernel_call(
-        react_body, [block, block, (GATES, *dense)], [SM, SM] + [VM] * 5, [dense] * 6
-    )(jnp.maximum(holder, 0).reshape(-1), par, coming, voltage, base, tissue, mask)
+        react_body,
+        [block, block, (GATES, *dense)],
+        [SM] + [HB] * 4 + [VM],
+        [block, block, whole_i, smem] + [dense] * 5 + [dma(4)],
+    )(worker, voltage, base, tissue, par, coming)
 
     low, high = shift_pair(
         "slab", jnp.concatenate([v1[-2:], current[-1:]]), jnp.concatenate([v1[:2], current[:1]])
     )
-    (parts,) = kernel_call(second_body, [(4, *block)], [SM, VM, VM], [dense, (4, *dense)])(par, states, v1)
+    (parts,) = kernel_call(second_body, [(4, *block)], [HB, VM, VM], [dense, (4, *dense), smem, pltpu.SemaphoreType.DMA])(par, states, v1)
     side = (2 * NI + CX + 2, CZ)
     up, down = kernel_call(columns2_body, [side, side], [VM] * 4)(v1, current, low, high)
     left, right = shift_pair("blk", up, down)
@@ -502,10 +560,10 @@
     v3, ours, used = kernel_call(
         functools.partial(steps_body, slots),
         [block, block, (slots, 16, LANES)],
-        [SM, SM] + [VM] * 8 + [HB, VM, VM],
-        [sheets, wide, wide, wide, (TILES * 16, LANES), pltpu.SemaphoreType.DMA],
-        limit=12,
-    )(tile_of, par, voltage, v1, current, low, high, left, right, weights_e, faces, parts, mask)
+        [SM] + [HB] * 2 + [VM] * 10,
+        [pltpu.SMEM((LANES,), jnp.int32), smem, wide, wide, wide, (TILES * 16, LANES), dma(2)],
+        limit=24,
+    )(worker, jnp.pad(tile_of, (0, LANES - slots)), par, voltage, weights_e, faces, v1, current, low, high, left, right, parts)
     returned = swap_blocks(used)
 
     below, above = shift_pair("slab", ours[-1:], ours[:1])
@@ -516,7 +574,7 @@
     )
 
     (gates_out,) = kernel_call(
-        functools.partial(last_body, slots), [gates.shape], [SM, SM, VM, VM], [((CAP + 1) * 16, LANES)]
+        functools.partial(last_body, slots), [gates.shape], [SM, SM, VM, VM], [((CAP + 1) * 16, LANES), (STEPS, CAP, CZ)]
     )(arrived, par, returned, gates)
     return (v3, gates_out, charge)
 

time: 116 us -> 115 us (level)
  local copies, waits for them, and re-layouts: 10.5 us -> 5.45 us
  Pallas kernels: 15.9 us -> 18.8 us
  starting transfers between devices: 65 us -> 66.6 us
    unnamed x50, local copies, waits for them, and re-layouts: 6.48 us -> 3.36 us
    pallas_call x5, Pallas kernels: 7.01 us -> 9.88 us  [the longest x1 5.2 us: on_device(): kernel_call(faces_body, [sheets, wide, block, lags], [HB] * 4 + [VM] * 4,...]
    reshape x2 -> x0, local copies, waits for them, and re-layouts: 1.2 us -> none  [the longest x1 0.61 us: on_device(): jnp.maximum(holder, 0).reshape(-1)]
  transfers between devices with their start and end apart: 15 -> 15, of which waited for: 4 -> 5; matrix products, arithmetic and copies ran while one was open for 2% -> 1% of each run, Pallas kernels for 6% -> 8%
where the time goes in v4:
time: 115 us; the launch traced here: 114 us
  starting transfers between devices  66.6 us (58%)
  waiting for transfers between devices  21.5 us (19%)
  Pallas kernels  18.8 us (16%)
  local copies, waits for them, and re-layouts  5.45 us (5%)
  between operations  1.21 us (1%)
    ppermute x6, starting transfers between devices, shift_pair(): lax.ppermute(last, axis, up)  24.2 us
    all_to_all x3, starting transfers between devices, swap_blocks(): return lax.all_to_all(x, 'blk', split_axis=0, concat_axis=0, tiled=True)  22.5 us
    ppermute x6, starting transfers between devices, shift_pair(): lax.ppermute(first, axis, [(b, a) for a, b in up])  19.8 us
    ppermute x6, waiting for transfers between devices, shift_pair(): lax.ppermute(first, axis, [(b, a) for a, b in up])  11 us
    all_to_all x3, waiting for transfers between devices, swap_blocks(): return lax.all_to_all(x, 'blk', split_axis=0, concat_axis=0, tiled=True)  5.84 us
    pallas_call x1, Pallas kernels, on_device(): kernel_call(faces_body, [sheets, wide, block, lags], [HB] * 4 + [VM] * 4,...  5.2 us
    ppermute x6, waiting for transfers between devices, shift_pair(): lax.ppermute(last, axis, up)  4.58 us
    unnamed x50, local copies, waits for them, and re-layouts  3.36 us
  transfers between devices with their start and end apart: 15, of which 5 were waited for; matrix products, arithmetic and copies ran while one was open for 1% of the time, Pallas kernels for 8%

profile of v4, /device:TPU:199, one launch (start us, length us, event | category | flops | bytes accessed | tf_op | source)
XLA Modules:
  0.0 114.4 jit_solution(1225025292850557500)
XLA Ops:
  0.6 0.0 copy-start.3
  0.7 0.8 fusion
  1.5 0.1 select_reduce_fusion
  1.6 0.7 broadcast_in_dim.34
  2.3 9.7 %all-to-all-start = ((s32[32,1,128]{2,1,0:T(1,128)}), s32[32,1,128]{2,1,0:T(1,128)S(1)}, u32[]{:S(2)}, u32[]{:S(2)}) async-start(s32[32,1,128]{2,1,0:T(1,128)} %broadcast_in_dim.34), calls=%async_computation | async-start | bytes 32768 | tf_op jit(solution)/shard_map/all_to_all | solution.py:486
  12.0 0.0 copy-start.1
  12.0 1.0 copy-done.1
  13.0 0.0 copy-start.16
  13.0 0.1 shard_map.142.by_row
  13.2 5.8 %all-to-all-done = s32[32,1,128]{2,1,0:T(1,128)S(1)} async-done(((s32[32,1,128]{2,1,0:T(1,128)}), s32[32,1,128]{2,1,0:T(1,128)S(1)}, u32[]{:S(2)}, u32[]{:S(2)}) %all-to-all-start) | async-done | bytes 16416 | tf_op jit(solution)/shard_map/all_to_all | solution.py:486
  19.0 0.7 slice_reduce_fusion.arrived
  19.7 1.5 %shard_map.143 = f32[32,48,128]{2,1,0:T(8,128)} custom-call(s32[32]{0:T(128)S(1)} %slice_reduce_fusion.arrived, f32[768,128]{1,0:T(8,128)S(1)} %shard_map.142.by_row), custom_call_target="tpu_custom_call" | custom-call | flops 1000000 | bytes 1000000 | tf_op jit(solution)/shard_map/pallas_call | solution.py:527
  21.2 5.5 %all-to-all-start.1 = ((f32[32,48,128]{2,1,0:T(8,128)}), f32[32,48,128]{2,1,0:T(8,128)S(1)}, u32[]{:S(2)}, u32[]{:S(2)}) async-start(f32[32,48,128]{2,1,0:T(8,128)} %shard_map.143), calls=%async_computation.1 | async-start | bytes 1572864 | tf_op jit(solution)/shard_map/all_to_all | solution.py:486
  26.7 0.4 shard_map.139
  27.2 7.5 %collective-permute-start = (f32[6,8,512]{2,1,0:T(8,128)S(1)}, f32[6,8,512]{2,1,0:T(8,128)S(1)}, u32[]{:S(2)}, u32[]{:S(2)}) collective-permute-start(f32[6,8,512]{2,1,0:T(8,128)S(1)} %get-tuple-element.21), channel_id=1, source_target_pairs={{0,32},{32,64},{64,96},{96,128},{128,160},{160,192},{192,224},{224... | collective-permute-start | bytes 294920 | tf_op jit(solution)/shard_map/ppermute | solution.py:482
  34.7 1.9 %collective-permute-start.1 = (f32[6,8,512]{2,1,0:T(8,128)S(1)}, f32[6,8,512]{2,1,0:T(8,128)S(1)}, u32[]{:S(2)}, u32[]{:S(2)}) collective-permute-start(f32[6,8,512]{2,1,0:T(8,128)S(1)} %get-tuple-element.22), channel_id=1, source_target_pairs={{32,0},{64,32},{96,64},{128,96},{160,128},{192,160},{224,192},{256... | collective-permute-start | bytes 294920 | tf_op jit(solution)/shard_map/ppermute | solution.py:482
  36.6 0.0 collective-permute-done.low
  36.6 0.0 copy-start.7
  36.6 5.5 %collective-permute-done.1.high = f32[6,8,512]{2,1,0:T(8,128)S(1)} collective-permute-done((f32[6,8,512]{2,1,0:T(8,128)S(1)}, f32[6,8,512]{2,1,0:T(8,128)S(1)}, u32[]{:S(2)}, u32[]{:S(2)}) %collective-permute-start.1) | collective-permute-done | bytes 98336 | tf_op jit(solution)/shard_map/ppermute | solution.py:482
  42.1 3.1 %collective-permute-start.2 = (f32[42,512]{1,0:T(8,128)S(1)}, f32[42,512]{1,0:T(8,128)S(1)}, u32[]{:S(2)}, u32[]{:S(2)}) collective-permute-start(f32[42,512]{1,0:T(8,128)S(1)} %get-tuple-element.25), channel_id=1, source_target_pairs={{0,1},{1,2},{2,3},{3,4},{4,5},{5,6},{6,7},{7,8},{8,9},{9,10},{10,1... | collective-permute-start | bytes 258056 | tf_op jit(solution)/shard_map/ppermute | solution.py:482
  45.2 4.3 %collective-permute-start.3 = (f32[42,512]{1,0:T(8,128)S(1)}, f32[42,512]{1,0:T(8,128)S(1)}, u32[]{:S(2)}, u32[]{:S(2)}) collective-permute-start(f32[42,512]{1,0:T(8,128)S(1)} %get-tuple-element.26), channel_id=1, source_target_pairs={{1,0},{2,1},{3,2},{4,3},{5,4},{6,5},{7,6},{8,7},{9,8},{10,9},{11,1... | collective-permute-start | bytes 258056 | tf_op jit(solution)/shard_map/ppermute | solution.py:482
  49.6 0.1 concatenate.9
  49.7 0.6 pad.9.par_in.par
  50.3 0.0 collective-permute-done.2.left
  50.3 0.9 collective-permute-done.3.right
  51.2 0.6 copy-done.18
  51.8 5.2 %shard_map.141 = (f32[8,9,16,512]{3,2,1,0:T(8,128)}, f32[8,16,512]{2,1,0:T(8,128)}, f32[4,8,512]{2,1,0:T(8,128)}, f32[24,512]{1,0:T(8,128)}) custom-call(f32[4,8,512]{2,1,0:T(8,128)} %v0.1, s32[4,8,512]{2,1,0:T(8,128)} %tissue.1, s32[4,8,512]{2,1,0:T(8,128)} %fiber_in.3, f32[256]{0:T(256)} %pad.9.par_in.par, f32[6,8,512]{2,1,0:T(8,128)} %copy-done.7, ...), custom_call_target="tpu_custom_call" | custom-call | flops 1000000 | bytes 1000000 | tf_op jit(solution)/shard_map/pallas_call | solution.py:535
  57.0 0.0 copy-start.9
  57.1 0.0 copy-start.12
  57.1 1.0 copy-done.12
  58.1 0.7 copy-done.14
  58.7 2.7 %shard_map.144 = (f32[4,8,512]{2,1,0:T(8,128)S(1)}, f32[4,8,512]{2,1,0:T(8,128)S(1)}, f32[12,128,128]{2,1,0:T(8,128)S(1)}) custom-call(s32[4,8]{1,0:T(4,128)S(1)} %copy-done.16, f32[4,8,512]{2,1,0:T(8,128)S(1)} %copy-done.4, f32[4,8,512]{2,1,0:T(8,128)S(1)} %copy-done.12, s32[4,8,512]{2,1,0:T(8,128)S(1)} %copy-done.6, f32[256]{0:T(256)S(1)} %copy-done.14, ...), custom_call_target="tpu_custom_call" | custom-call | flops 1000000 | bytes 1000000 | tf_op jit(solution)/shard_map/pallas_call | solution.py:545
  61.5 4.6 %collective-permute-start.4 = (f32[3,8,512]{2,1,0:T(8,128)S(1)}, f32[3,8,512]{2,1,0:T(8,128)S(1)}, u32[]{:S(2)}, u32[]{:S(2)}) collective-permute-start(f32[3,8,512]{2,1,0:T(8,128)S(1)} %pad_maximum_fusion), channel_id=1, source_target_pairs={{0,32},{32,64},{64,96},{96,128},{128,160},{160,192},{192,224},{224... | collective-permute-start | bytes 147464 | tf_op jit(solution)/shard_map/ppermute | solution.py:482
  66.2 1.9 %collective-permute-start.5 = (f32[3,8,512]{2,1,0:T(8,128)S(1)}, f32[3,8,512]{2,1,0:T(8,128)S(1)}, u32[]{:S(2)}, u32[]{:S(2)}) collective-permute-start(f32[3,8,512]{2,1,0:T(8,128)S(1)} %pad_maximum_fusion.1), channel_id=1, source_target_pairs={{32,0},{64,32},{96,64},{128,96},{160,128},{192,160},{224,192},{256... | collective-permute-start | bytes 147464 | tf_op jit(solution)/shard_map/ppermute | solution.py:482
  68.1 4.7 %collective-permute-done.5.high = f32[3,8,512]{2,1,0:T(8,128)S(1)} collective-permute-done((f32[3,8,512]{2,1,0:T(8,128)S(1)}, f32[3,8,512]{2,1,0:T(8,128)S(1)}, u32[]{:S(2)}, u32[]{:S(2)}) %collective-permute-start.5) | collective-permute-done | bytes 49184 | tf_op jit(solution)/shard_map/ppermute | solution.py:482
  72.8 2.2 %collective-permute-start.6 = (f32[22,512]{1,0:T(8,128)S(1)}, f32[22,512]{1,0:T(8,128)S(1)}, u32[]{:S(2)}, u32[]{:S(2)}) collective-permute-start(f32[22,512]{1,0:T(8,128)S(1)} %get-tuple-element.32), channel_id=1, source_target_pairs={{0,1},{1,2},{2,3},{3,4},{4,5},{5,6},{6,7},{7,8},{8,9},{9,10},{10,1... | collective-permute-start | bytes 135176 | tf_op jit(solution)/shard_map/ppermute | solution.py:482
  75.0 5.2 %collective-permute-start.7 = (f32[22,512]{1,0:T(8,128)S(1)}, f32[22,512]{1,0:T(8,128)S(1)}, u32[]{:S(2)}, u32[]{:S(2)}) collective-permute-start(f32[22,512]{1,0:T(8,128)S(1)} %get-tuple-element.33), channel_id=1, source_target_pairs={{1,0},{2,1},{3,2},{4,3},{5,4},{6,5},{7,6},{8,7},{9,8},{10,9},{11,1... | collective-permute-start | bytes 135176 | tf_op jit(solution)/shard_map/ppermute | solution.py:482
  80.2 1.5 %shard_map.146.parts = f32[4,4,8,512]{3,2,1,0:T(8,128)S(1)} custom-call(f32[256]{0:T(256)S(1)} %copy-done.14, f32[12,128,128]{2,1,0:T(8,128)S(1)} %get-tuple-element.34.states_in, f32[4,8,512]{2,1,0:T(8,128)S(1)} %get-tuple-element.30.v1), custom_call_target="tpu_custom_call" | custom-call | flops 1000000 | bytes 1000000 | tf_op jit(solution)/shard_map/pallas_call | solution.py:555
  81.7 0.0 copy-start.2
  81.8 3.1 %shard_map.147 = (f32[4,8,512]{2,1,0:T(8,128)}, f32[4,8,512]{2,1,0:T(8,128)S(1)}, f32[32,16,128]{2,1,0:T(8,128)}) custom-call(s32[4,8]{1,0:T(4,128)S(1)} %copy-done.16, s32[128]{0:T(128)S(1)} %pad.8.tile_of_in, f32[256]{0:T(256)S(1)} %copy-done.14, f32[4,8,512]{2,1,0:T(8,128)S(1)} %copy-done.4, f32[8,16,512]{2,1,0:T(8,128)S(1)} %copy-done.9, ...), custom_call_target="tpu_custom_call" | custom-call | flops 1000000 | bytes 1000000 | tf_op jit(solution)/shard_map/pallas_call | solution.py:560
  84.9 7.3 %all-to-all-start.2 = ((f32[32,16,128]{2,1,0:T(8,128)}), f32[32,16,128]{2,1,0:T(8,128)S(1)}, u32[]{:S(2)}, u32[]{:S(2)}) async-start(f32[32,16,128]{2,1,0:T(8,128)} %get-tuple-element.36), calls=%async_computation.2 | async-start | bytes 524288 | tf_op jit(solution)/shard_map/all_to_all | solution.py:486
  92.2 1.9 %collective-permute-start.9 = (f32[1,8,512]{2,1,0:T(8,128)S(1)}, f32[1,8,512]{2,1,0:T(8,128)S(1)}, u32[]{:S(2)}, u32[]{:S(2)}) collective-permute-start(f32[1,8,512]{2,1,0:T(8,128)S(1)} %get-tuple-element.43), channel_id=1, source_target_pairs={{32,0},{64,32},{96,64},{128,96},{160,128},{192,160},{224,192},{256... | collective-permute-start | bytes 49160 | tf_op jit(solution)/shard_map/ppermute | solution.py:482
  94.2 4.9 %collective-permute-start.8 = (f32[1,8,512]{2,1,0:T(8,128)S(1)}, f32[1,8,512]{2,1,0:T(8,128)S(1)}, u32[]{:S(2)}, u32[]{:S(2)}) collective-permute-start(f32[1,8,512]{2,1,0:T(8,128)S(1)} %get-tuple-element.44), channel_id=1, source_target_pairs={{0,32},{32,64},{64,96},{96,128},{128,160},{160,192},{192,224},{224... | collective-permute-start | bytes 49160 | tf_op jit(solution)/shard_map/ppermute | solution.py:482
  99.0 4.6 %collective-permute-start.11 = (f32[4,1,512]{2,1,0:T(1,128)S(1)}, f32[4,1,512]{2,1,0:T(1,128)S(1)}, u32[]{:S(2)}, u32[]{:S(2)}) collective-permute-start(f32[4,1,512]{2,1,0:T(1,128)S(1)} %get-tuple-element.41), channel_id=1, source_target_pairs={{1,0},{2,1},{3,2},{4,3},{5,4},{6,5},{7,6},{8,7},{9,8},{10,9},{11,1... | collective-permute-start | bytes 24584 | tf_op jit(solution)/shard_map/ppermute | solution.py:482
  103.6 1.9 %collective-permute-start.10 = (f32[4,1,512]{2,1,0:T(1,128)S(1)}, f32[4,1,512]{2,1,0:T(1,128)S(1)}, u32[]{:S(2)}, u32[]{:S(2)}) collective-permute-start(f32[4,1,512]{2,1,0:T(1,128)S(1)} %get-tuple-element.42), channel_id=1, source_target_pairs={{0,1},{1,2},{2,3},{3,4},{4,5},{5,6},{6,7},{7,8},{8,9},{9,10},{10,1... | collective-permute-start | bytes 24584 | tf_op jit(solution)/shard_map/ppermute | solution.py:482
  105.6 4.6 %collective-permute-done.10.left = f32[4,1,512]{2,1,0:T(1,128)S(1)} collective-permute-done((f32[4,1,512]{2,1,0:T(1,128)S(1)}, f32[4,1,512]{2,1,0:T(1,128)S(1)}, u32[]{:S(2)}, u32[]{:S(2)}) %collective-permute-start.10) | collective-permute-done | bytes 8224 | tf_op jit(solution)/shard_map/ppermute | solution.py:482
  110.2 1.9 %shard_map.149 = f32[3,4,8,512]{3,2,1,0:T(8,128)} custom-call(f32[4,8,512]{2,1,0:T(8,128)S(1)} %get-tuple-element.37.ours, f32[1,8,512]{2,1,0:T(8,128)S(1)} %collective-permute-done.8.below, f32[1,8,512]{2,1,0:T(8,128)S(1)} %collective-permute-done.9.above, f32[4,1,512]{2,1,0:T(1,128)S(1)} %collective-permute-done.10.left, ...), custom_call_target="tpu_custom_call" | custom-call | flops 1000000 | bytes 1000000 | tf_op jit(solution)/shard_map/pallas_call | solution.py:572
  112.0 2.4 %shard_map.148 = f32[12,16,512]{2,1,0:T(8,128)} custom-call(s32[32]{0:T(128)S(1)} %slice_reduce_fusion.arrived, f32[256]{0:T(256)S(1)} %copy-done.15, f32[32,16,128]{2,1,0:T(8,128)S(1)} %all-to-all-done.2.returned, f32[12,16,512]{2,1,0:T(8,128)S(1)} %copy-done.2), custom_call_target="tpu_custom_call" | custom-call | flops 1000000 | bytes 1000000 | tf_op jit(solution)/shard_map/pallas_call | solution.py:576
  (59 shorter events, 0.2 us)
Async XLA Ops:
  0.6 26.1 %copy-start.3 = (f32[4,8,512]{2,1,0:T(8,128)S(1)}, f32[4,8,512]{2,1,0:T(8,128)}, u32[]{:S(2)}) copy-start(f32[4,8,512]{2,1,0:T(8,128)} %v0.1) | copy-start | bytes 196612
  0.6 48.9 %copy-start.19 = (f32[6,16]{1,0:T(8,128)S(1)}, f32[6,16]{1,0:T(8,128)}, u32[]{:S(2)}) copy-start(f32[6,16]{1,0:T(8,128)} %param.16) | copy-start | bytes 1156
  0.7 48.9 %copy-start.24 = (f32[6]{0:T(128)S(1)}, f32[6]{0:T(128)}, u32[]{:S(2)}) copy-start(f32[6]{0:T(128)} %param.23) | copy-start | bytes 76
  0.7 48.9 %copy-start.23 = (f32[12]{0:T(128)S(1)}, f32[12]{0:T(128)}, u32[]{:S(2)}) copy-start(f32[12]{0:T(128)} %param.22) | copy-start | bytes 148
  0.7 48.9 %copy-start.22 = (f32[12]{0:T(128)S(1)}, f32[12]{0:T(128)}, u32[]{:S(2)}) copy-start(f32[12]{0:T(128)} %param.21) | copy-start | bytes 148
  0.7 48.9 %copy-start.21 = (f32[12]{0:T(128)S(1)}, f32[12]{0:T(128)}, u32[]{:S(2)}) copy-start(f32[12]{0:T(128)} %param.20) | copy-start | bytes 148
  0.7 48.9 %copy-start.20 = (f32[12]{0:T(128)S(1)}, f32[12]{0:T(128)}, u32[]{:S(2)}) copy-start(f32[12]{0:T(128)} %param.19) | copy-start | bytes 148
  2.3 16.7 %all-to-all-start = ((s32[32,1,128]{2,1,0:T(1,128)}), s32[32,1,128]{2,1,0:T(1,128)S(1)}, u32[]{:S(2)}, u32[]{:S(2)}) async-start(s32[32,1,128]{2,1,0:T(1,128)} %broadcast_in_dim.34), calls=%async_computation | async-start | bytes 32768 | tf_op jit(solution)/shard_map/all_to_all | solution.py:486
  12.0 1.0 copy-start.1
  13.0 13.7 %copy-start.5 = (s32[4,8,512]{2,1,0:T(8,128)S(1)}, s32[4,8,512]{2,1,0:T(8,128)}, u32[]{:S(2)}) copy-start(s32[4,8,512]{2,1,0:T(8,128)} %tissue.1) | copy-start | bytes 196612
  13.0 13.7 %copy-start.10 = (s32[4,8,512]{2,1,0:T(8,128)S(1)}, s32[4,8,512]{2,1,0:T(8,128)}, u32[]{:S(2)}) copy-start(s32[4,8,512]{2,1,0:T(8,128)} %fiber_in.3) | copy-start | bytes 196612
  13.0 13.7 %copy-start.11 = (f32[4,8,512]{2,1,0:T(8,128)S(1)}, f32[4,8,512]{2,1,0:T(8,128)}, u32[]{:S(2)}) copy-start(f32[4,8,512]{2,1,0:T(8,128)} %lag.1) | copy-start | bytes 196612
  13.0 44.0 %copy-start.4 = (f32[4,8,512]{2,1,0:T(8,128)S(1)}, f32[4,8,512]{2,1,0:T(8,128)}, u32[]{:S(2)}) copy-start(f32[4,8,512]{2,1,0:T(8,128)} %v0.1) | copy-start | bytes 196612
  13.0 44.0 %copy-start.6 = (s32[4,8,512]{2,1,0:T(8,128)S(1)}, s32[4,8,512]{2,1,0:T(8,128)}, u32[]{:S(2)}) copy-start(s32[4,8,512]{2,1,0:T(8,128)} %tissue.1) | copy-start | bytes 196612
  13.0 44.0 %copy-start.16 = (s32[4,8]{1,0:T(4,128)S(1)}, s32[4,8]{1,0:T(4,128)}, u32[]{:S(2)}) copy-start(s32[4,8]{1,0:T(4,128)} %worker.3) | copy-start | bytes 388
  21.2 35.9 %all-to-all-start.1 = ((f32[32,48,128]{2,1,0:T(8,128)}), f32[32,48,128]{2,1,0:T(8,128)S(1)}, u32[]{:S(2)}, u32[]{:S(2)}) async-start(f32[32,48,128]{2,1,0:T(8,128)} %shard_map.143), calls=%async_computation.1 | async-start | bytes 1572864 | tf_op jit(solution)/shard_map/all_to_all | solution.py:486
  27.2 9.4 %collective-permute-start = (f32[6,8,512]{2,1,0:T(8,128)S(1)}, f32[6,8,512]{2,1,0:T(8,128)S(1)}, u32[]{:S(2)}, u32[]{:S(2)}) collective-permute-start(f32[6,8,512]{2,1,0:T(8,128)S(1)} %get-tuple-element.21), channel_id=1, source_target_pairs={{0,32},{32,64},{64,96},{96,128},{128,160},{160,192},{192,224},{224... | collective-permute-start | bytes 294920 | tf_op jit(solution)/shard_map/ppermute | solution.py:482
  34.7 7.4 %collective-permute-start.1 = (f32[6,8,512]{2,1,0:T(8,128)S(1)}, f32[6,8,512]{2,1,0:T(8,128)S(1)}, u32[]{:S(2)}, u32[]{:S(2)}) collective-permute-start(f32[6,8,512]{2,1,0:T(8,128)S(1)} %get-tuple-element.22), channel_id=1, source_target_pairs={{32,0},{64,32},{96,64},{128,96},{160,128},{192,160},{224,192},{256... | collective-permute-start | bytes 294920 | tf_op jit(solution)/shard_map/ppermute | solution.py:482
  36.6 14.6 %copy-start.7 = (f32[6,8,512]{2,1,0:T(8,128)}, f32[6,8,512]{2,1,0:T(8,128)S(1)}, u32[]{:S(2)}) copy-start(f32[6,8,512]{2,1,0:T(8,128)S(1)} %collective-permute-done.low) | copy-start | bytes 294916
  42.1 9.1 %copy-start.8 = (f32[6,8,512]{2,1,0:T(8,128)}, f32[6,8,512]{2,1,0:T(8,128)S(1)}, u32[]{:S(2)}) copy-start(f32[6,8,512]{2,1,0:T(8,128)S(1)} %collective-permute-done.1.high) | copy-start | bytes 294916
  42.1 8.2 %collective-permute-start.2 = (f32[42,512]{1,0:T(8,128)S(1)}, f32[42,512]{1,0:T(8,128)S(1)}, u32[]{:S(2)}, u32[]{:S(2)}) collective-permute-start(f32[42,512]{1,0:T(8,128)S(1)} %get-tuple-element.25), channel_id=1, source_target_pairs={{0,1},{1,2},{2,3},{3,4},{4,5},{5,6},{6,7},{7,8},{8,9},{9,10},{10,1... | collective-permute-start | bytes 258056 | tf_op jit(solution)/shard_map/ppermute | solution.py:482
  45.2 5.9 %collective-permute-start.3 = (f32[42,512]{1,0:T(8,128)S(1)}, f32[42,512]{1,0:T(8,128)S(1)}, u32[]{:S(2)}, u32[]{:S(2)}) collective-permute-start(f32[42,512]{1,0:T(8,128)S(1)} %get-tuple-element.26), channel_id=1, source_target_pairs={{1,0},{2,1},{3,2},{4,3},{5,4},{6,5},{7,6},{8,7},{9,8},{10,9},{11,1... | collective-permute-start | bytes 258056 | tf_op jit(solution)/shard_map/ppermute | solution.py:482
  50.3 0.9 copy-start.17
  51.2 0.6 copy-start.18
  57.0 24.8 %copy-start.9 = (f32[8,16,512]{2,1,0:T(8,128)S(1)}, f32[8,16,512]{2,1,0:T(8,128)}, u32[]{:S(2)}) copy-start(f32[8,16,512]{2,1,0:T(8,128)} %get-tuple-element.27.weights) | copy-start | bytes 786436
  57.0 24.8 %copy-start = (f32[8,9,16,512]{3,2,1,0:T(8,128)S(1)}, f32[8,9,16,512]{3,2,1,0:T(8,128)}, u32[]{:S(2)}) copy-start(f32[8,9,16,512]{3,2,1,0:T(8,128)} %get-tuple-element.28.faces) | copy-start | bytes 7077892
  57.1 1.0 copy-start.12
  58.1 0.7 copy-start.14
  61.5 6.6 %collective-permute-start.4 = (f32[3,8,512]{2,1,0:T(8,128)S(1)}, f32[3,8,512]{2,1,0:T(8,128)S(1)}, u32[]{:S(2)}, u32[]{:S(2)}) collective-permute-start(f32[3,8,512]{2,1,0:T(8,128)S(1)} %pad_maximum_fusion), channel_id=1, source_target_pairs={{0,32},{32,64},{64,96},{96,128},{128,160},{160,192},{192,224},{224... | collective-permute-start | bytes 147464 | tf_op jit(solution)/shard_map/ppermute | solution.py:482
  66.2 6.6 %collective-permute-start.5 = (f32[3,8,512]{2,1,0:T(8,128)S(1)}, f32[3,8,512]{2,1,0:T(8,128)S(1)}, u32[]{:S(2)}, u32[]{:S(2)}) collective-permute-start(f32[3,8,512]{2,1,0:T(8,128)S(1)} %pad_maximum_fusion.1), channel_id=1, source_target_pairs={{32,0},{64,32},{96,64},{128,96},{160,128},{192,160},{224,192},{256... | collective-permute-start | bytes 147464 | tf_op jit(solution)/shard_map/ppermute | solution.py:482
  72.8 8.9 %collective-permute-start.6 = (f32[22,512]{1,0:T(8,128)S(1)}, f32[22,512]{1,0:T(8,128)S(1)}, u32[]{:S(2)}, u32[]{:S(2)}) collective-permute-start(f32[22,512]{1,0:T(8,128)S(1)} %get-tuple-element.32), channel_id=1, source_target_pairs={{0,1},{1,2},{2,3},{3,4},{4,5},{5,6},{6,7},{7,8},{8,9},{9,10},{10,1... | collective-permute-start | bytes 135176 | tf_op jit(solution)/shard_map/ppermute | solution.py:482
  75.0 6.7 %collective-permute-start.7 = (f32[22,512]{1,0:T(8,128)S(1)}, f32[22,512]{1,0:T(8,128)S(1)}, u32[]{:S(2)}, u32[]{:S(2)}) collective-permute-start(f32[22,512]{1,0:T(8,128)S(1)} %get-tuple-element.33), channel_id=1, source_target_pairs={{1,0},{2,1},{3,2},{4,3},{5,4},{6,5},{7,6},{8,7},{9,8},{10,9},{11,1... | collective-permute-start | bytes 135176 | tf_op jit(solution)/shard_map/ppermute | solution.py:482
  80.2 29.9 %copy-start.13 = (f32[24,512]{1,0:T(8,128)S(1)}, f32[24,512]{1,0:T(8,128)}, u32[]{:S(2)}) copy-start(f32[24,512]{1,0:T(8,128)} %get-tuple-element.38.lag_rim) | copy-start | bytes 147460
  81.7 30.3 %copy-start.2 = (f32[12,16,512]{2,1,0:T(8,128)S(1)}, f32[12,16,512]{2,1,0:T(8,128)}, u32[]{:S(2)}) copy-start(f32[12,16,512]{2,1,0:T(8,128)} %gates.3) | copy-start | bytes 1179652
  81.7 30.3 %copy-start.15 = (f32[256]{0:T(256)S(1)}, f32[256]{0:T(256)}, u32[]{:S(2)}) copy-start(f32[256]{0:T(256)} %pad.9.par_in.par) | copy-start | bytes 3076
  84.9 27.2 %all-to-all-start.2 = ((f32[32,16,128]{2,1,0:T(8,128)}), f32[32,16,128]{2,1,0:T(8,128)S(1)}, u32[]{:S(2)}, u32[]{:S(2)}) async-start(f32[32,16,128]{2,1,0:T(8,128)} %get-tuple-element.36), calls=%async_computation.2 | async-start | bytes 524288 | tf_op jit(solution)/shard_map/all_to_all | solution.py:486
  92.2 17.9 %collective-permute-start.9 = (f32[1,8,512]{2,1,0:T(8,128)S(1)}, f32[1,8,512]{2,1,0:T(8,128)S(1)}, u32[]{:S(2)}, u32[]{:S(2)}) collective-permute-start(f32[1,8,512]{2,1,0:T(8,128)S(1)} %get-tuple-element.43), channel_id=1, source_target_pairs={{32,0},{64,32},{96,64},{128,96},{160,128},{192,160},{224,192},{256... | collective-permute-start | bytes 49160 | tf_op jit(solution)/shard_map/ppermute | solution.py:482
  94.2 16.0 %collective-permute-start.8 = (f32[1,8,512]{2,1,0:T(8,128)S(1)}, f32[1,8,512]{2,1,0:T(8,128)S(1)}, u32[]{:S(2)}, u32[]{:S(2)}) collective-permute-start(f32[1,8,512]{2,1,0:T(8,128)S(1)} %get-tuple-element.44), channel_id=1, source_target_pairs={{0,32},{32,64},{64,96},{96,128},{128,160},{160,192},{192,224},{224... | collective-permute-start | bytes 49160 | tf_op jit(solution)/shard_map/ppermute | solution.py:482
  99.0 6.5 %collective-permute-start.11 = (f32[4,1,512]{2,1,0:T(1,128)S(1)}, f32[4,1,512]{2,1,0:T(1,128)S(1)}, u32[]{:S(2)}, u32[]{:S(2)}) collective-permute-start(f32[4,1,512]{2,1,0:T(1,128)S(1)} %get-tuple-element.41), channel_id=1, source_target_pairs={{1,0},{2,1},{3,2},{4,3},{5,4},{6,5},{7,6},{8,7},{9,8},{10,9},{11,1... | collective-permute-start | bytes 24584 | tf_op jit(solution)/shard_map/ppermute | solution.py:482
  103.6 6.5 %collective-permute-start.10 = (f32[4,1,512]{2,1,0:T(1,128)S(1)}, f32[4,1,512]{2,1,0:T(1,128)S(1)}, u32[]{:S(2)}, u32[]{:S(2)}) collective-permute-start(f32[4,1,512]{2,1,0:T(1,128)S(1)} %get-tuple-element.42), channel_id=1, source_target_pairs={{0,1},{1,2},{2,3},{3,4},{4,5},{5,6},{6,7},{7,8},{8,9},{9,10},{10,1... | collective-permute-start | bytes 24584 | tf_op jit(solution)/shard_map/ppermute | solution.py:482

commit v5 on v4

--- a/solution.py
+++ b/solution.py
@@ -33,7 +33,7 @@
 def kernel_call(body, outs, ins, scratch=(), flops=1_000_000, limit=6, specs=None):
     return pl.pallas_call(
         body,
-        out_shape=[jax.ShapeDtypeStruct(shape, f32) for shape in outs],
+        out_shape=[jax.ShapeDtypeStruct(s, f32) if isinstance(s, tuple) else s for s in outs],
         in_specs=ins,
         out_specs=specs or [VM] * len(outs),
         scratch_shapes=[pltpu.VMEM(s, f32) if isinstance(s, tuple) else s for s in scratch],
@@ -55,6 +55,10 @@
     for j in range(CY):
         mask = jnp.where(row == j, jnp.where(worker[i, j] >= 0, 1.0, 0.0), mask)
     return mask
+
+
+def face_at(n, i):
+    return 3 * i + n if n < 3 else 3 * (NI - 1) + 6 * (i - 1) + n - 3
 
 
 def chunk(c):
@@ -198,18 +202,14 @@
 
 
 def faces_body(
-    voltage_in, tissue_in, fiber_in, par_in, low, high, left, right,
-    faces_out, weights_out, base_out, lag_out,
-    voltage, tissue, fiber, cond, faces_ref, weights_ref, base_ref, lag_ref, field_ref, fib_ref, stack_ref, sems, in_sems,
+    par, voltage, tissue, fiber, low, high, left, right,
+    faces_ref, flags_ref, base_ref, lag_ref, weights_ref, field_ref, fib_ref, stack_ref,
 ):
-    coming = fetched(((voltage_in, voltage), (tissue_in, tissue), (fiber_in, fiber), (par_in, cond)), in_sems)
     zero = jnp.zeros((NI, NJ, CZ), f32)
     field_ref[...] = zero
     fib_ref[...] = zero
     weights_ref[...] = zero
     own = slice(2, 2 + CY)
-    for copy in coming:
-        copy.wait()
     for i in range(CX):
         w = tissue[i].astype(f32)
         field_ref[2 + i, own, :] = w * voltage[i]
@@ -233,10 +233,10 @@
         for c in range(CHUNKS):
             fib = fib_ref[i, :, chunk(c)]
             w = weights_ref[i, :, chunk(c)]
-            found = [jnp.full((NJ, LANES), cond[COND + n * FIB]) for n in range(6)]
+            found = [jnp.full((NJ, LANES), par[COND + n * FIB]) for n in range(6)]
             for k in range(1, FIB):
                 here = fib == float(k)
-                found = [jnp.where(here, cond[COND + n * FIB + k], old) for n, old in enumerate(found)]
+                found = [jnp.where(here, par[COND + n * FIB + k], old) for n, old in enumerate(found)]
             for n in range(6):
                 stack_ref[n, i, :, chunk(c)] = 0.5 * (w * found[n])
         return carry
@@ -247,46 +247,30 @@
     lag_ref[2 * CY : 2 * CY + CX] = left[CX + 2 : 2 * CX + 2]
     lag_ref[2 * CY + CX : 2 * CY + 2 * CX] = right[CX + 2 : 2 * CX + 2]
     z = lax.broadcasted_iota(jnp.int32, (NJ, CZ), 1)
-    copies = fetched(((weights_ref, weights_out), (lag_ref, lag_out)), sems)
-    late = 2
     for i in range(NI - 1):
-        if i > 1:
-            copies.append(pltpu.make_async_copy(faces_ref.at[i - 1], faces_out.at[i - 1], sems.at[late + i - 1]))
-            copies[-1].start()
         w = weights_ref[i]
         both = w * weights_ref[i + 1]
         for n, comp in enumerate(COMPONENT[0]):
-            faces_ref[i, n] = (stack_ref[comp, i] + stack_ref[comp, i + 1]) * both
+            faces_ref[face_at(n, i)] = (stack_ref[comp, i] + stack_ref[comp, i + 1]) * both
         if i == 0:
-            faces_ref[0, 3:] = jnp.zeros((6, NJ, CZ), f32)
             continue
         both = w * up_j(w)
         for n, comp in enumerate(COMPONENT[1]):
             here = stack_ref[comp, i]
-            faces_ref[i, 3 + n] = (here + up_j(here)) * both
+            faces_ref[face_at(3 + n, i)] = (here + up_j(here)) * both
         both = w * jnp.where(z == CZ - 1, 0.0, up_z(w))
         for n, comp in enumerate(COMPONENT[2]):
             here = stack_ref[comp, i]
-            faces_ref[i, 6 + n] = (here + up_z(here)) * both
-    for i in (0, NI - 2):
-        copies.append(pltpu.make_async_copy(faces_ref.at[i], faces_out.at[i], sems.at[late + i]))
-        copies[-1].start()
+            faces_ref[face_at(6 + n, i)] = (here + up_z(here)) * both
+    for i in range(NI):
+        flags_ref[i] = weights_ref[i].astype(jnp.bfloat16)
     field = {i: field_ref[i] for i in range(1, NI - 1)}
-    spread = spread_of(field, lambda n, i: faces_ref[i, n], 2, CX + 1)
+    spread = spread_of(field, lambda n, i: faces_ref[face_at(n, i)], 2, CX + 1)
     for i in range(CX):
         base_ref[i] = voltage[i] + tissue[i].astype(f32) * spread[2 + i][2 : 2 + CY]
-    copies.append(pltpu.make_async_copy(base_ref, base_out, sems.at[late + NI - 1]))
-    copies[-1].start()
-    for copy in copies:
-        copy.wait()
-
-
-def react_body(
-    worker, voltage_in, base_in, tissue_in, par_in, coming,
-    v1_ref, current_ref, states_ref, voltage, base, tissue, par, v_d, base_d, w_d, out_d, cur_d, sems,
-):
-    for copy in fetched(((voltage_in, voltage), (base_in, base), (tissue_in, tissue), (par_in, par)), sems):
-        copy.wait()
+
+
+def react_body(worker, par, voltage, base, tissue, coming, v1_ref, current_ref, states_ref, v_d, base_d, w_d, out_d, cur_d):
     for i in range(CX):
         to_dense(v_d, voltage[i], i)
         to_dense(base_d, base[i], i)
@@ -318,10 +302,7 @@
             current_ref[i, :, chunk(c)] = from_dense(cur_d, i, c)
 
 
-def second_body(par_in, states_in, v1, parts_ref, v_d, parts_d, par, sem):
-    fetch = pltpu.make_async_copy(par_in, par, sem)
-    fetch.start()
-    fetch.wait()
+def second_body(par, states_in, v1, parts_ref, v_d, parts_d):
     for i in range(CX):
         to_dense(v_d, v1[i], i)
 
@@ -359,12 +340,9 @@
 
 
 def steps_body(
-    slots, worker, tile_of_in, par_in, v0, weights, faces, v1, current, low, high, left, right, parts,
-    v3_ref, ours_ref, used_ref, tile_of, par, v_ref, cur_ref, next_ref, rows_ref, sems,
+    slots, worker, tile_of, par, v0, flags, faces, v1, current, low, high, left, right, parts,
+    v3_ref, ours_ref, used_ref, v_ref, cur_ref, next_ref, rows_ref,
 ):
-    fetches = fetched(
-        ((par_in, par), (tile_of_in, tile_of)), sems
-    )
     v_ref[...] = jnp.zeros((NI, NJ, CZ), f32)
     cur_ref[...] = jnp.zeros((NI, NJ, CZ), f32)
     own = slice(2, 2 + CY)
@@ -382,9 +360,8 @@
                 v_ref[i, j : j + 1, :] = ref[n * NI + i : n * NI + i + 1, :]
         for i in range(CX + 2):
             cur_ref[1 + i, outer : outer + 1, :] = ref[2 * NI + i : 2 * NI + i + 1, :]
-    face = lambda n, i: faces[i, n]
-    for fetch in fetches:
-        fetch.wait()
+    face = lambda n, i: faces[face_at(n, i)]
+    weights = {i: flags[i].astype(f32) for i in range(NI)}
     field = {i: weights[i] * v_ref[i] for i in range(NI)}
     spread = spread_of(field, face, 1, NI - 2)
     for i in range(1, NI - 1):
@@ -393,7 +370,7 @@
     spread = spread_of(field, face, 2, CX + 1)
     for i in range(CX):
         v2 = next_ref[2 + i, own, :]
-        w = weights[2 + i, own, :]
+        w = weights[2 + i][own]
         found = live_plane(worker, i) * current_from(v2, [parts[n, i] for n in range(4)], par)
         v3 = v2 + w * (spread[2 + i][own] - STEP_DT * found)
         v3_ref[i] = v3
@@ -504,7 +481,6 @@
     slots = lax.axis_size("blk")
     par = jnp.concatenate([gate_half, gate_steep, gate_tmin, gate_tspan, channel, *conductivity])
     par = jnp.pad(par, (0, PARAMS - par.shape[0]))
-    smem = pltpu.SMEM((PARAMS,), f32)
     dma = lambda n: pltpu.SemaphoreType.DMA((n,))
     whole_i = pltpu.VMEM(block, jnp.int32)
 
@@ -530,29 +506,25 @@
     up, down = kernel_call(columns_body, [side, side], [VM] * 4)(right, left, low, high)
     left, right = shift_pair("blk", up, down)
     wide = (NI, NJ, CZ)
-    sheets = (NI, 9, NJ, CZ)
+    sheets = (3 * (NI - 1) + 6 * (NI - 2), NJ, CZ)
     lags = (2 * CY + 2 * CX, CZ)
-    faces, weights_e, base, lag_rim = kernel_call(
+    faces, flags, base, lag_rim = kernel_call(
         faces_body,
-        [sheets, wide, block, lags],
-        [HB] * 4 + [VM] * 4,
-        [block, whole_i, whole_i, smem, sheets, wide, block, lags, wide, wide, (6, *wide), dma(NI + 2), dma(4)],
-        limit=61,
-        specs=[HB] * 4,
-    )(voltage, tissue, fiber, par, low, high, left, right)
+        [sheets, jax.ShapeDtypeStruct(wide, jnp.bfloat16), block, lags],
+        [SM] + [VM] * 7,
+        [wide, wide, wide, (6, *wide)],
+        limit=12,
+    )(par, voltage, tissue, fiber, low, high, left, right)
 
     dense = (TILES * CHUNKS, LANES)
     v1, current, states = kernel_call(
-        react_body,
-        [block, block, (GATES, *dense)],
-        [SM] + [HB] * 4 + [VM],
-        [block, block, whole_i, smem] + [dense] * 5 + [dma(4)],
-    )(worker, voltage, base, tissue, par, coming)
+        react_body, [block, block, (GATES, *dense)], [SM, SM] + [VM] * 4, [dense] * 5
+    )(worker, par, voltage, base, tissue, coming)
 
     low, high = shift_pair(
         "slab", jnp.concatenate([v1[-2:], current[-1:]]), jnp.concatenate([v1[:2], current[:1]])
     )
-    (parts,) = kernel_call(second_body, [(4, *block)], [HB, VM, VM], [dense, (4, *dense), smem, pltpu.SemaphoreType.DMA])(par, states, v1)
+    (parts,) = kernel_call(second_body, [(4, *block)], [SM, VM, VM], [dense, (4, *dense)])(par, states, v1)
     side = (2 * NI + CX + 2, CZ)
     up, down = kernel_call(columns2_body, [side, side], [VM] * 4)(v1, current, low, high)
     left, right = shift_pair("blk", up, down)
@@ -560,10 +532,10 @@
     v3, ours, used = kernel_call(
         functools.partial(steps_body, slots),
         [block, block, (slots, 16, LANES)],
-        [SM] + [HB] * 2 + [VM] * 10,
-        [pltpu.SMEM((LANES,), jnp.int32), smem, wide, wide, wide, (TILES * 16, LANES), dma(2)],
-        limit=24,
-    )(worker, jnp.pad(tile_of, (0, LANES - slots)), par, voltage, weights_e, faces, v1, current, low, high, left, right, parts)
+        [SM] * 3 + [VM] * 10,
+        [wide, wide, wide, (TILES * 16, LANES)],
+        limit=12,
+    )(worker, tile_of, par, voltage, flags, faces, v1, current, low, high, left, right, parts)
     returned = swap_blocks(used)
 
     below, above = shift_pair("slab", ours[-1:], ours[:1])

time: 115 us -> 112 us (0.974)
  Pallas kernels: 18.8 us -> 15.1 us
    pallas_call x3, Pallas kernels: 9.42 us -> 6.29 us  [the longest x1 2.91 us: on_device(): kernel_call(faces_body, [sheets, jax.ShapeDtypeStruct(wide, jnp.bfloat16)...]
    unnamed x50 -> x38, local copies, waits for them, and re-layouts: 3.36 us -> 3.63 us
  transfers between devices with their start and end apart: 15 -> 15, of which waited for: 5 -> 5; matrix products, arithmetic and copies ran while one was open for 1% -> 0% of each run, Pallas kernels for 8% -> 6%
where the time goes in v5:
time: 112 us; the launch traced here: 111 us
  starting transfers between devices  66.1 us (59%)
  waiting for transfers between devices  22 us (20%)
  Pallas kernels  15.1 us (13%)
  local copies, waits for them, and re-layouts  5.14 us (5%)
  other arithmetic  1.41 us (1%)
    ppermute x6, starting transfers between devices, shift_pair(): lax.ppermute(last, axis, up)  24.2 us
    all_to_all x3, starting transfers between devices, swap_blocks(): return lax.all_to_all(x, 'blk', split_axis=0, concat_axis=0, tiled=True)  22.8 us
    ppermute x6, starting transfers between devices, shift_pair(): lax.ppermute(first, axis, [(b, a) for a, b in up])  19.2 us
    ppermute x6, waiting for transfers between devices, shift_pair(): lax.ppermute(first, axis, [(b, a) for a, b in up])  11.6 us
    all_to_all x3, waiting for transfers between devices, swap_blocks(): return lax.all_to_all(x, 'blk', split_axis=0, concat_axis=0, tiled=True)  5.79 us
    ppermute x6, waiting for transfers between devices, shift_pair(): lax.ppermute(last, axis, up)  4.58 us
    unnamed x38, local copies, waits for them, and re-layouts  3.63 us
    pallas_call x1, Pallas kernels, on_device(): kernel_call(faces_body, [sheets, jax.ShapeDtypeStruct(wide, jnp.bfloat16)...  2.91 us
  transfers between devices with their start and end apart: 15, of which 5 were waited for; matrix products, arithmetic and copies ran while one was open for 0% of the time, Pallas kernels for 6%

profile of v5, /device:TPU:199, one launch (start us, length us, event | category | flops | bytes accessed | tf_op | source)
XLA Modules:
  0.0 110.9 jit_solution(9152951369512974620)
XLA Ops:
  0.6 0.8 fusion
  1.4 0.6 select_reduce_fusion
  2.0 0.7 broadcast_in_dim.34
  2.8 9.7 %all-to-all-start = ((s32[32,1,128]{2,1,0:T(1,128)}), s32[32,1,128]{2,1,0:T(1,128)S(1)}, u32[]{:S(2)}, u32[]{:S(2)}) async-start(s32[32,1,128]{2,1,0:T(1,128)} %broadcast_in_dim.34), calls=%async_computation | async-start | bytes 32768 | tf_op jit(solution)/shard_map/all_to_all | solution.py:463
  12.4 0.0 copy-start
  12.5 1.0 copy-done
  13.4 0.1 shard_map.142.by_row
  13.6 0.0 copy-start.13
  13.6 0.0 copy-start.14
  13.6 0.0 copy-start.15
  13.6 0.0 copy-start.16
  13.6 0.0 copy-start.17
  13.6 0.0 copy-start.18
  13.6 5.8 %all-to-all-done = s32[32,1,128]{2,1,0:T(1,128)S(1)} async-done(((s32[32,1,128]{2,1,0:T(1,128)}), s32[32,1,128]{2,1,0:T(1,128)S(1)}, u32[]{:S(2)}, u32[]{:S(2)}) %all-to-all-start) | async-done | bytes 16416 | tf_op jit(solution)/shard_map/all_to_all | solution.py:463
  19.4 0.7 slice_reduce_fusion.arrived
  20.1 1.5 %shard_map.143 = f32[32,48,128]{2,1,0:T(8,128)} custom-call(s32[32]{0:T(128)S(1)} %slice_reduce_fusion.arrived, f32[768,128]{1,0:T(8,128)S(1)} %shard_map.142.by_row), custom_call_target="tpu_custom_call" | custom-call | flops 1000000 | bytes 1000000 | tf_op jit(solution)/shard_map/pallas_call | solution.py:503
  21.6 5.5 %all-to-all-start.1 = ((f32[32,48,128]{2,1,0:T(8,128)}), f32[32,48,128]{2,1,0:T(8,128)S(1)}, u32[]{:S(2)}, u32[]{:S(2)}) async-start(f32[32,48,128]{2,1,0:T(8,128)} %shard_map.143), calls=%async_computation.1 | async-start | bytes 1572864 | tf_op jit(solution)/shard_map/all_to_all | solution.py:463
  27.2 0.4 shard_map.139
  27.6 7.5 %collective-permute-start = (f32[6,8,512]{2,1,0:T(8,128)S(1)}, f32[6,8,512]{2,1,0:T(8,128)S(1)}, u32[]{:S(2)}, u32[]{:S(2)}) collective-permute-start(f32[6,8,512]{2,1,0:T(8,128)S(1)} %get-tuple-element.21), channel_id=1, source_target_pairs={{0,32},{32,64},{64,96},{96,128},{128,160},{160,192},{192,224},{224... | collective-permute-start | bytes 294920 | tf_op jit(solution)/shard_map/ppermute | solution.py:459
  35.1 1.9 %collective-permute-start.1 = (f32[6,8,512]{2,1,0:T(8,128)S(1)}, f32[6,8,512]{2,1,0:T(8,128)S(1)}, u32[]{:S(2)}, u32[]{:S(2)}) collective-permute-start(f32[6,8,512]{2,1,0:T(8,128)S(1)} %get-tuple-element.22), channel_id=1, source_target_pairs={{32,0},{64,32},{96,64},{128,96},{160,128},{192,160},{224,192},{256... | collective-permute-start | bytes 294920 | tf_op jit(solution)/shard_map/ppermute | solution.py:459
  37.0 0.0 collective-permute-done.low
  37.0 5.5 %collective-permute-done.1.high = f32[6,8,512]{2,1,0:T(8,128)S(1)} collective-permute-done((f32[6,8,512]{2,1,0:T(8,128)S(1)}, f32[6,8,512]{2,1,0:T(8,128)S(1)}, u32[]{:S(2)}, u32[]{:S(2)}) %collective-permute-start.1) | collective-permute-done | bytes 98336 | tf_op jit(solution)/shard_map/ppermute | solution.py:459
  42.6 3.1 %collective-permute-start.2 = (f32[42,512]{1,0:T(8,128)S(1)}, f32[42,512]{1,0:T(8,128)S(1)}, u32[]{:S(2)}, u32[]{:S(2)}) collective-permute-start(f32[42,512]{1,0:T(8,128)S(1)} %get-tuple-element.25), channel_id=1, source_target_pairs={{0,1},{1,2},{2,3},{3,4},{4,5},{5,6},{6,7},{7,8},{8,9},{9,10},{10,1... | collective-permute-start | bytes 258056 | tf_op jit(solution)/shard_map/ppermute | solution.py:459
  45.7 4.3 %collective-permute-start.3 = (f32[42,512]{1,0:T(8,128)S(1)}, f32[42,512]{1,0:T(8,128)S(1)}, u32[]{:S(2)}, u32[]{:S(2)}) collective-permute-start(f32[42,512]{1,0:T(8,128)S(1)} %get-tuple-element.26), channel_id=1, source_target_pairs={{1,0},{2,1},{3,2},{4,3},{5,4},{6,5},{7,6},{8,7},{9,8},{10,9},{11,1... | collective-permute-start | bytes 258056 | tf_op jit(solution)/shard_map/ppermute | solution.py:459
  50.1 0.1 concatenate.9
  50.2 1.4 %collective-permute-done.3.right = f32[42,512]{1,0:T(8,128)S(1)} collective-permute-done((f32[42,512]{1,0:T(8,128)S(1)}, f32[42,512]{1,0:T(8,128)S(1)}, u32[]{:S(2)}, u32[]{:S(2)}) %collective-permute-start.3) | collective-permute-done | bytes 86048 | tf_op jit(solution)/shard_map/ppermute | solution.py:459
  51.6 2.9 %shard_map.141 = (f32[57,16,512]{2,1,0:T(8,128)S(1)}, bf16[8,16,512]{2,1,0:T(8,128)(2,1)S(1)}, f32[4,8,512]{2,1,0:T(8,128)S(1)}, f32[24,512]{1,0:T(8,128)S(1)}) custom-call(f32[256]{0:T(256)S(1)} %pad.4.par, f32[4,8,512]{2,1,0:T(8,128)S(1)} %copy-done.2, s32[4,8,512]{2,1,0:T(8,128)S(1)} %copy-done.3, s32[4,8,512]{2,1,0:T(8,128)S(1)} %copy-done.4, ...), custom_call_target="tpu_custom_call" | custom-call | flops 1000000 | bytes 1000000 | tf_op jit(solution)/shard_map/pallas_call | solution.py:511
  54.5 0.6 copy-done.6
  55.1 0.7 copy-done.7
  55.8 0.7 copy-done.9
  56.5 1.9 %shard_map.144 = (f32[4,8,512]{2,1,0:T(8,128)S(1)}, f32[4,8,512]{2,1,0:T(8,128)S(1)}, f32[12,128,128]{2,1,0:T(8,128)S(1)}) custom-call(s32[4,8]{1,0:T(4,128)S(1)} %copy-done.9, f32[256]{0:T(256)S(1)} %copy-done.7, f32[4,8,512]{2,1,0:T(8,128)S(1)} %copy-done.2, f32[4,8,512]{2,1,0:T(8,128)S(1)} %get-tuple-element.29.base, s32[4,8,512]{2,1,0:T(8,128)S(1)} %copy-done.3, ...), custom_call_target="tpu_custom_call" | custom-call | flops 1000000 | bytes 1000000 | tf_op jit(solution)/shard_map/pallas_call | solution.py:520
  58.4 4.0 %collective-permute-start.4 = (f32[3,8,512]{2,1,0:T(8,128)S(1)}, f32[3,8,512]{2,1,0:T(8,128)S(1)}, u32[]{:S(2)}, u32[]{:S(2)}) collective-permute-start(f32[3,8,512]{2,1,0:T(8,128)S(1)} %pad_maximum_fusion), channel_id=1, source_target_pairs={{0,32},{32,64},{64,96},{96,128},{128,160},{160,192},{192,224},{224... | collective-permute-start | bytes 147464 | tf_op jit(solution)/shard_map/ppermute | solution.py:459
  62.4 1.9 %collective-permute-start.5 = (f32[3,8,512]{2,1,0:T(8,128)S(1)}, f32[3,8,512]{2,1,0:T(8,128)S(1)}, u32[]{:S(2)}, u32[]{:S(2)}) collective-permute-start(f32[3,8,512]{2,1,0:T(8,128)S(1)} %pad_maximum_fusion.1), channel_id=1, source_target_pairs={{32,0},{64,32},{96,64},{128,96},{160,128},{192,160},{224,192},{256... | collective-permute-start | bytes 147464 | tf_op jit(solution)/shard_map/ppermute | solution.py:459
  64.4 4.7 %collective-permute-done.5.high = f32[3,8,512]{2,1,0:T(8,128)S(1)} collective-permute-done((f32[3,8,512]{2,1,0:T(8,128)S(1)}, f32[3,8,512]{2,1,0:T(8,128)S(1)}, u32[]{:S(2)}, u32[]{:S(2)}) %collective-permute-start.5) | collective-permute-done | bytes 49184 | tf_op jit(solution)/shard_map/ppermute | solution.py:459
  69.1 2.8 %collective-permute-start.6 = (f32[22,512]{1,0:T(8,128)S(1)}, f32[22,512]{1,0:T(8,128)S(1)}, u32[]{:S(2)}, u32[]{:S(2)}) collective-permute-start(f32[22,512]{1,0:T(8,128)S(1)} %get-tuple-element.32), channel_id=1, source_target_pairs={{0,1},{1,2},{2,3},{3,4},{4,5},{5,6},{6,7},{7,8},{8,9},{9,10},{10,1... | collective-permute-start | bytes 135176 | tf_op jit(solution)/shard_map/ppermute | solution.py:459
  71.9 4.5 %collective-permute-start.7 = (f32[22,512]{1,0:T(8,128)S(1)}, f32[22,512]{1,0:T(8,128)S(1)}, u32[]{:S(2)}, u32[]{:S(2)}) collective-permute-start(f32[22,512]{1,0:T(8,128)S(1)} %get-tuple-element.33), channel_id=1, source_target_pairs={{1,0},{2,1},{3,2},{4,3},{5,4},{6,5},{7,6},{8,7},{9,8},{10,9},{11,1... | collective-permute-start | bytes 135176 | tf_op jit(solution)/shard_map/ppermute | solution.py:459
  76.5 1.5 %shard_map.146.parts = f32[4,4,8,512]{3,2,1,0:T(8,128)S(1)} custom-call(f32[256]{0:T(256)S(1)} %copy-done.7, f32[12,128,128]{2,1,0:T(8,128)S(1)} %get-tuple-element.34.states_in, f32[4,8,512]{2,1,0:T(8,128)S(1)} %get-tuple-element.30.v1), custom_call_target="tpu_custom_call" | custom-call | flops 1000000 | bytes 1000000 | tf_op jit(solution)/shard_map/pallas_call | solution.py:527
  78.0 0.0 copy-start.12
  78.0 0.6 copy-done.12
  78.6 2.5 %shard_map.147 = (f32[4,8,512]{2,1,0:T(8,128)}, f32[4,8,512]{2,1,0:T(8,128)S(1)}, f32[32,16,128]{2,1,0:T(8,128)}) custom-call(s32[4,8]{1,0:T(4,128)S(1)} %copy-done.9, s32[32]{0:T(128)S(1)} %copy-done.12, f32[256]{0:T(256)S(1)} %copy-done.7, f32[4,8,512]{2,1,0:T(8,128)S(1)} %copy-done.2, bf16[8,16,512]{2,1,0:T(8,128)(2,1)S(1)} %get-tuple-element.27.flags, ...), custom_call_target="tpu_custom_call" | custom-call | flops 1000000 | bytes 1000000 | tf_op jit(solution)/shard_map/pallas_call | solution.py:532
  81.1 7.6 %all-to-all-start.2 = ((f32[32,16,128]{2,1,0:T(8,128)}), f32[32,16,128]{2,1,0:T(8,128)S(1)}, u32[]{:S(2)}, u32[]{:S(2)}) async-start(f32[32,16,128]{2,1,0:T(8,128)} %get-tuple-element.36), calls=%async_computation.2 | async-start | bytes 524288 | tf_op jit(solution)/shard_map/all_to_all | solution.py:463
  88.7 1.9 %collective-permute-start.9 = (f32[1,8,512]{2,1,0:T(8,128)S(1)}, f32[1,8,512]{2,1,0:T(8,128)S(1)}, u32[]{:S(2)}, u32[]{:S(2)}) collective-permute-start(f32[1,8,512]{2,1,0:T(8,128)S(1)} %get-tuple-element.43), channel_id=1, source_target_pairs={{32,0},{64,32},{96,64},{128,96},{160,128},{192,160},{224,192},{256... | collective-permute-start | bytes 49160 | tf_op jit(solution)/shard_map/ppermute | solution.py:459
  90.6 4.9 %collective-permute-start.8 = (f32[1,8,512]{2,1,0:T(8,128)S(1)}, f32[1,8,512]{2,1,0:T(8,128)S(1)}, u32[]{:S(2)}, u32[]{:S(2)}) collective-permute-start(f32[1,8,512]{2,1,0:T(8,128)S(1)} %get-tuple-element.44), channel_id=1, source_target_pairs={{0,32},{32,64},{64,96},{96,128},{128,160},{160,192},{192,224},{224... | collective-permute-start | bytes 49160 | tf_op jit(solution)/shard_map/ppermute | solution.py:459
  95.5 4.6 %collective-permute-start.11 = (f32[4,1,512]{2,1,0:T(1,128)S(1)}, f32[4,1,512]{2,1,0:T(1,128)S(1)}, u32[]{:S(2)}, u32[]{:S(2)}) collective-permute-start(f32[4,1,512]{2,1,0:T(1,128)S(1)} %get-tuple-element.41), channel_id=1, source_target_pairs={{1,0},{2,1},{3,2},{4,3},{5,4},{6,5},{7,6},{8,7},{9,8},{10,9},{11,1... | collective-permute-start | bytes 24584 | tf_op jit(solution)/shard_map/ppermute | solution.py:459
  100.1 1.9 %collective-permute-start.10 = (f32[4,1,512]{2,1,0:T(1,128)S(1)}, f32[4,1,512]{2,1,0:T(1,128)S(1)}, u32[]{:S(2)}, u32[]{:S(2)}) collective-permute-start(f32[4,1,512]{2,1,0:T(1,128)S(1)} %get-tuple-element.42), channel_id=1, source_target_pairs={{0,1},{1,2},{2,3},{3,4},{4,5},{5,6},{6,7},{7,8},{8,9},{9,10},{10,1... | collective-permute-start | bytes 24584 | tf_op jit(solution)/shard_map/ppermute | solution.py:459
  102.0 4.6 %collective-permute-done.10.left = f32[4,1,512]{2,1,0:T(1,128)S(1)} collective-permute-done((f32[4,1,512]{2,1,0:T(1,128)S(1)}, f32[4,1,512]{2,1,0:T(1,128)S(1)}, u32[]{:S(2)}, u32[]{:S(2)}) %collective-permute-start.10) | collective-permute-done | bytes 8224 | tf_op jit(solution)/shard_map/ppermute | solution.py:459
  106.6 1.9 %shard_map.149 = f32[3,4,8,512]{3,2,1,0:T(8,128)} custom-call(f32[4,8,512]{2,1,0:T(8,128)S(1)} %get-tuple-element.37.ours, f32[1,8,512]{2,1,0:T(8,128)S(1)} %collective-permute-done.8.below, f32[1,8,512]{2,1,0:T(8,128)S(1)} %collective-permute-done.9.above, f32[4,1,512]{2,1,0:T(1,128)S(1)} %collective-permute-done.10.left, ...), custom_call_target="tpu_custom_call" | custom-call | flops 1000000 | bytes 1000000 | tf_op jit(solution)/shard_map/pallas_call | solution.py:544
  108.5 2.4 %shard_map.148 = f32[12,16,512]{2,1,0:T(8,128)} custom-call(s32[32]{0:T(128)S(1)} %copy-done.11, f32[256]{0:T(256)S(1)} %copy-done.8, f32[32,16,128]{2,1,0:T(8,128)S(1)} %all-to-all-done.2.returned, f32[12,16,512]{2,1,0:T(8,128)S(1)} %copy-done.1), custom_call_target="tpu_custom_call" | custom-call | flops 1000000 | bytes 1000000 | tf_op jit(solution)/shard_map/pallas_call | solution.py:548
  (46 shorter events, 0.2 us)
Async XLA Ops:
  0.6 26.5 %copy-start.2 = (f32[4,8,512]{2,1,0:T(8,128)S(1)}, f32[4,8,512]{2,1,0:T(8,128)}, u32[]{:S(2)}) copy-start(f32[4,8,512]{2,1,0:T(8,128)} %v0.1) | copy-start | bytes 196612
  2.8 16.7 %all-to-all-start = ((s32[32,1,128]{2,1,0:T(1,128)}), s32[32,1,128]{2,1,0:T(1,128)S(1)}, u32[]{:S(2)}, u32[]{:S(2)}) async-start(s32[32,1,128]{2,1,0:T(1,128)} %broadcast_in_dim.34), calls=%async_computation | async-start | bytes 32768 | tf_op jit(solution)/shard_map/all_to_all | solution.py:463
  12.4 1.0 copy-start
  13.4 13.7 %copy-start.3 = (s32[4,8,512]{2,1,0:T(8,128)S(1)}, s32[4,8,512]{2,1,0:T(8,128)}, u32[]{:S(2)}) copy-start(s32[4,8,512]{2,1,0:T(8,128)} %tissue.5) | copy-start | bytes 196612
  13.4 13.7 %copy-start.4 = (s32[4,8,512]{2,1,0:T(8,128)S(1)}, s32[4,8,512]{2,1,0:T(8,128)}, u32[]{:S(2)}) copy-start(s32[4,8,512]{2,1,0:T(8,128)} %fiber.1) | copy-start | bytes 196612
  13.4 13.7 %copy-start.5 = (f32[4,8,512]{2,1,0:T(8,128)S(1)}, f32[4,8,512]{2,1,0:T(8,128)}, u32[]{:S(2)}) copy-start(f32[4,8,512]{2,1,0:T(8,128)} %lag.1) | copy-start | bytes 196612
  13.6 36.4 %copy-start.13 = (f32[6,16]{1,0:T(8,128)S(1)}, f32[6,16]{1,0:T(8,128)}, u32[]{:S(2)}) copy-start(f32[6,16]{1,0:T(8,128)} %param.16) | copy-start | bytes 1156
  13.6 36.4 %copy-start.14 = (f32[12]{0:T(128)S(1)}, f32[12]{0:T(128)}, u32[]{:S(2)}) copy-start(f32[12]{0:T(128)} %param.19) | copy-start | bytes 148
  13.6 36.4 %copy-start.15 = (f32[12]{0:T(128)S(1)}, f32[12]{0:T(128)}, u32[]{:S(2)}) copy-start(f32[12]{0:T(128)} %param.20) | copy-start | bytes 148
  13.6 36.4 %copy-start.16 = (f32[12]{0:T(128)S(1)}, f32[12]{0:T(128)}, u32[]{:S(2)}) copy-start(f32[12]{0:T(128)} %param.21) | copy-start | bytes 148
  13.6 36.4 %copy-start.17 = (f32[12]{0:T(128)S(1)}, f32[12]{0:T(128)}, u32[]{:S(2)}) copy-start(f32[12]{0:T(128)} %param.22) | copy-start | bytes 148
  13.6 36.4 %copy-start.18 = (f32[6]{0:T(128)S(1)}, f32[6]{0:T(128)}, u32[]{:S(2)}) copy-start(f32[6]{0:T(128)} %param.23) | copy-start | bytes 76
  20.1 7.5 %copy-start.10 = (s32[32]{0:T(128)}, s32[32]{0:T(128)S(1)}, u32[]{:S(2)}) copy-start(s32[32]{0:T(128)S(1)} %slice_reduce_fusion.arrived) | copy-start | bytes 388
  21.6 33.5 %all-to-all-start.1 = ((f32[32,48,128]{2,1,0:T(8,128)}), f32[32,48,128]{2,1,0:T(8,128)S(1)}, u32[]{:S(2)}, u32[]{:S(2)}) async-start(f32[32,48,128]{2,1,0:T(8,128)} %shard_map.143), calls=%async_computation.1 | async-start | bytes 1572864 | tf_op jit(solution)/shard_map/all_to_all | solution.py:463
  27.6 9.4 %collective-permute-start = (f32[6,8,512]{2,1,0:T(8,128)S(1)}, f32[6,8,512]{2,1,0:T(8,128)S(1)}, u32[]{:S(2)}, u32[]{:S(2)}) collective-permute-start(f32[6,8,512]{2,1,0:T(8,128)S(1)} %get-tuple-element.21), channel_id=1, source_target_pairs={{0,32},{32,64},{64,96},{96,128},{128,160},{160,192},{192,224},{224... | collective-permute-start | bytes 294920 | tf_op jit(solution)/shard_map/ppermute | solution.py:459
  35.1 7.4 %collective-permute-start.1 = (f32[6,8,512]{2,1,0:T(8,128)S(1)}, f32[6,8,512]{2,1,0:T(8,128)S(1)}, u32[]{:S(2)}, u32[]{:S(2)}) collective-permute-start(f32[6,8,512]{2,1,0:T(8,128)S(1)} %get-tuple-element.22), channel_id=1, source_target_pairs={{32,0},{64,32},{96,64},{128,96},{160,128},{192,160},{224,192},{256... | collective-permute-start | bytes 294920 | tf_op jit(solution)/shard_map/ppermute | solution.py:459
  42.6 7.6 %collective-permute-start.2 = (f32[42,512]{1,0:T(8,128)S(1)}, f32[42,512]{1,0:T(8,128)S(1)}, u32[]{:S(2)}, u32[]{:S(2)}) collective-permute-start(f32[42,512]{1,0:T(8,128)S(1)} %get-tuple-element.25), channel_id=1, source_target_pairs={{0,1},{1,2},{2,3},{3,4},{4,5},{5,6},{6,7},{7,8},{8,9},{9,10},{10,1... | collective-permute-start | bytes 258056 | tf_op jit(solution)/shard_map/ppermute | solution.py:459
  45.7 5.9 %collective-permute-start.3 = (f32[42,512]{1,0:T(8,128)S(1)}, f32[42,512]{1,0:T(8,128)S(1)}, u32[]{:S(2)}, u32[]{:S(2)}) collective-permute-start(f32[42,512]{1,0:T(8,128)S(1)} %get-tuple-element.26), channel_id=1, source_target_pairs={{1,0},{2,1},{3,2},{4,3},{5,4},{6,5},{7,6},{8,7},{9,8},{10,9},{11,1... | collective-permute-start | bytes 258056 | tf_op jit(solution)/shard_map/ppermute | solution.py:459
  54.5 0.6 copy-start.6
  55.1 0.7 copy-start.7
  55.8 0.7 copy-start.9
  58.4 5.9 %collective-permute-start.4 = (f32[3,8,512]{2,1,0:T(8,128)S(1)}, f32[3,8,512]{2,1,0:T(8,128)S(1)}, u32[]{:S(2)}, u32[]{:S(2)}) collective-permute-start(f32[3,8,512]{2,1,0:T(8,128)S(1)} %pad_maximum_fusion), channel_id=1, source_target_pairs={{0,32},{32,64},{64,96},{96,128},{128,160},{160,192},{192,224},{224... | collective-permute-start | bytes 147464 | tf_op jit(solution)/shard_map/ppermute | solution.py:459
  62.4 6.6 %collective-permute-start.5 = (f32[3,8,512]{2,1,0:T(8,128)S(1)}, f32[3,8,512]{2,1,0:T(8,128)S(1)}, u32[]{:S(2)}, u32[]{:S(2)}) collective-permute-start(f32[3,8,512]{2,1,0:T(8,128)S(1)} %pad_maximum_fusion.1), channel_id=1, source_target_pairs={{32,0},{64,32},{96,64},{128,96},{160,128},{192,160},{224,192},{256... | collective-permute-start | bytes 147464 | tf_op jit(solution)/shard_map/ppermute | solution.py:459
  69.1 8.9 %collective-permute-start.6 = (f32[22,512]{1,0:T(8,128)S(1)}, f32[22,512]{1,0:T(8,128)S(1)}, u32[]{:S(2)}, u32[]{:S(2)}) collective-permute-start(f32[22,512]{1,0:T(8,128)S(1)} %get-tuple-element.32), channel_id=1, source_target_pairs={{0,1},{1,2},{2,3},{3,4},{4,5},{5,6},{6,7},{7,8},{8,9},{9,10},{10,1... | collective-permute-start | bytes 135176 | tf_op jit(solution)/shard_map/ppermute | solution.py:459
  71.9 6.0 %collective-permute-start.7 = (f32[22,512]{1,0:T(8,128)S(1)}, f32[22,512]{1,0:T(8,128)S(1)}, u32[]{:S(2)}, u32[]{:S(2)}) collective-permute-start(f32[22,512]{1,0:T(8,128)S(1)} %get-tuple-element.33), channel_id=1, source_target_pairs={{1,0},{2,1},{3,2},{4,3},{5,4},{6,5},{7,6},{8,7},{9,8},{10,9},{11,1... | collective-permute-start | bytes 135176 | tf_op jit(solution)/shard_map/ppermute | solution.py:459
  78.0 0.7 copy-start.12
  78.6 29.8 %copy-start.1 = (f32[12,16,512]{2,1,0:T(8,128)S(1)}, f32[12,16,512]{2,1,0:T(8,128)}, u32[]{:S(2)}) copy-start(f32[12,16,512]{2,1,0:T(8,128)} %gates.3) | copy-start | bytes 1179652
  78.6 29.9 %copy-start.8 = (f32[256]{0:T(256)S(1)}, f32[256]{0:T(256)}, u32[]{:S(2)}) copy-start(f32[256]{0:T(256)} %copy-done.6) | copy-start | bytes 3076
  78.6 29.9 %copy-start.11 = (s32[32]{0:T(128)S(1)}, s32[32]{0:T(128)}, u32[]{:S(2)}) copy-start(s32[32]{0:T(128)} %copy-done.10) | copy-start | bytes 388
  81.1 27.4 %all-to-all-start.2 = ((f32[32,16,128]{2,1,0:T(8,128)}), f32[32,16,128]{2,1,0:T(8,128)S(1)}, u32[]{:S(2)}, u32[]{:S(2)}) async-start(f32[32,16,128]{2,1,0:T(8,128)} %get-tuple-element.36), calls=%async_computation.2 | async-start | bytes 524288 | tf_op jit(solution)/shard_map/all_to_all | solution.py:463
  88.7 17.9 %collective-permute-start.9 = (f32[1,8,512]{2,1,0:T(8,128)S(1)}, f32[1,8,512]{2,1,0:T(8,128)S(1)}, u32[]{:S(2)}, u32[]{:S(2)}) collective-permute-start(f32[1,8,512]{2,1,0:T(8,128)S(1)} %get-tuple-element.43), channel_id=1, source_target_pairs={{32,0},{64,32},{96,64},{128,96},{160,128},{192,160},{224,192},{256... | collective-permute-start | bytes 49160 | tf_op jit(solution)/shard_map/ppermute | solution.py:459
  90.6 16.0 %collective-permute-start.8 = (f32[1,8,512]{2,1,0:T(8,128)S(1)}, f32[1,8,512]{2,1,0:T(8,128)S(1)}, u32[]{:S(2)}, u32[]{:S(2)}) collective-permute-start(f32[1,8,512]{2,1,0:T(8,128)S(1)} %get-tuple-element.44), channel_id=1, source_target_pairs={{0,32},{32,64},{64,96},{96,128},{128,160},{160,192},{192,224},{224... | collective-permute-start | bytes 49160 | tf_op jit(solution)/shard_map/ppermute | solution.py:459
  95.5 6.5 %collective-permute-start.11 = (f32[4,1,512]{2,1,0:T(1,128)S(1)}, f32[4,1,512]{2,1,0:T(1,128)S(1)}, u32[]{:S(2)}, u32[]{:S(2)}) collective-permute-start(f32[4,1,512]{2,1,0:T(1,128)S(1)} %get-tuple-element.41), channel_id=1, source_target_pairs={{1,0},{2,1},{3,2},{4,3},{5,4},{6,5},{7,6},{8,7},{9,8},{10,9},{11,1... | collective-permute-start | bytes 24584 | tf_op jit(solution)/shard_map/ppermute | solution.py:459
  100.1 6.5 %collective-permute-start.10 = (f32[4,1,512]{2,1,0:T(1,128)S(1)}, f32[4,1,512]{2,1,0:T(1,128)S(1)}, u32[]{:S(2)}, u32[]{:S(2)}) collective-permute-start(f32[4,1,512]{2,1,0:T(1,128)S(1)} %get-tuple-element.42), channel_id=1, source_target_pairs={{0,1},{1,2},{2,3},{3,4},{4,5},{5,6},{6,7},{7,8},{8,9},{9,10},{10,1... | collective-permute-start | bytes 24584 | tf_op jit(solution)/shard_map/ppermute | solution.py:459

commit v6 on v5

--- a/solution.py
+++ b/solution.py
@@ -142,6 +142,15 @@
                     ref[base + CX + 2 + m : base + CX + 3 + m] = high[kind + m, one]
 
 
+def claims_body(slots, worker, claims_ref, held_ref):
+    held_ref[...] = jnp.full(held_ref.shape, -1, jnp.int32)
+    for t in range(TILES):
+        k = worker[t // CY, t % CY]
+        at = jnp.where(k >= 0, jnp.maximum(k, 0) // CAP, slots)
+        held_ref[at] = jnp.full((1, LANES), jnp.maximum(k, 0) % CAP, jnp.int32)
+    claims_ref[...] = held_ref[0:slots]
+
+
 def by_row_body(gates, out_ref):
     for g in range(GATES):
         for c in range(CHUNKS):
@@ -151,7 +160,7 @@
 
 def pack_body(slots, arrived, by_row, out_ref):
     for d in range(slots):
-        k = jnp.maximum(arrived[d], 0)
+        k = jnp.maximum(arrived[d, 0, 0], 0)
         out_ref[d] = by_row[pl.ds(pl.multiple_of(k * GATES * CHUNKS, 8), GATES * CHUNKS), :]
 
 
@@ -270,11 +279,11 @@
         base_ref[i] = voltage[i] + tissue[i].astype(f32) * spread[2 + i][2 : 2 + CY]
 
 
-def react_body(worker, par, voltage, base, tissue, coming, v1_ref, current_ref, states_ref, v_d, base_d, w_d, out_d, cur_d):
+def react_body(worker, par, voltage, base, flags, coming, v1_ref, current_ref, states_ref, v_d, base_d, w_d, out_d, cur_d):
     for i in range(CX):
         to_dense(v_d, voltage[i], i)
         to_dense(base_d, base[i], i)
-        to_dense(w_d, tissue[i].astype(f32), i)
+        to_dense(w_d, flags[2 + i].astype(f32)[2 : 2 + CY], i)
     low_half = lax.broadcasted_iota(jnp.int32, (8, LANES), 0) < CHUNKS
 
     def pair(p, carry):
@@ -340,8 +349,8 @@
 
 
 def steps_body(
-    slots, worker, tile_of, par, v0, flags, faces, v1, current, low, high, left, right, parts,
-    v3_ref, ours_ref, used_ref, v_ref, cur_ref, next_ref, rows_ref,
+    slots, worker, par, v0, flags, faces, v1, current, low, high, left, right, parts,
+    v3_ref, ours_ref, used_ref, v_ref, cur_ref, next_ref, rows_ref, tile_of,
 ):
     v_ref[...] = jnp.zeros((NI, NJ, CZ), f32)
     cur_ref[...] = jnp.zeros((NI, NJ, CZ), f32)
@@ -360,6 +369,11 @@
                 v_ref[i, j : j + 1, :] = ref[n * NI + i : n * NI + i + 1, :]
         for i in range(CX + 2):
             cur_ref[1 + i, outer : outer + 1, :] = ref[2 * NI + i : 2 * NI + i + 1, :]
+    for d in range(slots):
+        tile_of[d] = 0
+    for t in range(TILES):
+        k = worker[t // CY, t % CY]
+        tile_of[jnp.where(k >= 0, jnp.maximum(k, 0) // CAP, slots)] = t
     face = lambda n, i: faces[face_at(n, i)]
     weights = {i: flags[i].astype(f32) for i in range(NI)}
     field = {i: weights[i] * v_ref[i] for i in range(NI)}
@@ -386,7 +400,7 @@
 
 def last_body(slots, arrived, par, returned, gates, out_ref, rows_ref, seen_ref):
     for d in range(slots):
-        k = arrived[d]
+        k = arrived[d, 0, 0]
         row = jnp.where(k >= 0, k, CAP)
         rows_ref[pl.ds(pl.multiple_of(row * 16, 16), 16), :] = returned[d]
     for n in range(STEPS):
@@ -484,17 +498,19 @@
     dma = lambda n: pltpu.SemaphoreType.DMA((n,))
     whole_i = pltpu.VMEM(block, jnp.int32)
 
-    live = worker >= 0
-    holder = jnp.where(live, worker // CAP, -1)
-    claimed = holder[None] == jnp.arange(slots, dtype=jnp.int32)[:, None, None]
-    tiles = CY * jnp.arange(CX, dtype=jnp.int32)[:, None] + jnp.arange(CY, dtype=jnp.int32)[None, :]
-    claims = jnp.sum(jnp.where(claimed, worker % CAP + 1, 0), axis=(1, 2)) - 1
-    tile_of = jnp.sum(jnp.where(claimed, tiles[None], 0), axis=(1, 2))
-    arrived = swap_blocks(jnp.broadcast_to(claims[:, None, None], (slots, 1, LANES)))[:, 0, 0]
+    slip = (slots, 1, LANES)
+    (claims,) = kernel_call(
+        functools.partial(claims_body, slots),
+        [jax.ShapeDtypeStruct(slip, jnp.int32)],
+        [SM],
+        [pltpu.VMEM((slots + 1, 1, LANES), jnp.int32)],
+    )(worker)
+    arrived = swap_blocks(claims)
+
     rim = (6, CY, CZ)
     side = (2 * CX + 2 + 4 * NI, CZ)
     up, down, right, left = kernel_call(
-        start_body, [rim, rim, side, side], [HB] * 4, [block, block, whole_i, whole_i, dma(4)]
+        start_body, [rim, rim, side, side], [HB] * 4, [block, block, whole_i, whole_i, dma(4)], limit=62
     )(voltage, voltage_lag, tissue, fiber)
     low, high = shift_pair("slab", up, down)
     (by_row,) = kernel_call(by_row_body, [(CAP * GATES * CHUNKS, LANES)], [VM])(gates)
@@ -519,7 +535,7 @@
     dense = (TILES * CHUNKS, LANES)
     v1, current, states = kernel_call(
         react_body, [block, block, (GATES, *dense)], [SM, SM] + [VM] * 4, [dense] * 5
-    )(worker, par, voltage, base, tissue, coming)
+    )(worker, par, voltage, base, flags, coming)
 
     low, high = shift_pair(
         "slab", jnp.concatenate([v1[-2:], current[-1:]]), jnp.concatenate([v1[:2], current[:1]])
@@ -532,10 +548,10 @@
     v3, ours, used = kernel_call(
         functools.partial(steps_body, slots),
         [block, block, (slots, 16, LANES)],
-        [SM] * 3 + [VM] * 10,
-        [wide, wide, wide, (TILES * 16, LANES)],
+        [SM] * 2 + [VM] * 10,
+        [wide, wide, wide, (TILES * 16, LANES), pltpu.SMEM((slots + 1,), jnp.int32)],
         limit=12,
-    )(worker, tile_of, par, voltage, flags, faces, v1, current, low, high, left, right, parts)
+    )(worker, par, voltage, flags, faces, v1, current, low, high, left, right, parts)
     returned = swap_blocks(used)
 
     below, above = shift_pair("slab", ours[-1:], ours[:1])

time: 112 us -> 113 us (level)
  Pallas kernels: 15.1 us -> 18.3 us
  other arithmetic: 1.41 us -> 0.01 us
    pallas_call x0 -> x1, Pallas kernels: none -> 1.3 us  [on_device(): kernel_call(functools.partial(claims_body, slots), [jax.ShapeDtypeStruct(...]
    pallas_call x1, Pallas kernels: 0.43 us -> 1.72 us  [on_device(): kernel_call(start_body, [rim, rim, side, side], [HB] * 4, [block, block,...]
    unnamed x38 -> x36, local copies, waits for them, and re-layouts: 3.63 us -> 4.82 us
  transfers between devices with their start and end apart: 15 -> 15, of which waited for: 5 -> 5; matrix products, arithmetic and copies ran while one was open for 0% -> 0% of each run, Pallas kernels for 6% -> 7%
where the time goes in v6:
time: 113 us
  starting transfers between devices  66.1 us (58%)
  waiting for transfers between devices  22.2 us (20%)
  Pallas kernels  18.3 us (16%)
  local copies, waits for them, and re-layouts  4.94 us (4%)
    ppermute x6, starting transfers between devices, shift_pair(): lax.ppermute(last, axis, up)  23.4 us
    all_to_all x3, starting transfers between devices, swap_blocks(): return lax.all_to_all(x, 'blk', split_axis=0, concat_axis=0, tiled=True)  22.8 us
    ppermute x6, starting transfers between devices, shift_pair(): lax.ppermute(first, axis, [(b, a) for a, b in up])  19.9 us
    ppermute x6, waiting for transfers between devices, shift_pair(): lax.ppermute(first, axis, [(b, a) for a, b in up])  11.8 us
    all_to_all x3, waiting for transfers between devices, swap_blocks(): return lax.all_to_all(x, 'blk', split_axis=0, concat_axis=0, tiled=True)  5.75 us
    unnamed x36, local copies, waits for them, and re-layouts  4.82 us
    ppermute x6, waiting for transfers between devices, shift_pair(): lax.ppermute(last, axis, up)  4.58 us
    pallas_call x1, Pallas kernels, on_device(): kernel_call(faces_body, [sheets, jax.ShapeDtypeStruct(wide, jnp.bfloat16)...  2.96 us
  transfers between devices with their start and end apart: 15, of which 5 were waited for; matrix products, arithmetic and copies ran while one was open for 0% of the time, Pallas kernels for 7%

profile of v6, /device:TPU:199, one launch (start us, length us, event | category | flops | bytes accessed | tf_op | source)
XLA Modules:
  0.0 112.6 jit_solution(14948507916729804523)
XLA Ops:
  0.6 0.0 copy-start.10
  0.6 0.7 copy-done.10
  1.3 1.3 %shard_map.142 = s32[32,1,128]{2,1,0:T(1,128)} custom-call(s32[4,8]{1,0:T(4,128)S(1)} %copy-done.10), custom_call_target="tpu_custom_call" | custom-call | flops 1000000 | bytes 1000000 | tf_op jit(solution)/shard_map/pallas_call | solution.py:502
  2.6 9.7 %all-to-all-start = ((s32[32,1,128]{2,1,0:T(1,128)}), s32[32,1,128]{2,1,0:T(1,128)S(1)}, u32[]{:S(2)}, u32[]{:S(2)}) async-start(s32[32,1,128]{2,1,0:T(1,128)} %shard_map.142), calls=%async_computation | async-start | bytes 32768 | tf_op jit(solution)/shard_map/all_to_all | solution.py:477
  12.3 0.0 copy-start.2
  12.3 1.0 copy-done.2
  13.3 0.1 shard_map.143.by_row
  13.4 0.0 copy-start.12
  13.4 0.0 copy-start.13
  13.4 0.0 copy-start.14
  13.4 0.0 copy-start.15
  13.5 0.0 copy-start.16
  13.5 0.0 copy-start.17
  13.5 0.0 copy-start.5
  13.5 0.0 copy-start.6
  13.5 5.7 %all-to-all-done.arrived = s32[32,1,128]{2,1,0:T(1,128)S(1)} async-done(((s32[32,1,128]{2,1,0:T(1,128)}), s32[32,1,128]{2,1,0:T(1,128)S(1)}, u32[]{:S(2)}, u32[]{:S(2)}) %all-to-all-start) | async-done | bytes 16416 | tf_op jit(solution)/shard_map/all_to_all | solution.py:477
  19.3 1.7 %shard_map.144 = f32[32,48,128]{2,1,0:T(8,128)} custom-call(s32[32,1,128]{2,1,0:T(1,128)S(1)} %all-to-all-done.arrived, f32[768,128]{1,0:T(8,128)S(1)} %shard_map.143.by_row), custom_call_target="tpu_custom_call" | custom-call | flops 1000000 | bytes 1000000 | tf_op jit(solution)/shard_map/pallas_call | solution.py:519
  21.0 5.5 %all-to-all-start.1 = ((f32[32,48,128]{2,1,0:T(8,128)}), f32[32,48,128]{2,1,0:T(8,128)S(1)}, u32[]{:S(2)}, u32[]{:S(2)}) async-start(f32[32,48,128]{2,1,0:T(8,128)} %shard_map.144), calls=%async_computation.1 | async-start | bytes 1572864 | tf_op jit(solution)/shard_map/all_to_all | solution.py:477
  26.5 1.7 %shard_map.139 = (f32[6,8,512]{2,1,0:T(8,128)}, f32[6,8,512]{2,1,0:T(8,128)}, f32[42,512]{1,0:T(8,128)}, f32[42,512]{1,0:T(8,128)}) custom-call(f32[4,8,512]{2,1,0:T(8,128)} %v0.1, f32[4,8,512]{2,1,0:T(8,128)} %lag.1, s32[4,8,512]{2,1,0:T(8,128)} %tissue.3, s32[4,8,512]{2,1,0:T(8,128)} %fiber.1), custom_call_target="tpu_custom_call" | custom-call | flops 1000000 | bytes 1000000 | tf_op jit(solution)/shard_map/pallas_call | solution.py:512
  28.3 7.5 %collective-permute-start = (f32[6,8,512]{2,1,0:T(8,128)}, f32[6,8,512]{2,1,0:T(8,128)S(1)}, u32[]{:S(2)}, u32[]{:S(2)}) collective-permute-start(f32[6,8,512]{2,1,0:T(8,128)} %get-tuple-element.21), channel_id=1, source_target_pairs={{0,32},{32,64},{64,96},{96,128},{128,160},{160,192},{192,224},{224... | collective-permute-start | bytes 294920 | tf_op jit(solution)/shard_map/ppermute | solution.py:473
  35.8 1.9 %collective-permute-start.1 = (f32[6,8,512]{2,1,0:T(8,128)}, f32[6,8,512]{2,1,0:T(8,128)S(1)}, u32[]{:S(2)}, u32[]{:S(2)}) collective-permute-start(f32[6,8,512]{2,1,0:T(8,128)} %get-tuple-element.22), channel_id=1, source_target_pairs={{32,0},{64,32},{96,64},{128,96},{160,128},{192,160},{224,192},{256... | collective-permute-start | bytes 294920 | tf_op jit(solution)/shard_map/ppermute | solution.py:473
  37.7 0.0 collective-permute-done.low
  37.7 5.7 %collective-permute-done.1.high = f32[6,8,512]{2,1,0:T(8,128)S(1)} collective-permute-done((f32[6,8,512]{2,1,0:T(8,128)}, f32[6,8,512]{2,1,0:T(8,128)S(1)}, u32[]{:S(2)}, u32[]{:S(2)}) %collective-permute-start.1) | collective-permute-done | bytes 98336 | tf_op jit(solution)/shard_map/ppermute | solution.py:473
  43.4 0.9 copy-done.8
  44.3 0.9 copy-done.9
  45.2 3.1 %collective-permute-start.2 = (f32[42,512]{1,0:T(8,128)S(1)}, f32[42,512]{1,0:T(8,128)S(1)}, u32[]{:S(2)}, u32[]{:S(2)}) collective-permute-start(f32[42,512]{1,0:T(8,128)S(1)} %get-tuple-element.25), channel_id=1, source_target_pairs={{0,1},{1,2},{2,3},{3,4},{4,5},{5,6},{6,7},{7,8},{8,9},{9,10},{10,1... | collective-permute-start | bytes 258056 | tf_op jit(solution)/shard_map/ppermute | solution.py:473
  48.3 4.3 %collective-permute-start.3 = (f32[42,512]{1,0:T(8,128)S(1)}, f32[42,512]{1,0:T(8,128)S(1)}, u32[]{:S(2)}, u32[]{:S(2)}) collective-permute-start(f32[42,512]{1,0:T(8,128)S(1)} %get-tuple-element.26), channel_id=1, source_target_pairs={{1,0},{2,1},{3,2},{4,3},{5,4},{6,5},{7,6},{8,7},{9,8},{10,9},{11,1... | collective-permute-start | bytes 258056 | tf_op jit(solution)/shard_map/ppermute | solution.py:473
  52.7 0.1 concatenate.9
  52.8 1.4 %collective-permute-done.3.right = f32[42,512]{1,0:T(8,128)S(1)} collective-permute-done((f32[42,512]{1,0:T(8,128)S(1)}, f32[42,512]{1,0:T(8,128)S(1)}, u32[]{:S(2)}, u32[]{:S(2)}) %collective-permute-start.3) | collective-permute-done | bytes 86048 | tf_op jit(solution)/shard_map/ppermute | solution.py:473
  54.3 3.0 %shard_map.141 = (f32[57,16,512]{2,1,0:T(8,128)S(1)}, bf16[8,16,512]{2,1,0:T(8,128)(2,1)S(1)}, f32[4,8,512]{2,1,0:T(8,128)S(1)}, f32[24,512]{1,0:T(8,128)S(1)}) custom-call(f32[256]{0:T(256)S(1)} %pad.4.par, f32[4,8,512]{2,1,0:T(8,128)S(1)} %copy-done.4, s32[4,8,512]{2,1,0:T(8,128)S(1)} %copy-done.5, s32[4,8,512]{2,1,0:T(8,128)S(1)} %copy-done.6, ...), custom_call_target="tpu_custom_call" | custom-call | flops 1000000 | bytes 1000000 | tf_op jit(solution)/shard_map/pallas_call | solution.py:527
  57.3 1.3 %copy-done = f32[57,16,512]{2,1,0:T(8,128)} copy-done((f32[57,16,512]{2,1,0:T(8,128)}, f32[57,16,512]{2,1,0:T(8,128)S(1)}, u32[]{:S(2)}) %copy-start) | copy-done | bytes 1867800
  58.5 1.9 %shard_map.145 = (f32[4,8,512]{2,1,0:T(8,128)S(1)}, f32[4,8,512]{2,1,0:T(8,128)S(1)}, f32[12,128,128]{2,1,0:T(8,128)S(1)}) custom-call(s32[4,8]{1,0:T(4,128)S(1)} %copy-done.11, f32[256]{0:T(256)S(1)} %pad.4.par, f32[4,8,512]{2,1,0:T(8,128)S(1)} %copy-done.4, f32[4,8,512]{2,1,0:T(8,128)S(1)} %get-tuple-element.29.base, ...), custom_call_target="tpu_custom_call" | custom-call | flops 1000000 | bytes 1000000 | tf_op jit(solution)/shard_map/pallas_call | solution.py:536
  60.5 3.1 %collective-permute-start.4 = (f32[3,8,512]{2,1,0:T(8,128)S(1)}, f32[3,8,512]{2,1,0:T(8,128)S(1)}, u32[]{:S(2)}, u32[]{:S(2)}) collective-permute-start(f32[3,8,512]{2,1,0:T(8,128)S(1)} %pad_maximum_fusion), channel_id=1, source_target_pairs={{0,32},{32,64},{64,96},{96,128},{128,160},{160,192},{192,224},{224... | collective-permute-start | bytes 147464 | tf_op jit(solution)/shard_map/ppermute | solution.py:473
  63.7 1.9 %collective-permute-start.5 = (f32[3,8,512]{2,1,0:T(8,128)S(1)}, f32[3,8,512]{2,1,0:T(8,128)S(1)}, u32[]{:S(2)}, u32[]{:S(2)}) collective-permute-start(f32[3,8,512]{2,1,0:T(8,128)S(1)} %pad_maximum_fusion.1), channel_id=1, source_target_pairs={{32,0},{64,32},{96,64},{128,96},{160,128},{192,160},{224,192},{256... | collective-permute-start | bytes 147464 | tf_op jit(solution)/shard_map/ppermute | solution.py:473
  65.6 4.7 %collective-permute-done.5.high = f32[3,8,512]{2,1,0:T(8,128)S(1)} collective-permute-done((f32[3,8,512]{2,1,0:T(8,128)S(1)}, f32[3,8,512]{2,1,0:T(8,128)S(1)}, u32[]{:S(2)}, u32[]{:S(2)}) %collective-permute-start.5) | collective-permute-done | bytes 49184 | tf_op jit(solution)/shard_map/ppermute | solution.py:473
  70.3 2.9 %collective-permute-start.6 = (f32[22,512]{1,0:T(8,128)S(1)}, f32[22,512]{1,0:T(8,128)S(1)}, u32[]{:S(2)}, u32[]{:S(2)}) collective-permute-start(f32[22,512]{1,0:T(8,128)S(1)} %get-tuple-element.32), channel_id=1, source_target_pairs={{0,1},{1,2},{2,3},{3,4},{4,5},{5,6},{6,7},{7,8},{8,9},{9,10},{10,1... | collective-permute-start | bytes 135176 | tf_op jit(solution)/shard_map/ppermute | solution.py:473
  73.2 5.2 %collective-permute-start.7 = (f32[22,512]{1,0:T(8,128)S(1)}, f32[22,512]{1,0:T(8,128)S(1)}, u32[]{:S(2)}, u32[]{:S(2)}) collective-permute-start(f32[22,512]{1,0:T(8,128)S(1)} %get-tuple-element.33), channel_id=1, source_target_pairs={{1,0},{2,1},{3,2},{4,3},{5,4},{6,5},{7,6},{8,7},{9,8},{10,9},{11,1... | collective-permute-start | bytes 135176 | tf_op jit(solution)/shard_map/ppermute | solution.py:473
  78.5 1.5 %shard_map.147.parts = f32[4,4,8,512]{3,2,1,0:T(8,128)S(1)} custom-call(f32[256]{0:T(256)S(1)} %pad.4.par, f32[12,128,128]{2,1,0:T(8,128)S(1)} %get-tuple-element.34.states_in, f32[4,8,512]{2,1,0:T(8,128)S(1)} %get-tuple-element.30.v1), custom_call_target="tpu_custom_call" | custom-call | flops 1000000 | bytes 1000000 | tf_op jit(solution)/shard_map/pallas_call | solution.py:543
  80.0 0.0 copy-start.3
  80.0 2.6 %shard_map.148 = (f32[4,8,512]{2,1,0:T(8,128)}, f32[4,8,512]{2,1,0:T(8,128)S(1)}, f32[32,16,128]{2,1,0:T(8,128)}) custom-call(s32[4,8]{1,0:T(4,128)S(1)} %copy-done.11, f32[256]{0:T(256)S(1)} %pad.4.par, f32[4,8,512]{2,1,0:T(8,128)S(1)} %copy-done.4, bf16[8,16,512]{2,1,0:T(8,128)(2,1)S(1)} %get-tuple-element.27.flags, f32[57,16,512]{2,1,0:T(8,128)S(1)} %copy-done.1, ...), custom_call_target="tpu_custom_call" | custom-call | flops 1000000 | bytes 1000000 | tf_op jit(solution)/shard_map/pallas_call | solution.py:548
  82.6 7.6 %all-to-all-start.2 = ((f32[32,16,128]{2,1,0:T(8,128)}), f32[32,16,128]{2,1,0:T(8,128)S(1)}, u32[]{:S(2)}, u32[]{:S(2)}) async-start(f32[32,16,128]{2,1,0:T(8,128)} %get-tuple-element.36), calls=%async_computation.2 | async-start | bytes 524288 | tf_op jit(solution)/shard_map/all_to_all | solution.py:477
  90.2 1.9 %collective-permute-start.9 = (f32[1,8,512]{2,1,0:T(8,128)S(1)}, f32[1,8,512]{2,1,0:T(8,128)S(1)}, u32[]{:S(2)}, u32[]{:S(2)}) collective-permute-start(f32[1,8,512]{2,1,0:T(8,128)S(1)} %get-tuple-element.41), channel_id=1, source_target_pairs={{32,0},{64,32},{96,64},{128,96},{160,128},{192,160},{224,192},{256... | collective-permute-start | bytes 49160 | tf_op jit(solution)/shard_map/ppermute | solution.py:473
  92.2 4.9 %collective-permute-start.8 = (f32[1,8,512]{2,1,0:T(8,128)S(1)}, f32[1,8,512]{2,1,0:T(8,128)S(1)}, u32[]{:S(2)}, u32[]{:S(2)}) collective-permute-start(f32[1,8,512]{2,1,0:T(8,128)S(1)} %get-tuple-element.42), channel_id=1, source_target_pairs={{0,32},{32,64},{64,96},{96,128},{128,160},{160,192},{192,224},{224... | collective-permute-start | bytes 49160 | tf_op jit(solution)/shard_map/ppermute | solution.py:473
  97.0 4.6 %collective-permute-start.11 = (f32[4,1,512]{2,1,0:T(1,128)S(1)}, f32[4,1,512]{2,1,0:T(1,128)S(1)}, u32[]{:S(2)}, u32[]{:S(2)}) collective-permute-start(f32[4,1,512]{2,1,0:T(1,128)S(1)} %get-tuple-element.39), channel_id=1, source_target_pairs={{1,0},{2,1},{3,2},{4,3},{5,4},{6,5},{7,6},{8,7},{9,8},{10,9},{11,1... | collective-permute-start | bytes 24584 | tf_op jit(solution)/shard_map/ppermute | solution.py:473
  101.6 1.9 %collective-permute-start.10 = (f32[4,1,512]{2,1,0:T(1,128)S(1)}, f32[4,1,512]{2,1,0:T(1,128)S(1)}, u32[]{:S(2)}, u32[]{:S(2)}) collective-permute-start(f32[4,1,512]{2,1,0:T(1,128)S(1)} %get-tuple-element.40), channel_id=1, source_target_pairs={{0,1},{1,2},{2,3},{3,4},{4,5},{5,6},{6,7},{7,8},{8,9},{9,10},{10,1... | collective-permute-start | bytes 24584 | tf_op jit(solution)/shard_map/ppermute | solution.py:473
  103.6 4.6 %collective-permute-done.10.left = f32[4,1,512]{2,1,0:T(1,128)S(1)} collective-permute-done((f32[4,1,512]{2,1,0:T(1,128)S(1)}, f32[4,1,512]{2,1,0:T(1,128)S(1)}, u32[]{:S(2)}, u32[]{:S(2)}) %collective-permute-start.10) | collective-permute-done | bytes 8224 | tf_op jit(solution)/shard_map/ppermute | solution.py:473
  108.1 1.9 %shard_map.150 = f32[3,4,8,512]{3,2,1,0:T(8,128)} custom-call(f32[4,8,512]{2,1,0:T(8,128)S(1)} %get-tuple-element.37.ours, f32[1,8,512]{2,1,0:T(8,128)S(1)} %collective-permute-done.8.below, f32[1,8,512]{2,1,0:T(8,128)S(1)} %collective-permute-done.9.above, f32[4,1,512]{2,1,0:T(1,128)S(1)} %collective-permute-done.10.left, ...), custom_call_target="tpu_custom_call" | custom-call | flops 1000000 | bytes 1000000 | tf_op jit(solution)/shard_map/pallas_call | solution.py:560
  110.0 2.6 %shard_map.149 = f32[12,16,512]{2,1,0:T(8,128)} custom-call(s32[32,1,128]{2,1,0:T(1,128)S(1)} %all-to-all-done.arrived, f32[256]{0:T(256)S(1)} %pad.4.par, f32[32,16,128]{2,1,0:T(8,128)S(1)} %all-to-all-done.2.returned, f32[12,16,512]{2,1,0:T(8,128)S(1)} %copy-done.3), custom_call_target="tpu_custom_call" | custom-call | flops 1000000 | bytes 1000000 | tf_op jit(solution)/shard_map/pallas_call | solution.py:564
  (39 shorter events, 0.2 us)
Async XLA Ops:
  0.6 0.7 copy-start.10
  2.6 16.7 %all-to-all-start = ((s32[32,1,128]{2,1,0:T(1,128)}), s32[32,1,128]{2,1,0:T(1,128)S(1)}, u32[]{:S(2)}, u32[]{:S(2)}) async-start(s32[32,1,128]{2,1,0:T(1,128)} %shard_map.142), calls=%async_computation | async-start | bytes 32768 | tf_op jit(solution)/shard_map/all_to_all | solution.py:477
  12.3 1.0 copy-start.2
  13.4 39.2 %copy-start.12 = (f32[6,16]{1,0:T(8,128)S(1)}, f32[6,16]{1,0:T(8,128)}, u32[]{:S(2)}) copy-start(f32[6,16]{1,0:T(8,128)} %param.16) | copy-start | bytes 1156
  13.4 39.3 %copy-start.13 = (f32[12]{0:T(128)S(1)}, f32[12]{0:T(128)}, u32[]{:S(2)}) copy-start(f32[12]{0:T(128)} %param.19) | copy-start | bytes 148
  13.4 39.2 %copy-start.14 = (f32[12]{0:T(128)S(1)}, f32[12]{0:T(128)}, u32[]{:S(2)}) copy-start(f32[12]{0:T(128)} %param.20) | copy-start | bytes 148
  13.4 39.2 %copy-start.15 = (f32[12]{0:T(128)S(1)}, f32[12]{0:T(128)}, u32[]{:S(2)}) copy-start(f32[12]{0:T(128)} %param.21) | copy-start | bytes 148
  13.5 39.2 %copy-start.16 = (f32[12]{0:T(128)S(1)}, f32[12]{0:T(128)}, u32[]{:S(2)}) copy-start(f32[12]{0:T(128)} %param.22) | copy-start | bytes 148
  13.5 39.2 %copy-start.17 = (f32[6]{0:T(128)S(1)}, f32[6]{0:T(128)}, u32[]{:S(2)}) copy-start(f32[6]{0:T(128)} %param.23) | copy-start | bytes 76
  13.5 40.8 %copy-start.4 = (f32[4,8,512]{2,1,0:T(8,128)S(1)}, f32[4,8,512]{2,1,0:T(8,128)}, u32[]{:S(2)}) copy-start(f32[4,8,512]{2,1,0:T(8,128)} %v0.1) | copy-start | bytes 196612
  13.5 40.8 %copy-start.5 = (s32[4,8,512]{2,1,0:T(8,128)S(1)}, s32[4,8,512]{2,1,0:T(8,128)}, u32[]{:S(2)}) copy-start(s32[4,8,512]{2,1,0:T(8,128)} %tissue.3) | copy-start | bytes 196612
  13.5 40.8 %copy-start.6 = (s32[4,8,512]{2,1,0:T(8,128)S(1)}, s32[4,8,512]{2,1,0:T(8,128)}, u32[]{:S(2)}) copy-start(s32[4,8,512]{2,1,0:T(8,128)} %fiber.1) | copy-start | bytes 196612
  13.5 45.0 %copy-start.11 = (s32[4,8]{1,0:T(4,128)S(1)}, s32[4,8]{1,0:T(4,128)}, u32[]{:S(2)}) copy-start(s32[4,8]{1,0:T(4,128)} %worker.5) | copy-start | bytes 388
  21.0 37.5 %all-to-all-start.1 = ((f32[32,48,128]{2,1,0:T(8,128)}), f32[32,48,128]{2,1,0:T(8,128)S(1)}, u32[]{:S(2)}, u32[]{:S(2)}) async-start(f32[32,48,128]{2,1,0:T(8,128)} %shard_map.144), calls=%async_computation.1 | async-start | bytes 1572864 | tf_op jit(solution)/shard_map/all_to_all | solution.py:477
  28.3 9.4 %collective-permute-start = (f32[6,8,512]{2,1,0:T(8,128)}, f32[6,8,512]{2,1,0:T(8,128)S(1)}, u32[]{:S(2)}, u32[]{:S(2)}) collective-permute-start(f32[6,8,512]{2,1,0:T(8,128)} %get-tuple-element.21), channel_id=1, source_target_pairs={{0,32},{32,64},{64,96},{96,128},{128,160},{160,192},{192,224},{224... | collective-permute-start | bytes 294920 | tf_op jit(solution)/shard_map/ppermute | solution.py:473
  35.8 7.7 %collective-permute-start.1 = (f32[6,8,512]{2,1,0:T(8,128)}, f32[6,8,512]{2,1,0:T(8,128)S(1)}, u32[]{:S(2)}, u32[]{:S(2)}) collective-permute-start(f32[6,8,512]{2,1,0:T(8,128)} %get-tuple-element.22), channel_id=1, source_target_pairs={{32,0},{64,32},{96,64},{128,96},{160,128},{192,160},{224,192},{256... | collective-permute-start | bytes 294920 | tf_op jit(solution)/shard_map/ppermute | solution.py:473
  43.4 0.9 copy-start.8
  44.3 0.9 copy-start.9
  45.2 7.6 %collective-permute-start.2 = (f32[42,512]{1,0:T(8,128)S(1)}, f32[42,512]{1,0:T(8,128)S(1)}, u32[]{:S(2)}, u32[]{:S(2)}) collective-permute-start(f32[42,512]{1,0:T(8,128)S(1)} %get-tuple-element.25), channel_id=1, source_target_pairs={{0,1},{1,2},{2,3},{3,4},{4,5},{5,6},{6,7},{7,8},{8,9},{9,10},{10,1... | collective-permute-start | bytes 258056 | tf_op jit(solution)/shard_map/ppermute | solution.py:473
  48.3 5.9 %collective-permute-start.3 = (f32[42,512]{1,0:T(8,128)S(1)}, f32[42,512]{1,0:T(8,128)S(1)}, u32[]{:S(2)}, u32[]{:S(2)}) collective-permute-start(f32[42,512]{1,0:T(8,128)S(1)} %get-tuple-element.26), channel_id=1, source_target_pairs={{1,0},{2,1},{3,2},{4,3},{5,4},{6,5},{7,6},{8,7},{9,8},{10,9},{11,1... | collective-permute-start | bytes 258056 | tf_op jit(solution)/shard_map/ppermute | solution.py:473
  57.2 1.3 %copy-start = (f32[57,16,512]{2,1,0:T(8,128)}, f32[57,16,512]{2,1,0:T(8,128)S(1)}, u32[]{:S(2)}) copy-start(f32[57,16,512]{2,1,0:T(8,128)S(1)} %get-tuple-element.28.faces) | copy-start | bytes 5603332
  58.5 21.4 %copy-start.1 = (f32[57,16,512]{2,1,0:T(8,128)S(1)}, f32[57,16,512]{2,1,0:T(8,128)}, u32[]{:S(2)}) copy-start(f32[57,16,512]{2,1,0:T(8,128)} %copy-done) | copy-start | bytes 5603332
  60.5 5.1 %collective-permute-start.4 = (f32[3,8,512]{2,1,0:T(8,128)S(1)}, f32[3,8,512]{2,1,0:T(8,128)S(1)}, u32[]{:S(2)}, u32[]{:S(2)}) collective-permute-start(f32[3,8,512]{2,1,0:T(8,128)S(1)} %pad_maximum_fusion), channel_id=1, source_target_pairs={{0,32},{32,64},{64,96},{96,128},{128,160},{160,192},{192,224},{224... | collective-permute-start | bytes 147464 | tf_op jit(solution)/shard_map/ppermute | solution.py:473
  63.7 6.6 %collective-permute-start.5 = (f32[3,8,512]{2,1,0:T(8,128)S(1)}, f32[3,8,512]{2,1,0:T(8,128)S(1)}, u32[]{:S(2)}, u32[]{:S(2)}) collective-permute-start(f32[3,8,512]{2,1,0:T(8,128)S(1)} %pad_maximum_fusion.1), channel_id=1, source_target_pairs={{32,0},{64,32},{96,64},{128,96},{160,128},{192,160},{224,192},{256... | collective-permute-start | bytes 147464 | tf_op jit(solution)/shard_map/ppermute | solution.py:473
  70.3 9.6 %collective-permute-start.6 = (f32[22,512]{1,0:T(8,128)S(1)}, f32[22,512]{1,0:T(8,128)S(1)}, u32[]{:S(2)}, u32[]{:S(2)}) collective-permute-start(f32[22,512]{1,0:T(8,128)S(1)} %get-tuple-element.32), channel_id=1, source_target_pairs={{0,1},{1,2},{2,3},{3,4},{4,5},{5,6},{6,7},{7,8},{8,9},{9,10},{10,1... | collective-permute-start | bytes 135176 | tf_op jit(solution)/shard_map/ppermute | solution.py:473
  73.2 6.7 %collective-permute-start.7 = (f32[22,512]{1,0:T(8,128)S(1)}, f32[22,512]{1,0:T(8,128)S(1)}, u32[]{:S(2)}, u32[]{:S(2)}) collective-permute-start(f32[22,512]{1,0:T(8,128)S(1)} %get-tuple-element.33), channel_id=1, source_target_pairs={{1,0},{2,1},{3,2},{4,3},{5,4},{6,5},{7,6},{8,7},{9,8},{10,9},{11,1... | collective-permute-start | bytes 135176 | tf_op jit(solution)/shard_map/ppermute | solution.py:473
  80.0 28.2 %copy-start.7 = (f32[4,8,512]{2,1,0:T(8,128)S(1)}, f32[4,8,512]{2,1,0:T(8,128)}, u32[]{:S(2)}) copy-start(f32[4,8,512]{2,1,0:T(8,128)} %lag.1) | copy-start | bytes 196612
  80.0 30.0 %copy-start.3 = (f32[12,16,512]{2,1,0:T(8,128)S(1)}, f32[12,16,512]{2,1,0:T(8,128)}, u32[]{:S(2)}) copy-start(f32[12,16,512]{2,1,0:T(8,128)} %gates.3) | copy-start | bytes 1179652
  82.6 27.4 %all-to-all-start.2 = ((f32[32,16,128]{2,1,0:T(8,128)}), f32[32,16,128]{2,1,0:T(8,128)S(1)}, u32[]{:S(2)}, u32[]{:S(2)}) async-start(f32[32,16,128]{2,1,0:T(8,128)} %get-tuple-element.36), calls=%async_computation.2 | async-start | bytes 524288 | tf_op jit(solution)/shard_map/all_to_all | solution.py:477
  90.2 17.9 %collective-permute-start.9 = (f32[1,8,512]{2,1,0:T(8,128)S(1)}, f32[1,8,512]{2,1,0:T(8,128)S(1)}, u32[]{:S(2)}, u32[]{:S(2)}) collective-permute-start(f32[1,8,512]{2,1,0:T(8,128)S(1)} %get-tuple-element.41), channel_id=1, source_target_pairs={{32,0},{64,32},{96,64},{128,96},{160,128},{192,160},{224,192},{256... | collective-permute-start | bytes 49160 | tf_op jit(solution)/shard_map/ppermute | solution.py:473
  92.2 16.0 %collective-permute-start.8 = (f32[1,8,512]{2,1,0:T(8,128)S(1)}, f32[1,8,512]{2,1,0:T(8,128)S(1)}, u32[]{:S(2)}, u32[]{:S(2)}) collective-permute-start(f32[1,8,512]{2,1,0:T(8,128)S(1)} %get-tuple-element.42), channel_id=1, source_target_pairs={{0,32},{32,64},{64,96},{96,128},{128,160},{160,192},{192,224},{224... | collective-permute-start | bytes 49160 | tf_op jit(solution)/shard_map/ppermute | solution.py:473
  97.0 6.5 %collective-permute-start.11 = (f32[4,1,512]{2,1,0:T(1,128)S(1)}, f32[4,1,512]{2,1,0:T(1,128)S(1)}, u32[]{:S(2)}, u32[]{:S(2)}) collective-permute-start(f32[4,1,512]{2,1,0:T(1,128)S(1)} %get-tuple-element.39), channel_id=1, source_target_pairs={{1,0},{2,1},{3,2},{4,3},{5,4},{6,5},{7,6},{8,7},{9,8},{10,9},{11,1... | collective-permute-start | bytes 24584 | tf_op jit(solution)/shard_map/ppermute | solution.py:473
  101.6 6.5 %collective-permute-start.10 = (f32[4,1,512]{2,1,0:T(1,128)S(1)}, f32[4,1,512]{2,1,0:T(1,128)S(1)}, u32[]{:S(2)}, u32[]{:S(2)}) collective-permute-start(f32[4,1,512]{2,1,0:T(1,128)S(1)} %get-tuple-element.40), channel_id=1, source_target_pairs={{0,1},{1,2},{2,3},{3,4},{4,5},{5,6},{6,7},{7,8},{8,9},{9,10},{10,1... | collective-permute-start | bytes 24584 | tf_op jit(solution)/shard_map/ppermute | solution.py:473

commit v7 on v6

--- a/solution.py
+++ b/solution.py
@@ -158,10 +158,15 @@
                 out_ref[pl.ds(k * GATES * CHUNKS + g * CHUNKS + c, 8, stride=GATES * CHUNKS), :] = gates[g, k : k + 8, chunk(c)]
 
 
-def pack_body(slots, arrived, by_row, out_ref):
+def pack_body(slots, arrived, by_row, out_ref, sems):
+    copies = []
     for d in range(slots):
         k = jnp.maximum(arrived[d, 0, 0], 0)
-        out_ref[d] = by_row[pl.ds(pl.multiple_of(k * GATES * CHUNKS, 8), GATES * CHUNKS), :]
+        rows = pl.ds(pl.multiple_of(k * GATES * CHUNKS, 8), GATES * CHUNKS)
+        copies.append(pltpu.make_async_copy(by_row.at[rows, :], out_ref.at[d], sems.at[d]))
+        copies[-1].start()
+    for copy in copies:
+        copy.wait()
 
 
 def up_j(x):
@@ -504,19 +509,20 @@
         [jax.ShapeDtypeStruct(slip, jnp.int32)],
         [SM],
         [pltpu.VMEM((slots + 1, 1, LANES), jnp.int32)],
+        limit=62,
     )(worker)
     arrived = swap_blocks(claims)
 
     rim = (6, CY, CZ)
     side = (2 * CX + 2 + 4 * NI, CZ)
     up, down, right, left = kernel_call(
-        start_body, [rim, rim, side, side], [HB] * 4, [block, block, whole_i, whole_i, dma(4)], limit=62
+        start_body, [rim, rim, side, side], [HB] * 4, [block, block, whole_i, whole_i, dma(4)]
     )(voltage, voltage_lag, tissue, fiber)
     low, high = shift_pair("slab", up, down)
     (by_row,) = kernel_call(by_row_body, [(CAP * GATES * CHUNKS, LANES)], [VM])(gates)
 
     run = (slots, GATES * CHUNKS, LANES)
-    (leaving,) = kernel_call(functools.partial(pack_body, slots), [run], [SM, VM])(arrived, by_row)
+    (leaving,) = kernel_call(functools.partial(pack_body, slots), [run], [SM, VM], [dma(slots)], specs=[HB])(arrived, by_row)
     coming = swap_blocks(leaving)
 
     up, down = kernel_call(columns_body, [side, side], [VM] * 4)(right, left, low, high)
@@ -554,8 +560,8 @@
     )(worker, par, voltage, flags, faces, v1, current, low, high, left, right, parts)
     returned = swap_blocks(used)
 
+    left, right = shift_pair("blk", ours[:, -1:], ours[:, :1])
     below, above = shift_pair("slab", ours[-1:], ours[:1])
-    left, right = shift_pair("blk", ours[:, -1:], ours[:, :1])
 
     (charge,) = kernel_call(charge_body, [(3, *block)], [VM] * 8)(
         ours, below, above, left, right, voltage_lag, tissue, lag_rim

time: 113 us -> 109 us (0.965)
  local copies, waits for them, and re-layouts: 4.94 us -> 1.8 us
    unnamed x36 -> x30, local copies, waits for them, and re-layouts: 4.82 us -> 1.68 us
    pallas_call x1, Pallas kernels: 1.72 us -> 0.43 us  [on_device(): kernel_call(start_body, [rim, rim, side, side], [HB] * 4, [block, block,...]
  transfers between devices with their start and end apart: 15 -> 15, of which waited for: 5 -> 5; matrix products, arithmetic and copies ran while one was open for 0% -> 0% of each run, Pallas kernels for 7% -> 6%
where the time goes in v7:
time: 109 us; the launch traced here: 108 us
  starting transfers between devices  66.1 us (61%)
  waiting for transfers between devices  22 us (20%)
  Pallas kernels  17.4 us (16%)
  local copies, waits for them, and re-layouts  1.8 us (2%)
    ppermute x6, starting transfers between devices, shift_pair(): lax.ppermute(last, axis, up)  24.2 us
    all_to_all x3, starting transfers between devices, swap_blocks(): return lax.all_to_all(x, 'blk', split_axis=0, concat_axis=0, tiled=True)  22.7 us
    ppermute x6, starting transfers between devices, shift_pair(): lax.ppermute(first, axis, [(b, a) for a, b in up])  19.2 us
    ppermute x6, waiting for transfers between devices, shift_pair(): lax.ppermute(first, axis, [(b, a) for a, b in up])  11.6 us
    all_to_all x3, waiting for transfers between devices, swap_blocks(): return lax.all_to_all(x, 'blk', split_axis=0, concat_axis=0, tiled=True)  5.78 us
    ppermute x6, waiting for transfers between devices, shift_pair(): lax.ppermute(last, axis, up)  4.58 us
    pallas_call x1, Pallas kernels, on_device(): kernel_call(faces_body, [sheets, jax.ShapeDtypeStruct(wide, jnp.bfloat16)...  2.96 us
    pallas_call x1, Pallas kernels, on_device(): kernel_call(functools.partial(last_body, slots), [gates.shape], [SM, SM,...  2.63 us
  transfers between devices with their start and end apart: 15, of which 5 were waited for; matrix products, arithmetic and copies ran while one was open for 0% of the time, Pallas kernels for 6%

profile of v7, /device:TPU:199, one launch (start us, length us, event | category | flops | bytes accessed | tf_op | source)
XLA Modules:
  0.0 108.4 jit_solution(2459515248071639796)
XLA Ops:
  0.6 1.4 %shard_map.142 = s32[32,1,128]{2,1,0:T(1,128)} custom-call(s32[4,8]{1,0:T(4,128)} %worker.5), custom_call_target="tpu_custom_call" | custom-call | flops 1000000 | bytes 1000000 | tf_op jit(solution)/shard_map/pallas_call | solution.py:507
  2.1 9.7 %all-to-all-start = ((s32[32,1,128]{2,1,0:T(1,128)}), s32[32,1,128]{2,1,0:T(1,128)S(1)}, u32[]{:S(2)}, u32[]{:S(2)}) async-start(s32[32,1,128]{2,1,0:T(1,128)} %shard_map.142), calls=%async_computation | async-start | bytes 32768 | tf_op jit(solution)/shard_map/all_to_all | solution.py:482
  11.7 0.0 copy-start
  11.7 1.0 copy-done
  12.7 0.1 shard_map.143.by_row
  12.9 0.0 copy-start.9
  12.9 0.0 copy-start.10
  12.9 0.0 copy-start.11
  12.9 0.0 copy-start.12
  12.9 0.0 copy-start.13
  12.9 0.0 copy-start.14
  12.9 0.0 copy-start.8
  12.9 5.8 %all-to-all-done.arrived = s32[32,1,128]{2,1,0:T(1,128)S(1)} async-done(((s32[32,1,128]{2,1,0:T(1,128)}), s32[32,1,128]{2,1,0:T(1,128)S(1)}, u32[]{:S(2)}, u32[]{:S(2)}) %all-to-all-start) | async-done | bytes 16416 | tf_op jit(solution)/shard_map/all_to_all | solution.py:482
  18.7 2.0 %shard_map.144 = f32[32,48,128]{2,1,0:T(8,128)} custom-call(s32[32,1,128]{2,1,0:T(1,128)S(1)} %all-to-all-done.arrived, f32[768,128]{1,0:T(8,128)S(1)} %shard_map.143.by_row), custom_call_target="tpu_custom_call" | custom-call | flops 1000000 | bytes 1000000 | tf_op jit(solution)/shard_map/pallas_call | solution.py:525
  20.7 5.5 %all-to-all-start.1 = ((f32[32,48,128]{2,1,0:T(8,128)}), f32[32,48,128]{2,1,0:T(8,128)S(1)}, u32[]{:S(2)}, u32[]{:S(2)}) async-start(f32[32,48,128]{2,1,0:T(8,128)} %shard_map.144), calls=%async_computation.1 | async-start | bytes 1572864 | tf_op jit(solution)/shard_map/all_to_all | solution.py:482
  26.3 0.4 shard_map.139
  26.7 7.5 %collective-permute-start = (f32[6,8,512]{2,1,0:T(8,128)S(1)}, f32[6,8,512]{2,1,0:T(8,128)S(1)}, u32[]{:S(2)}, u32[]{:S(2)}) collective-permute-start(f32[6,8,512]{2,1,0:T(8,128)S(1)} %get-tuple-element.21), channel_id=1, source_target_pairs={{0,32},{32,64},{64,96},{96,128},{128,160},{160,192},{192,224},{224... | collective-permute-start | bytes 294920 | tf_op jit(solution)/shard_map/ppermute | solution.py:478
  34.2 1.9 %collective-permute-start.1 = (f32[6,8,512]{2,1,0:T(8,128)S(1)}, f32[6,8,512]{2,1,0:T(8,128)S(1)}, u32[]{:S(2)}, u32[]{:S(2)}) collective-permute-start(f32[6,8,512]{2,1,0:T(8,128)S(1)} %get-tuple-element.22), channel_id=1, source_target_pairs={{32,0},{64,32},{96,64},{128,96},{160,128},{192,160},{224,192},{256... | collective-permute-start | bytes 294920 | tf_op jit(solution)/shard_map/ppermute | solution.py:478
  36.2 5.5 %collective-permute-done.1.high = f32[6,8,512]{2,1,0:T(8,128)S(1)} collective-permute-done((f32[6,8,512]{2,1,0:T(8,128)S(1)}, f32[6,8,512]{2,1,0:T(8,128)S(1)}, u32[]{:S(2)}, u32[]{:S(2)}) %collective-permute-start.1) | collective-permute-done | bytes 98336 | tf_op jit(solution)/shard_map/ppermute | solution.py:478
  41.7 3.1 %collective-permute-start.2 = (f32[42,512]{1,0:T(8,128)S(1)}, f32[42,512]{1,0:T(8,128)S(1)}, u32[]{:S(2)}, u32[]{:S(2)}) collective-permute-start(f32[42,512]{1,0:T(8,128)S(1)} %get-tuple-element.25), channel_id=1, source_target_pairs={{0,1},{1,2},{2,3},{3,4},{4,5},{5,6},{6,7},{7,8},{8,9},{9,10},{10,1... | collective-permute-start | bytes 258056 | tf_op jit(solution)/shard_map/ppermute | solution.py:478
  44.8 4.3 %collective-permute-start.3 = (f32[42,512]{1,0:T(8,128)S(1)}, f32[42,512]{1,0:T(8,128)S(1)}, u32[]{:S(2)}, u32[]{:S(2)}) collective-permute-start(f32[42,512]{1,0:T(8,128)S(1)} %get-tuple-element.26), channel_id=1, source_target_pairs={{1,0},{2,1},{3,2},{4,3},{5,4},{6,5},{7,6},{8,7},{9,8},{10,9},{11,1... | collective-permute-start | bytes 258056 | tf_op jit(solution)/shard_map/ppermute | solution.py:478
  49.2 0.1 concatenate.9
  49.3 0.0 collective-permute-done.2.left
  49.3 1.4 %collective-permute-done.3.right = f32[42,512]{1,0:T(8,128)S(1)} collective-permute-done((f32[42,512]{1,0:T(8,128)S(1)}, f32[42,512]{1,0:T(8,128)S(1)}, u32[]{:S(2)}, u32[]{:S(2)}) %collective-permute-start.3) | collective-permute-done | bytes 86048 | tf_op jit(solution)/shard_map/ppermute | solution.py:478
  50.7 3.0 %shard_map.141 = (f32[57,16,512]{2,1,0:T(8,128)S(1)}, bf16[8,16,512]{2,1,0:T(8,128)(2,1)S(1)}, f32[4,8,512]{2,1,0:T(8,128)S(1)}, f32[24,512]{1,0:T(8,128)S(1)}) custom-call(f32[256]{0:T(256)S(1)} %pad.4.par, f32[4,8,512]{2,1,0:T(8,128)S(1)} %copy-done.2, s32[4,8,512]{2,1,0:T(8,128)S(1)} %copy-done.3, s32[4,8,512]{2,1,0:T(8,128)S(1)} %copy-done.4, ...), custom_call_target="tpu_custom_call" | custom-call | flops 1000000 | bytes 1000000 | tf_op jit(solution)/shard_map/pallas_call | solution.py:533
  53.7 0.0 copy-start.6
  53.7 0.6 copy-done.6
  54.3 0.0 all-to-all-done.1.coming
  54.3 1.9 %shard_map.145 = (f32[4,8,512]{2,1,0:T(8,128)S(1)}, f32[4,8,512]{2,1,0:T(8,128)S(1)}, f32[12,128,128]{2,1,0:T(8,128)S(1)}) custom-call(s32[4,8]{1,0:T(4,128)S(1)} %copy-done.8, f32[256]{0:T(256)S(1)} %pad.4.par, f32[4,8,512]{2,1,0:T(8,128)S(1)} %copy-done.2, f32[4,8,512]{2,1,0:T(8,128)S(1)} %get-tuple-element.29.base, ...), custom_call_target="tpu_custom_call" | custom-call | flops 1000000 | bytes 1000000 | tf_op jit(solution)/shard_map/pallas_call | solution.py:542
  56.3 4.0 %collective-permute-start.4 = (f32[3,8,512]{2,1,0:T(8,128)S(1)}, f32[3,8,512]{2,1,0:T(8,128)S(1)}, u32[]{:S(2)}, u32[]{:S(2)}) collective-permute-start(f32[3,8,512]{2,1,0:T(8,128)S(1)} %pad_maximum_fusion), channel_id=1, source_target_pairs={{0,32},{32,64},{64,96},{96,128},{128,160},{160,192},{192,224},{224... | collective-permute-start | bytes 147464 | tf_op jit(solution)/shard_map/ppermute | solution.py:478
  60.3 1.9 %collective-permute-start.5 = (f32[3,8,512]{2,1,0:T(8,128)S(1)}, f32[3,8,512]{2,1,0:T(8,128)S(1)}, u32[]{:S(2)}, u32[]{:S(2)}) collective-permute-start(f32[3,8,512]{2,1,0:T(8,128)S(1)} %pad_maximum_fusion.1), channel_id=1, source_target_pairs={{32,0},{64,32},{96,64},{128,96},{160,128},{192,160},{224,192},{256... | collective-permute-start | bytes 147464 | tf_op jit(solution)/shard_map/ppermute | solution.py:478
  62.2 0.0 collective-permute-done.4.low
  62.2 4.7 %collective-permute-done.5.high = f32[3,8,512]{2,1,0:T(8,128)S(1)} collective-permute-done((f32[3,8,512]{2,1,0:T(8,128)S(1)}, f32[3,8,512]{2,1,0:T(8,128)S(1)}, u32[]{:S(2)}, u32[]{:S(2)}) %collective-permute-start.5) | collective-permute-done | bytes 49184 | tf_op jit(solution)/shard_map/ppermute | solution.py:478
  67.0 2.8 %collective-permute-start.6 = (f32[22,512]{1,0:T(8,128)S(1)}, f32[22,512]{1,0:T(8,128)S(1)}, u32[]{:S(2)}, u32[]{:S(2)}) collective-permute-start(f32[22,512]{1,0:T(8,128)S(1)} %get-tuple-element.32), channel_id=1, source_target_pairs={{0,1},{1,2},{2,3},{3,4},{4,5},{5,6},{6,7},{7,8},{8,9},{9,10},{10,1... | collective-permute-start | bytes 135176 | tf_op jit(solution)/shard_map/ppermute | solution.py:478
  69.8 4.6 %collective-permute-start.7 = (f32[22,512]{1,0:T(8,128)S(1)}, f32[22,512]{1,0:T(8,128)S(1)}, u32[]{:S(2)}, u32[]{:S(2)}) collective-permute-start(f32[22,512]{1,0:T(8,128)S(1)} %get-tuple-element.33), channel_id=1, source_target_pairs={{1,0},{2,1},{3,2},{4,3},{5,4},{6,5},{7,6},{8,7},{9,8},{10,9},{11,1... | collective-permute-start | bytes 135176 | tf_op jit(solution)/shard_map/ppermute | solution.py:478
  74.4 1.5 %shard_map.147.parts = f32[4,4,8,512]{3,2,1,0:T(8,128)S(1)} custom-call(f32[256]{0:T(256)S(1)} %pad.4.par, f32[12,128,128]{2,1,0:T(8,128)S(1)} %get-tuple-element.34.states_in, f32[4,8,512]{2,1,0:T(8,128)S(1)} %get-tuple-element.30.v1), custom_call_target="tpu_custom_call" | custom-call | flops 1000000 | bytes 1000000 | tf_op jit(solution)/shard_map/pallas_call | solution.py:549
  75.8 0.0 copy-start.7
  75.8 0.0 collective-permute-done.6.left
  75.9 0.0 copy-start.1
  75.9 2.6 %shard_map.148 = (f32[4,8,512]{2,1,0:T(8,128)}, f32[4,8,512]{2,1,0:T(8,128)S(1)}, f32[32,16,128]{2,1,0:T(8,128)}) custom-call(s32[4,8]{1,0:T(4,128)S(1)} %copy-done.8, f32[256]{0:T(256)S(1)} %pad.4.par, f32[4,8,512]{2,1,0:T(8,128)S(1)} %copy-done.2, bf16[8,16,512]{2,1,0:T(8,128)(2,1)S(1)} %get-tuple-element.27.flags, ...), custom_call_target="tpu_custom_call" | custom-call | flops 1000000 | bytes 1000000 | tf_op jit(solution)/shard_map/pallas_call | solution.py:554
  78.4 7.5 %all-to-all-start.2 = ((f32[32,16,128]{2,1,0:T(8,128)}), f32[32,16,128]{2,1,0:T(8,128)S(1)}, u32[]{:S(2)}, u32[]{:S(2)}) async-start(f32[32,16,128]{2,1,0:T(8,128)} %get-tuple-element.36), calls=%async_computation.2 | async-start | bytes 524288 | tf_op jit(solution)/shard_map/all_to_all | solution.py:482
  86.0 1.9 %collective-permute-start.9 = (f32[1,8,512]{2,1,0:T(8,128)S(1)}, f32[1,8,512]{2,1,0:T(8,128)S(1)}, u32[]{:S(2)}, u32[]{:S(2)}) collective-permute-start(f32[1,8,512]{2,1,0:T(8,128)S(1)} %get-tuple-element.41), channel_id=1, source_target_pairs={{32,0},{64,32},{96,64},{128,96},{160,128},{192,160},{224,192},{256... | collective-permute-start | bytes 49160 | tf_op jit(solution)/shard_map/ppermute | solution.py:478
  87.9 4.9 %collective-permute-start.8 = (f32[1,8,512]{2,1,0:T(8,128)S(1)}, f32[1,8,512]{2,1,0:T(8,128)S(1)}, u32[]{:S(2)}, u32[]{:S(2)}) collective-permute-start(f32[1,8,512]{2,1,0:T(8,128)S(1)} %get-tuple-element.42), channel_id=1, source_target_pairs={{0,32},{32,64},{64,96},{96,128},{128,160},{160,192},{192,224},{224... | collective-permute-start | bytes 49160 | tf_op jit(solution)/shard_map/ppermute | solution.py:478
  92.8 4.6 %collective-permute-start.11 = (f32[4,1,512]{2,1,0:T(1,128)S(1)}, f32[4,1,512]{2,1,0:T(1,128)S(1)}, u32[]{:S(2)}, u32[]{:S(2)}) collective-permute-start(f32[4,1,512]{2,1,0:T(1,128)S(1)} %get-tuple-element.39), channel_id=1, source_target_pairs={{1,0},{2,1},{3,2},{4,3},{5,4},{6,5},{7,6},{8,7},{9,8},{10,9},{11,1... | collective-permute-start | bytes 24584 | tf_op jit(solution)/shard_map/ppermute | solution.py:478
  97.4 1.9 %collective-permute-start.10 = (f32[4,1,512]{2,1,0:T(1,128)S(1)}, f32[4,1,512]{2,1,0:T(1,128)S(1)}, u32[]{:S(2)}, u32[]{:S(2)}) collective-permute-start(f32[4,1,512]{2,1,0:T(1,128)S(1)} %get-tuple-element.40), channel_id=1, source_target_pairs={{0,1},{1,2},{2,3},{3,4},{4,5},{5,6},{6,7},{7,8},{8,9},{9,10},{10,1... | collective-permute-start | bytes 24584 | tf_op jit(solution)/shard_map/ppermute | solution.py:478
  99.3 4.6 %collective-permute-done.10.left = f32[4,1,512]{2,1,0:T(1,128)S(1)} collective-permute-done((f32[4,1,512]{2,1,0:T(1,128)S(1)}, f32[4,1,512]{2,1,0:T(1,128)S(1)}, u32[]{:S(2)}, u32[]{:S(2)}) %collective-permute-start.10) | collective-permute-done | bytes 8224 | tf_op jit(solution)/shard_map/ppermute | solution.py:478
  103.9 1.9 %shard_map.150 = f32[3,4,8,512]{3,2,1,0:T(8,128)} custom-call(f32[4,8,512]{2,1,0:T(8,128)S(1)} %get-tuple-element.37.ours, f32[1,8,512]{2,1,0:T(8,128)S(1)} %collective-permute-done.8.below, f32[1,8,512]{2,1,0:T(8,128)S(1)} %collective-permute-done.9.above, f32[4,1,512]{2,1,0:T(1,128)S(1)} %collective-permute-done.10.left, ...), custom_call_target="tpu_custom_call" | custom-call | flops 1000000 | bytes 1000000 | tf_op jit(solution)/shard_map/pallas_call | solution.py:566
  105.8 2.6 %shard_map.149 = f32[12,16,512]{2,1,0:T(8,128)} custom-call(s32[32,1,128]{2,1,0:T(1,128)S(1)} %all-to-all-done.arrived, f32[256]{0:T(256)S(1)} %pad.4.par, f32[32,16,128]{2,1,0:T(8,128)S(1)} %all-to-all-done.2.returned, f32[12,16,512]{2,1,0:T(8,128)S(1)} %copy-done.1), custom_call_target="tpu_custom_call" | custom-call | flops 1000000 | bytes 1000000 | tf_op jit(solution)/shard_map/pallas_call | solution.py:570
  (33 shorter events, 0.2 us)
Async XLA Ops:
  2.1 16.7 %all-to-all-start = ((s32[32,1,128]{2,1,0:T(1,128)}), s32[32,1,128]{2,1,0:T(1,128)S(1)}, u32[]{:S(2)}, u32[]{:S(2)}) async-start(s32[32,1,128]{2,1,0:T(1,128)} %shard_map.142), calls=%async_computation | async-start | bytes 32768 | tf_op jit(solution)/shard_map/all_to_all | solution.py:482
  11.7 1.0 copy-start
  12.7 13.5 %copy-start.2 = (f32[4,8,512]{2,1,0:T(8,128)S(1)}, f32[4,8,512]{2,1,0:T(8,128)}, u32[]{:S(2)}) copy-start(f32[4,8,512]{2,1,0:T(8,128)} %v0.1) | copy-start | bytes 196612
  12.7 13.5 %copy-start.3 = (s32[4,8,512]{2,1,0:T(8,128)S(1)}, s32[4,8,512]{2,1,0:T(8,128)}, u32[]{:S(2)}) copy-start(s32[4,8,512]{2,1,0:T(8,128)} %tissue.3) | copy-start | bytes 196612
  12.7 13.5 %copy-start.4 = (s32[4,8,512]{2,1,0:T(8,128)S(1)}, s32[4,8,512]{2,1,0:T(8,128)}, u32[]{:S(2)}) copy-start(s32[4,8,512]{2,1,0:T(8,128)} %fiber.1) | copy-start | bytes 196612
  12.7 13.6 %copy-start.5 = (f32[4,8,512]{2,1,0:T(8,128)S(1)}, f32[4,8,512]{2,1,0:T(8,128)}, u32[]{:S(2)}) copy-start(f32[4,8,512]{2,1,0:T(8,128)} %lag.1) | copy-start | bytes 196612
  12.9 36.3 %copy-start.9 = (f32[6,16]{1,0:T(8,128)S(1)}, f32[6,16]{1,0:T(8,128)}, u32[]{:S(2)}) copy-start(f32[6,16]{1,0:T(8,128)} %param.16) | copy-start | bytes 1156
  12.9 36.3 %copy-start.10 = (f32[12]{0:T(128)S(1)}, f32[12]{0:T(128)}, u32[]{:S(2)}) copy-start(f32[12]{0:T(128)} %param.19) | copy-start | bytes 148
  12.9 36.3 %copy-start.11 = (f32[12]{0:T(128)S(1)}, f32[12]{0:T(128)}, u32[]{:S(2)}) copy-start(f32[12]{0:T(128)} %param.20) | copy-start | bytes 148
  12.9 36.3 %copy-start.12 = (f32[12]{0:T(128)S(1)}, f32[12]{0:T(128)}, u32[]{:S(2)}) copy-start(f32[12]{0:T(128)} %param.21) | copy-start | bytes 148
  12.9 36.3 %copy-start.13 = (f32[12]{0:T(128)S(1)}, f32[12]{0:T(128)}, u32[]{:S(2)}) copy-start(f32[12]{0:T(128)} %param.22) | copy-start | bytes 148
  12.9 36.3 %copy-start.14 = (f32[6]{0:T(128)S(1)}, f32[6]{0:T(128)}, u32[]{:S(2)}) copy-start(f32[6]{0:T(128)} %param.23) | copy-start | bytes 76
  12.9 41.4 %copy-start.8 = (s32[4,8]{1,0:T(4,128)S(1)}, s32[4,8]{1,0:T(4,128)}, u32[]{:S(2)}) copy-start(s32[4,8]{1,0:T(4,128)} %worker.5) | copy-start | bytes 388
  20.7 33.6 %all-to-all-start.1 = ((f32[32,48,128]{2,1,0:T(8,128)}), f32[32,48,128]{2,1,0:T(8,128)S(1)}, u32[]{:S(2)}, u32[]{:S(2)}) async-start(f32[32,48,128]{2,1,0:T(8,128)} %shard_map.144), calls=%async_computation.1 | async-start | bytes 1572864 | tf_op jit(solution)/shard_map/all_to_all | solution.py:482
  26.7 9.4 %collective-permute-start = (f32[6,8,512]{2,1,0:T(8,128)S(1)}, f32[6,8,512]{2,1,0:T(8,128)S(1)}, u32[]{:S(2)}, u32[]{:S(2)}) collective-permute-start(f32[6,8,512]{2,1,0:T(8,128)S(1)} %get-tuple-element.21), channel_id=1, source_target_pairs={{0,32},{32,64},{64,96},{96,128},{128,160},{160,192},{192,224},{224... | collective-permute-start | bytes 294920 | tf_op jit(solution)/shard_map/ppermute | solution.py:478
  34.2 7.4 %collective-permute-start.1 = (f32[6,8,512]{2,1,0:T(8,128)S(1)}, f32[6,8,512]{2,1,0:T(8,128)S(1)}, u32[]{:S(2)}, u32[]{:S(2)}) collective-permute-start(f32[6,8,512]{2,1,0:T(8,128)S(1)} %get-tuple-element.22), channel_id=1, source_target_pairs={{32,0},{64,32},{96,64},{128,96},{160,128},{192,160},{224,192},{256... | collective-permute-start | bytes 294920 | tf_op jit(solution)/shard_map/ppermute | solution.py:478
  41.7 7.6 %collective-permute-start.2 = (f32[42,512]{1,0:T(8,128)S(1)}, f32[42,512]{1,0:T(8,128)S(1)}, u32[]{:S(2)}, u32[]{:S(2)}) collective-permute-start(f32[42,512]{1,0:T(8,128)S(1)} %get-tuple-element.25), channel_id=1, source_target_pairs={{0,1},{1,2},{2,3},{3,4},{4,5},{5,6},{6,7},{7,8},{8,9},{9,10},{10,1... | collective-permute-start | bytes 258056 | tf_op jit(solution)/shard_map/ppermute | solution.py:478
  44.8 5.9 %collective-permute-start.3 = (f32[42,512]{1,0:T(8,128)S(1)}, f32[42,512]{1,0:T(8,128)S(1)}, u32[]{:S(2)}, u32[]{:S(2)}) collective-permute-start(f32[42,512]{1,0:T(8,128)S(1)} %get-tuple-element.26), channel_id=1, source_target_pairs={{1,0},{2,1},{3,2},{4,3},{5,4},{6,5},{7,6},{8,7},{9,8},{10,9},{11,1... | collective-permute-start | bytes 258056 | tf_op jit(solution)/shard_map/ppermute | solution.py:478
  53.7 0.6 copy-start.6
  56.3 6.0 %collective-permute-start.4 = (f32[3,8,512]{2,1,0:T(8,128)S(1)}, f32[3,8,512]{2,1,0:T(8,128)S(1)}, u32[]{:S(2)}, u32[]{:S(2)}) collective-permute-start(f32[3,8,512]{2,1,0:T(8,128)S(1)} %pad_maximum_fusion), channel_id=1, source_target_pairs={{0,32},{32,64},{64,96},{96,128},{128,160},{160,192},{192,224},{224... | collective-permute-start | bytes 147464 | tf_op jit(solution)/shard_map/ppermute | solution.py:478
  60.3 6.6 %collective-permute-start.5 = (f32[3,8,512]{2,1,0:T(8,128)S(1)}, f32[3,8,512]{2,1,0:T(8,128)S(1)}, u32[]{:S(2)}, u32[]{:S(2)}) collective-permute-start(f32[3,8,512]{2,1,0:T(8,128)S(1)} %pad_maximum_fusion.1), channel_id=1, source_target_pairs={{32,0},{64,32},{96,64},{128,96},{160,128},{192,160},{224,192},{256... | collective-permute-start | bytes 147464 | tf_op jit(solution)/shard_map/ppermute | solution.py:478
  67.0 8.9 %collective-permute-start.6 = (f32[22,512]{1,0:T(8,128)S(1)}, f32[22,512]{1,0:T(8,128)S(1)}, u32[]{:S(2)}, u32[]{:S(2)}) collective-permute-start(f32[22,512]{1,0:T(8,128)S(1)} %get-tuple-element.32), channel_id=1, source_target_pairs={{0,1},{1,2},{2,3},{3,4},{4,5},{5,6},{6,7},{7,8},{8,9},{9,10},{10,1... | collective-permute-start | bytes 135176 | tf_op jit(solution)/shard_map/ppermute | solution.py:478
  69.8 6.1 %collective-permute-start.7 = (f32[22,512]{1,0:T(8,128)S(1)}, f32[22,512]{1,0:T(8,128)S(1)}, u32[]{:S(2)}, u32[]{:S(2)}) collective-permute-start(f32[22,512]{1,0:T(8,128)S(1)} %get-tuple-element.33), channel_id=1, source_target_pairs={{1,0},{2,1},{3,2},{4,3},{5,4},{6,5},{7,6},{8,7},{9,8},{10,9},{11,1... | collective-permute-start | bytes 135176 | tf_op jit(solution)/shard_map/ppermute | solution.py:478
  75.8 28.1 %copy-start.7 = (f32[24,512]{1,0:T(8,128)S(1)}, f32[24,512]{1,0:T(8,128)}, u32[]{:S(2)}) copy-start(f32[24,512]{1,0:T(8,128)} %copy-done.6) | copy-start | bytes 147460
  75.9 29.9 %copy-start.1 = (f32[12,16,512]{2,1,0:T(8,128)S(1)}, f32[12,16,512]{2,1,0:T(8,128)}, u32[]{:S(2)}) copy-start(f32[12,16,512]{2,1,0:T(8,128)} %gates.3) | copy-start | bytes 1179652
  78.4 27.4 %all-to-all-start.2 = ((f32[32,16,128]{2,1,0:T(8,128)}), f32[32,16,128]{2,1,0:T(8,128)S(1)}, u32[]{:S(2)}, u32[]{:S(2)}) async-start(f32[32,16,128]{2,1,0:T(8,128)} %get-tuple-element.36), calls=%async_computation.2 | async-start | bytes 524288 | tf_op jit(solution)/shard_map/all_to_all | solution.py:482
  86.0 17.9 %collective-permute-start.9 = (f32[1,8,512]{2,1,0:T(8,128)S(1)}, f32[1,8,512]{2,1,0:T(8,128)S(1)}, u32[]{:S(2)}, u32[]{:S(2)}) collective-permute-start(f32[1,8,512]{2,1,0:T(8,128)S(1)} %get-tuple-element.41), channel_id=1, source_target_pairs={{32,0},{64,32},{96,64},{128,96},{160,128},{192,160},{224,192},{256... | collective-permute-start | bytes 49160 | tf_op jit(solution)/shard_map/ppermute | solution.py:478
  87.9 16.0 %collective-permute-start.8 = (f32[1,8,512]{2,1,0:T(8,128)S(1)}, f32[1,8,512]{2,1,0:T(8,128)S(1)}, u32[]{:S(2)}, u32[]{:S(2)}) collective-permute-start(f32[1,8,512]{2,1,0:T(8,128)S(1)} %get-tuple-element.42), channel_id=1, source_target_pairs={{0,32},{32,64},{64,96},{96,128},{128,160},{160,192},{192,224},{224... | collective-permute-start | bytes 49160 | tf_op jit(solution)/shard_map/ppermute | solution.py:478
  92.8 6.5 %collective-permute-start.11 = (f32[4,1,512]{2,1,0:T(1,128)S(1)}, f32[4,1,512]{2,1,0:T(1,128)S(1)}, u32[]{:S(2)}, u32[]{:S(2)}) collective-permute-start(f32[4,1,512]{2,1,0:T(1,128)S(1)} %get-tuple-element.39), channel_id=1, source_target_pairs={{1,0},{2,1},{3,2},{4,3},{5,4},{6,5},{7,6},{8,7},{9,8},{10,9},{11,1... | collective-permute-start | bytes 24584 | tf_op jit(solution)/shard_map/ppermute | solution.py:478
  97.4 6.5 %collective-permute-start.10 = (f32[4,1,512]{2,1,0:T(1,128)S(1)}, f32[4,1,512]{2,1,0:T(1,128)S(1)}, u32[]{:S(2)}, u32[]{:S(2)}) collective-permute-start(f32[4,1,512]{2,1,0:T(1,128)S(1)} %get-tuple-element.40), channel_id=1, source_target_pairs={{0,1},{1,2},{2,3},{3,4},{4,5},{5,6},{6,7},{7,8},{8,9},{9,10},{10,1... | collective-permute-start | bytes 24584 | tf_op jit(solution)/shard_map/ppermute | solution.py:478

commit v8 on v6

--- a/solution.py
+++ b/solution.py
@@ -398,7 +398,7 @@
         used_ref[d] = rows_ref[pl.ds(pl.multiple_of(tile_of[d] * 16, 16), 16), :]
 
 
-def last_body(slots, arrived, par, returned, gates, out_ref, rows_ref, seen_ref):
+def last_body(slots, arrived, par, returned, gates, gates_out, rows_ref, seen_ref, out_ref, sems):
     for d in range(slots):
         k = arrived[d, 0, 0]
         row = jnp.where(k >= 0, k, CAP)
@@ -415,9 +415,12 @@
                 for n in range(STEPS):
                     state = updated(seen_ref[n, k : k + 8, chunk(c)], state, par, g)
                 out_ref[g, k : k + 8, chunk(c)] = state
+        pltpu.make_async_copy(out_ref.at[g], gates_out.at[g], sems.at[g]).start()
         return carry
 
     lax.fori_loop(0, GATES, one, 0)
+    for g in range(GATES):
+        pltpu.make_async_copy(out_ref.at[g], gates_out.at[g], sems.at[g]).wait()
 
 
 def arctan_of(cross, den):
@@ -504,13 +507,14 @@
         [jax.ShapeDtypeStruct(slip, jnp.int32)],
         [SM],
         [pltpu.VMEM((slots + 1, 1, LANES), jnp.int32)],
+        limit=62,
     )(worker)
     arrived = swap_blocks(claims)
 
     rim = (6, CY, CZ)
     side = (2 * CX + 2 + 4 * NI, CZ)
     up, down, right, left = kernel_call(
-        start_body, [rim, rim, side, side], [HB] * 4, [block, block, whole_i, whole_i, dma(4)], limit=62
+        start_body, [rim, rim, side, side], [HB] * 4, [block, block, whole_i, whole_i, dma(4)]
     )(voltage, voltage_lag, tissue, fiber)
     low, high = shift_pair("slab", up, down)
     (by_row,) = kernel_call(by_row_body, [(CAP * GATES * CHUNKS, LANES)], [VM])(gates)
@@ -554,15 +558,15 @@
     )(worker, par, voltage, flags, faces, v1, current, low, high, left, right, parts)
     returned = swap_blocks(used)
 
+    left, right = shift_pair("blk", ours[:, -1:], ours[:, :1])
     below, above = shift_pair("slab", ours[-1:], ours[:1])
-    left, right = shift_pair("blk", ours[:, -1:], ours[:, :1])
 
     (charge,) = kernel_call(charge_body, [(3, *block)], [VM] * 8)(
         ours, below, above, left, right, voltage_lag, tissue, lag_rim
     )
 
     (gates_out,) = kernel_call(
-        functools.partial(last_body, slots), [gates.shape], [SM, SM, VM, VM], [((CAP + 1) * 16, LANES), (STEPS, CAP, CZ)]
+        functools.partial(last_body, slots), [gates.shape], [SM, SM, VM, VM], [((CAP + 1) * 16, LANES), (STEPS, CAP, CZ), gates.shape, dma(GATES)], specs=[HB]
     )(arrived, par, returned, gates)
     return (v3, gates_out, charge)
 

time: 113 us -> 109 us (0.965)
  local copies, waits for them, and re-layouts: 4.94 us -> 1.8 us
    unnamed x36 -> x30, local copies, waits for them, and re-layouts: 4.82 us -> 1.68 us
    pallas_call x1, Pallas kernels: 1.72 us -> 0.43 us  [on_device(): kernel_call(start_body, [rim, rim, side, side], [HB] * 4, [block, block,...]
  transfers between devices with their start and end apart: 15 -> 15, of which waited for: 5 -> 5; matrix products, arithmetic and copies ran while one was open for 0% -> 0% of each run, Pallas kernels for 7% -> 6%
where the time goes in v8:
time: 109 us; the launch traced here: 108 us
  starting transfers between devices  66.1 us (61%)
  waiting for transfers between devices  22 us (20%)
  Pallas kernels  17.2 us (16%)
  local copies, waits for them, and re-layouts  1.8 us (2%)
    ppermute x6, starting transfers between devices, shift_pair(): lax.ppermute(last, axis, up)  24.2 us
    all_to_all x3, starting transfers between devices, swap_blocks(): return lax.all_to_all(x, 'blk', split_axis=0, concat_axis=0, tiled=True)  22.7 us
    ppermute x6, starting transfers between devices, shift_pair(): lax.ppermute(first, axis, [(b, a) for a, b in up])  19.2 us
    ppermute x6, waiting for transfers between devices, shift_pair(): lax.ppermute(first, axis, [(b, a) for a, b in up])  11.6 us
    all_to_all x3, waiting for transfers between devices, swap_blocks(): return lax.all_to_all(x, 'blk', split_axis=0, concat_axis=0, tiled=True)  5.78 us
    ppermute x6, waiting for transfers between devices, shift_pair(): lax.ppermute(last, axis, up)  4.58 us
    pallas_call x1, Pallas kernels, on_device(): kernel_call(faces_body, [sheets, jax.ShapeDtypeStruct(wide, jnp.bfloat16)...  2.96 us
    pallas_call x1, Pallas kernels, on_device(): kernel_call(functools.partial(last_body, slots), [gates.shape], [SM, SM,...  2.61 us
  transfers between devices with their start and end apart: 15, of which 5 were waited for; matrix products, arithmetic and copies ran while one was open for 0% of the time, Pallas kernels for 6%

profile of v8, /device:TPU:199, one launch (start us, length us, event | category | flops | bytes accessed | tf_op | source)
XLA Modules:
  0.0 108.2 jit_solution(8720845857881842664)
XLA Ops:
  0.6 1.4 %shard_map.142 = s32[32,1,128]{2,1,0:T(1,128)} custom-call(s32[4,8]{1,0:T(4,128)} %worker.5), custom_call_target="tpu_custom_call" | custom-call | flops 1000000 | bytes 1000000 | tf_op jit(solution)/shard_map/pallas_call | solution.py:505
  2.1 9.7 %all-to-all-start = ((s32[32,1,128]{2,1,0:T(1,128)}), s32[32,1,128]{2,1,0:T(1,128)S(1)}, u32[]{:S(2)}, u32[]{:S(2)}) async-start(s32[32,1,128]{2,1,0:T(1,128)} %shard_map.142), calls=%async_computation | async-start | bytes 32768 | tf_op jit(solution)/shard_map/all_to_all | solution.py:480
  11.7 0.0 copy-start
  11.7 1.0 copy-done
  12.7 0.1 shard_map.143.by_row
  12.9 0.0 copy-start.9
  12.9 0.0 copy-start.10
  12.9 0.0 copy-start.11
  12.9 0.0 copy-start.12
  12.9 0.0 copy-start.13
  12.9 0.0 copy-start.14
  12.9 0.0 copy-start.8
  12.9 5.8 %all-to-all-done.arrived = s32[32,1,128]{2,1,0:T(1,128)S(1)} async-done(((s32[32,1,128]{2,1,0:T(1,128)}), s32[32,1,128]{2,1,0:T(1,128)S(1)}, u32[]{:S(2)}, u32[]{:S(2)}) %all-to-all-start) | async-done | bytes 16416 | tf_op jit(solution)/shard_map/all_to_all | solution.py:480
  18.7 1.8 %shard_map.144 = f32[32,48,128]{2,1,0:T(8,128)} custom-call(s32[32,1,128]{2,1,0:T(1,128)S(1)} %all-to-all-done.arrived, f32[768,128]{1,0:T(8,128)S(1)} %shard_map.143.by_row), custom_call_target="tpu_custom_call" | custom-call | flops 1000000 | bytes 1000000 | tf_op jit(solution)/shard_map/pallas_call | solution.py:523
  20.5 5.5 %all-to-all-start.1 = ((f32[32,48,128]{2,1,0:T(8,128)}), f32[32,48,128]{2,1,0:T(8,128)S(1)}, u32[]{:S(2)}, u32[]{:S(2)}) async-start(f32[32,48,128]{2,1,0:T(8,128)} %shard_map.144), calls=%async_computation.1 | async-start | bytes 1572864 | tf_op jit(solution)/shard_map/all_to_all | solution.py:480
  26.0 0.4 shard_map.139
  26.5 7.5 %collective-permute-start = (f32[6,8,512]{2,1,0:T(8,128)S(1)}, f32[6,8,512]{2,1,0:T(8,128)S(1)}, u32[]{:S(2)}, u32[]{:S(2)}) collective-permute-start(f32[6,8,512]{2,1,0:T(8,128)S(1)} %get-tuple-element.21), channel_id=1, source_target_pairs={{0,32},{32,64},{64,96},{96,128},{128,160},{160,192},{192,224},{224... | collective-permute-start | bytes 294920 | tf_op jit(solution)/shard_map/ppermute | solution.py:476
  34.0 1.9 %collective-permute-start.1 = (f32[6,8,512]{2,1,0:T(8,128)S(1)}, f32[6,8,512]{2,1,0:T(8,128)S(1)}, u32[]{:S(2)}, u32[]{:S(2)}) collective-permute-start(f32[6,8,512]{2,1,0:T(8,128)S(1)} %get-tuple-element.22), channel_id=1, source_target_pairs={{32,0},{64,32},{96,64},{128,96},{160,128},{192,160},{224,192},{256... | collective-permute-start | bytes 294920 | tf_op jit(solution)/shard_map/ppermute | solution.py:476
  35.9 0.0 collective-permute-done.low
  35.9 5.5 %collective-permute-done.1.high = f32[6,8,512]{2,1,0:T(8,128)S(1)} collective-permute-done((f32[6,8,512]{2,1,0:T(8,128)S(1)}, f32[6,8,512]{2,1,0:T(8,128)S(1)}, u32[]{:S(2)}, u32[]{:S(2)}) %collective-permute-start.1) | collective-permute-done | bytes 98336 | tf_op jit(solution)/shard_map/ppermute | solution.py:476
  41.4 3.1 %collective-permute-start.2 = (f32[42,512]{1,0:T(8,128)S(1)}, f32[42,512]{1,0:T(8,128)S(1)}, u32[]{:S(2)}, u32[]{:S(2)}) collective-permute-start(f32[42,512]{1,0:T(8,128)S(1)} %get-tuple-element.25), channel_id=1, source_target_pairs={{0,1},{1,2},{2,3},{3,4},{4,5},{5,6},{6,7},{7,8},{8,9},{9,10},{10,1... | collective-permute-start | bytes 258056 | tf_op jit(solution)/shard_map/ppermute | solution.py:476
  44.6 4.3 %collective-permute-start.3 = (f32[42,512]{1,0:T(8,128)S(1)}, f32[42,512]{1,0:T(8,128)S(1)}, u32[]{:S(2)}, u32[]{:S(2)}) collective-permute-start(f32[42,512]{1,0:T(8,128)S(1)} %get-tuple-element.26), channel_id=1, source_target_pairs={{1,0},{2,1},{3,2},{4,3},{5,4},{6,5},{7,6},{8,7},{9,8},{10,9},{11,1... | collective-permute-start | bytes 258056 | tf_op jit(solution)/shard_map/ppermute | solution.py:476
  48.9 0.1 concatenate.9
  49.0 0.0 collective-permute-done.2.left
  49.0 1.4 %collective-permute-done.3.right = f32[42,512]{1,0:T(8,128)S(1)} collective-permute-done((f32[42,512]{1,0:T(8,128)S(1)}, f32[42,512]{1,0:T(8,128)S(1)}, u32[]{:S(2)}, u32[]{:S(2)}) %collective-permute-start.3) | collective-permute-done | bytes 86048 | tf_op jit(solution)/shard_map/ppermute | solution.py:476
  50.5 3.0 %shard_map.141 = (f32[57,16,512]{2,1,0:T(8,128)S(1)}, bf16[8,16,512]{2,1,0:T(8,128)(2,1)S(1)}, f32[4,8,512]{2,1,0:T(8,128)S(1)}, f32[24,512]{1,0:T(8,128)S(1)}) custom-call(f32[256]{0:T(256)S(1)} %pad.4.par, f32[4,8,512]{2,1,0:T(8,128)S(1)} %copy-done.2, s32[4,8,512]{2,1,0:T(8,128)S(1)} %copy-done.3, s32[4,8,512]{2,1,0:T(8,128)S(1)} %copy-done.4, ...), custom_call_target="tpu_custom_call" | custom-call | flops 1000000 | bytes 1000000 | tf_op jit(solution)/shard_map/pallas_call | solution.py:531
  53.4 0.0 copy-start.6
  53.5 0.6 copy-done.6
  54.1 0.0 all-to-all-done.1.coming
  54.1 1.9 %shard_map.145 = (f32[4,8,512]{2,1,0:T(8,128)S(1)}, f32[4,8,512]{2,1,0:T(8,128)S(1)}, f32[12,128,128]{2,1,0:T(8,128)S(1)}) custom-call(s32[4,8]{1,0:T(4,128)S(1)} %copy-done.8, f32[256]{0:T(256)S(1)} %pad.4.par, f32[4,8,512]{2,1,0:T(8,128)S(1)} %copy-done.2, f32[4,8,512]{2,1,0:T(8,128)S(1)} %get-tuple-element.29.base, ...), custom_call_target="tpu_custom_call" | custom-call | flops 1000000 | bytes 1000000 | tf_op jit(solution)/shard_map/pallas_call | solution.py:540
  56.0 4.0 %collective-permute-start.4 = (f32[3,8,512]{2,1,0:T(8,128)S(1)}, f32[3,8,512]{2,1,0:T(8,128)S(1)}, u32[]{:S(2)}, u32[]{:S(2)}) collective-permute-start(f32[3,8,512]{2,1,0:T(8,128)S(1)} %pad_maximum_fusion), channel_id=1, source_target_pairs={{0,32},{32,64},{64,96},{96,128},{128,160},{160,192},{192,224},{224... | collective-permute-start | bytes 147464 | tf_op jit(solution)/shard_map/ppermute | solution.py:476
  60.1 1.9 %collective-permute-start.5 = (f32[3,8,512]{2,1,0:T(8,128)S(1)}, f32[3,8,512]{2,1,0:T(8,128)S(1)}, u32[]{:S(2)}, u32[]{:S(2)}) collective-permute-start(f32[3,8,512]{2,1,0:T(8,128)S(1)} %pad_maximum_fusion.1), channel_id=1, source_target_pairs={{32,0},{64,32},{96,64},{128,96},{160,128},{192,160},{224,192},{256... | collective-permute-start | bytes 147464 | tf_op jit(solution)/shard_map/ppermute | solution.py:476
  62.0 4.7 %collective-permute-done.5.high = f32[3,8,512]{2,1,0:T(8,128)S(1)} collective-permute-done((f32[3,8,512]{2,1,0:T(8,128)S(1)}, f32[3,8,512]{2,1,0:T(8,128)S(1)}, u32[]{:S(2)}, u32[]{:S(2)}) %collective-permute-start.5) | collective-permute-done | bytes 49184 | tf_op jit(solution)/shard_map/ppermute | solution.py:476
  66.7 2.8 %collective-permute-start.6 = (f32[22,512]{1,0:T(8,128)S(1)}, f32[22,512]{1,0:T(8,128)S(1)}, u32[]{:S(2)}, u32[]{:S(2)}) collective-permute-start(f32[22,512]{1,0:T(8,128)S(1)} %get-tuple-element.32), channel_id=1, source_target_pairs={{0,1},{1,2},{2,3},{3,4},{4,5},{5,6},{6,7},{7,8},{8,9},{9,10},{10,1... | collective-permute-start | bytes 135176 | tf_op jit(solution)/shard_map/ppermute | solution.py:476
  69.5 4.6 %collective-permute-start.7 = (f32[22,512]{1,0:T(8,128)S(1)}, f32[22,512]{1,0:T(8,128)S(1)}, u32[]{:S(2)}, u32[]{:S(2)}) collective-permute-start(f32[22,512]{1,0:T(8,128)S(1)} %get-tuple-element.33), channel_id=1, source_target_pairs={{1,0},{2,1},{3,2},{4,3},{5,4},{6,5},{7,6},{8,7},{9,8},{10,9},{11,1... | collective-permute-start | bytes 135176 | tf_op jit(solution)/shard_map/ppermute | solution.py:476
  74.1 1.5 %shard_map.147.parts = f32[4,4,8,512]{3,2,1,0:T(8,128)S(1)} custom-call(f32[256]{0:T(256)S(1)} %pad.4.par, f32[12,128,128]{2,1,0:T(8,128)S(1)} %get-tuple-element.34.states_in, f32[4,8,512]{2,1,0:T(8,128)S(1)} %get-tuple-element.30.v1), custom_call_target="tpu_custom_call" | custom-call | flops 1000000 | bytes 1000000 | tf_op jit(solution)/shard_map/pallas_call | solution.py:547
  75.6 0.0 copy-start.7
  75.6 0.0 copy-start.1
  75.6 2.6 %shard_map.148 = (f32[4,8,512]{2,1,0:T(8,128)}, f32[4,8,512]{2,1,0:T(8,128)S(1)}, f32[32,16,128]{2,1,0:T(8,128)}) custom-call(s32[4,8]{1,0:T(4,128)S(1)} %copy-done.8, f32[256]{0:T(256)S(1)} %pad.4.par, f32[4,8,512]{2,1,0:T(8,128)S(1)} %copy-done.2, bf16[8,16,512]{2,1,0:T(8,128)(2,1)S(1)} %get-tuple-element.27.flags, ...), custom_call_target="tpu_custom_call" | custom-call | flops 1000000 | bytes 1000000 | tf_op jit(solution)/shard_map/pallas_call | solution.py:552
  78.2 7.5 %all-to-all-start.2 = ((f32[32,16,128]{2,1,0:T(8,128)}), f32[32,16,128]{2,1,0:T(8,128)S(1)}, u32[]{:S(2)}, u32[]{:S(2)}) async-start(f32[32,16,128]{2,1,0:T(8,128)} %get-tuple-element.36), calls=%async_computation.2 | async-start | bytes 524288 | tf_op jit(solution)/shard_map/all_to_all | solution.py:480
  85.7 1.9 %collective-permute-start.9 = (f32[1,8,512]{2,1,0:T(8,128)S(1)}, f32[1,8,512]{2,1,0:T(8,128)S(1)}, u32[]{:S(2)}, u32[]{:S(2)}) collective-permute-start(f32[1,8,512]{2,1,0:T(8,128)S(1)} %get-tuple-element.41), channel_id=1, source_target_pairs={{32,0},{64,32},{96,64},{128,96},{160,128},{192,160},{224,192},{256... | collective-permute-start | bytes 49160 | tf_op jit(solution)/shard_map/ppermute | solution.py:476
  87.7 4.9 %collective-permute-start.8 = (f32[1,8,512]{2,1,0:T(8,128)S(1)}, f32[1,8,512]{2,1,0:T(8,128)S(1)}, u32[]{:S(2)}, u32[]{:S(2)}) collective-permute-start(f32[1,8,512]{2,1,0:T(8,128)S(1)} %get-tuple-element.42), channel_id=1, source_target_pairs={{0,32},{32,64},{64,96},{96,128},{128,160},{160,192},{192,224},{224... | collective-permute-start | bytes 49160 | tf_op jit(solution)/shard_map/ppermute | solution.py:476
  92.5 4.6 %collective-permute-start.11 = (f32[4,1,512]{2,1,0:T(1,128)S(1)}, f32[4,1,512]{2,1,0:T(1,128)S(1)}, u32[]{:S(2)}, u32[]{:S(2)}) collective-permute-start(f32[4,1,512]{2,1,0:T(1,128)S(1)} %get-tuple-element.39), channel_id=1, source_target_pairs={{1,0},{2,1},{3,2},{4,3},{5,4},{6,5},{7,6},{8,7},{9,8},{10,9},{11,1... | collective-permute-start | bytes 24584 | tf_op jit(solution)/shard_map/ppermute | solution.py:476
  97.1 1.9 %collective-permute-start.10 = (f32[4,1,512]{2,1,0:T(1,128)S(1)}, f32[4,1,512]{2,1,0:T(1,128)S(1)}, u32[]{:S(2)}, u32[]{:S(2)}) collective-permute-start(f32[4,1,512]{2,1,0:T(1,128)S(1)} %get-tuple-element.40), channel_id=1, source_target_pairs={{0,1},{1,2},{2,3},{3,4},{4,5},{5,6},{6,7},{7,8},{8,9},{9,10},{10,1... | collective-permute-start | bytes 24584 | tf_op jit(solution)/shard_map/ppermute | solution.py:476
  99.1 4.6 %collective-permute-done.10.left = f32[4,1,512]{2,1,0:T(1,128)S(1)} collective-permute-done((f32[4,1,512]{2,1,0:T(1,128)S(1)}, f32[4,1,512]{2,1,0:T(1,128)S(1)}, u32[]{:S(2)}, u32[]{:S(2)}) %collective-permute-start.10) | collective-permute-done | bytes 8224 | tf_op jit(solution)/shard_map/ppermute | solution.py:476
  103.7 1.9 %shard_map.150 = f32[3,4,8,512]{3,2,1,0:T(8,128)} custom-call(f32[4,8,512]{2,1,0:T(8,128)S(1)} %get-tuple-element.37.ours, f32[1,8,512]{2,1,0:T(8,128)S(1)} %collective-permute-done.8.below, f32[1,8,512]{2,1,0:T(8,128)S(1)} %collective-permute-done.9.above, f32[4,1,512]{2,1,0:T(1,128)S(1)} %collective-permute-done.10.left, ...), custom_call_target="tpu_custom_call" | custom-call | flops 1000000 | bytes 1000000 | tf_op jit(solution)/shard_map/pallas_call | solution.py:564
  105.5 0.0 all-to-all-done.2.returned
  105.5 2.6 %shard_map.149 = f32[12,16,512]{2,1,0:T(8,128)} custom-call(s32[32,1,128]{2,1,0:T(1,128)S(1)} %all-to-all-done.arrived, f32[256]{0:T(256)S(1)} %pad.4.par, f32[32,16,128]{2,1,0:T(8,128)S(1)} %all-to-all-done.2.returned, f32[12,16,512]{2,1,0:T(8,128)S(1)} %copy-done.1), custom_call_target="tpu_custom_call" | custom-call | flops 1000000 | bytes 1000000 | tf_op jit(solution)/shard_map/pallas_call | solution.py:568
  (33 shorter events, 0.2 us)
Async XLA Ops:
  2.1 16.7 %all-to-all-start = ((s32[32,1,128]{2,1,0:T(1,128)}), s32[32,1,128]{2,1,0:T(1,128)S(1)}, u32[]{:S(2)}, u32[]{:S(2)}) async-start(s32[32,1,128]{2,1,0:T(1,128)} %shard_map.142), calls=%async_computation | async-start | bytes 32768 | tf_op jit(solution)/shard_map/all_to_all | solution.py:480
  11.7 1.0 copy-start
  12.7 13.3 %copy-start.2 = (f32[4,8,512]{2,1,0:T(8,128)S(1)}, f32[4,8,512]{2,1,0:T(8,128)}, u32[]{:S(2)}) copy-start(f32[4,8,512]{2,1,0:T(8,128)} %v0.1) | copy-start | bytes 196612
  12.7 13.3 %copy-start.3 = (s32[4,8,512]{2,1,0:T(8,128)S(1)}, s32[4,8,512]{2,1,0:T(8,128)}, u32[]{:S(2)}) copy-start(s32[4,8,512]{2,1,0:T(8,128)} %tissue.3) | copy-start | bytes 196612
  12.7 13.3 %copy-start.4 = (s32[4,8,512]{2,1,0:T(8,128)S(1)}, s32[4,8,512]{2,1,0:T(8,128)}, u32[]{:S(2)}) copy-start(s32[4,8,512]{2,1,0:T(8,128)} %fiber.1) | copy-start | bytes 196612
  12.7 13.3 %copy-start.5 = (f32[4,8,512]{2,1,0:T(8,128)S(1)}, f32[4,8,512]{2,1,0:T(8,128)}, u32[]{:S(2)}) copy-start(f32[4,8,512]{2,1,0:T(8,128)} %lag.1) | copy-start | bytes 196612
  12.9 36.0 %copy-start.9 = (f32[6,16]{1,0:T(8,128)S(1)}, f32[6,16]{1,0:T(8,128)}, u32[]{:S(2)}) copy-start(f32[6,16]{1,0:T(8,128)} %param.16) | copy-start | bytes 1156
  12.9 36.0 %copy-start.10 = (f32[12]{0:T(128)S(1)}, f32[12]{0:T(128)}, u32[]{:S(2)}) copy-start(f32[12]{0:T(128)} %param.19) | copy-start | bytes 148
  12.9 36.0 %copy-start.11 = (f32[12]{0:T(128)S(1)}, f32[12]{0:T(128)}, u32[]{:S(2)}) copy-start(f32[12]{0:T(128)} %param.20) | copy-start | bytes 148
  12.9 36.0 %copy-start.12 = (f32[12]{0:T(128)S(1)}, f32[12]{0:T(128)}, u32[]{:S(2)}) copy-start(f32[12]{0:T(128)} %param.21) | copy-start | bytes 148
  12.9 36.0 %copy-start.13 = (f32[12]{0:T(128)S(1)}, f32[12]{0:T(128)}, u32[]{:S(2)}) copy-start(f32[12]{0:T(128)} %param.22) | copy-start | bytes 148
  12.9 36.0 %copy-start.14 = (f32[6]{0:T(128)S(1)}, f32[6]{0:T(128)}, u32[]{:S(2)}) copy-start(f32[6]{0:T(128)} %param.23) | copy-start | bytes 76
  12.9 41.1 %copy-start.8 = (s32[4,8]{1,0:T(4,128)S(1)}, s32[4,8]{1,0:T(4,128)}, u32[]{:S(2)}) copy-start(s32[4,8]{1,0:T(4,128)} %worker.5) | copy-start | bytes 388
  20.5 33.6 %all-to-all-start.1 = ((f32[32,48,128]{2,1,0:T(8,128)}), f32[32,48,128]{2,1,0:T(8,128)S(1)}, u32[]{:S(2)}, u32[]{:S(2)}) async-start(f32[32,48,128]{2,1,0:T(8,128)} %shard_map.144), calls=%async_computation.1 | async-start | bytes 1572864 | tf_op jit(solution)/shard_map/all_to_all | solution.py:480
  26.5 9.4 %collective-permute-start = (f32[6,8,512]{2,1,0:T(8,128)S(1)}, f32[6,8,512]{2,1,0:T(8,128)S(1)}, u32[]{:S(2)}, u32[]{:S(2)}) collective-permute-start(f32[6,8,512]{2,1,0:T(8,128)S(1)} %get-tuple-element.21), channel_id=1, source_target_pairs={{0,32},{32,64},{64,96},{96,128},{128,160},{160,192},{192,224},{224... | collective-permute-start | bytes 294920 | tf_op jit(solution)/shard_map/ppermute | solution.py:476
  34.0 7.4 %collective-permute-start.1 = (f32[6,8,512]{2,1,0:T(8,128)S(1)}, f32[6,8,512]{2,1,0:T(8,128)S(1)}, u32[]{:S(2)}, u32[]{:S(2)}) collective-permute-start(f32[6,8,512]{2,1,0:T(8,128)S(1)} %get-tuple-element.22), channel_id=1, source_target_pairs={{32,0},{64,32},{96,64},{128,96},{160,128},{192,160},{224,192},{256... | collective-permute-start | bytes 294920 | tf_op jit(solution)/shard_map/ppermute | solution.py:476
  41.4 7.6 %collective-permute-start.2 = (f32[42,512]{1,0:T(8,128)S(1)}, f32[42,512]{1,0:T(8,128)S(1)}, u32[]{:S(2)}, u32[]{:S(2)}) collective-permute-start(f32[42,512]{1,0:T(8,128)S(1)} %get-tuple-element.25), channel_id=1, source_target_pairs={{0,1},{1,2},{2,3},{3,4},{4,5},{5,6},{6,7},{7,8},{8,9},{9,10},{10,1... | collective-permute-start | bytes 258056 | tf_op jit(solution)/shard_map/ppermute | solution.py:476
  44.6 5.9 %collective-permute-start.3 = (f32[42,512]{1,0:T(8,128)S(1)}, f32[42,512]{1,0:T(8,128)S(1)}, u32[]{:S(2)}, u32[]{:S(2)}) collective-permute-start(f32[42,512]{1,0:T(8,128)S(1)} %get-tuple-element.26), channel_id=1, source_target_pairs={{1,0},{2,1},{3,2},{4,3},{5,4},{6,5},{7,6},{8,7},{9,8},{10,9},{11,1... | collective-permute-start | bytes 258056 | tf_op jit(solution)/shard_map/ppermute | solution.py:476
  53.4 0.6 copy-start.6
  56.0 6.0 %collective-permute-start.4 = (f32[3,8,512]{2,1,0:T(8,128)S(1)}, f32[3,8,512]{2,1,0:T(8,128)S(1)}, u32[]{:S(2)}, u32[]{:S(2)}) collective-permute-start(f32[3,8,512]{2,1,0:T(8,128)S(1)} %pad_maximum_fusion), channel_id=1, source_target_pairs={{0,32},{32,64},{64,96},{96,128},{128,160},{160,192},{192,224},{224... | collective-permute-start | bytes 147464 | tf_op jit(solution)/shard_map/ppermute | solution.py:476
  60.1 6.6 %collective-permute-start.5 = (f32[3,8,512]{2,1,0:T(8,128)S(1)}, f32[3,8,512]{2,1,0:T(8,128)S(1)}, u32[]{:S(2)}, u32[]{:S(2)}) collective-permute-start(f32[3,8,512]{2,1,0:T(8,128)S(1)} %pad_maximum_fusion.1), channel_id=1, source_target_pairs={{32,0},{64,32},{96,64},{128,96},{160,128},{192,160},{224,192},{256... | collective-permute-start | bytes 147464 | tf_op jit(solution)/shard_map/ppermute | solution.py:476
  66.7 8.9 %collective-permute-start.6 = (f32[22,512]{1,0:T(8,128)S(1)}, f32[22,512]{1,0:T(8,128)S(1)}, u32[]{:S(2)}, u32[]{:S(2)}) collective-permute-start(f32[22,512]{1,0:T(8,128)S(1)} %get-tuple-element.32), channel_id=1, source_target_pairs={{0,1},{1,2},{2,3},{3,4},{4,5},{5,6},{6,7},{7,8},{8,9},{9,10},{10,1... | collective-permute-start | bytes 135176 | tf_op jit(solution)/shard_map/ppermute | solution.py:476
  69.5 6.1 %collective-permute-start.7 = (f32[22,512]{1,0:T(8,128)S(1)}, f32[22,512]{1,0:T(8,128)S(1)}, u32[]{:S(2)}, u32[]{:S(2)}) collective-permute-start(f32[22,512]{1,0:T(8,128)S(1)} %get-tuple-element.33), channel_id=1, source_target_pairs={{1,0},{2,1},{3,2},{4,3},{5,4},{6,5},{7,6},{8,7},{9,8},{10,9},{11,1... | collective-permute-start | bytes 135176 | tf_op jit(solution)/shard_map/ppermute | solution.py:476
  75.6 28.1 %copy-start.7 = (f32[24,512]{1,0:T(8,128)S(1)}, f32[24,512]{1,0:T(8,128)}, u32[]{:S(2)}) copy-start(f32[24,512]{1,0:T(8,128)} %copy-done.6) | copy-start | bytes 147460
  75.6 29.9 %copy-start.1 = (f32[12,16,512]{2,1,0:T(8,128)S(1)}, f32[12,16,512]{2,1,0:T(8,128)}, u32[]{:S(2)}) copy-start(f32[12,16,512]{2,1,0:T(8,128)} %gates.3) | copy-start | bytes 1179652
  78.2 27.4 %all-to-all-start.2 = ((f32[32,16,128]{2,1,0:T(8,128)}), f32[32,16,128]{2,1,0:T(8,128)S(1)}, u32[]{:S(2)}, u32[]{:S(2)}) async-start(f32[32,16,128]{2,1,0:T(8,128)} %get-tuple-element.36), calls=%async_computation.2 | async-start | bytes 524288 | tf_op jit(solution)/shard_map/all_to_all | solution.py:480
  85.7 17.9 %collective-permute-start.9 = (f32[1,8,512]{2,1,0:T(8,128)S(1)}, f32[1,8,512]{2,1,0:T(8,128)S(1)}, u32[]{:S(2)}, u32[]{:S(2)}) collective-permute-start(f32[1,8,512]{2,1,0:T(8,128)S(1)} %get-tuple-element.41), channel_id=1, source_target_pairs={{32,0},{64,32},{96,64},{128,96},{160,128},{192,160},{224,192},{256... | collective-permute-start | bytes 49160 | tf_op jit(solution)/shard_map/ppermute | solution.py:476
  87.7 16.0 %collective-permute-start.8 = (f32[1,8,512]{2,1,0:T(8,128)S(1)}, f32[1,8,512]{2,1,0:T(8,128)S(1)}, u32[]{:S(2)}, u32[]{:S(2)}) collective-permute-start(f32[1,8,512]{2,1,0:T(8,128)S(1)} %get-tuple-element.42), channel_id=1, source_target_pairs={{0,32},{32,64},{64,96},{96,128},{128,160},{160,192},{192,224},{224... | collective-permute-start | bytes 49160 | tf_op jit(solution)/shard_map/ppermute | solution.py:476
  92.5 6.5 %collective-permute-start.11 = (f32[4,1,512]{2,1,0:T(1,128)S(1)}, f32[4,1,512]{2,1,0:T(1,128)S(1)}, u32[]{:S(2)}, u32[]{:S(2)}) collective-permute-start(f32[4,1,512]{2,1,0:T(1,128)S(1)} %get-tuple-element.39), channel_id=1, source_target_pairs={{1,0},{2,1},{3,2},{4,3},{5,4},{6,5},{7,6},{8,7},{9,8},{10,9},{11,1... | collective-permute-start | bytes 24584 | tf_op jit(solution)/shard_map/ppermute | solution.py:476
  97.1 6.5 %collective-permute-start.10 = (f32[4,1,512]{2,1,0:T(1,128)S(1)}, f32[4,1,512]{2,1,0:T(1,128)S(1)}, u32[]{:S(2)}, u32[]{:S(2)}) collective-permute-start(f32[4,1,512]{2,1,0:T(1,128)S(1)} %get-tuple-element.40), channel_id=1, source_target_pairs={{0,1},{1,2},{2,3},{3,4},{4,5},{5,6},{6,7},{7,8},{8,9},{9,10},{10,1... | collective-permute-start | bytes 24584 | tf_op jit(solution)/shard_map/ppermute | solution.py:476
